TPU v7x, 64 devices: a 2x2x8 block of a 4x4x8 slice. The times are simulated.
64 devices in a mesh: dp: 4 (over x, y), sp: 16 (over z, core).
Axes of the slice: x: 2, y: 2, z: 8, core: 2. Of those that a mesh axis runs over, the one named last changes fastest.
The devices are a block of a 4x4x8 slice.
Arguments:
- x_in: bfloat16 [8, 4096, 1536], P('dp', 'sp'), parts along dimension 0
- positions: int32 [8, 4096], P('dp', 'sp'), parts along dimension 0
- keep_mask: int32 [8, 4096], P('dp', 'sp'), parts along dimension 0
- ln_gain: float32 [1536], replicated
- ln_bias: float32 [1536], replicated
- w_qkv: bfloat16 [1536, 16, 3, 96], replicated
- b_qkv: float32 [16, 3, 96], replicated
- w_out: bfloat16 [1536, 1536], replicated
- b_out: float32 [1536], replicated
- grad_y: bfloat16 [8, 4096, 1536], P('dp', 'sp'), parts along dimension 0
Outputs:
- output 1: bfloat16 [8, 4096, 1536], P('dp', 'sp'), parts along dimension 0
- output 2: bfloat16 [8, 4096, 1536], P('dp', 'sp'), parts along dimension 0
- output 3: float32 [6144, 16, 3, 96], P('dp'), parts along dimension 0
- output 4: float32 [64, 3, 96], P('dp'), parts along dimension 0
- output 5: float32 [6144, 1536], P('dp'), parts along dimension 0
- output 6: float32 [6144], P('dp'), parts along dimension 0
- output 7: float32 [6144], P('dp'), parts along dimension 0
- output 8: float32 [6144], P('dp'), parts along dimension 0
There are 4 independent parts. A program takes and returns all parts, laid end to end along the dimension named above; an argument that names none is the same for every part.
All inputs are finite; a program needn't handle non-finite values.
Results may differ from a plain program's by a relative error of at most 0.00974613.
Values are sent between devices in bfloat16 or wider.
A program may use at most 768 MiB of HBM per device.

v0:
```python
import jax
import jax.numpy as jnp
from jax import lax
from jax.sharding import PartitionSpec as P

NORM_EPS = 1e-5
MASK_FILL = -1e30


def norm_forward(x_blk, ln_gain, ln_bias):
    x_f32 = x_blk.astype(jnp.float32)
    centered = x_f32 - jnp.mean(x_f32, axis=-1, keepdims=True)
    inv_std = lax.rsqrt(jnp.mean(centered * centered, axis=-1, keepdims=True) + NORM_EPS)
    x_hat = centered * inv_std
    x_norm = (x_hat * ln_gain + ln_bias).astype(jnp.bfloat16)
    return x_f32, x_hat, inv_std, x_norm


def norm_backward(d_norm, x_hat, inv_std, ln_gain):
    d_hat = d_norm * ln_gain
    d_mean = jnp.mean(d_hat, axis=-1, keepdims=True)
    d_proj = jnp.mean(d_hat * x_hat, axis=-1, keepdims=True)
    return inv_std * (d_hat - d_mean - x_hat * d_proj)


def attn_probs(q_part, k_part, q_pos, k_pos, k_keep, q_index, k_index, slopes, qk_scale):
    scores = jnp.einsum("bqnd,bknd->bnqk", q_part, k_part, preferred_element_type=jnp.float32) * qk_scale
    pos_gap = (q_pos[:, :, None] - k_pos[:, None, :]).astype(jnp.float32)
    scores = scores - slopes[None, :, None, None] * pos_gap[:, None, :, :]
    allowed = (k_index[None, :] <= q_index[:, None])[None, None] & (k_keep[:, None, None, :] > 0)
    return jax.nn.softmax(jnp.where(allowed, scores, MASK_FILL), axis=-1)


def attn_backward(attn_prob, prob_lo, q_part, k_part, v_part, o_part, do_part, qk_scale):
    dv_part = jnp.einsum("bnqk,bqnd->bknd", prob_lo, do_part, preferred_element_type=jnp.float32)
    grad_prob = jnp.einsum("bqnd,bknd->bnqk", do_part, v_part, preferred_element_type=jnp.float32)
    row_dot = jnp.einsum("bqnd,bqnd->bnq", do_part, o_part, preferred_element_type=jnp.float32)
    ds_lo = (attn_prob * (grad_prob - row_dot[:, :, :, None])).astype(jnp.bfloat16)
    dq_part = jnp.einsum("bnqk,bknd->bqnd", ds_lo, k_part, preferred_element_type=jnp.float32) * qk_scale
    dk_part = jnp.einsum("bnqk,bqnd->bknd", ds_lo, q_part, preferred_element_type=jnp.float32) * qk_scale
    return dq_part, dk_part, dv_part


def solution(mesh):
    sp_size = mesh.shape["sp"]

    def block_fn(x_blk, pos_blk, keep_blk, ln_gain, ln_bias, w_qkv, b_qkv, w_out, b_out, dy_blk):
        batch_loc, seq_loc, hidden = x_blk.shape
        num_heads = w_qkv.shape[1]
        head_dim = w_qkv.shape[3]
        heads_loc = num_heads // sp_size
        seq_len = seq_loc * sp_size
        qk_scale = head_dim ** -0.5
        sp_rank = lax.axis_index("sp")
        x_f32, x_hat, inv_std, x_norm = norm_forward(x_blk, ln_gain, ln_bias)
        qkv_loc = (jnp.einsum("bsh,hnct->bsnct", x_norm, w_qkv, preferred_element_type=jnp.float32) + b_qkv).astype(jnp.bfloat16)
        qkv_head = lax.all_to_all(qkv_loc, "sp", 2, 1, tiled=True)
        pos_full = lax.all_gather(pos_blk, "sp", axis=1, tiled=True)
        keep_full = lax.all_gather(keep_blk, "sp", axis=1, tiled=True)
        q_head = qkv_head[:, :, :, 0]
        k_head = qkv_head[:, :, :, 1]
        v_head = qkv_head[:, :, :, 2]
        head_ids = sp_rank * heads_loc + jnp.arange(heads_loc)
        slopes = jnp.exp2(-8.0 * (head_ids + 1).astype(jnp.float32) / num_heads)
        tok_index = jnp.arange(seq_len)
        attn_prob = attn_probs(q_head, k_head, pos_full, pos_full, keep_full, tok_index, tok_index, slopes, qk_scale)
        prob_lo = attn_prob.astype(jnp.bfloat16)
        o_head = jnp.einsum("bnqk,bknd->bqnd", prob_lo, v_head, preferred_element_type=jnp.float32).astype(jnp.bfloat16)
        o_loc = lax.all_to_all(o_head, "sp", 1, 2, tiled=True).reshape(batch_loc, seq_loc, hidden)
        y_blk = (x_f32 + jnp.einsum("bsh,hk->bsk", o_loc, w_out, preferred_element_type=jnp.float32) + b_out).astype(jnp.bfloat16)
        grad_b_out = jnp.sum(dy_blk.astype(jnp.float32), axis=(0, 1))
        grad_w_out = jnp.einsum("bsh,bsk->hk", o_loc, dy_blk, preferred_element_type=jnp.float32)
        do_loc = jnp.einsum("bsk,hk->bsh", dy_blk, w_out, preferred_element_type=jnp.float32).astype(jnp.bfloat16)
        do_head = lax.all_to_all(do_loc.reshape(batch_loc, seq_loc, num_heads, head_dim), "sp", 2, 1, tiled=True)
        dq_head, dk_head, dv_head = attn_backward(attn_prob, prob_lo, q_head, k_head, v_head, o_head, do_head, qk_scale)
        dqkv_head = jnp.stack([dq_head, dk_head, dv_head], axis=3).astype(jnp.bfloat16)
        dqkv_loc = lax.all_to_all(dqkv_head, "sp", 1, 2, tiled=True)
        grad_b_qkv = jnp.sum(dqkv_loc.astype(jnp.float32), axis=(0, 1))
        grad_w_qkv = jnp.einsum("bsh,bsnct->hnct", x_norm, dqkv_loc, preferred_element_type=jnp.float32)
        d_norm = jnp.einsum("bsnct,hnct->bsh", dqkv_loc, w_qkv, preferred_element_type=jnp.float32)
        grad_gain = jnp.sum(d_norm * x_hat, axis=(0, 1))
        grad_bias = jnp.sum(d_norm, axis=(0, 1))
        grad_x = (dy_blk.astype(jnp.float32) + norm_backward(d_norm, x_hat, inv_std, ln_gain)).astype(jnp.bfloat16)
        summed = lax.psum((grad_w_qkv, grad_b_qkv, grad_w_out, grad_b_out, grad_gain, grad_bias), "sp")
        return (y_blk, grad_x) + tuple(summed)

    act_spec = P("dp", "sp", None)
    tok_spec = P("dp", "sp")
    in_specs = (act_spec, tok_spec, tok_spec, P(), P(), P(), P(), P(), P(), act_spec)
    out_specs = (act_spec, act_spec, P("dp", None, None, None), P("dp", None, None), P("dp", None), P("dp"), P("dp"), P("dp"))
    return jax.shard_map(block_fn, mesh=mesh, in_specs=in_specs, out_specs=out_specs, check_vma=False)
```

profile of v0, /device:TPU:21, one launch (start us, length us, event | category | flops | bytes accessed | tf_op | source)
XLA Modules:
  0.0 1207.3 jit_solution(8103120511393380534)
XLA Ops:
  7.2 5.4 fusion.46
  12.6 0.7 copy.100
  13.3 0.0 copy-start.8
  13.4 0.0 copy-start.1
  13.4 1.3 copy.101
  14.6 10.9 all-to-all-start.2
  25.5 0.0 copy-done.8
  25.5 0.0 copy-done.1
  25.5 0.3 convert_reduce_fusion.1
  25.8 0.0 copy-start.9
  25.8 0.5 fusion.39
  26.4 0.0 copy-done.11
  26.4 0.0 copy-start.13
  26.4 11.6 add_convert_fusion
  38.1 0.0 copy-done.9
  38.1 0.0 copy-done.13
  38.1 2.6 copy.90
  40.7 23.1 %all-to-all-done.2 = bf16[2,256,16,96]{1,3,0,2:T(8,128)(2,1)S(1)} async-done(((bf16[2,256,16,96]{1,3,0,2:T(8,128)(2,1)}), bf16[2,256,16,96]{1,3,0,2:T(8,128)(2,1)S(1)}, u32[]{:S(2)}, u32[]{:S(2)}) %all-to-all-start.2) | async-done | bytes 1572896 | tf_op jit(solution)/shard_map/all_to_all | solution.py:74
  63.8 4.7 all-to-all-start
  68.6 117.0 %all_gather.7 = s32[2,4096]{1,0:T(2,128)S(1)} all-gather(s32[2,256]{1,0:T(2,128)S(1)} %copy-done.15), channel_id=1, replica_groups=mesh['dp'=4,'sp'=16] {'sp'}, dimensions={1}, use_global_device_ids=true | all-gather | bytes 34816 | tf_op jit(solution)/shard_map/all_gather | solution.py:58
  185.6 16.7 %all_gather.6 = s32[2,4096]{1,0:T(2,128)S(1)} all-gather(s32[2,256]{1,0:T(2,128)S(1)} %copy-done.16), channel_id=1, replica_groups=mesh['dp'=4,'sp'=16] {'sp'}, dimensions={1}, use_global_device_ids=true | all-gather | bytes 34816 | tf_op jit(solution)/shard_map/all_gather | solution.py:59
  202.3 11.0 iota_compare_fusion
  213.3 0.9 copy.102
  214.2 2.1 reshape.215
  216.3 0.0 all-to-all-done
  216.3 7.4 copy.134
  223.7 8.3 reshape.227
  232.0 89.8 %fusion.57 = (f32[2,4096]{1,0:T(2,128)S(1)}, f32[2,4096,4096]{1,2,0:T(8,128)}) fusion(s32[2,4096]{1,0:T(2,128)S(1)} %all_gather.7, f32[]{:T(128)S(6)} %exp2.9, pred[2,4096]{1,0:T(4,128)(4,1)S(1)} %broadcast_compare_fusion, pred[4096,4096]{0,1:T(8,128)(4,1)} %iota_compare_fusion, bf16[2,4096,1,3,96]{1,4,0,3,2:T(8,128)(2,1)} %reshape.227), kind=kOutput, calls=%fused_computation.75 | convolution fusion | flops 6744444928 | bytes 154255360 | tf_op jit(solution)/shard_map/sub | solution.py:31
  321.8 0.0 copy-start
  321.8 64.4 %fusion.6 = bf16[2,4096,4096]{1,2,0:T(8,128)(2,1)} fusion(f32[2,4096,4096]{1,2,0:T(8,128)} %get-tuple-element.29, f32[2,4096]{1,0:T(2,128)S(1)} %get-tuple-element.28), kind=kLoop, calls=%fused_computation.11 | loop fusion | flops 67108864 | bytes 201359360 | tf_op jit(solution)/shard_map/convert_element_type | solution.py:67
  386.2 28.3 %fusion.11 = bf16[2,4096,1,1,96]{1,4,0,3,2:T(8,128)(2,1)} fusion(bf16[2,4096,96]{1,2,0:T(8,128)(2,1)S(1)} %copy-done, bf16[2,4096,4096]{1,2,0:T(8,128)(2,1)} %fusion.6), kind=kOutput, calls=%fused_computation.21 | convolution fusion | flops 6443237376 | bytes 70254592 | tf_op jit(solution)/shard_map/bnqk,bqnd->bknd/dot_general | solution.py:35
  414.5 24.8 %fusion.43 = (f32[2,4096]{1,0:T(2,128)S(1)}, bf16[2,96,4096]{2,1,0:T(8,128)(2,1)S(1)}) fusion(bf16[2,4096,96]{1,2,0:T(8,128)(2,1)S(1)} %copy-done, bf16[2,4096,4096]{1,2,0:T(8,128)(2,1)} %fusion.6, bf16[2,4096,1,3,96]{1,4,0,3,2:T(8,128)(2,1)} %reshape.227), kind=kOutput, calls=%fused_computation.58 | convolution fusion | flops 6446374912 | bytes 71860224 | tf_op jit(solution)/shard_map/bnqk,bknd->bqnd/dot_general | solution.py:68
  439.3 66.7 %multiply_convert_fusion = bf16[2,4096,4096]{1,2,0:T(8,128)(2,1)} fusion(f32[2,4096]{1,0:T(2,128)S(1)} %get-tuple-element.30, f32[2,4096,4096]{1,2,0:T(8,128)} %get-tuple-element.29, f32[2,4096]{1,0:T(2,128)S(1)} %get-tuple-element.28, bf16[2,4096,96]{1,2,0:T(8,128)(2,1)S(1)} %copy-done, bf16[2,4096,1,3,96]{1,4,0,3,2:T(8,128)(2,1)} %reshape.227), kind=kOutput, calls=%fused_computation.1 | convolution fusion | flops 6576668672 | bytes 204537856 | tf_op jit(solution)/shard_map/bqnd,bknd->bnqk/dot_general | solution.py:36
  506.0 3.9 copy.96
  509.9 5.1 all-to-all-start.1
  515.0 25.7 %fusion.15 = bf16[2,4096,1,1,96]{1,4,0,3,2:T(8,128)(2,1)} fusion(bf16[2,4096,4096]{1,2,0:T(8,128)(2,1)} %multiply_convert_fusion, bf16[2,4096,1,3,96]{1,4,0,3,2:T(8,128)(2,1)} %reshape.227), kind=kOutput, calls=%fused_computation.27 | convolution fusion | flops 6444023808 | bytes 70254592 | tf_op jit(solution)/shard_map/bnqk,bknd->bqnd/dot_general | solution.py:39
  540.7 28.7 %fusion.13 = bf16[2,4096,1,1,96]{1,4,0,3,2:T(8,128)(2,1)} fusion(bf16[2,4096,4096]{1,2,0:T(8,128)(2,1)} %multiply_convert_fusion, bf16[2,4096,1,3,96]{1,4,0,3,2:T(8,128)(2,1)} %reshape.227), kind=kOutput, calls=%fused_computation.24 | convolution fusion | flops 6444023808 | bytes 70254592 | tf_op jit(solution)/shard_map/bnqk,bqnd->bknd/dot_general | solution.py:40
  569.4 3.6 pad_maximum_fusion
  573.0 14.8 %copy.107 = bf16[2,4096,1,3,96]{4,0,3,2,1:T(2,128)(2,1)} copy(bf16[2,4096,1,3,96]{1,4,0,3,2:T(8,128)(2,1)} %pad_maximum_fusion) | data formatting | bytes 9437184 | tf_op jit(solution)/shard_map/stack | solution.py:76
  587.7 0.0 all-to-all-done.1
  587.7 7.2 all-to-all-start.3
  595.0 0.1 all-reduce.4.cloned.1.call-start
  595.1 4.0 copy.128
  599.1 8.2 convolution_bitcast_fusion.1
  607.3 128.9 %all-to-all-done.3 = bf16[2,4096,1,3,96]{4,0,3,2,1:T(2,128)(2,1)} async-done(((bf16[2,4096,1,3,96]{4,0,3,2,1:T(2,128)(2,1)}), bf16[2,4096,1,3,96]{4,0,3,2,1:T(2,128)(2,1)}, u32[]{:S(2)}, u32[]{:S(2)}) %all-to-all-start.3) | async-done | bytes 4718624 | tf_op jit(solution)/shard_map/all_to_all | solution.py:77
  736.2 0.0 copy-start.18
  736.2 15.6 %copy.133 = bf16[2,16,256,1,3,96]{2,5,0,4,1,3:T(8,128)(2,1)} copy(bf16[2,16,256,1,3,96]{5,0,4,2,1,3:T(2,128)(2,1)} %bitcast.29) | data formatting | bytes 9437184 | tf_op jit(solution)/shard_map/all_to_all | solution.py:77
  751.8 0.0 copy-done.14
  751.8 0.0 copy-done.18
  751.8 15.3 %convolution_bitcast_fusion = f32[1536,16,3,96]{0,3,2,1:T(8,128)} fusion(bf16[2,16,256,1,3,96]{2,5,0,4,1,3:T(8,128)(2,1)} %copy.133, bf16[2,256,1536]{2,1,0:T(8,128)(2,1)S(1)} %copy-done.2, f32[1536]{0:T(1024)S(1)} %copy-done.18, f32[1536]{0:T(1024)S(1)} %copy-done.12, f32[2,256]{1,0:T(2,128)S(1)} %copy-done.14, f32[2,256]{1,0:T(2,128)S(1)} %copy-done.10), kind=kOutput, calls=%fused_computation.13 | convolution fusion | flops 7252475904 | bytes 34619392 | tf_op jit(solution)/shard_map/bsh,bsnct->hnct/dot_general | solution.py:79
  767.2 0.1 all-reduce.4.cloned.1.call-update
  767.2 1.3 copy-done.6
  768.6 6.1 fusion.42
  774.6 10.8 copy.130
  785.4 18.0 %fusion.38 = (f32[1536]{0:T(1024)S(1)}, f32[2,256]{1,0:T(2,128)S(1)}, f32[2,256]{1,0:T(2,128)S(1)}, f32[1536]{0:T(1024)S(1)}, f32[2,256,1536]{2,1,0:T(8,128)S(1)}) fusion(bf16[2,256,1536]{2,1,0:T(8,128)(2,1)S(1)} %copy-done.2, f32[2,256]{1,0:T(2,128)S(1)} %copy-done.14, f32[2,256]{1,0:T(2,128)S(1)} %copy-done.10, f32[1536]{0:T(1024)S(1)} %copy-done.12, ...), kind=kOutput, calls=%fused_computation.52 | convolution fusion | flops 7255617536 | bytes 23619584 | tf_op jit(solution)/shard_map/bsnct,hnct->bsh/dot_general | solution.py:80
  803.5 0.0 copy-start.7
  803.5 0.8 convert_reduce_fusion
  804.3 0.6 copy-done.7
  804.9 2.5 convert_reduce_fusion.2
  807.4 46.1 %all-reduce = (f32[16,3,96]{0,2,1:T(8,128)S(1)}, f32[1536]{0:T(1024)}, f32[1536]{0:T(1024)}, f32[1536]{0:T(1024)}) all-reduce(f32[16,3,96]{0,2,1:T(8,128)S(1)} %convert_reduce_fusion, f32[1536]{0:T(1024)S(1)} %get-tuple-element.26, f32[1536]{0:T(1024)S(1)} %get-tuple-element.16, ...), channel_id=1, replica_groups=mesh['dp'=4,'sp'=16] {'sp'}, use_global_device_ids=true, to_apply=%region_8.9 | all-reduce | flops 9216 | bytes 73728 | tf_op jit(solution)/shard_map/psum | solution.py:84
  853.5 0.7 copy.111
  854.2 321.1 %all-reduce.4.cloned.1.call-done = (f32[1536,16,3,96]{0,3,2,1:T(8,128)}, f32[1536,1536]{1,0:T(8,128)}) async-done(((f32[1536,16,3,96]{0,3,2,1:T(8,128)}, f32[1536,1536]{1,0:T(8,128)}), (f32[1536,16,3,96]{0,3,2,1:T(8,128)}, f32[1536,1536]{1,0:T(8,128)})) %all-reduce.4.cloned.1.call-update) | async-done | bytes 37748752 | tf_op jit(solution)/shard_map/psum | solution.py:84
  1175.3 21.2 %copy.144 = f32[1536,16,3,96]{0,3,2,1:T(8,128)} copy(f32[1536,16,3,96]{0,3,2,1:T(8,128)} %get-tuple-element.37) | data formatting | bytes 56623104
  1196.5 3.7 copy.145
  (34 shorter events, 0.1 us)
Async XLA Ops:
  13.3 12.2 %copy-start.8 = (f32[16,3,96]{2,0,1:T(8,128)S(1)}, f32[16,3,96]{2,0,1:T(8,128)}, u32[]{:S(2)}) copy-start(f32[16,3,96]{2,0,1:T(8,128)} %param.16) | copy-start | bytes 55300
  13.4 12.2 %copy-start.1 = (bf16[2,256,1536]{2,1,0:T(8,128)(2,1)S(1)}, bf16[2,256,1536]{2,1,0:T(8,128)(2,1)}, u32[]{:S(2)}) copy-start(bf16[2,256,1536]{2,1,0:T(8,128)(2,1)} %param.10) | copy-start | bytes 4718596
  14.6 11.8 copy-start.11
  14.6 11.8 copy-start.17
  14.6 49.2 %all-to-all-start.2 = ((bf16[2,256,16,96]{1,3,0,2:T(8,128)(2,1)}), bf16[2,256,16,96]{1,3,0,2:T(8,128)(2,1)S(1)}, u32[]{:S(2)}, u32[]{:S(2)}) async-start(bf16[2,256,16,96]{1,3,0,2:T(8,128)(2,1)} %copy.101), calls=%async_computation.2 | async-start | bytes 3145728 | tf_op jit(solution)/shard_map/all_to_all | solution.py:74
  25.8 12.2 %copy-start.9 = (f32[2,256]{1,0:T(2,128)}, f32[2,256]{1,0:T(2,128)S(1)}, u32[]{:S(2)}) copy-start(f32[2,256]{1,0:T(2,128)S(1)} %broadcast_multiply_fusion.2) | copy-start | bytes 6148
  26.4 11.7 copy-start.13
  40.7 27.8 %copy-start.15 = (s32[2,256]{1,0:T(2,128)S(1)}, s32[2,256]{1,0:T(2,128)}, u32[]{:S(2)}) copy-start(s32[2,256]{1,0:T(2,128)} %param.11) | copy-start | bytes 6148
  40.7 144.9 %copy-start.16 = (s32[2,256]{1,0:T(2,128)S(1)}, s32[2,256]{1,0:T(2,128)}, u32[]{:S(2)}) copy-start(s32[2,256]{1,0:T(2,128)} %param.12) | copy-start | bytes 6148
  63.8 152.5 %all-to-all-start = ((bf16[2,256,16,3,96]{1,4,3,0,2:T(8,128)(2,1)}), bf16[2,256,16,3,96]{1,4,3,0,2:T(8,128)(2,1)}, u32[]{:S(2)}, u32[]{:S(2)}) async-start(bf16[2,256,16,3,96]{1,4,3,0,2:T(8,128)(2,1)} %copy.90), calls=%async_computation | async-start | bytes 9437184 | tf_op jit(solution)/shard_map/all_to_all | solution.py:57
  321.8 64.4 %copy-start = (bf16[2,4096,96]{1,2,0:T(8,128)(2,1)S(1)}, bf16[2,4096,96]{1,2,0:T(8,128)(2,1)}, u32[]{:S(2)}) copy-start(bf16[2,4096,96]{1,2,0:T(8,128)(2,1)} %reshape.215) | copy-start | bytes 4718596
  509.9 77.8 %all-to-all-start.1 = ((bf16[2,4096,1,96]{3,0,2,1:T(2,128)(2,1)}), bf16[2,4096,1,96]{3,0,2,1:T(2,128)(2,1)S(1)}, u32[]{:S(2)}, u32[]{:S(2)}) async-start(bf16[2,4096,1,96]{3,0,2,1:T(2,128)(2,1)} %copy.96), calls=%async_computation.1 | async-start | bytes 4194304 | tf_op jit(solution)/shard_map/all_to_all | solution.py:69
  540.7 28.7 %copy-start.4 = (bf16[2,4096,1,1,96]{1,4,0,3,2:T(8,128)(2,1)S(1)}, bf16[2,4096,1,1,96]{1,4,0,3,2:T(8,128)(2,1)}, u32[]{:S(2)}) copy-start(bf16[2,4096,1,1,96]{1,4,0,3,2:T(8,128)(2,1)} %fusion.11) | copy-start | bytes 4718596
  540.7 28.7 %copy-start.5 = (bf16[2,4096,1,1,96]{1,4,0,3,2:T(8,128)(2,1)S(1)}, bf16[2,4096,1,1,96]{1,4,0,3,2:T(8,128)(2,1)}, u32[]{:S(2)}) copy-start(bf16[2,4096,1,1,96]{1,4,0,3,2:T(8,128)(2,1)} %fusion.15) | copy-start | bytes 4718596
  587.7 148.4 %all-to-all-start.3 = ((bf16[2,4096,1,3,96]{4,0,3,2,1:T(2,128)(2,1)}), bf16[2,4096,1,3,96]{4,0,3,2,1:T(2,128)(2,1)}, u32[]{:S(2)}, u32[]{:S(2)}) async-start(bf16[2,4096,1,3,96]{4,0,3,2,1:T(2,128)(2,1)} %copy.107), calls=%async_computation.3 | async-start | bytes 12582912 | tf_op jit(solution)/shard_map/all_to_all | solution.py:77
  595.0 580.3 %all-reduce.4.cloned.1.call-start = ((), (), s32[]{:S(2)}) async-start(), calls=%async_computation.4 | async-start | bytes 75497472 | tf_op jit(solution)/shard_map/psum | solution.py:84
  736.2 15.6 %copy-start.2 = (bf16[2,256,1536]{2,1,0:T(8,128)(2,1)S(1)}, bf16[2,256,1536]{2,1,0:T(8,128)(2,1)}, u32[]{:S(2)}) copy-start(bf16[2,256,1536]{2,1,0:T(8,128)(2,1)} %param.10) | copy-start | bytes 4718596
  736.2 15.6 %copy-start.10 = (f32[2,256]{1,0:T(2,128)S(1)}, f32[2,256]{1,0:T(2,128)}, u32[]{:S(2)}) copy-start(f32[2,256]{1,0:T(2,128)} %copy-done.9) | copy-start | bytes 6148
  736.2 15.6 %copy-start.12 = (f32[1536]{0:T(1024)S(1)}, f32[1536]{0:T(1024)}, u32[]{:S(2)}) copy-start(f32[1536]{0:T(1024)} %param.13) | copy-start | bytes 18436
  736.2 15.6 %copy-start.14 = (f32[2,256]{1,0:T(2,128)S(1)}, f32[2,256]{1,0:T(2,128)}, u32[]{:S(2)}) copy-start(f32[2,256]{1,0:T(2,128)} %copy-done.13) | copy-start | bytes 6148
  736.2 15.6 %copy-start.18 = (f32[1536]{0:T(1024)S(1)}, f32[1536]{0:T(1024)}, u32[]{:S(2)}) copy-start(f32[1536]{0:T(1024)} %param.14) | copy-start | bytes 18436
  767.2 1.4 copy-start.6
  767.2 1.4 copy-start.19
  785.4 18.1 %slice-start = ((s8[4718592]{0:T(1024)(128)(4,1)}), s8[4194304]{0:T(1024)(128)(4,1)S(1)}, s32[]{:S(2)}) async-start(s8[4718592]{0:T(1024)(128)(4,1)} %bitcast.126), calls=%async_computation.5 | async-start | bytes 8388608
  785.4 18.1 %slice-start.1 = ((s8[4718592]{0:T(1024)(128)(4,1)}), s8[524288]{0:T(1024)(128)(4,1)S(1)}, s32[]{:S(2)}) async-start(s8[4718592]{0:T(1024)(128)(4,1)} %bitcast.126), calls=%async_computation.6 | async-start | bytes 1048576
  803.5 1.4 copy-start.7
  1175.3 21.2 %copy-start.3 = (f32[1536,1536]{1,0:T(8,128)S(1)}, f32[1536,1536]{1,0:T(8,128)}, u32[]{:S(2)}) copy-start(f32[1536,1536]{1,0:T(8,128)} %get-tuple-element.39) | copy-start | bytes 28311556
Sparse Core Ops, SparseCore 0:
  767.3 407.9 all-reduce.3
where the time goes:
time: 1220 us; the launch traced here: 1210 us
  waiting for transfers between devices  473 us (39%)
  matrix products  329 us (27%)
  blocking collectives  180 us (15%)
  local copies, waits for them, and re-layouts  100 us (8%)
  other arithmetic  83.1 us (7%)
  starting transfers between devices  27.9 us (2%)
  between operations  14.5 us (1%)
    psum x1, waiting for transfers between devices, block_fn(): lax.psum((grad_w_qkv, grad_b_qkv, grad_w_out, grad_b_out, grad_gain, grad...  321 us
    all_to_all x1, waiting for transfers between devices, block_fn(): dqkv_loc = lax.all_to_all(dqkv_head, 'sp', 1, 2, tiled=True)  129 us
    all_gather x1, blocking collectives, block_fn(): pos_full = lax.all_gather(pos_blk, 'sp', axis=1, tiled=True)  117 us
    sub x1, matrix products, attn_probs(): return jax.nn.softmax(jnp.where(allowed, scores, MASK_FILL), axis=-1)  89.8 us
    dot_general x1, matrix products, attn_backward(): jnp.einsum('bqnd,bknd->bnqk', do_part, v_part, preferred_element_type=jnp...  66.7 us
    convert_element_type x1, other arithmetic, block_fn(): prob_lo = attn_prob.astype(jnp.bfloat16)  64.4 us
    psum x1, blocking collectives, block_fn(): lax.psum((grad_w_qkv, grad_b_qkv, grad_w_out, grad_b_out, grad_gain, grad...  46.1 us
    dot_general x1, matrix products, attn_backward(): jnp.einsum('bnqk,bqnd->bknd', ds_lo, q_part, preferred_element_type=jnp.f...  28.7 us
  transfers between devices with their start and end apart: 5, of which 3 were waited for; matrix products, arithmetic and copies ran while one was open for 13% of the time, Pallas kernels for 0%

commit v1 on v0

v1 whole, which is shorter than its diff:
```python
import functools
import jax
import jax.numpy as jnp
from jax import lax
from jax.experimental import pallas as pl
from jax.experimental.pallas import tpu as pltpu
from jax.sharding import PartitionSpec as P

NORM_EPS = 1e-5

LOG2E = 1.4426950408889634
MASKED = -1e30
F32, BF16 = jnp.float32, jnp.bfloat16
NT = (((1,), (1,)), ((), ()))


def attn_body(slope_ref, qkvt_ref, dot_ref, posk_ref, pref_ref, out_ref,
              k_tok, v_tok, s_buf, q_pad, do_pad, o_acc, dq_acc, dk_acc, dv_acc, *, blk, tok):
    dim = dot_ref.shape[0]
    seq = dot_ref.shape[1]
    pad = k_tok.shape[1] - dim
    nq = blk // tok
    scale = dim ** -0.5
    i = pl.program_id(0)
    half = blk // 2

    @pl.when(i == 0)
    def _():
        dk_acc[...] = jnp.zeros_like(dk_acc)
        dv_acc[...] = jnp.zeros_like(dv_acc)
        q_pad[...] = jnp.zeros_like(q_pad)
        do_pad[...] = jnp.zeros_like(do_pad)

        @pl.loop(0, seq // 128)
        def _(t):
            cols = pl.ds(pl.multiple_of(t * 128, 128), 128)
            for base, dst in ((dim, k_tok), (2 * dim, v_tok)):
                part = qkvt_ref[base:base + dim, cols].astype(F32)
                full = jnp.concatenate([part, jnp.zeros((pad, 128), F32)], axis=0)
                dst[cols, :] = jnp.transpose(full).astype(BF16)

    qcols = pl.ds(pl.multiple_of(i * blk, blk), blk)
    q_pad[0:dim, :] = qkvt_ref[0:dim, qcols]
    do_pad[0:dim, :] = dot_ref[:, qcols]
    slope2 = slope_ref[0]
    ref_pos = pref_ref[pl.ds(i, 1), :]
    c = scale * LOG2E

    def scores(j, m8, diag):
        for sub in range(2):
            rows = pl.ds(pl.multiple_of(j * blk + sub * half, half), half)
            st = jnp.dot(k_tok[rows, :], q_pad[...], preferred_element_type=F32)
            bias = (posk_ref[rows, :] - ref_pos) * slope2
            st = st * c + jnp.concatenate([bias] * (blk // 128), axis=1)
            if diag:
                key = lax.broadcasted_iota(jnp.int32, (half, blk), 0) + sub * half
                qry = lax.broadcasted_iota(jnp.int32, (half, blk), 1)
                st = jnp.where(key <= qry, st, MASKED)
            s_buf[rows, :] = st
            m8 = jnp.maximum(m8, jnp.max(st.reshape(half // 8, 8, blk), axis=0))
        return m8

    m8 = lax.fori_loop(0, i, lambda j, m: scores(j, m, False), jnp.full((8, blk), MASKED, F32))
    m8 = scores(i, m8, True)
    m = jnp.max(m8, axis=0, keepdims=True)

    def exps(j, l8):
        for sub in range(2):
            rows = pl.ds(pl.multiple_of(j * blk + sub * half, half), half)
            e = jnp.exp2(s_buf[rows, :] - m)
            s_buf[rows, :] = e
            l8 = l8 + jnp.sum(e.reshape(half // 8, 8, blk), axis=0)
        return l8

    l8 = lax.fori_loop(0, i + 1, exps, jnp.zeros((8, blk), F32))
    inv = 1.0 / jnp.sum(l8, axis=0, keepdims=True)
    o_acc[...] = jnp.zeros_like(o_acc)
    dq_acc[...] = jnp.zeros_like(dq_acc)

    def values(j, _):
        rows = pl.ds(pl.multiple_of(j * blk, blk), blk)
        p = s_buf[rows, :] * inv
        s_buf[rows, :] = p
        pb = p.astype(BF16)
        o_acc[...] += jnp.dot(qkvt_ref[2 * dim:3 * dim, rows], pb, preferred_element_type=F32)
        dv_acc[:, rows] += lax.dot_general(do_pad[0:dim, :], pb, NT, preferred_element_type=F32)
        return 0

    lax.fori_loop(0, i + 1, values, 0)
    o_lo = o_acc[...].astype(BF16)
    do_f = do_pad[0:dim, :].astype(F32)
    r = jnp.sum(do_f * o_lo.astype(F32), axis=0, keepdims=True)

    def grads(j, _):
        rows = pl.ds(pl.multiple_of(j * blk, blk), blk)
        g = jnp.dot(v_tok[rows, :], do_pad[...], preferred_element_type=F32)
        ds = (s_buf[rows, :] * (g - r)).astype(BF16)
        dq_acc[...] += jnp.dot(qkvt_ref[dim:2 * dim, rows], ds, preferred_element_type=F32)
        dk_acc[:, rows] += lax.dot_general(q_pad[0:dim, :], ds, NT, preferred_element_type=F32)
        return 0

    lax.fori_loop(0, i + 1, grads, 0)
    dq_lo = (dq_acc[...] * scale).astype(BF16)
    for t in range(nq):
        out_ref[i * nq + t, 0] = o_lo[:, t * tok:(t + 1) * tok]
        out_ref[i * nq + t, 1] = dq_lo[:, t * tok:(t + 1) * tok]

    @pl.when(i == pl.num_programs(0) - 1)
    def _():
        @pl.loop(0, seq // tok)
        def _(t):
            cols = pl.ds(pl.multiple_of(t * tok, tok), tok)
            out_ref[t, 2] = (dk_acc[:, cols] * scale).astype(BF16)
            out_ref[t, 3] = dv_acc[:, cols].astype(BF16)


def attention(slope2, qkvt, dot_, posk, pref, *, blk, tok):
    dim, seq = dot_.shape
    wide = 128 * pl.cdiv(dim, 128)
    full = lambda a: pl.BlockSpec(a.shape, lambda i: (0,) * a.ndim, pipeline_mode=pl.Buffered(1))
    out = jax.ShapeDtypeStruct((seq // tok, 4, dim, tok), BF16)
    pairs = (seq // blk) * (seq // blk + 1) // 2
    return pl.pallas_call(
        functools.partial(attn_body, blk=blk, tok=tok),
        name="attention",
        out_shape=out,
        grid=(seq // blk,),
        in_specs=[pl.BlockSpec(memory_space=pltpu.SMEM)] + [full(a) for a in (qkvt, dot_, posk, pref)],
        out_specs=pl.BlockSpec(out.shape, lambda i: (0, 0, 0, 0), pipeline_mode=pl.Buffered(1)),
        scratch_shapes=[
            pltpu.VMEM((seq, wide), BF16), pltpu.VMEM((seq, wide), BF16),
            pltpu.VMEM((seq, blk), F32),
            pltpu.VMEM((wide, blk), BF16), pltpu.VMEM((wide, blk), BF16),
            pltpu.VMEM((dim, blk), F32), pltpu.VMEM((dim, blk), F32),
            pltpu.VMEM((dim, seq), F32), pltpu.VMEM((dim, seq), F32)],
        cost_estimate=pl.CostEstimate(flops=pairs * 6 * 2 * blk * blk * 256, bytes_accessed=12 << 20, transcendentals=pairs * blk * blk),
        compiler_params=pltpu.CompilerParams(dimension_semantics=("arbitrary",), vmem_limit_bytes=48 << 20),
    )(slope2, qkvt, dot_, posk, pref)


def exchange_body(x_ref, out_ref, send_sem, recv_sem, *, peers):
    me = lax.axis_index("sp")
    barrier = pltpu.get_barrier_semaphore()
    for d in range(1, peers):
        pl.semaphore_signal(barrier, inc=1, device_id={"sp": lax.rem(me + d, peers)}, device_id_type=pl.DeviceIdType.MESH)
    pl.semaphore_wait(barrier, peers - 1)
    copies = []
    for d in range(1, peers):
        copies.append(pltpu.make_async_remote_copy(
            src_ref=x_ref, dst_ref=out_ref.at[me], send_sem=send_sem.at[d - 1], recv_sem=recv_sem.at[d - 1],
            device_id={"sp": lax.rem(me + d, peers)}, device_id_type=pl.DeviceIdType.MESH))
        copies[-1].start()
    out_ref[me] = x_ref[...]
    for copy in copies:
        copy.wait()


def exchange(x, peers, collective_id, name):
    return pl.pallas_call(
        functools.partial(exchange_body, peers=peers),
        name=name,
        out_shape=jax.ShapeDtypeStruct((peers,) + x.shape, x.dtype),
        in_specs=[pl.BlockSpec(memory_space=pltpu.VMEM)],
        out_specs=pl.BlockSpec(memory_space=pltpu.VMEM),
        scratch_shapes=[pltpu.SemaphoreType.DMA((peers - 1,)), pltpu.SemaphoreType.DMA((peers - 1,))],
        compiler_params=pltpu.CompilerParams(collective_id=collective_id, has_side_effects=True, vmem_limit_bytes=8 << 20),
    )(x)


def swap_body(x_ref, out_ref, own, send_sem, recv_sem, own_sem, *, peers):
    me = lax.axis_index("sp")
    barrier = pltpu.get_barrier_semaphore()
    for d in range(1, peers):
        pl.semaphore_signal(barrier, inc=1, device_id={"sp": lax.rem(me + d, peers)}, device_id_type=pl.DeviceIdType.MESH)
    pl.semaphore_wait(barrier, peers - 1)
    copies = []
    for near in range(peers // 2):
        for d in sorted({peers // 2 - near, peers // 2 + near}):
            peer = lax.rem(me + d, peers)
            copies.append(pltpu.make_async_remote_copy(
                src_ref=x_ref.at[peer], dst_ref=out_ref.at[me], send_sem=send_sem.at[d - 1], recv_sem=recv_sem.at[d - 1],
                device_id={"sp": peer}, device_id_type=pl.DeviceIdType.MESH))
            copies[-1].start()
    take = pltpu.make_async_copy(x_ref.at[me], own, own_sem)
    take.start()
    take.wait()
    put = pltpu.make_async_copy(own, out_ref.at[me], own_sem)
    put.start()
    put.wait()
    for copy in copies:
        copy.wait()


def swap(x, peers, collective_id, name):
    hbm = pl.BlockSpec(memory_space=pltpu.HBM)
    return pl.pallas_call(
        functools.partial(swap_body, peers=peers),
        name=name,
        out_shape=jax.ShapeDtypeStruct(x.shape, x.dtype),
        in_specs=[hbm],
        out_specs=hbm,
        scratch_shapes=[pltpu.VMEM(x.shape[1:], x.dtype), pltpu.SemaphoreType.DMA((peers - 1,)),
                        pltpu.SemaphoreType.DMA((peers - 1,)), pltpu.SemaphoreType.DMA],
        compiler_params=pltpu.CompilerParams(collective_id=collective_id, has_side_effects=True, vmem_limit_bytes=48 << 20),
    )(x)


def norm_forward(x_blk, ln_gain, ln_bias):
    x_f32 = x_blk.astype(F32)
    centered = x_f32 - jnp.mean(x_f32, axis=-1, keepdims=True)
    inv_std = lax.rsqrt(jnp.mean(centered * centered, axis=-1, keepdims=True) + NORM_EPS)
    x_hat = centered * inv_std
    return x_f32, x_hat, inv_std, (x_hat * ln_gain + ln_bias).astype(BF16)


def solution(mesh):
    peers = mesh.shape["sp"]

    def block_fn(x_blk, pos_blk, keep_blk, ln_gain, ln_bias, w_qkv, b_qkv, w_out, b_out, dy_blk):
        batch, tok, hidden = x_blk.shape
        heads, dim = w_qkv.shape[1], w_qkv.shape[3]
        assert heads == peers
        seq = tok * peers
        blk = 2 * tok
        rank = lax.axis_index("sp")
        x_f32, x_hat, inv_std, x_norm = norm_forward(x_blk, ln_gain, ln_bias)
        marks = exchange(jnp.concatenate([pos_blk, keep_blk, jnp.zeros((8 - 2 * batch, tok), jnp.int32)]), peers, 0, "marks")
        w_t = jnp.transpose(w_qkv, (1, 2, 3, 0))
        w_head = lax.dynamic_index_in_dim(w_t, rank, 0, keepdims=False).reshape(3 * dim, hidden)
        b_head = lax.dynamic_index_in_dim(b_qkv, rank, 0, keepdims=False).reshape(3 * dim, 1)
        wo_head = lax.dynamic_slice_in_dim(w_out, rank * dim, dim, 0)
        slope = jnp.exp2(-8.0 * (rank + 1).astype(F32) / heads)
        slope2 = (slope * LOG2E).reshape(1)
        gw = jnp.zeros((3 * dim, hidden), F32)
        go = jnp.zeros((dim, hidden), F32)
        gb = jnp.zeros((3 * dim,), F32)
        got = []
        for b in range(batch):
            xn, dy = x_norm[b], dy_blk[b]
            if b:
                xn, dy, _, _ = lax.optimization_barrier((xn, dy, xf, df))
            xf = lax.all_gather(xn, "sp", axis=0, tiled=True)
            df = lax.all_gather(dy, "sp", axis=0, tiled=True)
            pos = marks[:, b].reshape(seq).astype(F32)
            keep = marks[:, batch + b].reshape(seq)
            posk = jnp.broadcast_to(jnp.where(keep > 0, pos, MASKED)[:, None], (seq, 128))
            pref = jnp.broadcast_to(pos[::blk][:, None], (seq // blk, 128))
            qkvt = (lax.dot_general(w_head, xf, NT, preferred_element_type=F32) + b_head).astype(BF16)
            dot_ = lax.dot_general(wo_head, df, NT, preferred_element_type=F32).astype(BF16)
            if b:
                slope2, _ = lax.optimization_barrier((slope2, got[-1]))
            att = attention(slope2, qkvt, dot_, posk, pref, blk=blk, tok=tok)
            got.append(swap(att, peers, 2 + b, "swap"))
            xf3, df3 = xf.reshape(peers, tok, hidden), df.reshape(peers, tok, hidden)
            gw += jnp.einsum("pcdt,pth->cdh", att[:, 1:], xf3, preferred_element_type=F32).reshape(3 * dim, hidden)
            go += jnp.einsum("pdt,pth->dh", att[:, 0], df3, preferred_element_type=F32)
            gb += jnp.sum(att[:, 1:].astype(F32), axis=(0, 3)).reshape(3 * dim)
        gw_all = lax.all_gather(gw, "sp", axis=0, tiled=True)
        go_all = lax.all_gather(go, "sp", axis=0, tiled=True)
        y, gx, gg, gbias = [], [], 0.0, 0.0
        for b in range(batch):
            o_t = got[b][:, 0].reshape(hidden, tok)
            dqkv_t = got[b][:, 1:].reshape(3 * hidden, tok)
            y.append((x_f32[b] + lax.dot_general(o_t, w_out, (((0,), (0,)), ((), ())), preferred_element_type=F32) + b_out).astype(BF16))
            d_norm = lax.dot_general(dqkv_t, w_t.reshape(3 * hidden, hidden), (((0,), (0,)), ((), ())), preferred_element_type=F32)
            gg += jnp.sum(d_norm * x_hat[b], axis=0)
            gbias += jnp.sum(d_norm, axis=0)
            d_hat = d_norm * ln_gain
            d_mean = jnp.mean(d_hat, axis=-1, keepdims=True)
            d_proj = jnp.mean(d_hat * x_hat[b], axis=-1, keepdims=True)
            gx.append((dy_blk[b].astype(F32) + inv_std[b] * (d_hat - d_mean - x_hat[b] * d_proj)).astype(BF16))
        g_out = jnp.sum(dy_blk.astype(F32), axis=(0, 1))
        rows = jnp.stack([gg, gbias, g_out, jnp.pad(gb, (0, hidden - 3 * dim))] + [jnp.zeros((hidden,), F32)] * 4)
        sums = exchange(rows, peers, 1, "sums")
        total = jnp.sum(sums[:, :3], axis=0)
        gb_all = sums[:, 3, :3 * dim].reshape(heads, 3, dim)
        gw_out = jnp.transpose(gw_all.reshape(heads, 3, dim, hidden), (3, 0, 1, 2))
        return jnp.stack(y), jnp.stack(gx), gw_out, gb_all, go_all, total[2], total[0], total[1]

    act_spec = P("dp", "sp", None)
    tok_spec = P("dp", "sp")
    in_specs = (act_spec, tok_spec, tok_spec, P(), P(), P(), P(), P(), P(), act_spec)
    out_specs = (act_spec, act_spec, P("dp", None, None, None), P("dp", None, None), P("dp", None), P("dp"), P("dp"), P("dp"))
    return jax.shard_map(block_fn, mesh=mesh, in_specs=in_specs, out_specs=out_specs, check_vma=False)
```

time: 1220 us -> 775 us (0.64); the launches traced: 1210 us -> 774 us
  Pallas kernels: 0 us -> 373 us
  matrix products: 329 us -> 91.8 us
  waiting for transfers between devices: 473 us -> 244 us
  blocking collectives: 180 us -> 0 us
  other arithmetic: 83.1 us -> 14.6 us
  local copies, waits for them, and re-layouts: 100 us -> 36 us
  starting transfers between devices: 27.9 us -> 0.37 us
    pallas_call x0 -> x6, Pallas kernels: none -> 373 us  [the longest x2 205 us: swap(): pl.pallas_call(functools.partial(swap_body, peers=peers), name=name, out_...]
    psum x1 -> x0, waiting for transfers between devices: 321 us -> none  [block_fn(): lax.psum((grad_w_qkv, grad_b_qkv, grad_w_out, grad_b_out, grad_gain, grad...]
    all_gather x0 -> x6, waiting for transfers between devices: none -> 242 us  [the longest x1 100 us: block_fn(): gw_all = lax.all_gather(gw, 'sp', axis=0, tiled=True)]
    all_to_all x4 -> x0, waiting for transfers between devices: 152 us -> none  [the longest x1 129 us: block_fn(): dqkv_loc = lax.all_to_all(dqkv_head, 'sp', 1, 2, tiled=True)]
    dot_general x11 -> x12, matrix products: 239 us -> 91.8 us  [the longest x2 21.7 us: block_fn(): lax.dot_general(w_head, xf, NT, preferred_element_type=F32) + b_head]
    all_gather x2 -> x0, blocking collectives: 134 us -> none  [the longest x1 117 us: block_fn(): pos_full = lax.all_gather(pos_blk, 'sp', axis=1, tiled=True)]
    sub x1 -> x0, matrix products: 89.8 us -> none  [attn_probs(): return jax.nn.softmax(jnp.where(allowed, scores, MASK_FILL), axis=-1)]
    convert_element_type x1 -> x2, other arithmetic: 64.4 us -> 3.59 us  [the longest x1 3.56 us: norm_forward(): x_f32 = x_blk.astype(F32)]
  transfers between devices with their start and end apart: 5 -> 6, of which waited for: 3 -> 4; matrix products, arithmetic and copies ran while one was open for 13% -> 10% of each run, Pallas kernels for 0% -> 41%
where the time goes in v1:
time: 775 us; the launch traced here: 774 us
  Pallas kernels  373 us (48%)
  waiting for transfers between devices  244 us (31%)
  matrix products  91.8 us (12%)
  local copies, waits for them, and re-layouts  36 us (5%)
  between operations  14.7 us (2%)
  other arithmetic  14.6 us (2%)
    pallas_call x2, Pallas kernels, swap(): pl.pallas_call(functools.partial(swap_body, peers=peers), name=name, out_...  205 us
    pallas_call x2, Pallas kernels, attention(): pl.pallas_call(functools.partial(attn_body, blk=blk, tok=tok), name='atte...  119 us
    all_gather x1, waiting for transfers between devices, block_fn(): gw_all = lax.all_gather(gw, 'sp', axis=0, tiled=True)  100 us
    all_gather x2, waiting for transfers between devices, block_fn(): xf = lax.all_gather(xn, 'sp', axis=0, tiled=True)  84 us
    all_gather x2, waiting for transfers between devices, block_fn(): df = lax.all_gather(dy, 'sp', axis=0, tiled=True)  57.6 us
    pallas_call x2, Pallas kernels, exchange(): pl.pallas_call(functools.partial(exchange_body, peers=peers), name=name,...  49 us
    unnamed x59, local copies, waits for them, and re-layouts  28.7 us
    dot_general x2, matrix products, block_fn(): lax.dot_general(w_head, xf, NT, preferred_element_type=F32) + b_head  21.7 us
  transfers between devices with their start and end apart: 6, of which 4 were waited for; matrix products, arithmetic and copies ran while one was open for 10% of the time, Pallas kernels for 41%

profile of v1, /device:TPU:21, one launch (start us, length us, event | category | flops | bytes accessed | tf_op | source)
XLA Modules:
  0.0 774.5 jit_solution(7781487254807210958)
XLA Ops:
  7.2 0.1 all-gather.19.cloned.1.call-start
  7.3 1.8 convert_reduce_fusion.3
  9.1 2.0 multiply_reduce_fusion
  11.1 2.3 subtract_multiply_fusion
  13.5 1.8 slice_bitcast_fusion.8
  15.3 0.1 all-gather.17.cloned.1.call-start
  15.4 0.7 all-gather.17.cloned.1.call-update
  16.1 0.1 all-gather.11.cloned.1.call-start
  16.2 0.7 all-gather.11.cloned.1.call-update
  16.9 0.1 all-gather.9.cloned.1.call-start
  17.0 0.6 all-gather.9.cloned.1.call-update
  17.5 0.1 all-gather.15.cloned.1.call-start
  17.7 0.1 pad.11.clone
  17.8 0.1 add.124
  17.8 0.1 add_add_fusion.x_ref
  17.9 15.7 %marks.1 = s32[16,8,256]{2,1,0:T(8,128)S(1)} custom-call(s32[8,256]{1,0:T(8,128)S(1)} %add_add_fusion.x_ref), custom_call_target="tpu_custom_call" | custom-call | tf_op jit(solution)/shard_map/marks/pallas_call | solution.py:159
  33.6 0.1 compare_reduce_fusion
  33.8 0.1 slice.102
  33.9 0.1 slice.109
  34.0 1.2 constant_dynamic-slice_fusion
  35.3 57.6 %all-gather.19.cloned.1.call-done = bf16[1,4096,1536]{2,1,0:T(8,128)(2,1)} async-done(((bf16[1,256,1536]{2,1,0:T(8,128)(2,1)}), bf16[1,4096,1536]{2,1,0:T(8,128)(2,1)}) %all-gather.19.cloned.1.call-update) | async-done | bytes 12582928 | tf_op jit(solution)/shard_map/all_gather | solution.py:243
  92.9 8.6 %convolution_convert_fusion.1.dot_ref = bf16[96,4096]{1,0:T(8,128)(2,1)S(1)} fusion(bf16[1536,1536]{1,0:T(8,128)(2,1)} %param.17, s32[]{:T(128)S(6)} %select_n.25, bf16[1,4096,1536]{2,1,0:T(8,128)(2,1)} %all-gather.19.cloned.1.call-done), kind=kOutput, calls=%fused_computation.11 | convolution fusion | flops 1208352768 | bytes 13664260 | tf_op jit(solution)/shard_map/dot_general | solution.py:249
  101.4 65.7 %all-gather.17.cloned.1.call-done = bf16[1,4096,1536]{2,1,0:T(8,128)(2,1)} async-done(((bf16[1,256,1536]{2,1,0:T(8,128)(2,1)}), bf16[1,4096,1536]{2,1,0:T(8,128)(2,1)}) %all-gather.17.cloned.1.call-update) | async-done | bytes 12582928 | tf_op jit(solution)/shard_map/all_gather | solution.py:242
  167.1 13.0 %fusion.4.qkvt_ref = bf16[288,4096]{1,0:T(8,128)(2,1)S(1)} fusion(bf16[288,1536]{1,0:T(8,128)(2,1)S(1)} %bitcast.134, f32[288]{0:T(512)S(1)} %add.124, bf16[1,4096,1536]{2,1,0:T(8,128)(2,1)} %all-gather.17.cloned.1.call-done), kind=kOutput, calls=%fused_computation.6 | convolution fusion | flops 3626237952 | bytes 15828096 | tf_op jit(solution)/shard_map/dot_general | solution.py:248
  180.1 0.1 broadcast_in_dim.18.pref_ref
  180.2 0.6 broadcast_in_dim.17.posk_ref
  180.8 59.3 %attention.2.x_ref = bf16[16,4,96,256]{3,2,1,0:T(8,128)(2,1)} custom-call(f32[1]{0:T(128)} %bitcast.1.slope_ref, bf16[288,4096]{1,0:T(8,128)(2,1)S(1)} %fusion.4.qkvt_ref, bf16[96,4096]{1,0:T(8,128)(2,1)S(1)} %convolution_convert_fusion.1.dot_ref, f32[4096,128]{1,0:T(8,128)S(1)} %broadcast_in_dim.17.posk_ref, f32[8,128]{1,0:T(8,128)S(1)} %broadcast_in_dim.18.pref_ref), custom_call_target="tpu_custom_call" | custom-call | flops 28991029248 | bytes 12582912 | tf_op jit(solution)/shard_map/attention/pallas_call | solution.py:123
  240.1 104.9 %swap.2 = bf16[16,4,96,256]{3,2,1,0:T(8,128)(2,1)S(1)} custom-call(bf16[16,4,96,256]{3,2,1,0:T(8,128)(2,1)} %attention.2.x_ref), custom_call_target="tpu_custom_call" | custom-call | tf_op jit(solution)/shard_map/swap/pallas_call | solution.py:196
  345.0 10.5 %convolution_convert_fusion.dot_ref = bf16[96,4096]{1,0:T(8,128)(2,1)} fusion(bf16[4096,1536]{1,0:T(8,128)(2,1)} %all-gather.11.cloned.1.call-done, bf16[1536,1536]{1,0:T(8,128)(2,1)} %param.17, s32[]{:T(128)S(6)} %select_n.25), kind=kOutput, calls=%fused_computation.10 | convolution fusion | flops 1208352768 | bytes 13664260 | tf_op jit(solution)/shard_map/dot_general | solution.py:249
  355.6 18.3 %all-gather.9.cloned.1.call-done = bf16[4096,1536]{1,0:T(8,128)(2,1)} async-done(((bf16[256,1536]{1,0:T(8,128)(2,1)}), bf16[4096,1536]{1,0:T(8,128)(2,1)}) %all-gather.9.cloned.1.call-update) | async-done | bytes 12582928 | tf_op jit(solution)/shard_map/all_gather | solution.py:242
  373.9 8.8 %fusion.5.qkvt_ref = bf16[288,4096]{1,0:T(8,128)(2,1)S(1)} fusion(bf16[288,1536]{1,0:T(8,128)(2,1)} %bitcast.135, bf16[4096,1536]{1,0:T(8,128)(2,1)} %all-gather.9.cloned.1.call-done, f32[288]{0:T(512)S(1)} %add.124), kind=kOutput, calls=%fused_computation.7 | convolution fusion | flops 3626237952 | bytes 15828096 | tf_op jit(solution)/shard_map/dot_general | solution.py:248
  382.7 0.1 broadcast_in_dim.20.pref_ref
  382.7 0.6 broadcast_in_dim.19.posk_ref
  383.3 59.3 %attention.3.x_ref = bf16[16,4,96,256]{3,2,1,0:T(8,128)(2,1)} custom-call(f32[1]{0:T(128)} %bitcast.1.slope_ref, bf16[288,4096]{1,0:T(8,128)(2,1)S(1)} %fusion.5.qkvt_ref, bf16[96,4096]{1,0:T(8,128)(2,1)S(1)} %copy-done.5, f32[4096,128]{1,0:T(8,128)S(1)} %broadcast_in_dim.19.posk_ref, f32[8,128]{1,0:T(8,128)S(1)} %broadcast_in_dim.20.pref_ref), custom_call_target="tpu_custom_call" | custom-call | flops 28991029248 | bytes 12582912 | tf_op jit(solution)/shard_map/attention/pallas_call | solution.py:123
  442.7 7.1 convolution_bitcast_fusion.2
  449.8 7.6 fusion.19
  457.4 0.1 all-gather.13.cloned.1.call-start
  457.5 1.6 slice-done.3
  459.1 7.1 convolution_bitcast_fusion
  466.2 1.0 slice-done.6
  467.3 5.0 fusion.6
  472.4 3.6 convert_element_type.70
  475.9 0.3 convert_reduce_fusion.2
  476.3 100.5 %swap.3 = bf16[16,4,96,256]{3,2,1,0:T(8,128)(2,1)S(1)} custom-call(bf16[16,4,96,256]{3,2,1,0:T(8,128)(2,1)} %attention.3.x_ref), custom_call_target="tpu_custom_call" | custom-call | tf_op jit(solution)/shard_map/swap/pallas_call | solution.py:196
  576.8 0.4 convert_reduce_fusion.1
  577.2 0.4 convert_reduce_fusion
  577.6 0.1 add.142
  577.7 0.8 copy-done.2
  578.6 7.2 fusion.10
  585.9 8.7 %multiply_reduce_fusion.2 = (f32[1536]{0:T(1024)S(1)}, f32[256]{0:T(256)S(1)}, f32[256]{0:T(256)S(1)}, f32[1536]{0:T(1024)S(1)}, f32[256]{0:T(256)S(1)}, /*index...) fusion(f32[2,256,1536]{2,1,0:T(8,128)S(1)} %copy-done.10, f32[1536]{0:T(1024)S(1)} %copy-done.20, ...), kind=kOutput, calls=%fused_computation.42 | convolution fusion | flops 3629376512 | bytes 23627776 | tf_op jit(solution)/shard_map/dot_general | solution.py:265
  594.7 33.4 %sums.1 = f32[16,8,1536]{2,1,0:T(8,128)S(1)} custom-call(f32[8,1536]{1,0:T(8,128)S(1)} %stack.41.x_ref), custom_call_target="tpu_custom_call" | custom-call | tf_op jit(solution)/shard_map/sums/pallas_call | solution.py:159
  628.1 0.1 slice_reduce_fusion.1
  628.2 0.1 reshape_squeeze.15
  628.3 0.6 copy.19
  628.9 0.6 slice_reduce_fusion.2
  629.6 4.4 fusion.17
  634.1 3.9 fusion.18
  638.0 1.3 pad_maximum_fusion
  639.3 1.2 copy-done.11
  640.4 1.0 fusion.22
  641.4 1.3 pad_maximum_fusion.1
  642.7 100.0 %all-gather.13.cloned.1.call-done = f32[4608,1536]{1,0:T(8,128)} async-done(((f32[288,1536]{1,0:T(8,128)}), f32[4608,1536]{1,0:T(8,128)}) %all-gather.13.cloned.1.call-update) | async-done | bytes 28311568 | tf_op jit(solution)/shard_map/all_gather | solution.py:258
  742.7 21.2 %copy.24 = f32[1536,16,3,96]{0,3,2,1:T(8,128)} copy(f32[1536,16,3,96]{0,3,2,1:T(8,128)} %bitcast.131) | data formatting | bytes 56623104
  763.9 3.7 copy.25
  (91 shorter events, 0.6 us)
Async XLA Ops:
  7.2 10.6 %copy-start = (f32[16,3,96]{2,0,1:T(8,128)S(1)}, f32[16,3,96]{2,0,1:T(8,128)}, u32[]{:S(2)}) copy-start(f32[16,3,96]{2,0,1:T(8,128)} %param.16) | copy-start | bytes 55300
  7.2 3.9 copy-start.6
  7.2 3.9 copy-start.20
  7.2 3.9 copy-start.21
  7.2 85.6 %all-gather.19.cloned.1.call-start = ((), (), s32[]{:S(2)}) async-start(), calls=%async_computation.5 | async-start | bytes 13369344 | tf_op jit(solution)/shard_map/all_gather | solution.py:243
  11.1 2.4 copy-start.14
  15.2 2.6 copy-start.22
  15.2 2.6 copy-start.23
  15.3 151.8 %all-gather.17.cloned.1.call-start = ((), (), s32[]{:S(2)}) async-start(), calls=%async_computation.4 | async-start | bytes 13369344 | tf_op jit(solution)/shard_map/all_gather | solution.py:242
  16.1 328.9 %all-gather.11.cloned.1.call-start = ((), (), s32[]{:S(2)}) async-start(), calls=%async_computation.1 | async-start | bytes 13369344 | tf_op jit(solution)/shard_map/all_gather | solution.py:243
  16.9 357.0 %all-gather.9.cloned.1.call-start = ((), (), s32[]{:S(2)}) async-start(), calls=%async_computation | async-start | bytes 13369344 | tf_op jit(solution)/shard_map/all_gather | solution.py:242
  17.5 625.2 %all-gather.15.cloned.1.call-start = ((), (), s32[]{:S(2)}) async-start(), calls=%async_computation.3 | async-start | bytes 10027008 | tf_op jit(solution)/shard_map/all_gather | solution.py:259
  35.2 131.9 %copy-start.19 = (bf16[1536,1,3,96]{0,3,2,1:T(8,128)(2,1)}, bf16[1536,1,3,96]{0,3,2,1:T(8,128)(2,1)S(1)}, u32[]{:S(2)}) copy-start(bf16[1536,1,3,96]{0,3,2,1:T(8,128)(2,1)S(1)} %constant_dynamic-slice_fusion) | copy-start | bytes 2654212
  345.0 131.2 %copy-start.3 = (bf16[16,4,96,256]{3,2,1,0:T(8,128)(2,1)}, bf16[16,4,96,256]{3,2,1,0:T(8,128)(2,1)S(1)}, u32[]{:S(2)}) copy-start(bf16[16,4,96,256]{3,2,1,0:T(8,128)(2,1)S(1)} %swap.2) | copy-start | bytes 9437188
  373.9 9.4 %copy-start.5 = (bf16[96,4096]{1,0:T(8,128)(2,1)S(1)}, bf16[96,4096]{1,0:T(8,128)(2,1)}, u32[]{:S(2)}) copy-start(bf16[96,4096]{1,0:T(8,128)(2,1)} %convolution_convert_fusion.dot_ref) | copy-start | bytes 2359300
  442.7 7.1 copy-start.7
  457.4 285.3 %all-gather.13.cloned.1.call-start = ((), (), s32[]{:S(2)}) async-start(), calls=%async_computation.2 | async-start | bytes 30081024 | tf_op jit(solution)/shard_map/all_gather | solution.py:258
  457.4 1.7 slice-start.3
  457.5 8.7 %slice-start.4 = ((s8[12582912]{0:T(1024)(128)(4,1)}), s8[4194304]{0:T(1024)(128)(4,1)S(1)}, s32[]{:S(2)}) async-start(s8[12582912]{0:T(1024)(128)(4,1)} %bitcast.142), calls=%async_computation.10 | async-start | bytes 8388608
  459.1 7.1 slice-start.2
  459.1 7.1 slice-start.5
  459.1 8.1 %slice-start.6 = ((s8[12582912]{0:T(1024)(128)(4,1)}), s8[4194304]{0:T(1024)(128)(4,1)S(1)}, s32[]{:S(2)}) async-start(s8[12582912]{0:T(1024)(128)(4,1)} %bitcast.142), calls=%async_computation.12 | async-start | bytes 8388608
  472.4 3.6 copy-start.15
  476.2 100.6 %copy-start.8 = (bf16[16,4,96,256]{3,2,1,0:T(8,128)(2,1)S(1)}, bf16[16,4,96,256]{3,2,1,0:T(8,128)(2,1)}, u32[]{:S(2)}) copy-start(bf16[16,4,96,256]{3,2,1,0:T(8,128)(2,1)} %attention.2.x_ref) | copy-start | bytes 9437188
  476.2 101.0 %copy-start.9 = (bf16[16,4,96,256]{3,2,1,0:T(8,128)(2,1)S(1)}, bf16[16,4,96,256]{3,2,1,0:T(8,128)(2,1)}, u32[]{:S(2)}) copy-start(bf16[16,4,96,256]{3,2,1,0:T(8,128)(2,1)} %attention.3.x_ref) | copy-start | bytes 9437188
  576.8 1.7 copy-start.2
  578.6 7.3 copy-start.4
  578.6 7.3 copy-start.10
  585.8 8.8 %copy-start.12 = (f32[256,1536]{1,0:T(8,128)}, f32[256,1536]{1,0:T(8,128)S(1)}, u32[]{:S(2)}) copy-start(f32[256,1536]{1,0:T(8,128)S(1)} %fusion.10) | copy-start | bytes 4718596
  585.8 43.8 %slice-start.1 = ((bf16[16,4,96,256]{3,2,1,0:T(8,128)(2,1)}), bf16[16,1,96,256]{3,2,1,0:T(8,128)(2,1)S(1)}, s32[]{:S(2)}) async-start(bf16[16,4,96,256]{3,2,1,0:T(8,128)(2,1)} %copy-done.3), calls=%async_computation.7 | async-start | bytes 1572864 | tf_op jit(solution)/shard_map/slice | solution.py:262
  585.8 43.8 %copy-start.24 = (f32[1536]{0:T(1024)S(1)}, f32[1536]{0:T(1024)}, u32[]{:S(2)}) copy-start(f32[1536]{0:T(1024)} %param.18) | copy-start | bytes 18436
  629.6 4.4 slice-start
  629.6 4.4 copy-start.18
  634.1 5.2 copy-start.13
  634.1 5.2 copy-start.16
  638.0 2.5 copy-start.11
  742.7 21.2 %copy-start.17 = (f32[1536,1536]{1,0:T(8,128)S(1)}, f32[1536,1536]{1,0:T(8,128)}, u32[]{:S(2)}) copy-start(f32[1536,1536]{1,0:T(8,128)} %all-gather.15.cloned.1.call-done) | copy-start | bytes 28311556
  763.9 3.7 copy-start.1
Sparse Core Ops, SparseCore 0:
  15.4 77.4 all-gather.18
  95.1 71.9 all-gather.16
  168.7 70.7 all-gather.10
  241.6 132.2 all-gather.8
  457.5 121.8 all-gather.14
  580.9 161.7 all-gather.12

commit v2 on v1

--- a/solution.py
+++ b/solution.py
@@ -14,15 +14,27 @@
 NT = (((1,), (1,)), ((), ()))
 
 
-def attn_body(slope_ref, qkvt_ref, dot_ref, posk_ref, pref_ref, out_ref,
-              k_tok, v_tok, s_buf, q_pad, do_pad, o_acc, dq_acc, dk_acc, dv_acc, *, blk, tok):
-    dim = dot_ref.shape[0]
-    seq = dot_ref.shape[1]
+def attn_body(slope_ref, qkvt_ref, dot_ref, posk_ref, pref_ref, *refs, blk, tok, peers):
+    if peers:
+        old_ref, out_ref, got_ref = refs[:3]
+        own, send_sem, recv_sem, own_sem = refs[-4:]
+        refs = refs[3:-4]
+    else:
+        out_ref, refs = refs[0], refs[1:]
+    k_tok, v_tok, s_buf, q_pad, do_pad, o_acc, dq_acc, dk_acc, dv_acc = refs
+    dim = dot_ref.shape[1]
+    seq = dot_ref.shape[0] * tok
     pad = k_tok.shape[1] - dim
     nq = blk // tok
     scale = dim ** -0.5
     i = pl.program_id(0)
     half = blk // 2
+
+    if peers:
+        @pl.when(i == 0)
+        def _():
+            meet(peers)
+            swap_start(old_ref, got_ref, own, send_sem, recv_sem, own_sem, peers)
 
     @pl.when(i == 0)
     def _():
@@ -41,7 +53,8 @@
 
     qcols = pl.ds(pl.multiple_of(i * blk, blk), blk)
     q_pad[0:dim, :] = qkvt_ref[0:dim, qcols]
-    do_pad[0:dim, :] = dot_ref[:, qcols]
+    for t in range(nq):
+        do_pad[0:dim, t * tok:(t + 1) * tok] = dot_ref[i * nq + t]
     slope2 = slope_ref[0]
     ref_pos = pref_ref[pl.ds(i, 1), :]
     c = scale * LOG2E
@@ -113,43 +126,123 @@
             out_ref[t, 2] = (dk_acc[:, cols] * scale).astype(BF16)
             out_ref[t, 3] = dv_acc[:, cols].astype(BF16)
 
-
-def attention(slope2, qkvt, dot_, posk, pref, *, blk, tok):
-    dim, seq = dot_.shape
+        if peers:
+            swap_wait(old_ref, got_ref, own, send_sem, recv_sem, own_sem, peers)
+
+
+def attention(slope2, qkvt, dot_, posk, pref, *, blk, tok, old=None, collective_id=None):
+    blocks, dim, _ = dot_.shape
+    seq = blocks * tok
     wide = 128 * pl.cdiv(dim, 128)
+    hbm = pl.BlockSpec(memory_space=pltpu.HBM)
     full = lambda a: pl.BlockSpec(a.shape, lambda i: (0,) * a.ndim, pipeline_mode=pl.Buffered(1))
-    out = jax.ShapeDtypeStruct((seq // tok, 4, dim, tok), BF16)
+    out = jax.ShapeDtypeStruct((blocks, 4, dim, tok), BF16)
     pairs = (seq // blk) * (seq // blk + 1) // 2
+    args = (slope2, qkvt, dot_, posk, pref)
+    in_specs = [pl.BlockSpec(memory_space=pltpu.SMEM)] + [full(a) for a in (qkvt, dot_, posk, pref)]
+    out_shape, out_specs = [out], [pl.BlockSpec(out.shape, lambda i: (0, 0, 0, 0), pipeline_mode=pl.Buffered(1))]
+    scratch = [
+        pltpu.VMEM((seq, wide), BF16), pltpu.VMEM((seq, wide), BF16),
+        pltpu.VMEM((seq, blk), F32),
+        pltpu.VMEM((wide, blk), BF16), pltpu.VMEM((wide, blk), BF16),
+        pltpu.VMEM((dim, blk), F32), pltpu.VMEM((dim, blk), F32),
+        pltpu.VMEM((dim, seq), F32), pltpu.VMEM((dim, seq), F32)]
+    peers = 0
+    if old is not None:
+        peers = old.shape[0]
+        args += (old,)
+        in_specs.append(hbm)
+        out_shape.append(jax.ShapeDtypeStruct(old.shape, old.dtype))
+        out_specs.append(hbm)
+        scratch += swap_scratch(old)
+    res = pl.pallas_call(
+        functools.partial(attn_body, blk=blk, tok=tok, peers=peers),
+        name="attention",
+        out_shape=out_shape,
+        grid=(seq // blk,),
+        in_specs=in_specs,
+        out_specs=out_specs,
+        scratch_shapes=scratch,
+        cost_estimate=pl.CostEstimate(flops=pairs * 6 * 2 * blk * blk * 256, bytes_accessed=12 << 20, transcendentals=pairs * blk * blk),
+        compiler_params=pltpu.CompilerParams(dimension_semantics=("arbitrary",), vmem_limit_bytes=44 << 20,
+                                             collective_id=collective_id, has_side_effects=old is not None),
+    )(*args)
+    return res if old is not None else res[0]
+
+
+def peer_at(d, peers):
+    return {"sp": lax.rem(lax.axis_index("sp") + d, peers)}
+
+
+def meet(peers):
+    barrier = pltpu.get_barrier_semaphore()
+    for d in range(1, peers):
+        pl.semaphore_signal(barrier, inc=1, device_id=peer_at(d, peers), device_id_type=pl.DeviceIdType.MESH)
+    pl.semaphore_wait(barrier, peers - 1)
+
+
+def swap_copies(x_ref, out_ref, send_sem, recv_sem, peers):
+    me = lax.axis_index("sp")
+    order = [d for near in range(peers // 2) for d in sorted({peers // 2 - near, peers // 2 + near})]
+    return [pltpu.make_async_remote_copy(
+        src_ref=x_ref.at[lax.rem(me + d, peers)], dst_ref=out_ref.at[me], send_sem=send_sem.at[d - 1], recv_sem=recv_sem.at[d - 1],
+        device_id=peer_at(d, peers), device_id_type=pl.DeviceIdType.MESH) for d in order]
+
+
+def swap_start(x_ref, out_ref, own, send_sem, recv_sem, own_sem, peers):
+    me = lax.axis_index("sp")
+    for copy in swap_copies(x_ref, out_ref, send_sem, recv_sem, peers):
+        copy.start()
+    take = pltpu.make_async_copy(x_ref.at[me], own, own_sem)
+    take.start()
+    take.wait()
+    pltpu.make_async_copy(own, out_ref.at[me], own_sem).start()
+
+
+def swap_wait(x_ref, out_ref, own, send_sem, recv_sem, own_sem, peers):
+    pltpu.make_async_copy(own, out_ref.at[lax.axis_index("sp")], own_sem).wait()
+    for copy in swap_copies(x_ref, out_ref, send_sem, recv_sem, peers):
+        copy.wait()
+
+
+def swap_scratch(x):
+    peers = x.shape[0]
+    return [pltpu.VMEM(x.shape[1:], x.dtype), pltpu.SemaphoreType.DMA((peers - 1,)), pltpu.SemaphoreType.DMA((peers - 1,)),
+            pltpu.SemaphoreType.DMA]
+
+
+def swap_body(*refs, peers, n):
+    ins, outs, scratch = refs[:n], refs[n:2 * n], refs[2 * n:]
+    meet(peers)
+    for k in range(n):
+        swap_start(ins[k], outs[k], *scratch[4 * k:4 * k + 4], peers)
+    for k in range(n):
+        swap_wait(ins[k], outs[k], *scratch[4 * k:4 * k + 4], peers)
+
+
+def swap(xs, collective_id, name):
+    hbm = pl.BlockSpec(memory_space=pltpu.HBM)
+    peers = xs[0].shape[0]
     return pl.pallas_call(
-        functools.partial(attn_body, blk=blk, tok=tok),
-        name="attention",
-        out_shape=out,
-        grid=(seq // blk,),
-        in_specs=[pl.BlockSpec(memory_space=pltpu.SMEM)] + [full(a) for a in (qkvt, dot_, posk, pref)],
-        out_specs=pl.BlockSpec(out.shape, lambda i: (0, 0, 0, 0), pipeline_mode=pl.Buffered(1)),
-        scratch_shapes=[
-            pltpu.VMEM((seq, wide), BF16), pltpu.VMEM((seq, wide), BF16),
-            pltpu.VMEM((seq, blk), F32),
-            pltpu.VMEM((wide, blk), BF16), pltpu.VMEM((wide, blk), BF16),
-            pltpu.VMEM((dim, blk), F32), pltpu.VMEM((dim, blk), F32),
-            pltpu.VMEM((dim, seq), F32), pltpu.VMEM((dim, seq), F32)],
-        cost_estimate=pl.CostEstimate(flops=pairs * 6 * 2 * blk * blk * 256, bytes_accessed=12 << 20, transcendentals=pairs * blk * blk),
-        compiler_params=pltpu.CompilerParams(dimension_semantics=("arbitrary",), vmem_limit_bytes=48 << 20),
-    )(slope2, qkvt, dot_, posk, pref)
+        functools.partial(swap_body, peers=peers, n=len(xs)),
+        name=name,
+        out_shape=[jax.ShapeDtypeStruct(x.shape, x.dtype) for x in xs],
+        in_specs=[hbm] * len(xs),
+        out_specs=[hbm] * len(xs),
+        scratch_shapes=sum((swap_scratch(x) for x in xs), []),
+        cost_estimate=pl.CostEstimate(flops=24000 * sum(x.size for x in xs), bytes_accessed=4 * sum(x.size for x in xs), transcendentals=0),
+        compiler_params=pltpu.CompilerParams(collective_id=collective_id, has_side_effects=True, vmem_limit_bytes=48 << 20),
+    )(*xs)
 
 
 def exchange_body(x_ref, out_ref, send_sem, recv_sem, *, peers):
     me = lax.axis_index("sp")
-    barrier = pltpu.get_barrier_semaphore()
-    for d in range(1, peers):
-        pl.semaphore_signal(barrier, inc=1, device_id={"sp": lax.rem(me + d, peers)}, device_id_type=pl.DeviceIdType.MESH)
-    pl.semaphore_wait(barrier, peers - 1)
-    copies = []
-    for d in range(1, peers):
-        copies.append(pltpu.make_async_remote_copy(
-            src_ref=x_ref, dst_ref=out_ref.at[me], send_sem=send_sem.at[d - 1], recv_sem=recv_sem.at[d - 1],
-            device_id={"sp": lax.rem(me + d, peers)}, device_id_type=pl.DeviceIdType.MESH))
-        copies[-1].start()
+    meet(peers)
+    copies = [pltpu.make_async_remote_copy(
+        src_ref=x_ref, dst_ref=out_ref.at[me], send_sem=send_sem.at[d - 1], recv_sem=recv_sem.at[d - 1],
+        device_id=peer_at(d, peers), device_id_type=pl.DeviceIdType.MESH) for d in range(1, peers)]
+    for copy in copies:
+        copy.start()
     out_ref[me] = x_ref[...]
     for copy in copies:
         copy.wait()
@@ -167,42 +260,15 @@
     )(x)
 
 
-def swap_body(x_ref, out_ref, own, send_sem, recv_sem, own_sem, *, peers):
-    me = lax.axis_index("sp")
-    barrier = pltpu.get_barrier_semaphore()
-    for d in range(1, peers):
-        pl.semaphore_signal(barrier, inc=1, device_id={"sp": lax.rem(me + d, peers)}, device_id_type=pl.DeviceIdType.MESH)
-    pl.semaphore_wait(barrier, peers - 1)
-    copies = []
-    for near in range(peers // 2):
-        for d in sorted({peers // 2 - near, peers // 2 + near}):
-            peer = lax.rem(me + d, peers)
-            copies.append(pltpu.make_async_remote_copy(
-                src_ref=x_ref.at[peer], dst_ref=out_ref.at[me], send_sem=send_sem.at[d - 1], recv_sem=recv_sem.at[d - 1],
-                device_id={"sp": peer}, device_id_type=pl.DeviceIdType.MESH))
-            copies[-1].start()
-    take = pltpu.make_async_copy(x_ref.at[me], own, own_sem)
-    take.start()
-    take.wait()
-    put = pltpu.make_async_copy(own, out_ref.at[me], own_sem)
-    put.start()
-    put.wait()
-    for copy in copies:
-        copy.wait()
-
-
-def swap(x, peers, collective_id, name):
-    hbm = pl.BlockSpec(memory_space=pltpu.HBM)
+def copy_body(x_ref, out_ref):
+    out_ref[...] = x_ref[...]
+
+
+def keep_copy(x, steps):
+    spec = pl.BlockSpec((x.shape[0] // steps, x.shape[1]), lambda i: (i, 0))
     return pl.pallas_call(
-        functools.partial(swap_body, peers=peers),
-        name=name,
-        out_shape=jax.ShapeDtypeStruct(x.shape, x.dtype),
-        in_specs=[hbm],
-        out_specs=hbm,
-        scratch_shapes=[pltpu.VMEM(x.shape[1:], x.dtype), pltpu.SemaphoreType.DMA((peers - 1,)),
-                        pltpu.SemaphoreType.DMA((peers - 1,)), pltpu.SemaphoreType.DMA],
-        compiler_params=pltpu.CompilerParams(collective_id=collective_id, has_side_effects=True, vmem_limit_bytes=48 << 20),
-    )(x)
+        copy_body, name="keep_copy", out_shape=jax.ShapeDtypeStruct(x.shape, x.dtype), grid=(steps,), in_specs=[spec], out_specs=spec,
+        cost_estimate=pl.CostEstimate(flops=10**10, bytes_accessed=8 * x.size, transcendentals=0))(x)
 
 
 def norm_forward(x_blk, ln_gain, ln_bias):
@@ -224,39 +290,40 @@
         blk = 2 * tok
         rank = lax.axis_index("sp")
         x_f32, x_hat, inv_std, x_norm = norm_forward(x_blk, ln_gain, ln_bias)
+        xf = [lax.all_gather(x_norm[0], "sp", axis=0, tiled=True)]
         marks = exchange(jnp.concatenate([pos_blk, keep_blk, jnp.zeros((8 - 2 * batch, tok), jnp.int32)]), peers, 0, "marks")
+        do_loc = [lax.dot_general(w_out, dy_blk[b], NT, preferred_element_type=F32).astype(BF16).reshape(heads, dim, tok) for b in range(batch)]
+        do_t = swap(do_loc, 1, "swap_do")
+        for b in range(1, batch):
+            xn, _ = lax.optimization_barrier((x_norm[b], xf[-1]))
+            xf.append(lax.all_gather(xn, "sp", axis=0, tiled=True))
         w_t = jnp.transpose(w_qkv, (1, 2, 3, 0))
         w_head = lax.dynamic_index_in_dim(w_t, rank, 0, keepdims=False).reshape(3 * dim, hidden)
         b_head = lax.dynamic_index_in_dim(b_qkv, rank, 0, keepdims=False).reshape(3 * dim, 1)
-        wo_head = lax.dynamic_slice_in_dim(w_out, rank * dim, dim, 0)
         slope = jnp.exp2(-8.0 * (rank + 1).astype(F32) / heads)
         slope2 = (slope * LOG2E).reshape(1)
         gw = jnp.zeros((3 * dim, hidden), F32)
-        go = jnp.zeros((dim, hidden), F32)
         gb = jnp.zeros((3 * dim,), F32)
-        got = []
+        att, got = [], []
         for b in range(batch):
-            xn, dy = x_norm[b], dy_blk[b]
-            if b:
-                xn, dy, _, _ = lax.optimization_barrier((xn, dy, xf, df))
-            xf = lax.all_gather(xn, "sp", axis=0, tiled=True)
-            df = lax.all_gather(dy, "sp", axis=0, tiled=True)
             pos = marks[:, b].reshape(seq).astype(F32)
             keep = marks[:, batch + b].reshape(seq)
             posk = jnp.broadcast_to(jnp.where(keep > 0, pos, MASKED)[:, None], (seq, 128))
             pref = jnp.broadcast_to(pos[::blk][:, None], (seq // blk, 128))
-            qkvt = (lax.dot_general(w_head, xf, NT, preferred_element_type=F32) + b_head).astype(BF16)
-            dot_ = lax.dot_general(wo_head, df, NT, preferred_element_type=F32).astype(BF16)
+            qkvt = (lax.dot_general(w_head, xf[b], NT, preferred_element_type=F32) + b_head).astype(BF16)
             if b:
-                slope2, _ = lax.optimization_barrier((slope2, got[-1]))
-            att = attention(slope2, qkvt, dot_, posk, pref, blk=blk, tok=tok)
-            got.append(swap(att, peers, 2 + b, "swap"))
-            xf3, df3 = xf.reshape(peers, tok, hidden), df.reshape(peers, tok, hidden)
-            gw += jnp.einsum("pcdt,pth->cdh", att[:, 1:], xf3, preferred_element_type=F32).reshape(3 * dim, hidden)
-            go += jnp.einsum("pdt,pth->dh", att[:, 0], df3, preferred_element_type=F32)
-            gb += jnp.sum(att[:, 1:].astype(F32), axis=(0, 3)).reshape(3 * dim)
+                slope2, gw = lax.optimization_barrier((slope2, gw))
+                cur, prev = attention(slope2, qkvt, do_t[b], posk, pref, blk=blk, tok=tok, old=att[-1], collective_id=2 + b)
+                got.append(prev)
+            else:
+                cur = attention(slope2, qkvt, do_t[b], posk, pref, blk=blk, tok=tok)
+            att.append(cur)
+            gw += jnp.einsum("pcdt,pth->cdh", cur[:, 1:], xf[b].reshape(peers, tok, hidden), preferred_element_type=F32).reshape(3 * dim, hidden)
+            gb += jnp.sum(cur[:, 1:].astype(F32), axis=(0, 3)).reshape(3 * dim)
         gw_all = lax.all_gather(gw, "sp", axis=0, tiled=True)
-        go_all = lax.all_gather(go, "sp", axis=0, tiled=True)
+        last, _ = lax.optimization_barrier((att[-1], gw))
+        got += swap([last], 2, "swap_last")
+        go = sum(lax.dot_general(got[b][:, 0].reshape(hidden, tok), dy_blk[b], (((1,), (0,)), ((), ())), preferred_element_type=F32) for b in range(batch))
         y, gx, gg, gbias = [], [], 0.0, 0.0
         for b in range(batch):
             o_t = got[b][:, 0].reshape(hidden, tok)
@@ -271,9 +338,14 @@
             gx.append((dy_blk[b].astype(F32) + inv_std[b] * (d_hat - d_mean - x_hat[b] * d_proj)).astype(BF16))
         g_out = jnp.sum(dy_blk.astype(F32), axis=(0, 1))
         rows = jnp.stack([gg, gbias, g_out, jnp.pad(gb, (0, hidden - 3 * dim))] + [jnp.zeros((hidden,), F32)] * 4)
-        sums = exchange(rows, peers, 1, "sums")
+        sums = exchange(rows, peers, 4, "sums")
         total = jnp.sum(sums[:, :3], axis=0)
         gb_all = sums[:, 3, :3 * dim].reshape(heads, 3, dim)
+        go, gw_all, _, _ = lax.optimization_barrier((go, gw_all, y, gx))
+        part = lax.psum_scatter(go, "sp", scatter_dimension=0, tiled=True)
+        gw_all = keep_copy(gw_all, heads)
+        part, gw_all = lax.optimization_barrier((part, gw_all))
+        go_all = lax.all_gather(part, "sp", axis=0, tiled=True)
         gw_out = jnp.transpose(gw_all.reshape(heads, 3, dim, hidden), (3, 0, 1, 2))
         return jnp.stack(y), jnp.stack(gx), gw_out, gb_all, go_all, total[2], total[0], total[1]
 

time: 775 us -> 674 us (0.87)
  waiting for transfers between devices: 244 us -> 174 us
  matrix products: 91.8 us -> 78.8 us
  local copies, waits for them, and re-layouts: 36 us -> 23 us
    all_gather x5 -> x3, waiting for transfers between devices: 142 us -> 60.6 us  [the longest x1 34.3 us: block_fn(): go_all = lax.all_gather(part, 'sp', axis=0, tiled=True)]
    reduce_scatter x0 -> x1, waiting for transfers between devices: none -> 43.6 us  [block_fn(): part = lax.psum_scatter(go, 'sp', scatter_dimension=0, tiled=True)]
    all_gather x1, waiting for transfers between devices: 100 us -> 68.8 us  [block_fn(): gw_all = lax.all_gather(gw, 'sp', axis=0, tiled=True)]
    dot_general x8, matrix products: 67.6 us -> 54.3 us  [the longest x2 26.1 us: block_fn(): lax.dot_general(w_head, xf[b], NT, preferred_element_type=F32) + b_head]
    unnamed x59 -> x54, local copies, waits for them, and re-layouts: 28.7 us -> 16.2 us
    pallas_call x4 -> x5, Pallas kernels: 324 us -> 320 us  [the longest x2 164 us: swap(): pl.pallas_call(functools.partial(swap_body, peers=peers, n=len(xs)), name...]
  transfers between devices with their start and end apart: 6 -> 5, of which waited for: 4 -> 4; matrix products, arithmetic and copies ran while one was open for 10% -> 11% of each run, Pallas kernels for 41% -> 44%
where the time goes in v2:
time: 674 us
  Pallas kernels  368 us (55%)
  waiting for transfers between devices  174 us (26%)
  matrix products  78.8 us (12%)
  local copies, waits for them, and re-layouts  23 us (3%)
  other arithmetic  15.4 us (2%)
  between operations  14.4 us (2%)
    pallas_call x2, Pallas kernels, swap(): pl.pallas_call(functools.partial(swap_body, peers=peers, n=len(xs)), name...  164 us
    pallas_call x2, Pallas kernels, attention(): pl.pallas_call(functools.partial(attn_body, blk=blk, tok=tok, peers=peers...  132 us
    all_gather x1, waiting for transfers between devices, block_fn(): gw_all = lax.all_gather(gw, 'sp', axis=0, tiled=True)  68.8 us
    pallas_call x2, Pallas kernels, exchange(): pl.pallas_call(functools.partial(exchange_body, peers=peers), name=name,...  47.9 us
    reduce_scatter x1, waiting for transfers between devices, block_fn(): part = lax.psum_scatter(go, 'sp', scatter_dimension=0, tiled=True)  43.6 us
    all_gather x1, waiting for transfers between devices, block_fn(): go_all = lax.all_gather(part, 'sp', axis=0, tiled=True)  34.3 us
    all_gather x1, waiting for transfers between devices, block_fn(): xf = [lax.all_gather(x_norm[0], 'sp', axis=0, tiled=True)]  26.3 us
    dot_general x2, matrix products, block_fn(): lax.dot_general(w_head, xf[b], NT, preferred_element_type=F32) + b_head  26.1 us
  transfers between devices with their start and end apart: 5, of which 4 were waited for; matrix products, arithmetic and copies ran while one was open for 11% of the time, Pallas kernels for 44%

profile of v2, /device:TPU:21, one launch (start us, length us, event | category | flops | bytes accessed | tf_op | source)
XLA Modules:
  0.0 673.8 jit_solution(13561741438979780082)
XLA Ops:
  7.2 0.1 all-gather.12.cloned.1.call-start
  7.3 1.8 convert_reduce_fusion.3
  9.1 0.5 multiply_reduce_fusion
  9.7 2.3 subtract_multiply_fusion
  12.0 1.2 slice_bitcast_fusion.4
  13.3 0.1 all-gather.6.cloned.1.call-start
  13.4 0.7 all-gather.6.cloned.1.call-update
  14.2 0.1 all-gather.8.cloned.1.call-start
  14.3 0.1 pad.11.clone
  14.4 0.1 add.123
  14.5 0.1 add_add_fusion.x_ref
  14.5 14.7 %marks.1 = s32[16,8,256]{2,1,0:T(8,128)S(1)} custom-call(s32[8,256]{1,0:T(8,128)S(1)} %add_add_fusion.x_ref), custom_call_target="tpu_custom_call" | custom-call | tf_op jit(solution)/shard_map/marks/pallas_call | solution.py:252
  29.3 0.1 compare_reduce_fusion
  29.5 0.1 slice.101
  29.6 0.1 slice.106
  29.7 2.3 constant_dynamic-slice_fusion
  32.0 3.8 convolution_convert_fusion
  35.9 1.4 convolution_convert_fusion.1
  37.3 58.3 %swap_do.1 = (bf16[16,96,256]{2,1,0:T(8,128)(2,1)S(1)}, bf16[16,96,256]{2,1,0:T(8,128)(2,1)S(1)}) custom-call(bf16[16,96,256]{2,1,0:T(8,128)(2,1)S(1)} %bitcast.111, bf16[16,96,256]{2,1,0:T(8,128)(2,1)S(1)} %bitcast.110), custom_call_target="tpu_custom_call" | custom-call | flops 18874368000 | bytes 3145728 | tf_op jit(solution)/shard_map/swap_do/pallas_call | solution.py:226
  95.6 0.9 copy-done.5
  96.5 0.9 copy-done.7
  97.4 26.3 %all-gather.12.cloned.1.call-done = bf16[1,4096,1536]{2,1,0:T(8,128)(2,1)} async-done(((bf16[1,256,1536]{2,1,0:T(8,128)(2,1)}), bf16[1,4096,1536]{2,1,0:T(8,128)(2,1)}) %all-gather.12.cloned.1.call-update) | async-done | bytes 12582928 | tf_op jit(solution)/shard_map/all_gather | solution.py:293
  123.7 13.0 %fusion.4.qkvt_ref = bf16[288,4096]{1,0:T(8,128)(2,1)S(1)} fusion(bf16[288,1536]{1,0:T(8,128)(2,1)S(1)} %bitcast.121, f32[288]{0:T(512)S(1)} %add.123, bf16[1,4096,1536]{2,1,0:T(8,128)(2,1)} %all-gather.12.cloned.1.call-done), kind=kOutput, calls=%fused_computation.7 | convolution fusion | flops 3626237952 | bytes 15828096 | tf_op jit(solution)/shard_map/dot_general | solution.py:313
  136.8 0.1 broadcast_in_dim.18.pref_ref
  136.8 0.6 broadcast_in_dim.17.posk_ref
  137.4 57.7 %attention.2.refs_0_ = bf16[16,4,96,256]{3,2,1,0:T(8,128)(2,1)S(1)} custom-call(f32[1]{0:T(128)} %bitcast.1.slope_ref, bf16[288,4096]{1,0:T(8,128)(2,1)S(1)} %fusion.4.qkvt_ref, bf16[16,96,256]{2,1,0:T(8,128)(2,1)S(1)} %copy-done.8, f32[4096,128]{1,0:T(8,128)S(1)} %broadcast_in_dim.17.posk_ref, f32[8,128]{1,0:T(8,128)S(1)} %broadcast_in_dim.18.pref_ref), custom_call_target="tpu_custom_call" | custom-call | flops 28991029248 | bytes 12582912 | tf_op jit(solution)/shard_map/attention/pallas_call | solution.py:158
  195.2 0.2 slice.124
  195.4 1.5 copy-done.2
  196.9 8.0 %convolution_bitcast_fusion.1 = f32[288,1536]{1,0:T(8,128)} fusion(bf16[288,16,256]{2,0,1:T(8,128)(2,1)S(1)} %bitcast.120, bf16[16,256,1536]{2,1,0:T(8,128)(2,1)} %bitcast.132), kind=kOutput, calls=%fused_computation.16 | convolution fusion | flops 3623878656 | bytes 16711680 | tf_op jit(solution)/shard_map/pcdt,pth->cdh/dot_general | solution.py:321
  204.9 13.0 %fusion.5.qkvt_ref = bf16[288,4096]{1,0:T(8,128)(2,1)S(1)} fusion(bf16[288,1536]{1,0:T(8,128)(2,1)S(1)} %bitcast.122, bf16[4096,1536]{1,0:T(8,128)(2,1)} %all-gather.6.cloned.1.call-done, f32[288]{0:T(512)S(1)} %add.123), kind=kOutput, calls=%fused_computation.8 | convolution fusion | flops 3626237952 | bytes 15828096 | tf_op jit(solution)/shard_map/dot_general | solution.py:313
  218.0 0.1 broadcast_in_dim.20.pref_ref
  218.0 0.6 broadcast_in_dim.19.posk_ref
  218.6 74.1 %attention.3 = (bf16[16,4,96,256]{3,2,1,0:T(8,128)(2,1)S(1)}, bf16[16,4,96,256]{3,2,1,0:T(8,128)(2,1)}) custom-call(f32[1]{0:T(128)} %bitcast.1.slope_ref, bf16[288,4096]{1,0:T(8,128)(2,1)S(1)} %fusion.5.qkvt_ref, bf16[16,96,256]{2,1,0:T(8,128)(2,1)S(1)} %copy-done.6, f32[4096,128]{1,0:T(8,128)S(1)} %broadcast_in_dim.19.posk_ref, ...), custom_call_target="tpu_custom_call" | custom-call | flops 28991029248 | bytes 12582912 | tf_op jit(solution)/shard_map/attention/pallas_call | solution.py:158
  292.8 0.2 slice.109
  293.0 1.4 copy-done.4
  294.4 1.0 copy-done.23
  295.4 8.2 %fusion.6 = f32[288,1536]{1,0:T(8,128)} fusion(f32[288,1536]{1,0:T(8,128)S(1)} %copy-done.23, bf16[288,16,256]{2,0,1:T(8,128)(2,1)S(1)} %bitcast.119, bf16[16,256,1536]{2,1,0:T(8,128)(2,1)} %bitcast.131), kind=kOutput, calls=%fused_computation.17 | convolution fusion | flops 3624321024 | bytes 18481152 | tf_op jit(solution)/shard_map/pcdt,pth->cdh/dot_general | solution.py:321
  303.7 0.1 reduce-scatter.2.cloned.1.call-start
  303.8 0.4 convert_element_type.70
  304.2 1.5 copy-done.13
  305.7 105.5 %swap_last.1 = bf16[16,4,96,256]{3,2,1,0:T(8,128)(2,1)S(1)} custom-call(bf16[16,4,96,256]{3,2,1,0:T(8,128)(2,1)} %copy-done.4), custom_call_target="tpu_custom_call" | custom-call | flops 37748736000 | bytes 6291456 | tf_op jit(solution)/shard_map/swap_last/pallas_call | solution.py:226
  411.3 7.3 %fusion.10 = f32[256,1536]{1,0:T(8,128)S(1)} fusion(bf16[16,4,96,256]{3,2,1,0:T(8,128)(2,1)S(1)} %swap_last.1, bf16[1536,16,3,96]{0,3,2,1:T(8,128)(2,1)} %param.15), kind=kOutput, calls=%fused_computation.19 | convolution fusion | flops 3623878656 | bytes 18874368 | tf_op jit(solution)/shard_map/dot_general | solution.py:332
  418.6 8.0 %multiply_reduce_fusion.2 = (f32[1536]{0:T(1024)S(1)}, f32[256]{0:T(256)S(1)}, f32[256]{0:T(256)S(1)}, f32[1536]{0:T(1024)S(1)}, f32[256]{0:T(256)S(1)}, /*index...) fusion(f32[2,256,1536]{2,1,0:T(8,128)S(1)} %copy-done.10, f32[1536]{0:T(1024)S(1)} %copy-done.18, ...), kind=kOutput, calls=%fused_computation.36 | convolution fusion | flops 3629376512 | bytes 23627776 | tf_op jit(solution)/shard_map/dot_general | solution.py:332
  426.7 1.4 fusion.19
  428.1 4.6 fusion.16
  432.7 4.6 fusion.15
  437.4 2.0 add_convert_fusion.2
  439.4 5.3 convolution_add_fusion
  444.7 68.8 %all-gather.8.cloned.1.call-done.x_ref = f32[4608,1536]{1,0:T(8,128)} async-done(((f32[288,1536]{1,0:T(8,128)}), f32[4608,1536]{1,0:T(8,128)}) %all-gather.8.cloned.1.call-update) | async-done | bytes 28311568 | tf_op jit(solution)/shard_map/all_gather | solution.py:323
  513.5 0.1 all-gather.10.cloned.1.call-start
  513.6 24.5 %keep_copy.1 = f32[4608,1536]{1,0:T(8,128)} custom-call(f32[4608,1536]{1,0:T(8,128)} %all-gather.8.cloned.1.call-done.x_ref), custom_call_target="tpu_custom_call" | custom-call | flops 10000000000 | bytes 56623104 | tf_op jit(solution)/shard_map/keep_copy/pallas_call | solution.py:269
  538.1 43.6 %reduce-scatter.2.cloned.1.call-done = f32[96,1536]{1,0:T(8,128)} async-done(((f32[1536,1536]{1,0:T(8,128)}), f32[96,1536]{1,0:T(8,128)}) %reduce-scatter.2.cloned.1.call-update) | async-done | bytes 589840 | tf_op jit(solution)/shard_map/reduce_scatter | solution.py:345
  581.8 1.7 convert_reduce_fusion.2
  583.4 2.4 convert_reduce_fusion
  585.8 0.1 add.141
  586.1 33.2 %sums.1 = f32[16,8,1536]{2,1,0:T(8,128)S(1)} custom-call(f32[8,1536]{1,0:T(8,128)S(1)} %stack.41.x_ref), custom_call_target="tpu_custom_call" | custom-call | tf_op jit(solution)/shard_map/sums/pallas_call | solution.py:252
  619.3 0.1 slice_reduce_fusion.1
  619.3 0.1 reshape_squeeze.8
  619.4 0.6 copy.19
  620.1 0.6 slice_reduce_fusion.2
  620.7 2.7 pad_maximum_fusion.1
  623.4 1.3 pad_maximum_fusion
  624.7 34.3 %all-gather.10.cloned.1.call-done = f32[1536,1536]{1,0:T(8,128)} async-done(((f32[96,1536]{1,0:T(8,128)}), f32[1536,1536]{1,0:T(8,128)}) %all-gather.10.cloned.1.call-update) | async-done | bytes 9437200 | tf_op jit(solution)/shard_map/all_gather | solution.py:348
  659.0 8.3 %copy.23 = f32[1536,1536]{1,0:T(8,128)} copy(f32[1536,1536]{1,0:T(8,128)} %all-gather.10.cloned.1.call-done) | data formatting | bytes 18874368
  (77 shorter events, 0.7 us)
Async XLA Ops:
  7.2 7.2 %copy-start = (f32[16,3,96]{2,0,1:T(8,128)S(1)}, f32[16,3,96]{2,0,1:T(8,128)}, u32[]{:S(2)}) copy-start(f32[16,3,96]{2,0,1:T(8,128)} %param.16) | copy-start | bytes 55300
  7.2 1.9 copy-start.9
  7.2 2.5 copy-start.17
  7.2 2.5 copy-start.19
  7.2 116.5 %all-gather.12.cloned.1.call-start = ((), (), s32[]{:S(2)}) async-start(), calls=%async_computation.5 | async-start | bytes 13369344 | tf_op jit(solution)/shard_map/all_gather | solution.py:293
  12.0 2.4 copy-start.20
  12.0 2.4 copy-start.21
  13.3 18.7 %copy-start.11 = (bf16[2,256,1536]{2,1,0:T(8,128)(2,1)S(1)}, bf16[2,256,1536]{2,1,0:T(8,128)(2,1)}, u32[]{:S(2)}) copy-start(bf16[2,256,1536]{2,1,0:T(8,128)(2,1)} %param.19) | copy-start | bytes 4718596
  13.3 191.6 %all-gather.6.cloned.1.call-start = ((), (), s32[]{:S(2)}) async-start(), calls=%async_computation.1 | async-start | bytes 13369344 | tf_op jit(solution)/shard_map/all_gather | solution.py:299
  14.2 499.3 %all-gather.8.cloned.1.call-start = ((), (), s32[]{:S(2)}) async-start(), calls=%async_computation.2 | async-start | bytes 30081024 | tf_op jit(solution)/shard_map/all_gather | solution.py:323
  29.7 6.1 slice-start
  32.0 3.8 slice-start.1
  37.3 86.4 %copy-start.14 = (bf16[1536,1,3,96]{0,3,2,1:T(8,128)(2,1)S(1)}, bf16[1536,1,3,96]{0,3,2,1:T(8,128)(2,1)}, u32[]{:S(2)}) copy-start(bf16[1536,1,3,96]{0,3,2,1:T(8,128)(2,1)} %constant_dynamic-slice_fusion) | copy-start | bytes 2654212
  95.6 0.9 copy-start.5
  96.5 0.9 copy-start.7
  123.7 13.7 %copy-start.8 = (bf16[16,96,256]{2,1,0:T(8,128)(2,1)S(1)}, bf16[16,96,256]{2,1,0:T(8,128)(2,1)}, u32[]{:S(2)}) copy-start(bf16[16,96,256]{2,1,0:T(8,128)(2,1)} %copy-done.7) | copy-start | bytes 2359300
  195.2 1.8 copy-start.2
  204.9 13.7 %copy-start.6 = (bf16[16,96,256]{2,1,0:T(8,128)(2,1)S(1)}, bf16[16,96,256]{2,1,0:T(8,128)(2,1)}, u32[]{:S(2)}) copy-start(bf16[16,96,256]{2,1,0:T(8,128)(2,1)} %copy-done.5) | copy-start | bytes 2359300
  292.8 1.6 copy-start.4
  292.8 2.6 copy-start.23
  303.7 278.0 %reduce-scatter.2.cloned.1.call-start = ((), (), s32[]{:S(2)}) async-start(), calls=%async_computation.3 | async-start | bytes 10027008 | tf_op jit(solution)/shard_map/reduce_scatter | solution.py:345
  303.8 1.9 copy-start.13
  411.3 7.3 %copy-start.10 = (f32[2,256,1536]{2,1,0:T(8,128)S(1)}, f32[2,256,1536]{2,1,0:T(8,128)}, u32[]{:S(2)}) copy-start(f32[2,256,1536]{2,1,0:T(8,128)} %get-tuple-element.65) | copy-start | bytes 9437188
  411.3 7.3 %copy-start.18 = (f32[1536]{0:T(1024)S(1)}, f32[1536]{0:T(1024)}, u32[]{:S(2)}) copy-start(f32[1536]{0:T(1024)} %param.13) | copy-start | bytes 18436
  418.6 8.1 %copy-start.12 = (bf16[2,256,1536]{2,1,0:T(8,128)(2,1)S(1)}, bf16[2,256,1536]{2,1,0:T(8,128)(2,1)}, u32[]{:S(2)}) copy-start(bf16[2,256,1536]{2,1,0:T(8,128)(2,1)} %param.19) | copy-start | bytes 4718596
  426.7 1.4 copy-start.22
  513.5 145.4 %all-gather.10.cloned.1.call-start = ((), (), s32[]{:S(2)}) async-start(), calls=%async_computation.4 | async-start | bytes 10027008 | tf_op jit(solution)/shard_map/all_gather | solution.py:348
  513.6 69.8 %copy-start.3 = (bf16[16,4,96,256]{3,2,1,0:T(8,128)(2,1)S(1)}, bf16[16,4,96,256]{3,2,1,0:T(8,128)(2,1)}, u32[]{:S(2)}) copy-start(bf16[16,4,96,256]{3,2,1,0:T(8,128)(2,1)} %copy-done.2) | copy-start | bytes 9437188
  586.0 37.4 %copy-start.15 = (bf16[256,1536]{1,0:T(8,128)(2,1)S(1)}, bf16[256,1536]{1,0:T(8,128)(2,1)}, u32[]{:S(2)}) copy-start(bf16[256,1536]{1,0:T(8,128)(2,1)} %fusion.16) | copy-start | bytes 2359300
  586.0 37.4 %copy-start.16 = (bf16[256,1536]{1,0:T(8,128)(2,1)S(1)}, bf16[256,1536]{1,0:T(8,128)(2,1)}, u32[]{:S(2)}) copy-start(bf16[256,1536]{1,0:T(8,128)(2,1)} %fusion.15) | copy-start | bytes 2359300
  659.0 8.3 %copy-start.1 = (f32[16,3,96]{2,0,1:T(8,128)S(1)}, f32[16,3,96]{2,0,1:T(8,128)}, u32[]{:S(2)}) copy-start(f32[16,3,96]{2,0,1:T(8,128)} %param.16) | copy-start | bytes 55300
Sparse Core Ops, SparseCore 0:
  13.5 110.2 all-gather.11
  125.9 71.6 all-gather.5
  303.8 209.5 all-gather.7
  516.3 65.3 reduce-scatter.1
  583.2 75.7 all-gather.9

commit v3 on v2

--- a/solution.py
+++ b/solution.py
@@ -16,11 +16,11 @@
 
 def attn_body(slope_ref, qkvt_ref, dot_ref, posk_ref, pref_ref, *refs, blk, tok, peers):
     if peers:
-        old_ref, out_ref, got_ref = refs[:3]
-        own, send_sem, recv_sem, own_sem = refs[-4:]
-        refs = refs[3:-4]
+        old, (o_ref, dqkv_ref), got = refs[:2], refs[2:4], refs[4:6]
+        swaps = [(old[n], got[n]) + refs[4 * n - 8:(4 * n - 4) or None] for n in range(2)]
+        refs = refs[6:-8]
     else:
-        out_ref, refs = refs[0], refs[1:]
+        (o_ref, dqkv_ref), refs = refs[:2], refs[2:]
     k_tok, v_tok, s_buf, q_pad, do_pad, o_acc, dq_acc, dk_acc, dv_acc = refs
     dim = dot_ref.shape[1]
     seq = dot_ref.shape[0] * tok
@@ -34,7 +34,8 @@
         @pl.when(i == 0)
         def _():
             meet(peers)
-            swap_start(old_ref, got_ref, own, send_sem, recv_sem, own_sem, peers)
+            for one in swaps:
+                swap_start(*one, peers)
 
     @pl.when(i == 0)
     def _():
@@ -115,19 +116,20 @@
     lax.fori_loop(0, i + 1, grads, 0)
     dq_lo = (dq_acc[...] * scale).astype(BF16)
     for t in range(nq):
-        out_ref[i * nq + t, 0] = o_lo[:, t * tok:(t + 1) * tok]
-        out_ref[i * nq + t, 1] = dq_lo[:, t * tok:(t + 1) * tok]
+        o_ref[i * nq + t] = o_lo[:, t * tok:(t + 1) * tok]
+        dqkv_ref[i * nq + t, 0] = dq_lo[:, t * tok:(t + 1) * tok]
 
     @pl.when(i == pl.num_programs(0) - 1)
     def _():
         @pl.loop(0, seq // tok)
         def _(t):
             cols = pl.ds(pl.multiple_of(t * tok, tok), tok)
-            out_ref[t, 2] = (dk_acc[:, cols] * scale).astype(BF16)
-            out_ref[t, 3] = dv_acc[:, cols].astype(BF16)
+            dqkv_ref[t, 1] = (dk_acc[:, cols] * scale).astype(BF16)
+            dqkv_ref[t, 2] = dv_acc[:, cols].astype(BF16)
 
         if peers:
-            swap_wait(old_ref, got_ref, own, send_sem, recv_sem, own_sem, peers)
+            for one in swaps:
+                swap_wait(*one, peers)
 
 
 def attention(slope2, qkvt, dot_, posk, pref, *, blk, tok, old=None, collective_id=None):
@@ -136,11 +138,11 @@
     wide = 128 * pl.cdiv(dim, 128)
     hbm = pl.BlockSpec(memory_space=pltpu.HBM)
     full = lambda a: pl.BlockSpec(a.shape, lambda i: (0,) * a.ndim, pipeline_mode=pl.Buffered(1))
-    out = jax.ShapeDtypeStruct((blocks, 4, dim, tok), BF16)
+    outs = [jax.ShapeDtypeStruct((blocks, dim, tok), BF16), jax.ShapeDtypeStruct((blocks, 3, dim, tok), BF16)]
     pairs = (seq // blk) * (seq // blk + 1) // 2
     args = (slope2, qkvt, dot_, posk, pref)
     in_specs = [pl.BlockSpec(memory_space=pltpu.SMEM)] + [full(a) for a in (qkvt, dot_, posk, pref)]
-    out_shape, out_specs = [out], [pl.BlockSpec(out.shape, lambda i: (0, 0, 0, 0), pipeline_mode=pl.Buffered(1))]
+    out_shape, out_specs = list(outs), [full(a) for a in outs]
     scratch = [
         pltpu.VMEM((seq, wide), BF16), pltpu.VMEM((seq, wide), BF16),
         pltpu.VMEM((seq, blk), F32),
@@ -149,12 +151,12 @@
         pltpu.VMEM((dim, seq), F32), pltpu.VMEM((dim, seq), F32)]
     peers = 0
     if old is not None:
-        peers = old.shape[0]
-        args += (old,)
-        in_specs.append(hbm)
-        out_shape.append(jax.ShapeDtypeStruct(old.shape, old.dtype))
-        out_specs.append(hbm)
-        scratch += swap_scratch(old)
+        peers = blocks
+        args += tuple(old)
+        in_specs += [hbm] * 2
+        out_shape += outs
+        out_specs += [hbm] * 2
+        scratch += swap_scratch(old[0]) + swap_scratch(old[1])
     res = pl.pallas_call(
         functools.partial(attn_body, blk=blk, tok=tok, peers=peers),
         name="attention",
@@ -167,7 +169,7 @@
         compiler_params=pltpu.CompilerParams(dimension_semantics=("arbitrary",), vmem_limit_bytes=44 << 20,
                                              collective_id=collective_id, has_side_effects=old is not None),
     )(*args)
-    return res if old is not None else res[0]
+    return res[:2], res[2:]
 
 
 def peer_at(d, peers):
@@ -209,6 +211,125 @@
     peers = x.shape[0]
     return [pltpu.VMEM(x.shape[1:], x.dtype), pltpu.SemaphoreType.DMA((peers - 1,)), pltpu.SemaphoreType.DMA((peers - 1,)),
             pltpu.SemaphoreType.DMA]
+
+
+def tail_body(o_ref, dqkv_ref, o_old, dy_ref, o_new, dqkv_new, full, mine, other, pair, landed, own_o, own_d,
+              os_sem, or_sem, oo_sem, ds_sem, dr_sem, do_sem, ps_sem, pr_sem, rs_sem, rr_sem, as_sem, ar_sem, fs_sem, fr_sem, *, peers):
+    ring = peers // 2
+    me = lax.axis_index("sp")
+    z, c = me // 2, me % 2
+    half = full.shape[-1] // 2
+    cols = (pl.ds(0, half), pl.ds(half, half))
+    at = lambda zz, cc: {"sp": 2 * zz + cc}
+    turn = lambda k: lax.rem(z + k + 2 * ring, ring)
+    step = (1, -1)
+    remote = functools.partial(pltpu.make_async_remote_copy, device_id_type=pl.DeviceIdType.MESH)
+    meet(peers)
+    swap_start(o_ref, o_new, own_o, os_sem, or_sem, oo_sem, peers)
+    swap_start(dqkv_ref, dqkv_new, own_d, ds_sem, dr_sem, do_sem, peers)
+    swap_wait(o_ref, o_new, own_o, os_sem, or_sem, oo_sem, peers)
+
+    def product(out, side):
+        @pl.loop(0, ring)
+        def _(k):
+            h = 2 * k + side
+            out[k] = (jnp.dot(o_old[h], dy_ref[0], preferred_element_type=F32)
+                      + jnp.dot(o_new[h], dy_ref[1], preferred_element_type=F32))
+
+    product(other, 1 - c)
+    to_pair = remote(src_ref=other, dst_ref=pair, send_sem=ps_sem, recv_sem=pr_sem, device_id=at(z, 1 - c))
+    product(mine, c)
+    to_pair.start()
+    to_pair.wait()
+
+    @pl.loop(0, ring)
+    def _(k):
+        mine[k] = mine[k] + pair[k]
+
+    def reduce_copy(w, t):
+        return remote(src_ref=mine.at[turn(-step[w] * (1 + t)), :, cols[w]], dst_ref=landed.at[w, t],
+                      send_sem=rs_sem.at[w, t], recv_sem=rr_sem.at[w, t], device_id=at(turn(step[w]), c))
+
+    def add(w, t, k):
+        reduce_copy(w, t).wait_recv()
+        mine[k, :, cols[w]] = mine[k, :, cols[w]] + landed[w, t]
+
+    for w in range(2):
+        reduce_copy(w, 0).start()
+
+    @pl.loop(1, ring - 1)
+    def _(t):
+        for w in range(2):
+            add(w, t - 1, turn(-step[w] * (1 + t)))
+            reduce_copy(w, t).start()
+
+    for w in range(2):
+        add(w, ring - 2, z)
+
+    def gather_copy(w, t):
+        k = turn(-step[w] * t)
+        return remote(src_ref=full.at[k, c, :, cols[w]], dst_ref=full.at[k, c, :, cols[w]],
+                      send_sem=as_sem.at[w, t], recv_sem=ar_sem.at[w, t], device_id=at(turn(step[w]), c))
+
+    def over_copy(w, t):
+        k = turn(-step[w] * t)
+        return remote(src_ref=full.at[k, c, :, cols[w]], dst_ref=full.at[k, c, :, cols[w]],
+                      send_sem=fs_sem.at[w, t], recv_sem=fr_sem.at[w, t], device_id=at(z, 1 - c))
+
+    full[z, c] = mine[z]
+    for w in range(2):
+        gather_copy(w, 0).start()
+    for w in range(2):
+        over_copy(w, 0).start()
+
+    @pl.loop(1, ring)
+    def _(t):
+        for w in range(2):
+            gather_copy(w, t - 1).wait_recv()
+
+            @pl.when(t < ring - 1)
+            def _():
+                gather_copy(w, t).start()
+
+            over_copy(w, t).start()
+
+    swap_wait(dqkv_ref, dqkv_new, own_d, ds_sem, dr_sem, do_sem, peers)
+
+    @pl.loop(0, ring - 1)
+    def _(t):
+        for w in range(2):
+            reduce_copy(w, t).wait_send()
+            gather_copy(w, t).wait_send()
+
+    @pl.loop(0, ring)
+    def _(t):
+        for w in range(2):
+            over_copy(w, t).wait_send()
+            remote(src_ref=full.at[turn(-step[w] * t), 1 - c, :, cols[w]], dst_ref=full.at[turn(-step[w] * t), 1 - c, :, cols[w]],
+                   send_sem=fs_sem.at[w, t], recv_sem=fr_sem.at[w, t], device_id=at(z, 1 - c)).wait_recv()
+
+
+def tail(o, dqkv, o_old, dy, collective_id):
+    peers, dim, tok = o.shape
+    ring = peers // 2
+    hidden = dy.shape[-1]
+    hbm, vmem = pl.BlockSpec(memory_space=pltpu.HBM), pl.BlockSpec(memory_space=pltpu.VMEM)
+    dma = pltpu.SemaphoreType.DMA
+    rows = lambda *lead: pltpu.VMEM(lead + (dim, hidden), F32)
+    return pl.pallas_call(
+        functools.partial(tail_body, peers=peers),
+        name="tail",
+        out_shape=[jax.ShapeDtypeStruct(o.shape, BF16), jax.ShapeDtypeStruct(dqkv.shape, BF16),
+                   jax.ShapeDtypeStruct((ring, 2, dim, hidden), F32)],
+        in_specs=[hbm, hbm, vmem, vmem],
+        out_specs=[vmem, hbm, vmem],
+        scratch_shapes=[rows(ring), rows(ring), rows(ring), pltpu.VMEM((2, ring - 1, dim, hidden // 2), F32),
+                        pltpu.VMEM(o.shape[1:], BF16), pltpu.VMEM(dqkv.shape[1:], BF16),
+                        dma((peers - 1,)), dma((peers - 1,)), dma, dma((peers - 1,)), dma((peers - 1,)), dma, dma, dma,
+                        dma((2, ring - 1)), dma((2, ring - 1)), dma((2, ring - 1)), dma((2, ring - 1)), dma((2, ring)), dma((2, ring))],
+        cost_estimate=pl.CostEstimate(flops=10**11, bytes_accessed=64 << 20, transcendentals=0),
+        compiler_params=pltpu.CompilerParams(collective_id=collective_id, has_side_effects=True, vmem_limit_bytes=48 << 20),
+    )(o, dqkv, o_old, dy)
 
 
 def swap_body(*refs, peers, n):
@@ -260,15 +381,26 @@
     )(x)
 
 
-def copy_body(x_ref, out_ref):
-    out_ref[...] = x_ref[...]
-
-
-def keep_copy(x, steps):
-    spec = pl.BlockSpec((x.shape[0] // steps, x.shape[1]), lambda i: (i, 0))
+def copy_body(x_ref, *refs):
+    refs[-1][...] = x_ref[...]
+
+
+def keep_copy(x):
+    spec = pl.BlockSpec((x.shape[0] // 8,) + x.shape[1:], lambda i: (i,) + (0,) * (x.ndim - 1))
     return pl.pallas_call(
-        copy_body, name="keep_copy", out_shape=jax.ShapeDtypeStruct(x.shape, x.dtype), grid=(steps,), in_specs=[spec], out_specs=spec,
-        cost_estimate=pl.CostEstimate(flops=10**10, bytes_accessed=8 * x.size, transcendentals=0))(x)
+        copy_body, name="keep_copy", out_shape=jax.ShapeDtypeStruct(x.shape, x.dtype), grid=(8,), in_specs=[spec], out_specs=spec,
+        cost_estimate=pl.CostEstimate(flops=10**9, bytes_accessed=8 * x.size, transcendentals=0))(x)
+
+
+def place(x, into, lanes, first):
+    heads, n, dim, hidden = x.shape
+    args, in_specs, alias = (x,), [pl.BlockSpec((1, n, dim, hidden), lambda i: (i, 0, 0, 0))], {}
+    if into is not None:
+        args, in_specs, alias = (x, into), in_specs + [pl.BlockSpec(memory_space=pltpu.HBM)], {1: 0}
+    return pl.pallas_call(
+        copy_body, name="place", out_shape=jax.ShapeDtypeStruct((heads, lanes, dim, hidden), x.dtype), grid=(heads,),
+        in_specs=in_specs, out_specs=pl.BlockSpec((1, n, dim, hidden), lambda i: (i, first // n, 0, 0)), input_output_aliases=alias,
+        cost_estimate=pl.CostEstimate(flops=10**9, bytes_accessed=8 * x.size, transcendentals=0))(*args)
 
 
 def norm_forward(x_blk, ln_gain, ln_bias):
@@ -302,7 +434,7 @@
         b_head = lax.dynamic_index_in_dim(b_qkv, rank, 0, keepdims=False).reshape(3 * dim, 1)
         slope = jnp.exp2(-8.0 * (rank + 1).astype(F32) / heads)
         slope2 = (slope * LOG2E).reshape(1)
-        gw = jnp.zeros((3 * dim, hidden), F32)
+        gw = jnp.zeros((3, dim, hidden), F32)
         gb = jnp.zeros((3 * dim,), F32)
         att, got = [], []
         for b in range(batch):
@@ -316,18 +448,20 @@
                 cur, prev = attention(slope2, qkvt, do_t[b], posk, pref, blk=blk, tok=tok, old=att[-1], collective_id=2 + b)
                 got.append(prev)
             else:
-                cur = attention(slope2, qkvt, do_t[b], posk, pref, blk=blk, tok=tok)
+                cur, _ = attention(slope2, qkvt, do_t[b], posk, pref, blk=blk, tok=tok)
             att.append(cur)
-            gw += jnp.einsum("pcdt,pth->cdh", cur[:, 1:], xf[b].reshape(peers, tok, hidden), preferred_element_type=F32).reshape(3 * dim, hidden)
-            gb += jnp.sum(cur[:, 1:].astype(F32), axis=(0, 3)).reshape(3 * dim)
-        gw_all = lax.all_gather(gw, "sp", axis=0, tiled=True)
-        last, _ = lax.optimization_barrier((att[-1], gw))
-        got += swap([last], 2, "swap_last")
-        go = sum(lax.dot_general(got[b][:, 0].reshape(hidden, tok), dy_blk[b], (((1,), (0,)), ((), ())), preferred_element_type=F32) for b in range(batch))
+            gw += jnp.einsum("pdt,pth->dh", cur[1].reshape(peers, 3 * dim, tok), xf[b].reshape(peers, tok, hidden), preferred_element_type=F32).reshape(3, dim, hidden)
+            gb += jnp.sum(cur[1].astype(F32), axis=(0, 3)).reshape(3 * dim)
+        cut = 2
+        gw_all = [lax.all_gather(gw[:cut], "sp", axis=0)]
+        gw_all.append(lax.all_gather(gw[cut:], "sp", axis=0))
+        o_last, dqkv_last, _ = lax.optimization_barrier((*att[-1], gw))
+        o_new, dqkv_new, go_all = tail(o_last, dqkv_last, got[0][0], dy_blk, 2)
+        got.append((o_new, dqkv_new))
         y, gx, gg, gbias = [], [], 0.0, 0.0
         for b in range(batch):
-            o_t = got[b][:, 0].reshape(hidden, tok)
-            dqkv_t = got[b][:, 1:].reshape(3 * hidden, tok)
+            o_t = got[b][0].reshape(hidden, tok)
+            dqkv_t = got[b][1].reshape(3 * hidden, tok)
             y.append((x_f32[b] + lax.dot_general(o_t, w_out, (((0,), (0,)), ((), ())), preferred_element_type=F32) + b_out).astype(BF16))
             d_norm = lax.dot_general(dqkv_t, w_t.reshape(3 * hidden, hidden), (((0,), (0,)), ((), ())), preferred_element_type=F32)
             gg += jnp.sum(d_norm * x_hat[b], axis=0)
@@ -341,12 +475,11 @@
         sums = exchange(rows, peers, 4, "sums")
         total = jnp.sum(sums[:, :3], axis=0)
         gb_all = sums[:, 3, :3 * dim].reshape(heads, 3, dim)
-        go, gw_all, _, _ = lax.optimization_barrier((go, gw_all, y, gx))
-        part = lax.psum_scatter(go, "sp", scatter_dimension=0, tiled=True)
-        gw_all = keep_copy(gw_all, heads)
-        part, gw_all = lax.optimization_barrier((part, gw_all))
-        go_all = lax.all_gather(part, "sp", axis=0, tiled=True)
-        gw_out = jnp.transpose(gw_all.reshape(heads, 3, dim, hidden), (3, 0, 1, 2))
+        go_all = keep_copy(go_all.reshape(hidden, hidden))
+        first, _, _, _ = lax.optimization_barrier((gw_all[0], go_all, y, gx))
+        gw_out = place(first, None, 3, 0)
+        gw_out = place(gw_all[1], gw_out, 3, cut)
+        gw_out = jnp.transpose(gw_out, (3, 0, 1, 2))
         return jnp.stack(y), jnp.stack(gx), gw_out, gb_all, go_all, total[2], total[0], total[1]
 
     act_spec = P("dp", "sp", None)

time: 674 us -> 711 us (1.055)
  Pallas kernels: 368 us -> 570 us
  waiting for transfers between devices: 174 us -> 29 us
  matrix products: 78.8 us -> 63.1 us
    pallas_call x0 -> x3, Pallas kernels: none -> 330 us  [the longest x1 299 us: tail(): pl.pallas_call(functools.partial(tail_body, peers=peers), name='tail', ou...]
    pallas_call x2 -> x1, Pallas kernels: 164 us -> 58.3 us  [swap(): pl.pallas_call(functools.partial(swap_body, peers=peers, n=len(xs)), name...]
    all_gather x2, waiting for transfers between devices: 103 us -> 0.01 us  [the longest x1 0.01 us: block_fn(): gw_all = [lax.all_gather(gw[:cut], 'sp', axis=0)]]
    reduce_scatter x1 -> x0, waiting for transfers between devices: 43.6 us -> none  [block_fn(): part = lax.psum_scatter(go, 'sp', scatter_dimension=0, tiled=True)]
    pallas_call x1, Pallas kernels: 24.5 us -> 9.55 us  [keep_copy(): pl.pallas_call(copy_body, name='keep_copy', out_shape=jax.ShapeDtypeStruc...]
    pallas_call x2, Pallas kernels: 47.9 us -> 39 us  [exchange(): pl.pallas_call(functools.partial(exchange_body, peers=peers), name=name,...]
    unnamed x54 -> x63, local copies, waits for them, and re-layouts: 16.2 us -> 7.72 us
    dot_general x2, matrix products: 26.1 us -> 18.9 us  [block_fn(): lax.dot_general(w_head, xf[b], NT, preferred_element_type=F32) + b_head]
  transfers between devices with their start and end apart: 5 -> 4, of which waited for: 4 -> 1; matrix products, arithmetic and copies ran while one was open for 11% -> 9% of each run, Pallas kernels for 44% -> 68%
where the time goes in v3:
time: 711 us; the launch traced here: 710 us
  Pallas kernels  570 us (80%)
  matrix products  63.1 us (9%)
  waiting for transfers between devices  29 us (4%)
  local copies, waits for them, and re-layouts  17 us (2%)
  other arithmetic  16.1 us (2%)
  between operations  14.4 us (2%)
    pallas_call x1, Pallas kernels, tail(): pl.pallas_call(functools.partial(tail_body, peers=peers), name='tail', ou...  299 us
    pallas_call x2, Pallas kernels, attention(): pl.pallas_call(functools.partial(attn_body, blk=blk, tok=tok, peers=peers...  134 us
    pallas_call x1, Pallas kernels, swap(): pl.pallas_call(functools.partial(swap_body, peers=peers, n=len(xs)), name...  58.3 us
    pallas_call x2, Pallas kernels, exchange(): pl.pallas_call(functools.partial(exchange_body, peers=peers), name=name,...  39 us
    pallas_call x2, Pallas kernels, place(): pl.pallas_call(copy_body, name='place', out_shape=jax.ShapeDtypeStruct((h...  30.9 us
    all_gather x1, waiting for transfers between devices, block_fn(): xf = [lax.all_gather(x_norm[0], 'sp', axis=0, tiled=True)]  28.1 us
    dot_general x2, matrix products, block_fn(): lax.dot_general(dqkv_t, w_t.reshape(3 * hidden, hidden), (((0,), (0,)), (...  19.3 us
    dot_general x2, matrix products, block_fn(): lax.dot_general(w_head, xf[b], NT, preferred_element_type=F32) + b_head  18.9 us
  transfers between devices with their start and end apart: 4, of which 1 were waited for; matrix products, arithmetic and copies ran while one was open for 9% of the time, Pallas kernels for 68%

profile of v3, /device:TPU:21, one launch (start us, length us, event | category | flops | bytes accessed | tf_op | source)
XLA Modules:
  0.0 710.1 jit_solution(3130442335929923418)
XLA Ops:
  7.2 0.1 all-gather.10.cloned.1.call-start
  7.3 1.8 convert_reduce_fusion.3
  9.1 0.5 multiply_reduce_fusion
  9.7 2.3 subtract_multiply_fusion
  12.0 1.2 slice_bitcast_fusion.4
  13.3 0.1 all-gather.10.cloned.1.call-update
  13.3 0.1 all-gather.8.cloned.1.call-start
  13.4 0.7 all-gather.8.cloned.1.call-update
  14.2 0.1 all-gather.14.cloned.1.call-start
  14.3 0.1 pad.11.clone
  14.4 0.1 add.118
  14.5 0.1 add_add_fusion.x_ref
  14.5 14.7 %marks.1 = s32[16,8,256]{2,1,0:T(8,128)S(1)} custom-call(s32[8,256]{1,0:T(8,128)S(1)} %add_add_fusion.x_ref), custom_call_target="tpu_custom_call" | custom-call | tf_op jit(solution)/shard_map/marks/pallas_call | solution.py:373
  29.3 0.1 compare_reduce_fusion
  29.5 0.1 slice.83
  29.6 0.1 slice.87
  29.7 2.3 constant_dynamic-slice_fusion
  32.0 3.8 convolution_convert_fusion
  35.9 1.4 convolution_convert_fusion.1
  37.3 58.3 %swap_do.1 = (bf16[16,96,256]{2,1,0:T(8,128)(2,1)S(1)}, bf16[16,96,256]{2,1,0:T(8,128)(2,1)S(1)}) custom-call(bf16[16,96,256]{2,1,0:T(8,128)(2,1)S(1)} %bitcast.128, bf16[16,96,256]{2,1,0:T(8,128)(2,1)S(1)} %bitcast.127), custom_call_target="tpu_custom_call" | custom-call | flops 18874368000 | bytes 3145728 | tf_op jit(solution)/shard_map/swap_do/pallas_call | solution.py:347
  95.6 28.1 %all-gather.10.cloned.1.call-done = bf16[1,4096,1536]{2,1,0:T(8,128)(2,1)} async-done(((bf16[1,256,1536]{2,1,0:T(8,128)(2,1)}), bf16[1,4096,1536]{2,1,0:T(8,128)(2,1)}) %all-gather.10.cloned.1.call-update) | async-done | bytes 12582928 | tf_op jit(solution)/shard_map/all_gather | solution.py:425
  123.7 8.7 %fusion.4.qkvt_ref = bf16[288,4096]{1,0:T(8,128)(2,1)S(1)} fusion(bf16[288,1536]{1,0:T(8,128)(2,1)} %bitcast.135, f32[288]{0:T(512)S(1)} %add.118, bf16[1,4096,1536]{2,1,0:T(8,128)(2,1)} %all-gather.10.cloned.1.call-done), kind=kOutput, calls=%fused_computation.6 | convolution fusion | flops 3626237952 | bytes 15828096 | tf_op jit(solution)/shard_map/dot_general | solution.py:445
  132.4 0.1 broadcast_in_dim.18.pref_ref
  132.5 0.6 broadcast_in_dim.17.posk_ref
  133.1 57.8 %attention.2 = (bf16[16,96,256]{2,1,0:T(8,128)(2,1)S(1)}, bf16[16,3,96,256]{3,2,1,0:T(8,128)(2,1)S(1)}) custom-call(f32[1]{0:T(128)} %bitcast.1.slope_ref, bf16[288,4096]{1,0:T(8,128)(2,1)S(1)} %fusion.4.qkvt_ref, bf16[16,96,256]{2,1,0:T(8,128)(2,1)S(1)} %get-tuple-element.25.dot_ref, f32[4096,128]{1,0:T(8,128)S(1)} %broadcast_in_dim.17.posk_ref, ...), custom_call_target="tpu_custom_call" | custom-call | flops 28991029248 | bytes 12582912 | tf_op jit(solution)/shard_map/attention/pallas_call | solution.py:160
  190.9 0.9 copy-done.13
  191.8 1.5 copy-done.3
  193.4 8.0 %convolution_bitcast_fusion.1 = f32[3,96,1536]{2,1,0:T(8,128)} fusion(bf16[16,256,1536,1]{2,1,3,0:T(8,128)(2,1)} %bitcast.146, bf16[16,3,96,256]{3,2,1,0:T(8,128)(2,1)S(1)} %get-tuple-element.26.refs_1_), kind=kOutput, calls=%fused_computation.15 | convolution fusion | flops 3623878656 | bytes 16711680 | tf_op jit(solution)/shard_map/pdt,pth->dh/dot_general | solution.py:453
  201.4 10.2 %fusion.5.qkvt_ref = bf16[288,4096]{1,0:T(8,128)(2,1)} fusion(bf16[288,1536]{1,0:T(8,128)(2,1)} %bitcast.136, bf16[4096,1536]{1,0:T(8,128)(2,1)} %all-gather.8.cloned.1.call-done, f32[288]{0:T(512)S(1)} %add.118), kind=kOutput, calls=%fused_computation.7 | convolution fusion | flops 3626237952 | bytes 15828096 | tf_op jit(solution)/shard_map/dot_general | solution.py:445
  211.6 0.1 broadcast_in_dim.20.pref_ref
  211.7 0.6 broadcast_in_dim.19.posk_ref
  212.3 75.7 %attention.3 = (bf16[16,96,256]{2,1,0:T(8,128)(2,1)S(1)}, bf16[16,3,96,256]{3,2,1,0:T(8,128)(2,1)S(1)}, bf16[16,96,256]{2,1,0:T(8,128)(2,1)S(1)}, bf16[16,3,96,256]{3,2,1,0:T(8,128)(2,1)S(1)}) custom-call(f32[1]{0:T(128)} %bitcast.1.slope_ref, bf16[288,4096]{1,0:T(8,128)(2,1)} %fusion.5.qkvt_ref, bf16[16,96,256]{2,1,0:T(8,128)(2,1)S(1)} %get-tuple-element.29.dot_ref, ...), custom_call_target="tpu_custom_call" | custom-call | flops 28991029248 | bytes 12582912 | tf_op jit(solution)/shard_map/attention/pallas_call | solution.py:160
  288.0 8.7 %fusion.6 = f32[3,96,1536]{2,1,0:T(8,128)S(1)} fusion(f32[3,96,1536]{2,1,0:T(8,128)S(1)} %copy-done.26, bf16[16,256,1536,1]{2,1,3,0:T(8,128)(2,1)} %bitcast.145, bf16[16,3,96,256]{3,2,1,0:T(8,128)(2,1)S(1)} %get-tuple-element.36.dqkv_ref), kind=kOutput, calls=%fused_computation.16 | convolution fusion | flops 3624321024 | bytes 18481152 | tf_op jit(solution)/shard_map/pdt,pth->dh/dot_general | solution.py:453
  296.8 1.2 copy-done.19
  298.0 1.1 slice.109
  299.1 0.1 all-gather.14.cloned.1.call-update
  299.2 0.1 all-gather.12.cloned.1.call-start
  299.3 1.9 slice.108
  301.3 3.6 convert_element_type.70
  304.9 0.3 convert_reduce_fusion.2
  305.2 0.4 convert_reduce_fusion.1
  305.6 1.0 copy-done.6
  306.5 0.4 convert_reduce_fusion
  307.0 0.1 add.135
  307.1 1.1 copy-done.12
  308.2 299.0 %tail.1 = (bf16[16,96,256]{2,1,0:T(8,128)(2,1)S(1)}, bf16[16,3,96,256]{3,2,1,0:T(8,128)(2,1)}, f32[8,2,96,1536]{3,2,1,0:T(8,128)}) custom-call(bf16[16,96,256]{2,1,0:T(8,128)(2,1)S(1)} %copy-done.12, bf16[16,3,96,256]{3,2,1,0:T(8,128)(2,1)} %copy-done.5, bf16[16,96,256]{2,1,0:T(8,128)(2,1)S(1)} %get-tuple-element.31.o_old, bf16[2,256,1536]{2,1,0:T(8,128)(2,1)S(1)} %copy-done.2), custom_call_target="tpu_custom_call" | custom-call | flops 99999997952 | bytes 67108864 | tf_op jit(solution)/shard_map/tail/pallas_call | solution.py:319
  607.2 8.1 %fusion.10 = f32[256,1536]{1,0:T(8,128)S(1)} fusion(bf16[16,3,96,256]{3,2,1,0:T(8,128)(2,1)} %get-tuple-element.39, bf16[1536,16,3,96]{0,3,2,1:T(8,128)(2,1)} %param.15), kind=kOutput, calls=%fused_computation.18 | convolution fusion | flops 3623878656 | bytes 18087936 | tf_op jit(solution)/shard_map/dot_general | solution.py:466
  615.3 11.2 %multiply_reduce_fusion.2 = (f32[1536]{0:T(1024)S(1)}, f32[256]{0:T(256)S(1)}, f32[256]{0:T(256)S(1)}, f32[1536]{0:T(1024)S(1)}, f32[256]{0:T(256)S(1)}, /*index...) fusion(f32[2,256,1536]{2,1,0:T(8,128)S(1)} %copy-done.16, f32[1536]{0:T(1024)S(1)} %copy-done.21, ...), kind=kOutput, calls=%fused_computation.37 | convolution fusion | flops 3629376512 | bytes 22841344 | tf_op jit(solution)/shard_map/dot_general | solution.py:466
  626.6 0.1 stack.41.x_ref
  626.7 24.3 %sums.1 = f32[16,8,1536]{2,1,0:T(8,128)S(1)} custom-call(f32[8,1536]{1,0:T(8,128)S(1)} %stack.41.x_ref), custom_call_target="tpu_custom_call" | custom-call | tf_op jit(solution)/shard_map/sums/pallas_call | solution.py:373
  651.0 0.1 slice_reduce_fusion.1
  651.1 0.1 reshape_squeeze.2
  651.2 0.6 copy.29
  651.8 9.6 %keep_copy.1 = f32[1536,1536]{1,0:T(8,128)} custom-call(f32[1536,1536]{1,0:T(8,128)} %bitcast.131), custom_call_target="tpu_custom_call" | custom-call | flops 1000000000 | bytes 18874368 | tf_op jit(solution)/shard_map/keep_copy/pallas_call | solution.py:390
  661.3 0.1 slice_reduce_fusion
  661.4 0.6 slice_reduce_fusion.2
  662.1 3.9 add_convert_fusion.2
  666.0 1.3 pad_maximum_fusion.1
  667.3 1.2 copy-done.18
  668.5 1.4 fusion.16
  669.9 1.4 fusion.15
  671.3 1.3 pad_maximum_fusion
  672.6 18.6 %place.2.refs_0_ = f32[16,3,96,1536]{3,2,1,0:T(8,128)} custom-call(f32[16,2,96,1536]{3,2,1,0:T(8,128)} %bitcast.130), custom_call_target="tpu_custom_call" | custom-call | flops 1000000000 | bytes 37748736 | tf_op jit(solution)/shard_map/place/pallas_call | solution.py:400
  691.2 12.3 %place.3 = f32[16,3,96,1536]{3,2,1,0:T(8,128)} custom-call(f32[16,1,96,1536]{3,2,1,0:T(8,128)} %bitcast.132, f32[16,3,96,1536]{3,2,1,0:T(8,128)} %place.2.refs_0_), custom_call_target="tpu_custom_call", output_to_operand_aliasing={{}: (1, {})} | custom-call | flops 1000000000 | bytes 18874368 | tf_op jit(solution)/shard_map/place/pallas_call | solution.py:400
  (83 shorter events, 0.4 us)
Async XLA Ops:
  7.2 7.2 %copy-start = (f32[16,3,96]{2,0,1:T(8,128)S(1)}, f32[16,3,96]{2,0,1:T(8,128)}, u32[]{:S(2)}) copy-start(f32[16,3,96]{2,0,1:T(8,128)} %param.16) | copy-start | bytes 55300
  7.2 1.9 copy-start.15
  7.2 2.5 copy-start.20
  7.2 2.5 copy-start.22
  7.2 116.5 %all-gather.10.cloned.1.call-start = ((), (), s32[]{:S(2)}) async-start(), calls=%async_computation.1 | async-start | bytes 13369344 | tf_op jit(solution)/shard_map/all_gather | solution.py:425
  12.0 2.4 copy-start.23
  12.0 2.4 copy-start.24
  13.3 18.7 %copy-start.2 = (bf16[2,256,1536]{2,1,0:T(8,128)(2,1)S(1)}, bf16[2,256,1536]{2,1,0:T(8,128)(2,1)}, u32[]{:S(2)}) copy-start(bf16[2,256,1536]{2,1,0:T(8,128)(2,1)} %dy_ref.1) | copy-start | bytes 4718596
  13.3 188.1 %all-gather.8.cloned.1.call-start = ((), (), s32[]{:S(2)}) async-start(), calls=%async_computation | async-start | bytes 13369344 | tf_op jit(solution)/shard_map/all_gather | solution.py:431
  14.2 658.4 %all-gather.14.cloned.1.call-start = ((), (), s32[]{:S(2)}) async-start(), calls=%async_computation.3 | async-start | bytes 20054016 | tf_op jit(solution)/shard_map/all_gather | solution.py:456
  29.7 6.2 slice-start
  32.0 3.9 slice-start.1
  190.9 0.9 copy-start.13
  191.8 1.5 copy-start.3
  201.4 10.8 %copy-start.14 = (bf16[16,96,256]{2,1,0:T(8,128)(2,1)S(1)}, bf16[16,96,256]{2,1,0:T(8,128)(2,1)}, u32[]{:S(2)}) copy-start(bf16[16,96,256]{2,1,0:T(8,128)(2,1)} %copy-done.13) | copy-start | bytes 2359300
  212.3 75.8 %copy-start.26 = (f32[3,96,1536]{2,1,0:T(8,128)S(1)}, f32[3,96,1536]{2,1,0:T(8,128)}, u32[]{:S(2)}) copy-start(f32[3,96,1536]{2,1,0:T(8,128)} %convolution_bitcast_fusion.1) | copy-start | bytes 5308420
  288.0 8.8 %copy-start.5 = (bf16[16,3,96,256]{3,2,1,0:T(8,128)(2,1)}, bf16[16,3,96,256]{3,2,1,0:T(8,128)(2,1)S(1)}, u32[]{:S(2)}) copy-start(bf16[16,3,96,256]{3,2,1,0:T(8,128)(2,1)S(1)} %get-tuple-element.36.dqkv_ref) | copy-start | bytes 7077892
  288.0 8.8 %copy-start.7 = (bf16[16,3,96,256]{3,2,1,0:T(8,128)(2,1)}, bf16[16,3,96,256]{3,2,1,0:T(8,128)(2,1)S(1)}, u32[]{:S(2)}) copy-start(bf16[16,3,96,256]{3,2,1,0:T(8,128)(2,1)S(1)} %get-tuple-element.38) | copy-start | bytes 7077892
  288.0 8.8 %copy-start.11 = (bf16[16,96,256]{2,1,0:T(8,128)(2,1)}, bf16[16,96,256]{2,1,0:T(8,128)(2,1)S(1)}, u32[]{:S(2)}) copy-start(bf16[16,96,256]{2,1,0:T(8,128)(2,1)S(1)} %get-tuple-element.35.o_ref) | copy-start | bytes 2359300
  296.8 1.2 copy-start.19
  299.2 392.0 %all-gather.12.cloned.1.call-start = ((), (), s32[]{:S(2)}) async-start(), calls=%async_computation.2 | async-start | bytes 10027008 | tf_op jit(solution)/shard_map/all_gather | solution.py:457
  301.3 3.9 copy-start.4
  304.9 1.7 copy-start.6
  307.1 1.1 copy-start.12
  607.2 8.1 %copy-start.9 = (bf16[16,96,256]{2,1,0:T(8,128)(2,1)}, bf16[16,96,256]{2,1,0:T(8,128)(2,1)S(1)}, u32[]{:S(2)}) copy-start(bf16[16,96,256]{2,1,0:T(8,128)(2,1)S(1)} %get-tuple-element.37) | copy-start | bytes 2359300
  607.2 8.2 %copy-start.8 = (bf16[16,3,96,256]{3,2,1,0:T(8,128)(2,1)S(1)}, bf16[16,3,96,256]{3,2,1,0:T(8,128)(2,1)}, u32[]{:S(2)}) copy-start(bf16[16,3,96,256]{3,2,1,0:T(8,128)(2,1)} %copy-done.7) | copy-start | bytes 7077892
  607.2 8.2 %copy-start.16 = (f32[2,256,1536]{2,1,0:T(8,128)S(1)}, f32[2,256,1536]{2,1,0:T(8,128)}, u32[]{:S(2)}) copy-start(f32[2,256,1536]{2,1,0:T(8,128)} %get-tuple-element.83) | copy-start | bytes 9437188
  607.2 8.2 %copy-start.21 = (f32[1536]{0:T(1024)S(1)}, f32[1536]{0:T(1024)}, u32[]{:S(2)}) copy-start(f32[1536]{0:T(1024)} %param.13) | copy-start | bytes 18436
  615.3 11.3 %copy-start.17 = (f32[256,1536]{1,0:T(8,128)}, f32[256,1536]{1,0:T(8,128)S(1)}, u32[]{:S(2)}) copy-start(f32[256,1536]{1,0:T(8,128)S(1)} %fusion.10) | copy-start | bytes 4718596
  662.0 5.2 slice-start.2
  662.0 5.2 slice-start.3
  665.9 2.5 copy-start.18
  666.0 2.5 copy-start.25
  668.5 1.4 copy-start.10
  691.2 12.3 %copy-start.1 = (f32[16,3,96]{2,0,1:T(8,128)S(1)}, f32[16,3,96]{2,0,1:T(8,128)}, u32[]{:S(2)}) copy-start(f32[16,3,96]{2,0,1:T(8,128)} %param.16) | copy-start | bytes 55300
Sparse Core Ops, SparseCore 0:
  13.5 110.2 all-gather.9
  125.9 71.6 all-gather.7
  299.3 205.5 all-gather.13
  506.4 94.2 all-gather.11

commit v4 on v3

--- a/solution.py
+++ b/solution.py
@@ -14,14 +14,11 @@
 NT = (((1,), (1,)), ((), ()))
 
 
-def attn_body(slope_ref, qkvt_ref, dot_ref, posk_ref, pref_ref, *refs, blk, tok, peers):
-    if peers:
-        old, (o_ref, dqkv_ref), got = refs[:2], refs[2:4], refs[4:6]
-        swaps = [(old[n], got[n]) + refs[4 * n - 8:(4 * n - 4) or None] for n in range(2)]
-        refs = refs[6:-8]
-    else:
-        (o_ref, dqkv_ref), refs = refs[:2], refs[2:]
-    k_tok, v_tok, s_buf, q_pad, do_pad, o_acc, dq_acc, dk_acc, dv_acc = refs
+def attn_body(slope_ref, w_ref, b_ref, x_ref, dot_ref, posk_ref, pref_ref, gw_old, *refs, blk, tok, n_swap):
+    peers = dot_ref.shape[0]
+    old, (o_ref, dqkv_ref, gw_ref), got = refs[:n_swap], refs[n_swap:n_swap + 3], refs[n_swap + 3:2 * n_swap + 3]
+    swaps = [(old[k], got[k]) + refs[len(refs) - 4 * n_swap + 4 * k:][:4] for k in range(n_swap)]
+    x_buf, qkvt_ref, k_tok, v_tok, s_buf, q_pad, do_pad, o_acc, dq_acc, dk_acc, dv_acc, x_sem = refs[2 * n_swap + 3:][:12]
     dim = dot_ref.shape[1]
     seq = dot_ref.shape[0] * tok
     pad = k_tok.shape[1] - dim
@@ -30,29 +27,35 @@
     i = pl.program_id(0)
     half = blk // 2
 
-    if peers:
-        @pl.when(i == 0)
-        def _():
+    def x_copy(k):
+        rows = pl.ds(pl.multiple_of(k * blk, blk), blk)
+        return pltpu.make_async_copy(x_ref.at[rows], x_buf.at[rows], x_sem.at[k])
+
+    @pl.when(i == 0)
+    def _():
+        for k in range(seq // blk):
+            x_copy(k).start()
+        if n_swap:
             meet(peers)
             for one in swaps:
                 swap_start(*one, peers)
-
-    @pl.when(i == 0)
-    def _():
         dk_acc[...] = jnp.zeros_like(dk_acc)
         dv_acc[...] = jnp.zeros_like(dv_acc)
         q_pad[...] = jnp.zeros_like(q_pad)
         do_pad[...] = jnp.zeros_like(do_pad)
 
-        @pl.loop(0, seq // 128)
-        def _(t):
-            cols = pl.ds(pl.multiple_of(t * 128, 128), 128)
-            for base, dst in ((dim, k_tok), (2 * dim, v_tok)):
-                part = qkvt_ref[base:base + dim, cols].astype(F32)
-                full = jnp.concatenate([part, jnp.zeros((pad, 128), F32)], axis=0)
-                dst[cols, :] = jnp.transpose(full).astype(BF16)
-
     qcols = pl.ds(pl.multiple_of(i * blk, blk), blk)
+    x_copy(i).wait()
+    qkvt_ref[:, qcols] = (lax.dot_general(w_ref[...], x_buf[qcols, :], NT, preferred_element_type=F32) + b_ref[...]).astype(BF16)
+
+    @pl.loop(0, blk // 128)
+    def _(t):
+        cols = pl.ds(pl.multiple_of(i * blk + t * 128, 128), 128)
+        for base, dst in ((dim, k_tok), (2 * dim, v_tok)):
+            part = qkvt_ref[base:base + dim, cols].astype(F32)
+            whole = jnp.concatenate([part, jnp.zeros((pad, 128), F32)], axis=0)
+            dst[cols, :] = jnp.transpose(whole).astype(BF16)
+
     q_pad[0:dim, :] = qkvt_ref[0:dim, qcols]
     for t in range(nq):
         do_pad[0:dim, t * tok:(t + 1) * tok] = dot_ref[i * nq + t]
@@ -127,49 +130,50 @@
             dqkv_ref[t, 1] = (dk_acc[:, cols] * scale).astype(BF16)
             dqkv_ref[t, 2] = dv_acc[:, cols].astype(BF16)
 
-        if peers:
-            for one in swaps:
-                swap_wait(*one, peers)
-
-
-def attention(slope2, qkvt, dot_, posk, pref, *, blk, tok, old=None, collective_id=None):
+        gw_ref[...] = gw_old[...]
+
+        @pl.loop(0, seq // blk)
+        def _(j):
+            total = gw_ref[...]
+            for t in range(nq):
+                rows = pl.ds(pl.multiple_of(j * blk + t * tok, tok), tok)
+                total = total + jnp.dot(dqkv_ref[j * nq + t].reshape(3 * dim, tok), x_buf[rows, :], preferred_element_type=F32)
+            gw_ref[...] = total
+
+        for one in swaps:
+            swap_wait(*one, peers)
+
+
+def attention(slope2, w_head, b_head, x, dot_, posk, pref, gw, old, *, blk, tok, collective_id):
     blocks, dim, _ = dot_.shape
-    seq = blocks * tok
+    seq, hidden = x.shape
     wide = 128 * pl.cdiv(dim, 128)
     hbm = pl.BlockSpec(memory_space=pltpu.HBM)
-    full = lambda a: pl.BlockSpec(a.shape, lambda i: (0,) * a.ndim, pipeline_mode=pl.Buffered(1))
-    outs = [jax.ShapeDtypeStruct((blocks, dim, tok), BF16), jax.ShapeDtypeStruct((blocks, 3, dim, tok), BF16)]
+    full = lambda a: pl.BlockSpec(a.shape, lambda i: (0,) * len(a.shape), pipeline_mode=pl.Buffered(1))
+    like = lambda a: jax.ShapeDtypeStruct(a.shape, a.dtype)
+    outs = [jax.ShapeDtypeStruct((blocks, dim, tok), BF16), jax.ShapeDtypeStruct((blocks, 3, dim, tok), BF16), like(gw)]
     pairs = (seq // blk) * (seq // blk + 1) // 2
-    args = (slope2, qkvt, dot_, posk, pref)
-    in_specs = [pl.BlockSpec(memory_space=pltpu.SMEM)] + [full(a) for a in (qkvt, dot_, posk, pref)]
-    out_shape, out_specs = list(outs), [full(a) for a in outs]
-    scratch = [
-        pltpu.VMEM((seq, wide), BF16), pltpu.VMEM((seq, wide), BF16),
-        pltpu.VMEM((seq, blk), F32),
-        pltpu.VMEM((wide, blk), BF16), pltpu.VMEM((wide, blk), BF16),
-        pltpu.VMEM((dim, blk), F32), pltpu.VMEM((dim, blk), F32),
-        pltpu.VMEM((dim, seq), F32), pltpu.VMEM((dim, seq), F32)]
-    peers = 0
-    if old is not None:
-        peers = blocks
-        args += tuple(old)
-        in_specs += [hbm] * 2
-        out_shape += outs
-        out_specs += [hbm] * 2
-        scratch += swap_scratch(old[0]) + swap_scratch(old[1])
     res = pl.pallas_call(
-        functools.partial(attn_body, blk=blk, tok=tok, peers=peers),
+        functools.partial(attn_body, blk=blk, tok=tok, n_swap=len(old)),
         name="attention",
-        out_shape=out_shape,
+        out_shape=outs + [like(a) for a in old],
         grid=(seq // blk,),
-        in_specs=in_specs,
-        out_specs=out_specs,
-        scratch_shapes=scratch,
-        cost_estimate=pl.CostEstimate(flops=pairs * 6 * 2 * blk * blk * 256, bytes_accessed=12 << 20, transcendentals=pairs * blk * blk),
-        compiler_params=pltpu.CompilerParams(dimension_semantics=("arbitrary",), vmem_limit_bytes=44 << 20,
-                                             collective_id=collective_id, has_side_effects=old is not None),
-    )(*args)
-    return res[:2], res[2:]
+        in_specs=[pl.BlockSpec(memory_space=pltpu.SMEM), full(w_head), full(b_head), hbm, full(dot_), full(posk), full(pref), full(gw)]
+        + [hbm] * len(old),
+        out_specs=[full(a) for a in outs] + [hbm] * len(old),
+        scratch_shapes=[
+            pltpu.VMEM((seq, hidden), BF16), pltpu.VMEM((3 * dim, seq), BF16),
+            pltpu.VMEM((seq, wide), BF16), pltpu.VMEM((seq, wide), BF16),
+            pltpu.VMEM((seq, blk), F32),
+            pltpu.VMEM((wide, blk), BF16), pltpu.VMEM((wide, blk), BF16),
+            pltpu.VMEM((dim, blk), F32), pltpu.VMEM((dim, blk), F32),
+            pltpu.VMEM((dim, seq), F32), pltpu.VMEM((dim, seq), F32), pltpu.SemaphoreType.DMA((seq // blk,))]
+        + sum((swap_scratch(a) for a in old), []),
+        cost_estimate=pl.CostEstimate(flops=pairs * 6 * 2 * blk * blk * 256, bytes_accessed=24 << 20, transcendentals=pairs * blk * blk),
+        compiler_params=pltpu.CompilerParams(dimension_semantics=("arbitrary",), vmem_limit_bytes=52 << 20,
+                                             collective_id=collective_id, has_side_effects=True),
+    )(slope2, w_head, b_head, x, dot_, posk, pref, gw, *old)
+    return res[:2], res[2], res[3:]
 
 
 def peer_at(d, peers):
@@ -213,12 +217,12 @@
             pltpu.SemaphoreType.DMA]
 
 
-def tail_body(o_ref, dqkv_ref, o_old, dy_ref, o_new, dqkv_new, full, mine, other, pair, landed, own_o, own_d,
-              os_sem, or_sem, oo_sem, ds_sem, dr_sem, do_sem, ps_sem, pr_sem, rs_sem, rr_sem, as_sem, ar_sem, fs_sem, fr_sem, *, peers):
+def tail_body(o_ref, dqkv_ref, o_old, dy_ref, o_new, dqkv_new, part, mine, other, pair, landed, own_o, own_d,
+              os_sem, or_sem, oo_sem, ds_sem, dr_sem, do_sem, ps_sem, pr_sem, rs_sem, rr_sem, *, peers):
     ring = peers // 2
     me = lax.axis_index("sp")
     z, c = me // 2, me % 2
-    half = full.shape[-1] // 2
+    half = part.shape[-1] // 2
     cols = (pl.ds(0, half), pl.ds(half, half))
     at = lambda zz, cc: {"sp": 2 * zz + cc}
     turn = lambda k: lax.rem(z + k + 2 * ring, ring)
@@ -266,47 +270,13 @@
     for w in range(2):
         add(w, ring - 2, z)
 
-    def gather_copy(w, t):
-        k = turn(-step[w] * t)
-        return remote(src_ref=full.at[k, c, :, cols[w]], dst_ref=full.at[k, c, :, cols[w]],
-                      send_sem=as_sem.at[w, t], recv_sem=ar_sem.at[w, t], device_id=at(turn(step[w]), c))
-
-    def over_copy(w, t):
-        k = turn(-step[w] * t)
-        return remote(src_ref=full.at[k, c, :, cols[w]], dst_ref=full.at[k, c, :, cols[w]],
-                      send_sem=fs_sem.at[w, t], recv_sem=fr_sem.at[w, t], device_id=at(z, 1 - c))
-
-    full[z, c] = mine[z]
-    for w in range(2):
-        gather_copy(w, 0).start()
-    for w in range(2):
-        over_copy(w, 0).start()
-
-    @pl.loop(1, ring)
-    def _(t):
-        for w in range(2):
-            gather_copy(w, t - 1).wait_recv()
-
-            @pl.when(t < ring - 1)
-            def _():
-                gather_copy(w, t).start()
-
-            over_copy(w, t).start()
-
+    part[...] = mine[z]
     swap_wait(dqkv_ref, dqkv_new, own_d, ds_sem, dr_sem, do_sem, peers)
 
     @pl.loop(0, ring - 1)
     def _(t):
         for w in range(2):
             reduce_copy(w, t).wait_send()
-            gather_copy(w, t).wait_send()
-
-    @pl.loop(0, ring)
-    def _(t):
-        for w in range(2):
-            over_copy(w, t).wait_send()
-            remote(src_ref=full.at[turn(-step[w] * t), 1 - c, :, cols[w]], dst_ref=full.at[turn(-step[w] * t), 1 - c, :, cols[w]],
-                   send_sem=fs_sem.at[w, t], recv_sem=fr_sem.at[w, t], device_id=at(z, 1 - c)).wait_recv()
 
 
 def tail(o, dqkv, o_old, dy, collective_id):
@@ -320,16 +290,86 @@
         functools.partial(tail_body, peers=peers),
         name="tail",
         out_shape=[jax.ShapeDtypeStruct(o.shape, BF16), jax.ShapeDtypeStruct(dqkv.shape, BF16),
-                   jax.ShapeDtypeStruct((ring, 2, dim, hidden), F32)],
+                   jax.ShapeDtypeStruct((dim, hidden), F32)],
         in_specs=[hbm, hbm, vmem, vmem],
         out_specs=[vmem, hbm, vmem],
         scratch_shapes=[rows(ring), rows(ring), rows(ring), pltpu.VMEM((2, ring - 1, dim, hidden // 2), F32),
                         pltpu.VMEM(o.shape[1:], BF16), pltpu.VMEM(dqkv.shape[1:], BF16),
                         dma((peers - 1,)), dma((peers - 1,)), dma, dma((peers - 1,)), dma((peers - 1,)), dma, dma, dma,
-                        dma((2, ring - 1)), dma((2, ring - 1)), dma((2, ring - 1)), dma((2, ring - 1)), dma((2, ring)), dma((2, ring))],
+                        dma((2, ring - 1)), dma((2, ring - 1))],
         cost_estimate=pl.CostEstimate(flops=10**11, bytes_accessed=64 << 20, transcendentals=0),
         compiler_params=pltpu.CompilerParams(collective_id=collective_id, has_side_effects=True, vmem_limit_bytes=48 << 20),
     )(o, dqkv, o_old, dy)
+
+
+def collect_body(part, rows_ref, full, sums, as_sem, ar_sem, fs_sem, fr_sem, xs_sem, xr_sem, *, peers):
+    ring = peers // 2
+    me = lax.axis_index("sp")
+    z, c = me // 2, me % 2
+    half = part.shape[-1] // 2
+    cols = (pl.ds(0, half), pl.ds(half, half))
+    turn = lambda k: lax.rem(z + k + 2 * ring, ring)
+    step = (1, -1)
+    remote = functools.partial(pltpu.make_async_remote_copy, device_id_type=pl.DeviceIdType.MESH)
+
+    def block_copy(w, t, side, send_sem, recv_sem, to):
+        ref = full.at[turn(-step[w] * t), side, :, cols[w]]
+        return remote(src_ref=ref, dst_ref=ref, send_sem=send_sem.at[w, t], recv_sem=recv_sem.at[w, t], device_id={"sp": to})
+
+    gather_copy = lambda w, t: block_copy(w, t, c, as_sem, ar_sem, 2 * turn(step[w]) + c)
+    over_copy = lambda w, t, side: block_copy(w, t, side, fs_sem, fr_sem, 2 * z + 1 - c)
+    full[z, c] = part[...]
+    meet(peers)
+    small = [remote(src_ref=rows_ref, dst_ref=sums.at[me], send_sem=xs_sem.at[d - 1], recv_sem=xr_sem.at[d - 1],
+                    device_id=peer_at(d, peers)) for d in range(1, peers)]
+    for copy in small:
+        copy.start()
+    for w in range(2):
+        gather_copy(w, 0).start()
+    for w in range(2):
+        over_copy(w, 0, c).start()
+    sums[me] = rows_ref[...]
+
+    @pl.loop(1, ring)
+    def _(t):
+        for w in range(2):
+            gather_copy(w, t - 1).wait_recv()
+
+            @pl.when(t < ring - 1)
+            def _():
+                gather_copy(w, t).start()
+
+            over_copy(w, t, c).start()
+
+    for copy in small:
+        copy.wait()
+
+    @pl.loop(0, ring - 1)
+    def _(t):
+        for w in range(2):
+            gather_copy(w, t).wait_send()
+
+    @pl.loop(0, ring)
+    def _(t):
+        for w in range(2):
+            over_copy(w, t, c).wait_send()
+            over_copy(w, t, 1 - c).wait_recv()
+
+
+def collect(part, rows, peers, collective_id):
+    ring = peers // 2
+    vmem = pl.BlockSpec(memory_space=pltpu.VMEM)
+    dma = pltpu.SemaphoreType.DMA
+    return pl.pallas_call(
+        functools.partial(collect_body, peers=peers),
+        name="collect",
+        out_shape=[jax.ShapeDtypeStruct((ring, 2) + part.shape, F32), jax.ShapeDtypeStruct((peers,) + rows.shape, F32)],
+        in_specs=[vmem, vmem],
+        out_specs=[vmem, vmem],
+        scratch_shapes=[dma((2, ring - 1)), dma((2, ring - 1)), dma((2, ring)), dma((2, ring)), dma((peers - 1,)), dma((peers - 1,))],
+        cost_estimate=pl.CostEstimate(flops=5 * 10**10, bytes_accessed=10 << 20, transcendentals=0),
+        compiler_params=pltpu.CompilerParams(collective_id=collective_id, has_side_effects=True, vmem_limit_bytes=24 << 20),
+    )(part, rows)
 
 
 def swap_body(*refs, peers, n):
@@ -381,26 +421,49 @@
     )(x)
 
 
-def copy_body(x_ref, *refs):
-    refs[-1][...] = x_ref[...]
-
-
-def keep_copy(x):
-    spec = pl.BlockSpec((x.shape[0] // 8,) + x.shape[1:], lambda i: (i,) + (0,) * (x.ndim - 1))
-    return pl.pallas_call(
-        copy_body, name="keep_copy", out_shape=jax.ShapeDtypeStruct(x.shape, x.dtype), grid=(8,), in_specs=[spec], out_specs=spec,
-        cost_estimate=pl.CostEstimate(flops=10**9, bytes_accessed=8 * x.size, transcendentals=0))(x)
+def place_body(*refs, first):
+    x_ref, (out_ref, buf, in_sem, out_sem) = refs[0], refs[-4:]
+    heads, n = x_ref.shape[:2]
+    reads = [pltpu.make_async_copy(x_ref.at[h], buf.at[h], in_sem.at[h]) for h in range(heads)]
+    writes = [pltpu.make_async_copy(buf.at[h], out_ref.at[h, pl.ds(first, n)], out_sem.at[h]) for h in range(heads)]
+    for copy in reads:
+        copy.start()
+    for read, write in zip(reads, writes):
+        read.wait()
+        write.start()
+    for copy in writes:
+        copy.wait()
 
 
 def place(x, into, lanes, first):
     heads, n, dim, hidden = x.shape
-    args, in_specs, alias = (x,), [pl.BlockSpec((1, n, dim, hidden), lambda i: (i, 0, 0, 0))], {}
-    if into is not None:
-        args, in_specs, alias = (x, into), in_specs + [pl.BlockSpec(memory_space=pltpu.HBM)], {1: 0}
+    hbm = pl.BlockSpec(memory_space=pltpu.HBM)
+    args, alias = ((x,), {}) if into is None else ((x, into), {1: 0})
+    dma = pltpu.SemaphoreType.DMA
     return pl.pallas_call(
-        copy_body, name="place", out_shape=jax.ShapeDtypeStruct((heads, lanes, dim, hidden), x.dtype), grid=(heads,),
-        in_specs=in_specs, out_specs=pl.BlockSpec((1, n, dim, hidden), lambda i: (i, first // n, 0, 0)), input_output_aliases=alias,
-        cost_estimate=pl.CostEstimate(flops=10**9, bytes_accessed=8 * x.size, transcendentals=0))(*args)
+        functools.partial(place_body, first=first), name="place",
+        out_shape=jax.ShapeDtypeStruct((heads, lanes, dim, hidden), x.dtype),
+        in_specs=[hbm] * len(args), out_specs=hbm, input_output_aliases=alias,
+        scratch_shapes=[pltpu.VMEM(x.shape, x.dtype), dma((heads,)), dma((heads,))],
+        cost_estimate=pl.CostEstimate(flops=10**9, bytes_accessed=8 * x.size, transcendentals=0),
+        compiler_params=pltpu.CompilerParams(vmem_limit_bytes=60 << 20))(*args)
+
+
+def lay_body(x_ref, out_ref, sem):
+    copies = [pltpu.make_async_copy(x_ref.at[k], out_ref.at[k], sem.at[k]) for k in range(x_ref.shape[0])]
+    for copy in copies:
+        copy.start()
+    for copy in copies:
+        copy.wait()
+
+
+def lay_down(x):
+    return pl.pallas_call(
+        lay_body, name="lay_down", out_shape=jax.ShapeDtypeStruct(x.shape, x.dtype),
+        in_specs=[pl.BlockSpec(memory_space=pltpu.VMEM)], out_specs=pl.BlockSpec(memory_space=pltpu.HBM),
+        scratch_shapes=[pltpu.SemaphoreType.DMA((x.shape[0],))],
+        cost_estimate=pl.CostEstimate(flops=10**9, bytes_accessed=8 * x.size, transcendentals=0),
+        compiler_params=pltpu.CompilerParams(vmem_limit_bytes=24 << 20))(x)
 
 
 def norm_forward(x_blk, ln_gain, ln_bias):
@@ -425,16 +488,15 @@
         xf = [lax.all_gather(x_norm[0], "sp", axis=0, tiled=True)]
         marks = exchange(jnp.concatenate([pos_blk, keep_blk, jnp.zeros((8 - 2 * batch, tok), jnp.int32)]), peers, 0, "marks")
         do_loc = [lax.dot_general(w_out, dy_blk[b], NT, preferred_element_type=F32).astype(BF16).reshape(heads, dim, tok) for b in range(batch)]
-        do_t = swap(do_loc, 1, "swap_do")
+        do_t = list(swap(do_loc[:1], 1, "swap_do"))
         for b in range(1, batch):
-            xn, _ = lax.optimization_barrier((x_norm[b], xf[-1]))
-            xf.append(lax.all_gather(xn, "sp", axis=0, tiled=True))
+            xf.append(lax.all_gather(x_norm[b], "sp", axis=0, tiled=True))
         w_t = jnp.transpose(w_qkv, (1, 2, 3, 0))
         w_head = lax.dynamic_index_in_dim(w_t, rank, 0, keepdims=False).reshape(3 * dim, hidden)
         b_head = lax.dynamic_index_in_dim(b_qkv, rank, 0, keepdims=False).reshape(3 * dim, 1)
         slope = jnp.exp2(-8.0 * (rank + 1).astype(F32) / heads)
         slope2 = (slope * LOG2E).reshape(1)
-        gw = jnp.zeros((3, dim, hidden), F32)
+        gw = jnp.zeros((3 * dim, hidden), F32)
         gb = jnp.zeros((3 * dim,), F32)
         att, got = [], []
         for b in range(batch):
@@ -442,22 +504,21 @@
             keep = marks[:, batch + b].reshape(seq)
             posk = jnp.broadcast_to(jnp.where(keep > 0, pos, MASKED)[:, None], (seq, 128))
             pref = jnp.broadcast_to(pos[::blk][:, None], (seq // blk, 128))
-            qkvt = (lax.dot_general(w_head, xf[b], NT, preferred_element_type=F32) + b_head).astype(BF16)
+            old = list(do_loc[b + 1:b + 2]) + (list(att[-1]) if b else [])
+            cur, gw, swapped = attention(slope2, w_head, b_head, xf[b], do_t[b], posk, pref, gw, old, blk=blk, tok=tok, collective_id=4 + b)
+            if b + 1 < batch:
+                do_t.append(swapped[0])
             if b:
-                slope2, gw = lax.optimization_barrier((slope2, gw))
-                cur, prev = attention(slope2, qkvt, do_t[b], posk, pref, blk=blk, tok=tok, old=att[-1], collective_id=2 + b)
-                got.append(prev)
-            else:
-                cur, _ = attention(slope2, qkvt, do_t[b], posk, pref, blk=blk, tok=tok)
+                got.append(swapped[-2:])
             att.append(cur)
-            gw += jnp.einsum("pdt,pth->dh", cur[1].reshape(peers, 3 * dim, tok), xf[b].reshape(peers, tok, hidden), preferred_element_type=F32).reshape(3, dim, hidden)
-            gb += jnp.sum(cur[1].astype(F32), axis=(0, 3)).reshape(3 * dim)
         cut = 2
-        gw_all = [lax.all_gather(gw[:cut], "sp", axis=0)]
-        gw_all.append(lax.all_gather(gw[cut:], "sp", axis=0))
-        o_last, dqkv_last, _ = lax.optimization_barrier((*att[-1], gw))
-        o_new, dqkv_new, go_all = tail(o_last, dqkv_last, got[0][0], dy_blk, 2)
+        gw3 = gw.reshape(3, dim, hidden)
+        gw_all = [lax.all_gather(gw3[:cut], "sp", axis=0), lax.all_gather(gw3[cut:], "sp", axis=0)]
+        o_last, dqkv_last, _ = lax.optimization_barrier((*att[-1], gw3))
+        o_new, dqkv_new, part = tail(o_last, dqkv_last, got[0][0], dy_blk, 2)
         got.append((o_new, dqkv_new))
+        late, _ = lax.optimization_barrier(([cur[1] for cur in att], part))
+        gb = sum(jnp.sum(one.astype(F32), axis=(0, 3)).reshape(3 * dim) for one in late)
         y, gx, gg, gbias = [], [], 0.0, 0.0
         for b in range(batch):
             o_t = got[b][0].reshape(hidden, tok)
@@ -472,15 +533,17 @@
             gx.append((dy_blk[b].astype(F32) + inv_std[b] * (d_hat - d_mean - x_hat[b] * d_proj)).astype(BF16))
         g_out = jnp.sum(dy_blk.astype(F32), axis=(0, 1))
         rows = jnp.stack([gg, gbias, g_out, jnp.pad(gb, (0, hidden - 3 * dim))] + [jnp.zeros((hidden,), F32)] * 4)
-        sums = exchange(rows, peers, 4, "sums")
+        y, gx = jnp.stack(y), jnp.stack(gx)
+        first, _, _ = lax.optimization_barrier((gw_all[0], y, gx))
+        gw_out = place(first, None, 3, 0)
+        rows, gw_out = lax.optimization_barrier((rows, gw_out))
+        go_all, sums = collect(part, rows, peers, 3)
+        go_all = lay_down(go_all.reshape(heads, dim, hidden)).reshape(hidden, hidden)
         total = jnp.sum(sums[:, :3], axis=0)
         gb_all = sums[:, 3, :3 * dim].reshape(heads, 3, dim)
-        go_all = keep_copy(go_all.reshape(hidden, hidden))
-        first, _, _, _ = lax.optimization_barrier((gw_all[0], go_all, y, gx))
-        gw_out = place(first, None, 3, 0)
-        gw_out = place(gw_all[1], gw_out, 3, cut)
-        gw_out = jnp.transpose(gw_out, (3, 0, 1, 2))
-        return jnp.stack(y), jnp.stack(gx), gw_out, gb_all, go_all, total[2], total[0], total[1]
+        second, go_all = lax.optimization_barrier((gw_all[1], go_all))
+        gw_out = jnp.transpose(place(second, gw_out, 3, cut), (3, 0, 1, 2))
+        return y, gx, gw_out, gb_all, go_all, total[2], total[0], total[1]
 
     act_spec = P("dp", "sp", None)
     tok_spec = P("dp", "sp")

time: 711 us -> 638 us (0.90)
  Pallas kernels: 570 us -> 513 us
  matrix products: 63.1 us -> 33.6 us
  waiting for transfers between devices: 29 us -> 41.7 us
    pallas_call x1, Pallas kernels: 299 us -> 203 us  [tail(): pl.pallas_call(functools.partial(tail_body, peers=peers), name='tail', ou...]
    pallas_call x5 -> x6, Pallas kernels: 174 us -> 263 us  [the longest x2 158 us: attention(): pl.pallas_call(functools.partial(attn_body, blk=blk, tok=tok, n_swap=len(...]
    dot_general x4 -> x0, matrix products: 35.7 us -> none  [the longest x2 18.9 us: block_fn(): lax.dot_general(w_head, xf[b], NT, preferred_element_type=F32) + b_head]
    pallas_call x1, Pallas kernels: 58.3 us -> 32.5 us  [swap(): pl.pallas_call(functools.partial(swap_body, peers=peers, n=len(xs)), name...]
    pallas_call x2 -> x1, Pallas kernels: 39 us -> 14.7 us  [exchange(): pl.pallas_call(functools.partial(exchange_body, peers=peers), name=name,...]
    all_gather x1, waiting for transfers between devices: 28.1 us -> 35.3 us  [block_fn(): xf = [lax.all_gather(x_norm[0], 'sp', axis=0, tiled=True)]]
  transfers between devices with their start and end apart: 4 -> 4, of which waited for: 1 -> 2; matrix products, arithmetic and copies ran while one was open for 9% -> 8% of each run, Pallas kernels for 68% -> 67%
where the time goes in v4:
time: 638 us; the launch traced here: 637 us
  Pallas kernels  513 us (80%)
  waiting for transfers between devices  41.7 us (7%)
  matrix products  33.6 us (5%)
  local copies, waits for them, and re-layouts  21.3 us (3%)
  between operations  14.4 us (2%)
  other arithmetic  13 us (2%)
    pallas_call x1, Pallas kernels, tail(): pl.pallas_call(functools.partial(tail_body, peers=peers), name='tail', ou...  203 us
    pallas_call x2, Pallas kernels, attention(): pl.pallas_call(functools.partial(attn_body, blk=blk, tok=tok, n_swap=len(...  158 us
    pallas_call x1, Pallas kernels, collect(): pl.pallas_call(functools.partial(collect_body, peers=peers), name='collec...  80.9 us
    all_gather x1, waiting for transfers between devices, block_fn(): xf = [lax.all_gather(x_norm[0], 'sp', axis=0, tiled=True)]  35.3 us
    pallas_call x1, Pallas kernels, swap(): pl.pallas_call(functools.partial(swap_body, peers=peers, n=len(xs)), name...  32.5 us
    pallas_call x2, Pallas kernels, place(): pl.pallas_call(functools.partial(place_body, first=first), name='place',...  20.8 us
    dot_general x2, matrix products, block_fn(): lax.dot_general(dqkv_t, w_t.reshape(3 * hidden, hidden), (((0,), (0,)), (...  19.1 us
    pallas_call x1, Pallas kernels, exchange(): pl.pallas_call(functools.partial(exchange_body, peers=peers), name=name,...  14.7 us
  transfers between devices with their start and end apart: 4, of which 2 were waited for; matrix products, arithmetic and copies ran while one was open for 8% of the time, Pallas kernels for 67%

profile of v4, /device:TPU:21, one launch (start us, length us, event | category | flops | bytes accessed | tf_op | source)
XLA Modules:
  0.0 637.3 jit_solution(9306383891691203253)
XLA Ops:
  7.2 0.1 all-gather.12.cloned.1.call-start
  7.3 1.8 convert_reduce_fusion.3
  9.1 0.5 multiply_reduce_fusion
  9.7 2.3 subtract_multiply_fusion
  12.0 1.3 fusion.22
  13.3 0.1 all-gather.12.cloned.1.call-update
  13.4 0.1 all-gather.10.cloned.1.call-start
  13.4 0.7 all-gather.10.cloned.1.call-update
  14.2 0.1 all-gather.8.cloned.1.call-start
  14.3 0.1 pad.11.clone
  14.4 0.1 add_add_fusion.x_ref
  14.5 14.7 %marks.1 = s32[16,8,256]{2,1,0:T(8,128)S(1)} custom-call(s32[8,256]{1,0:T(8,128)S(1)} %add_add_fusion.x_ref), custom_call_target="tpu_custom_call" | custom-call | tf_op jit(solution)/shard_map/marks/pallas_call | solution.py:413
  29.2 0.1 compare_reduce_fusion
  29.4 0.1 slice.85
  29.5 0.1 slice.89
  29.6 0.2 reshape.176.b_ref
  29.9 2.3 constant_dynamic-slice_fusion
  32.1 4.8 convolution_convert_fusion
  36.9 1.5 convolution_convert_fusion.1
  38.4 32.5 %swap_do.1.dot_ref = bf16[16,96,256]{2,1,0:T(8,128)(2,1)S(1)} custom-call(bf16[16,96,256]{2,1,0:T(8,128)(2,1)S(1)} %bitcast.93), custom_call_target="tpu_custom_call" | custom-call | flops 9437184000 | bytes 1572864 | tf_op jit(solution)/shard_map/swap_do/pallas_call | solution.py:387
  70.9 0.9 copy-done.3
  71.8 35.3 %all-gather.12.cloned.1.call-done = bf16[1,4096,1536]{2,1,0:T(8,128)(2,1)} async-done(((bf16[1,256,1536]{2,1,0:T(8,128)(2,1)}), bf16[1,4096,1536]{2,1,0:T(8,128)(2,1)}) %all-gather.12.cloned.1.call-update) | async-done | bytes 12582928 | tf_op jit(solution)/shard_map/all_gather | solution.py:488
  107.1 0.1 broadcast_in_dim.20.pref_ref
  107.2 1.9 broadcast_in_dim.19.posk_ref
  109.1 1.4 broadcast_in_dim.21.gw_old
  110.5 78.1 %attention.2 = (bf16[16,96,256]{2,1,0:T(8,128)(2,1)S(1)}, bf16[16,3,96,256]{3,2,1,0:T(8,128)(2,1)}, f32[288,1536]{1,0:T(8,128)}, bf16[16,96,256]{2,1,0:T(8,128)(2,1)S(1)}) custom-call(f32[1]{0:T(128)} %bitcast.1.slope_ref, bf16[288,1536]{1,0:T(8,128)(2,1)} %bitcast.98, f32[288,1]{1,0:T(8,128)S(1)} %reshape.176.b_ref, bf16[4096,1536]{1,0:T(8,128)(2,1)} %bitcast.107, ...), custom_call_target="tpu_custom_call" | custom-call | flops 28991029248 | bytes 25165824 | tf_op jit(solution)/shard_map/attention/pallas_call | solution.py:156
  188.6 0.9 copy-done.6
  189.5 0.9 copy-done.7
  190.4 5.5 all-gather.10.cloned.1.call-done
  195.9 0.1 broadcast_in_dim.23.pref_ref
  195.9 1.9 broadcast_in_dim.22.posk_ref
  197.9 79.6 %attention.3 = (bf16[16,96,256]{2,1,0:T(8,128)(2,1)S(1)}, bf16[16,3,96,256]{3,2,1,0:T(8,128)(2,1)}, f32[288,1536]{1,0:T(8,128)}, bf16[16,96,256]{2,1,0:T(8,128)(2,1)S(1)}, bf16[16,3,96,256]{3,2,1,0:T(8,128)(2,1)}) custom-call(f32[1]{0:T(128)} %bitcast.1.slope_ref, bf16[288,1536]{1,0:T(8,128)(2,1)} %bitcast.99, f32[288,1]{1,0:T(8,128)S(1)} %reshape.176.b_ref, ...), custom_call_target="tpu_custom_call" | custom-call | flops 28991029248 | bytes 25165824 | tf_op jit(solution)/shard_map/attention/pallas_call | solution.py:156
  277.5 0.9 copy-done.4
  278.4 2.4 slice.96
  280.8 0.1 all-gather.8.cloned.1.call-update
  280.8 0.1 all-gather.14.cloned.1.call-start
  280.9 3.5 convert_element_type.64
  284.4 0.3 convert_reduce_fusion.2
  284.7 1.9 slice.95
  286.6 0.1 all-gather.14.cloned.1.call-update
  286.7 1.1 copy-done.5
  287.8 202.7 %tail.1 = (bf16[16,96,256]{2,1,0:T(8,128)(2,1)S(1)}, bf16[16,3,96,256]{3,2,1,0:T(8,128)(2,1)}, f32[96,1536]{1,0:T(8,128)S(1)}) custom-call(bf16[16,96,256]{2,1,0:T(8,128)(2,1)S(1)} %copy-done.5, bf16[16,3,96,256]{3,2,1,0:T(8,128)(2,1)} %get-tuple-element.46.dqkv_ref, bf16[16,96,256]{2,1,0:T(8,128)(2,1)S(1)} %get-tuple-element.35.o_old, ...), custom_call_target="tpu_custom_call" | custom-call | flops 99999997952 | bytes 67108864 | tf_op jit(solution)/shard_map/tail/pallas_call | solution.py:289
  490.5 0.7 convert_reduce_fusion
  491.2 0.1 copy-done.8
  491.3 0.1 add.111
  491.4 7.9 %fusion.7 = f32[256,1536]{1,0:T(8,128)S(1)} fusion(bf16[16,3,96,256]{3,2,1,0:T(8,128)(2,1)} %get-tuple-element.42, bf16[1536,16,3,96]{0,3,2,1:T(8,128)(2,1)} %param.15), kind=kOutput, calls=%fused_computation.11 | convolution fusion | flops 3623878656 | bytes 18087936 | tf_op jit(solution)/shard_map/dot_general | solution.py:527
  499.4 11.1 %multiply_reduce_fusion.2 = (f32[1536]{0:T(1024)S(1)}, f32[256]{0:T(256)S(1)}, f32[256]{0:T(256)S(1)}, f32[1536]{0:T(1024)S(1)}, f32[256]{0:T(256)S(1)}, /*index...) fusion(f32[2,256,1536]{2,1,0:T(8,128)S(1)} %copy-done.11, f32[1536]{0:T(1024)S(1)} %copy-done.21, ...), kind=kOutput, calls=%fused_computation.30 | convolution fusion | flops 3629376512 | bytes 22841344 | tf_op jit(solution)/shard_map/dot_general | solution.py:527
  510.6 0.1 stack.41.rows_ref
  510.7 4.4 fusion.14
  515.1 3.9 fusion.15
  519.0 1.3 pad_maximum_fusion
  520.3 1.2 copy-done.12
  521.5 1.0 fusion.16
  522.4 1.3 pad_maximum_fusion.1
  523.7 13.4 %place.2.refs_1_ = f32[16,3,96,1536]{3,2,1,0:T(8,128)} custom-call(f32[16,2,96,1536]{3,2,1,0:T(8,128)} %all-gather.8.cloned.1.call-done.refs_0_), custom_call_target="tpu_custom_call" | custom-call | flops 1000000000 | bytes 37748736 | tf_op jit(solution)/shard_map/place/pallas_call | solution.py:443
  537.1 80.9 %collect.1 = (f32[8,2,96,1536]{3,2,1,0:T(8,128)S(1)}, f32[16,8,1536]{2,1,0:T(8,128)S(1)}) custom-call(f32[96,1536]{1,0:T(8,128)S(1)} %copy-done.9, f32[8,1536]{1,0:T(8,128)S(1)} %stack.41.rows_ref), custom_call_target="tpu_custom_call" | custom-call | flops 49999998976 | bytes 10485760 | tf_op jit(solution)/shard_map/collect/pallas_call | solution.py:363
  618.0 3.8 lay_down.1
  621.8 0.1 slice_reduce_fusion.1
  621.9 0.1 slice_reduce_fusion
  621.9 0.0 all-gather.14.cloned.1.call-done
  621.9 0.6 slice_reduce_fusion.2
  622.6 0.1 reshape_squeeze.2
  622.7 0.6 copy.25
  623.3 7.4 %place.3 = f32[16,3,96,1536]{3,2,1,0:T(8,128)} custom-call(f32[16,1,96,1536]{3,2,1,0:T(8,128)} %bitcast.96, f32[16,3,96,1536]{3,2,1,0:T(8,128)} %place.2.refs_1_), custom_call_target="tpu_custom_call", output_to_operand_aliasing={{}: (1, {})} | custom-call | flops 1000000000 | bytes 18874368 | tf_op jit(solution)/shard_map/place/pallas_call | solution.py:443
  (72 shorter events, 0.3 us)
Async XLA Ops:
  7.2 22.4 %copy-start = (f32[16,3,96]{2,0,1:T(8,128)S(1)}, f32[16,3,96]{2,0,1:T(8,128)}, u32[]{:S(2)}) copy-start(f32[16,3,96]{2,0,1:T(8,128)} %param.16) | copy-start | bytes 55300
  7.2 1.9 copy-start.10
  7.2 2.5 copy-start.20
  7.2 2.5 copy-start.22
  7.2 99.9 %all-gather.12.cloned.1.call-start = ((), (), s32[]{:S(2)}) async-start(), calls=%async_computation.2 | async-start | bytes 13369344 | tf_op jit(solution)/shard_map/all_gather | solution.py:488
  13.3 1.1 copy-start.23
  13.3 1.1 copy-start.24
  13.4 18.8 %copy-start.2 = (bf16[2,256,1536]{2,1,0:T(8,128)(2,1)S(1)}, bf16[2,256,1536]{2,1,0:T(8,128)(2,1)}, u32[]{:S(2)}) copy-start(bf16[2,256,1536]{2,1,0:T(8,128)(2,1)} %dy_ref.1) | copy-start | bytes 4718596
  13.4 182.5 %all-gather.10.cloned.1.call-start = ((), (), s32[]{:S(2)}) async-start(), calls=%async_computation.1 | async-start | bytes 13369344 | tf_op jit(solution)/shard_map/all_gather | solution.py:493
  14.2 509.5 %all-gather.8.cloned.1.call-start = ((), (), s32[]{:S(2)}) async-start(), calls=%async_computation | async-start | bytes 20054016 | tf_op jit(solution)/shard_map/all_gather | solution.py:516
  29.8 7.1 %slice-start = ((s8[4718592]{0:T(1024)(128)(4,1)}), s8[4194304]{0:T(1024)(128)(4,1)S(1)}, s32[]{:S(2)}) async-start(s8[4718592]{0:T(1024)(128)(4,1)} %bitcast.108), calls=%async_computation.4 | async-start | bytes 8388608
  32.1 4.8 slice-start.1
  70.9 0.9 copy-start.3
  188.6 0.9 copy-start.6
  189.5 0.9 copy-start.7
  277.5 0.9 copy-start.4
  280.8 341.1 %all-gather.14.cloned.1.call-start = ((), (), s32[]{:S(2)}) async-start(), calls=%async_computation.3 | async-start | bytes 10027008 | tf_op jit(solution)/shard_map/all_gather | solution.py:516
  286.7 1.1 copy-start.5
  287.8 202.7 %copy-start.17 = (bf16[16,3,96,256]{3,2,1,0:T(8,128)(2,1)S(1)}, bf16[16,3,96,256]{3,2,1,0:T(8,128)(2,1)}, u32[]{:S(2)}) copy-start(bf16[16,3,96,256]{3,2,1,0:T(8,128)(2,1)} %get-tuple-element.45.refs_1_) | copy-start | bytes 7077892
  287.8 202.7 %copy-start.18 = (bf16[16,3,96,256]{3,2,1,0:T(8,128)(2,1)S(1)}, bf16[16,3,96,256]{3,2,1,0:T(8,128)(2,1)}, u32[]{:S(2)}) copy-start(bf16[16,3,96,256]{3,2,1,0:T(8,128)(2,1)} %get-tuple-element.46.dqkv_ref) | copy-start | bytes 7077892
  490.5 0.8 copy-start.8
  491.4 8.0 %copy-start.11 = (f32[2,256,1536]{2,1,0:T(8,128)S(1)}, f32[2,256,1536]{2,1,0:T(8,128)}, u32[]{:S(2)}) copy-start(f32[2,256,1536]{2,1,0:T(8,128)} %get-tuple-element.95) | copy-start | bytes 9437188
  491.4 8.0 %copy-start.19 = (bf16[16,3,96,256]{3,2,1,0:T(8,128)(2,1)S(1)}, bf16[16,3,96,256]{3,2,1,0:T(8,128)(2,1)}, u32[]{:S(2)}) copy-start(bf16[16,3,96,256]{3,2,1,0:T(8,128)(2,1)} %get-tuple-element.41) | copy-start | bytes 7077892
  491.4 8.0 %copy-start.21 = (f32[1536]{0:T(1024)S(1)}, f32[1536]{0:T(1024)}, u32[]{:S(2)}) copy-start(f32[1536]{0:T(1024)} %param.13) | copy-start | bytes 18436
  499.3 11.2 %copy-start.13 = (f32[256,1536]{1,0:T(8,128)}, f32[256,1536]{1,0:T(8,128)S(1)}, u32[]{:S(2)}) copy-start(f32[256,1536]{1,0:T(8,128)S(1)} %fusion.7) | copy-start | bytes 4718596
  499.4 11.3 %copy-start.25 = (f32[1536]{0:T(1024)S(1)}, f32[1536]{0:T(1024)}, u32[]{:S(2)}) copy-start(f32[1536]{0:T(1024)} %param.18) | copy-start | bytes 18436
  510.7 4.4 copy-start.16
  515.1 5.2 copy-start.14
  515.1 5.2 copy-start.15
  519.0 2.5 copy-start.12
  523.7 13.4 %copy-start.9 = (f32[96,1536]{1,0:T(8,128)S(1)}, f32[96,1536]{1,0:T(8,128)}, u32[]{:S(2)}) copy-start(f32[96,1536]{1,0:T(8,128)} %copy-done.8) | copy-start | bytes 1769476
  623.3 7.4 %copy-start.1 = (f32[16,3,96]{2,0,1:T(8,128)S(1)}, f32[16,3,96]{2,0,1:T(8,128)}, u32[]{:S(2)}) copy-start(f32[16,3,96]{2,0,1:T(8,128)} %param.16) | copy-start | bytes 55300
Sparse Core Ops, SparseCore 0:
  13.5 93.6 all-gather.11
  108.8 87.0 all-gather.9
  281.0 207.1 all-gather.7
  489.7 62.2 all-gather.13

commit v5 on v4

--- a/solution.py
+++ b/solution.py
@@ -14,48 +14,79 @@
 NT = (((1,), (1,)), ((), ()))
 
 
-def attn_body(slope_ref, w_ref, b_ref, x_ref, dot_ref, posk_ref, pref_ref, gw_old, *refs, blk, tok, n_swap):
+def attn_body(slope_ref, w_ref, b_ref, x_ref, dot_ref, pos_ref, pref_ref, *refs, blk, tok, n_swap, n_old):
     peers = dot_ref.shape[0]
-    old, (o_ref, dqkv_ref, gw_ref), got = refs[:n_swap], refs[n_swap:n_swap + 3], refs[n_swap + 3:2 * n_swap + 3]
-    swaps = [(old[k], got[k]) + refs[len(refs) - 4 * n_swap + 4 * k:][:4] for k in range(n_swap)]
-    x_buf, qkvt_ref, k_tok, v_tok, s_buf, q_pad, do_pad, o_acc, dq_acc, dk_acc, dv_acc, x_sem = refs[2 * n_swap + 3:][:12]
+    gw_old, old, refs = refs[:n_old], refs[n_old:n_old + n_swap], refs[n_old + n_swap:]
+    (dqkv_ref, gwa_ref, gwb_ref, o_new), got, refs = refs[:4], refs[4:4 + n_swap], refs[4 + n_swap:]
+    x_buf, qkvt_ref, k_tok, v_tok, posk_ref, s_buf, q_pad, do_pad, o_acc, dq_acc, dk_acc, dv_acc, o_ref, x_sem, os_sem, or_sem = refs[:16]
+    swaps = [(old[k], got[k]) + refs[16 + 4 * k:20 + 4 * k] for k in range(n_swap)]
     dim = dot_ref.shape[1]
     seq = dot_ref.shape[0] * tok
     pad = k_tok.shape[1] - dim
     nq = blk // tok
+    steps = seq // blk
     scale = dim ** -0.5
-    i = pl.program_id(0)
+    me = lax.axis_index("sp")
+    step = pl.program_id(0)
+    i = lax.rem(me // nq + step, steps)
     half = blk // 2
 
     def x_copy(k):
         rows = pl.ds(pl.multiple_of(k * blk, blk), blk)
         return pltpu.make_async_copy(x_ref.at[rows], x_buf.at[rows], x_sem.at[k])
 
-    @pl.when(i == 0)
+    def o_send(to):
+        return pltpu.make_async_remote_copy(
+            src_ref=o_ref.at[to], dst_ref=o_new.at[me], send_sem=os_sem.at[to], recv_sem=or_sem.at[me],
+            device_id={"sp": to}, device_id_type=pl.DeviceIdType.MESH)
+
+    def o_keep():
+        return pltpu.make_async_copy(o_ref.at[me], o_new.at[me], os_sem.at[me])
+
+    def o_start(at):
+        for t in range(nq):
+            to = lax.rem(me // nq + at, steps) * nq + t
+
+            @pl.when(to != me)
+            def _():
+                o_send(to).start()
+
+            @pl.when(to == me)
+            def _():
+                o_keep().start()
+
+    @pl.when(step == 0)
     def _():
-        for k in range(seq // blk):
+        for k in range(steps):
             x_copy(k).start()
-        if n_swap:
-            meet(peers)
-            for one in swaps:
-                swap_start(*one, peers)
+        meet(peers)
+        for one in swaps:
+            swap_start(*one, peers)
         dk_acc[...] = jnp.zeros_like(dk_acc)
         dv_acc[...] = jnp.zeros_like(dv_acc)
         q_pad[...] = jnp.zeros_like(q_pad)
         do_pad[...] = jnp.zeros_like(do_pad)
 
+        @pl.loop(0, steps)
+        def _(k):
+            rows = pl.ds(pl.multiple_of(k * blk, blk), blk)
+            x_copy(k).wait()
+            qkvt_ref[:, rows] = (lax.dot_general(w_ref[...], x_buf[rows, :], NT, preferred_element_type=F32) + b_ref[...]).astype(BF16)
+
+            @pl.loop(0, blk // 128)
+            def _(t):
+                cols = pl.ds(pl.multiple_of(k * blk + t * 128, 128), 128)
+                for base, dst in ((dim, k_tok), (2 * dim, v_tok)):
+                    part = qkvt_ref[base:base + dim, cols].astype(F32)
+                    whole = jnp.concatenate([part, jnp.zeros((pad, 128), F32)], axis=0)
+                    dst[cols, :] = jnp.transpose(whole).astype(BF16)
+                posk_ref[cols, :] = jnp.transpose(jnp.broadcast_to(pos_ref[:, cols], (128, 128)))
+
+    @pl.when(step > 0)
+    def _():
+        o_start(step - 1)
+
     qcols = pl.ds(pl.multiple_of(i * blk, blk), blk)
-    x_copy(i).wait()
-    qkvt_ref[:, qcols] = (lax.dot_general(w_ref[...], x_buf[qcols, :], NT, preferred_element_type=F32) + b_ref[...]).astype(BF16)
-
-    @pl.loop(0, blk // 128)
-    def _(t):
-        cols = pl.ds(pl.multiple_of(i * blk + t * 128, 128), 128)
-        for base, dst in ((dim, k_tok), (2 * dim, v_tok)):
-            part = qkvt_ref[base:base + dim, cols].astype(F32)
-            whole = jnp.concatenate([part, jnp.zeros((pad, 128), F32)], axis=0)
-            dst[cols, :] = jnp.transpose(whole).astype(BF16)
-
     q_pad[0:dim, :] = qkvt_ref[0:dim, qcols]
     for t in range(nq):
         do_pad[0:dim, t * tok:(t + 1) * tok] = dot_ref[i * nq + t]
@@ -122,7 +153,7 @@
         o_ref[i * nq + t] = o_lo[:, t * tok:(t + 1) * tok]
         dqkv_ref[i * nq + t, 0] = dq_lo[:, t * tok:(t + 1) * tok]
 
-    @pl.when(i == pl.num_programs(0) - 1)
+    @pl.when(step == steps - 1)
     def _():
         @pl.loop(0, seq // tok)
         def _(t):
@@ -130,50 +161,65 @@
             dqkv_ref[t, 1] = (dk_acc[:, cols] * scale).astype(BF16)
             dqkv_ref[t, 2] = dv_acc[:, cols].astype(BF16)
 
-        gw_ref[...] = gw_old[...]
-
-        @pl.loop(0, seq // blk)
+        o_start(step)
+        if n_old:
+            gwa_ref[...] = gw_old[0][...]
+            gwb_ref[...] = gw_old[1][...]
+        else:
+            gwa_ref[...] = jnp.zeros_like(gwa_ref)
+            gwb_ref[...] = jnp.zeros_like(gwb_ref)
+
+        @pl.loop(0, steps)
         def _(j):
-            total = gw_ref[...]
-            for t in range(nq):
-                rows = pl.ds(pl.multiple_of(j * blk + t * tok, tok), tok)
-                total = total + jnp.dot(dqkv_ref[j * nq + t].reshape(3 * dim, tok), x_buf[rows, :], preferred_element_type=F32)
-            gw_ref[...] = total
-
+            rows = pl.ds(pl.multiple_of(j * blk, blk), blk)
+            for ref, lo, n in ((gwa_ref, 0, 2), (gwb_ref, 2, 1)):
+                lhs = jnp.concatenate([dqkv_ref[j * nq + t, lo:lo + n].reshape(n * dim, tok) for t in range(nq)], axis=1)
+                ref[...] += jnp.dot(lhs, x_buf[rows, :], preferred_element_type=F32)
+
+        o_keep().wait()
+        for d in range(1, peers):
+            o_send(lax.rem(me + d, peers)).wait_send()
+            frm = lax.rem(me + d, peers)
+            pltpu.make_async_remote_copy(
+                src_ref=o_ref.at[frm], dst_ref=o_new.at[frm], send_sem=os_sem.at[frm], recv_sem=or_sem.at[frm],
+                device_id={"sp": frm}, device_id_type=pl.DeviceIdType.MESH).wait_recv()
         for one in swaps:
             swap_wait(*one, peers)
 
 
-def attention(slope2, w_head, b_head, x, dot_, posk, pref, gw, old, *, blk, tok, collective_id):
+def attention(slope2, w_head, b_head, x, dot_, pos, pref, gw, old, *, blk, tok, collective_id):
     blocks, dim, _ = dot_.shape
     seq, hidden = x.shape
     wide = 128 * pl.cdiv(dim, 128)
     hbm = pl.BlockSpec(memory_space=pltpu.HBM)
     full = lambda a: pl.BlockSpec(a.shape, lambda i: (0,) * len(a.shape), pipeline_mode=pl.Buffered(1))
     like = lambda a: jax.ShapeDtypeStruct(a.shape, a.dtype)
-    outs = [jax.ShapeDtypeStruct((blocks, dim, tok), BF16), jax.ShapeDtypeStruct((blocks, 3, dim, tok), BF16), like(gw)]
+    outs = [jax.ShapeDtypeStruct((blocks, 3, dim, tok), BF16), jax.ShapeDtypeStruct((2 * dim, hidden), F32),
+            jax.ShapeDtypeStruct((dim, hidden), F32)]
     pairs = (seq // blk) * (seq // blk + 1) // 2
+    dma = pltpu.SemaphoreType.DMA
     res = pl.pallas_call(
-        functools.partial(attn_body, blk=blk, tok=tok, n_swap=len(old)),
+        functools.partial(attn_body, blk=blk, tok=tok, n_swap=len(old), n_old=len(gw)),
         name="attention",
-        out_shape=outs + [like(a) for a in old],
+        out_shape=outs + [like(dot_)] + [like(a) for a in old],
         grid=(seq // blk,),
-        in_specs=[pl.BlockSpec(memory_space=pltpu.SMEM), full(w_head), full(b_head), hbm, full(dot_), full(posk), full(pref), full(gw)]
-        + [hbm] * len(old),
-        out_specs=[full(a) for a in outs] + [hbm] * len(old),
+        in_specs=[pl.BlockSpec(memory_space=pltpu.SMEM), full(w_head), full(b_head), hbm, full(dot_), full(pos), full(pref)]
+        + [full(a) for a in gw] + [hbm] * len(old),
+        out_specs=[full(a) for a in outs] + [hbm] * (1 + len(old)),
         scratch_shapes=[
             pltpu.VMEM((seq, hidden), BF16), pltpu.VMEM((3 * dim, seq), BF16),
-            pltpu.VMEM((seq, wide), BF16), pltpu.VMEM((seq, wide), BF16),
+            pltpu.VMEM((seq, wide), BF16), pltpu.VMEM((seq, wide), BF16), pltpu.VMEM((seq, 128), F32),
             pltpu.VMEM((seq, blk), F32),
             pltpu.VMEM((wide, blk), BF16), pltpu.VMEM((wide, blk), BF16),
             pltpu.VMEM((dim, blk), F32), pltpu.VMEM((dim, blk), F32),
-            pltpu.VMEM((dim, seq), F32), pltpu.VMEM((dim, seq), F32), pltpu.SemaphoreType.DMA((seq // blk,))]
+            pltpu.VMEM((dim, seq), F32), pltpu.VMEM((dim, seq), F32), pltpu.VMEM(dot_.shape, BF16),
+            dma((seq // blk,)), dma((blocks,)), dma((blocks,))]
         + sum((swap_scratch(a) for a in old), []),
         cost_estimate=pl.CostEstimate(flops=pairs * 6 * 2 * blk * blk * 256, bytes_accessed=24 << 20, transcendentals=pairs * blk * blk),
         compiler_params=pltpu.CompilerParams(dimension_semantics=("arbitrary",), vmem_limit_bytes=52 << 20,
                                              collective_id=collective_id, has_side_effects=True),
-    )(slope2, w_head, b_head, x, dot_, posk, pref, gw, *old)
-    return res[:2], res[2], res[3:]
+    )(slope2, w_head, b_head, x, dot_, pos, pref, *gw, *old)
+    return res[0], res[1:3], res[3], res[4:]
 
 
 def peer_at(d, peers):
@@ -217,8 +263,7 @@
             pltpu.SemaphoreType.DMA]
 
 
-def tail_body(o_ref, dqkv_ref, o_old, dy_ref, o_new, dqkv_new, part, mine, other, pair, landed, own_o, own_d,
-              os_sem, or_sem, oo_sem, ds_sem, dr_sem, do_sem, ps_sem, pr_sem, rs_sem, rr_sem, *, peers):
+def tail_body(dqkv_ref, o_old, o_new, dy_ref, dqkv_new, part, mine, other, pair, landed, own_d, ds_sem, dr_sem, do_sem, ps_sem, pr_sem, rs_sem, rr_sem, *, peers):
     ring = peers // 2
     me = lax.axis_index("sp")
     z, c = me // 2, me % 2
@@ -229,9 +274,7 @@
     step = (1, -1)
     remote = functools.partial(pltpu.make_async_remote_copy, device_id_type=pl.DeviceIdType.MESH)
     meet(peers)
-    swap_start(o_ref, o_new, own_o, os_sem, or_sem, oo_sem, peers)
     swap_start(dqkv_ref, dqkv_new, own_d, ds_sem, dr_sem, do_sem, peers)
-    swap_wait(o_ref, o_new, own_o, os_sem, or_sem, oo_sem, peers)
 
     def product(out, side):
         @pl.loop(0, ring)
@@ -279,8 +322,8 @@
             reduce_copy(w, t).wait_send()
 
 
-def tail(o, dqkv, o_old, dy, collective_id):
-    peers, dim, tok = o.shape
+def tail(dqkv, o_old, o_new, dy, collective_id):
+    peers, dim, tok = o_old.shape
     ring = peers // 2
     hidden = dy.shape[-1]
     hbm, vmem = pl.BlockSpec(memory_space=pltpu.HBM), pl.BlockSpec(memory_space=pltpu.VMEM)
@@ -289,84 +332,83 @@
     return pl.pallas_call(
         functools.partial(tail_body, peers=peers),
         name="tail",
-        out_shape=[jax.ShapeDtypeStruct(o.shape, BF16), jax.ShapeDtypeStruct(dqkv.shape, BF16),
-                   jax.ShapeDtypeStruct((dim, hidden), F32)],
-        in_specs=[hbm, hbm, vmem, vmem],
-        out_specs=[vmem, hbm, vmem],
+        out_shape=[jax.ShapeDtypeStruct(dqkv.shape, BF16), jax.ShapeDtypeStruct((dim, hidden), F32)],
+        in_specs=[hbm, vmem, vmem, vmem],
+        out_specs=[hbm, vmem],
         scratch_shapes=[rows(ring), rows(ring), rows(ring), pltpu.VMEM((2, ring - 1, dim, hidden // 2), F32),
-                        pltpu.VMEM(o.shape[1:], BF16), pltpu.VMEM(dqkv.shape[1:], BF16),
-                        dma((peers - 1,)), dma((peers - 1,)), dma, dma((peers - 1,)), dma((peers - 1,)), dma, dma, dma,
+                        pltpu.VMEM(dqkv.shape[1:], BF16), dma((peers - 1,)), dma((peers - 1,)), dma, dma, dma,
                         dma((2, ring - 1)), dma((2, ring - 1))],
         cost_estimate=pl.CostEstimate(flops=10**11, bytes_accessed=64 << 20, transcendentals=0),
         compiler_params=pltpu.CompilerParams(collective_id=collective_id, has_side_effects=True, vmem_limit_bytes=48 << 20),
-    )(o, dqkv, o_old, dy)
-
-
-def collect_body(part, rows_ref, full, sums, as_sem, ar_sem, fs_sem, fr_sem, xs_sem, xr_sem, *, peers):
+    )(dqkv, o_old, o_new, dy)
+
+
+def collect_body(part, rows_ref, full, sums, as_sem, ar_sem, fs_sem, fr_sem, xs_sem, xr_sem, *, peers, cuts):
     ring = peers // 2
     me = lax.axis_index("sp")
     z, c = me // 2, me % 2
     half = part.shape[-1] // 2
-    cols = (pl.ds(0, half), pl.ds(half, half))
+    few = part.shape[0] // cuts
     turn = lambda k: lax.rem(z + k + 2 * ring, ring)
     step = (1, -1)
     remote = functools.partial(pltpu.make_async_remote_copy, device_id_type=pl.DeviceIdType.MESH)
 
-    def block_copy(w, t, side, send_sem, recv_sem, to):
-        ref = full.at[turn(-step[w] * t), side, :, cols[w]]
-        return remote(src_ref=ref, dst_ref=ref, send_sem=send_sem.at[w, t], recv_sem=recv_sem.at[w, t], device_id={"sp": to})
-
-    gather_copy = lambda w, t: block_copy(w, t, c, as_sem, ar_sem, 2 * turn(step[w]) + c)
-    over_copy = lambda w, t, side: block_copy(w, t, side, fs_sem, fr_sem, 2 * z + 1 - c)
+    def block_copy(w, t, u, side, send_sem, recv_sem, to):
+        ref = full.at[turn(-step[w] * t), side, pl.ds(u * few, few), pl.ds(w * half, half)]
+        return remote(src_ref=ref, dst_ref=ref, send_sem=send_sem.at[w, t, u], recv_sem=recv_sem.at[w, t, u], device_id={"sp": to})
+
+    gather_copy = lambda w, t, u: block_copy(w, t, u, c, as_sem, ar_sem, 2 * turn(step[w]) + c)
+    over_copy = lambda w, t, u, side: block_copy(w, t, u, side, fs_sem, fr_sem, 2 * z + 1 - c)
+    parts = [(w, u) for u in range(cuts) for w in range(2)]
     full[z, c] = part[...]
+    sums[me] = rows_ref[...]
     meet(peers)
+    for w, u in parts:
+        gather_copy(w, 0, u).start()
     small = [remote(src_ref=rows_ref, dst_ref=sums.at[me], send_sem=xs_sem.at[d - 1], recv_sem=xr_sem.at[d - 1],
                     device_id=peer_at(d, peers)) for d in range(1, peers)]
     for copy in small:
         copy.start()
-    for w in range(2):
-        gather_copy(w, 0).start()
-    for w in range(2):
-        over_copy(w, 0, c).start()
-    sums[me] = rows_ref[...]
+    for w, u in parts:
+        over_copy(w, 0, u, c).start()
 
     @pl.loop(1, ring)
     def _(t):
-        for w in range(2):
-            gather_copy(w, t - 1).wait_recv()
+        for w, u in parts:
+            gather_copy(w, t - 1, u).wait_recv()
 
             @pl.when(t < ring - 1)
             def _():
-                gather_copy(w, t).start()
-
-            over_copy(w, t, c).start()
+                gather_copy(w, t, u).start()
+
+            over_copy(w, t, u, c).start()
 
     for copy in small:
         copy.wait()
 
     @pl.loop(0, ring - 1)
     def _(t):
-        for w in range(2):
-            gather_copy(w, t).wait_send()
+        for w, u in parts:
+            gather_copy(w, t, u).wait_send()
 
     @pl.loop(0, ring)
     def _(t):
-        for w in range(2):
-            over_copy(w, t, c).wait_send()
-            over_copy(w, t, 1 - c).wait_recv()
-
-
-def collect(part, rows, peers, collective_id):
+        for w, u in parts:
+            over_copy(w, t, u, c).wait_send()
+            over_copy(w, t, u, 1 - c).wait_recv()
+
+
+def collect(part, rows, peers, collective_id, cuts=3):
     ring = peers // 2
     vmem = pl.BlockSpec(memory_space=pltpu.VMEM)
     dma = pltpu.SemaphoreType.DMA
     return pl.pallas_call(
-        functools.partial(collect_body, peers=peers),
+        functools.partial(collect_body, peers=peers, cuts=cuts),
         name="collect",
         out_shape=[jax.ShapeDtypeStruct((ring, 2) + part.shape, F32), jax.ShapeDtypeStruct((peers,) + rows.shape, F32)],
         in_specs=[vmem, vmem],
         out_specs=[vmem, vmem],
-        scratch_shapes=[dma((2, ring - 1)), dma((2, ring - 1)), dma((2, ring)), dma((2, ring)), dma((peers - 1,)), dma((peers - 1,))],
+        scratch_shapes=[dma((2, ring - 1, cuts)), dma((2, ring - 1, cuts)), dma((2, ring, cuts)), dma((2, ring, cuts)), dma((peers - 1,)), dma((peers - 1,))],
         cost_estimate=pl.CostEstimate(flops=5 * 10**10, bytes_accessed=10 << 20, transcendentals=0),
         compiler_params=pltpu.CompilerParams(collective_id=collective_id, has_side_effects=True, vmem_limit_bytes=24 << 20),
     )(part, rows)
@@ -496,34 +538,30 @@
         b_head = lax.dynamic_index_in_dim(b_qkv, rank, 0, keepdims=False).reshape(3 * dim, 1)
         slope = jnp.exp2(-8.0 * (rank + 1).astype(F32) / heads)
         slope2 = (slope * LOG2E).reshape(1)
-        gw = jnp.zeros((3 * dim, hidden), F32)
-        gb = jnp.zeros((3 * dim,), F32)
-        att, got = [], []
+        gw, att, o_got, d_got = (), [], [], []
         for b in range(batch):
-            pos = marks[:, b].reshape(seq).astype(F32)
-            keep = marks[:, batch + b].reshape(seq)
-            posk = jnp.broadcast_to(jnp.where(keep > 0, pos, MASKED)[:, None], (seq, 128))
-            pref = jnp.broadcast_to(pos[::blk][:, None], (seq // blk, 128))
-            old = list(do_loc[b + 1:b + 2]) + (list(att[-1]) if b else [])
-            cur, gw, swapped = attention(slope2, w_head, b_head, xf[b], do_t[b], posk, pref, gw, old, blk=blk, tok=tok, collective_id=4 + b)
+            pos = marks[:, b].reshape(1, seq).astype(F32)
+            keep = marks[:, batch + b].reshape(1, seq)
+            pref = jnp.broadcast_to(pos[0, ::blk][:, None], (seq // blk, 128))
+            old = list(do_loc[b + 1:b + 2]) + att[b - 1:b]
+            cur, gw, o_new, swapped = attention(slope2, w_head, b_head, xf[b], do_t[b], jnp.where(keep > 0, pos, MASKED), pref, gw, old,
+                                                blk=blk, tok=tok, collective_id=4 + b)
             if b + 1 < batch:
                 do_t.append(swapped[0])
-            if b:
-                got.append(swapped[-2:])
+            d_got += swapped[-1:] if b else []
+            o_got.append(o_new)
             att.append(cur)
-        cut = 2
-        gw3 = gw.reshape(3, dim, hidden)
-        gw_all = [lax.all_gather(gw3[:cut], "sp", axis=0), lax.all_gather(gw3[cut:], "sp", axis=0)]
-        o_last, dqkv_last, _ = lax.optimization_barrier((*att[-1], gw3))
-        o_new, dqkv_new, part = tail(o_last, dqkv_last, got[0][0], dy_blk, 2)
-        got.append((o_new, dqkv_new))
-        late, _ = lax.optimization_barrier(([cur[1] for cur in att], part))
+        gw_all = [lax.all_gather(one, "sp", axis=0, tiled=True).reshape(heads, -1, dim, hidden) for one in gw]
+        cut = gw_all[0].shape[1]
+        dqkv_new, part = tail(att[-1], *o_got, dy_blk, 2)
+        d_got.append(dqkv_new)
+        late, x_late, _ = lax.optimization_barrier((att, x_blk, part))
         gb = sum(jnp.sum(one.astype(F32), axis=(0, 3)).reshape(3 * dim) for one in late)
         y, gx, gg, gbias = [], [], 0.0, 0.0
         for b in range(batch):
-            o_t = got[b][0].reshape(hidden, tok)
-            dqkv_t = got[b][1].reshape(3 * hidden, tok)
-            y.append((x_f32[b] + lax.dot_general(o_t, w_out, (((0,), (0,)), ((), ())), preferred_element_type=F32) + b_out).astype(BF16))
+            o_t = o_got[b].reshape(hidden, tok)
+            dqkv_t = d_got[b].reshape(3 * hidden, tok)
+            y.append((x_late[b].astype(F32) + lax.dot_general(o_t, w_out, (((0,), (0,)), ((), ())), preferred_element_type=F32) + b_out).astype(BF16))
             d_norm = lax.dot_general(dqkv_t, w_t.reshape(3 * hidden, hidden), (((0,), (0,)), ((), ())), preferred_element_type=F32)
             gg += jnp.sum(d_norm * x_hat[b], axis=0)
             gbias += jnp.sum(d_norm, axis=0)

time: 638 us -> 629 us (0.986)
  waiting for transfers between devices: 41.7 us -> 58.2 us
  local copies, waits for them, and re-layouts: 21.3 us -> 8.37 us
  Pallas kernels: 513 us -> 505 us
    pallas_call x1, Pallas kernels: 203 us -> 176 us  [tail(): pl.pallas_call(functools.partial(tail_body, peers=peers), name='tail', ou...]
    all_gather x1, waiting for transfers between devices: 5.49 us -> 21.8 us  [block_fn(): xf.append(lax.all_gather(x_norm[b], 'sp', axis=0, tiled=True))]
    pallas_call x2, Pallas kernels: 158 us -> 170 us  [attention(): pl.pallas_call(functools.partial(attn_body, blk=blk, tok=tok, n_swap=len(...]
    pallas_call x1, Pallas kernels: 80.9 us -> 87.4 us  [collect(): pl.pallas_call(functools.partial(collect_body, peers=peers, cuts=cuts), n...]
  transfers between devices with their start and end apart: 4 -> 4, of which waited for: 2 -> 2; matrix products, arithmetic and copies ran while one was open for 8% -> 6% of each run, Pallas kernels for 67% -> 66%
where the time goes in v5:
time: 629 us
  Pallas kernels  505 us (80%)
  waiting for transfers between devices  58.2 us (9%)
  matrix products  32.7 us (5%)
  between operations  14.4 us (2%)
  other arithmetic  9.49 us (2%)
  local copies, waits for them, and re-layouts  8.37 us (1%)
    pallas_call x1, Pallas kernels, tail(): pl.pallas_call(functools.partial(tail_body, peers=peers), name='tail', ou...  176 us
    pallas_call x2, Pallas kernels, attention(): pl.pallas_call(functools.partial(attn_body, blk=blk, tok=tok, n_swap=len(...  170 us
    pallas_call x1, Pallas kernels, collect(): pl.pallas_call(functools.partial(collect_body, peers=peers, cuts=cuts), n...  87.4 us
    all_gather x1, waiting for transfers between devices, block_fn(): xf = [lax.all_gather(x_norm[0], 'sp', axis=0, tiled=True)]  35.4 us
    pallas_call x1, Pallas kernels, swap(): pl.pallas_call(functools.partial(swap_body, peers=peers, n=len(xs)), name...  32.5 us
    all_gather x1, waiting for transfers between devices, block_fn(): xf.append(lax.all_gather(x_norm[b], 'sp', axis=0, tiled=True))  21.8 us
    pallas_call x2, Pallas kernels, place(): pl.pallas_call(functools.partial(place_body, first=first), name='place',...  20.8 us
    dot_general x2, matrix products, block_fn(): lax.dot_general(dqkv_t, w_t.reshape(3 * hidden, hidden), (((0,), (0,)), (...  18.6 us
  transfers between devices with their start and end apart: 4, of which 2 were waited for; matrix products, arithmetic and copies ran while one was open for 6% of the time, Pallas kernels for 66%

profile of v5, /device:TPU:21, one launch (start us, length us, event | category | flops | bytes accessed | tf_op | source)
XLA Modules:
  0.0 629.0 jit_solution(1908640697170529136)
XLA Ops:
  7.2 0.0 copy-start
  7.2 0.0 copy-start.9
  7.2 0.0 copy-start.17
  7.2 0.1 all-gather.11.cloned.1.call-start
  7.3 1.8 convert_reduce_fusion.2
  9.1 0.5 fusion.6
  9.7 2.3 fusion.4
  12.0 1.2 fusion.25
  13.3 0.1 all-gather.11.cloned.1.call-update
  13.3 0.0 copy-start.2
  13.4 0.1 all-gather.13.cloned.1.call-start
  13.4 0.7 all-gather.13.cloned.1.call-update
  14.2 0.1 all-gather.9.cloned.1.call-start
  14.3 0.1 pad.11.clone
  14.4 0.1 add_add_fusion.x_ref
  14.4 14.7 %marks.1 = s32[16,8,256]{2,1,0:T(8,128)S(1)} custom-call(s32[8,256]{1,0:T(8,128)S(1)} %add_add_fusion.x_ref), custom_call_target="tpu_custom_call" | custom-call | tf_op jit(solution)/shard_map/marks/pallas_call | solution.py:455
  29.2 0.1 slice.75
  29.3 0.1 slice.80
  29.5 0.2 reshape.226.b_ref
  29.6 0.1 slice_compare_fusion
  29.7 0.0 slice-start
  29.7 2.3 constant_dynamic-slice_fusion
  32.0 4.7 convolution_convert_fusion
  36.8 1.4 convolution_convert_fusion.1
  38.2 32.5 %swap_do.1.dot_ref = bf16[16,96,256]{2,1,0:T(8,128)(2,1)S(1)} custom-call(bf16[16,96,256]{2,1,0:T(8,128)(2,1)S(1)} %bitcast.95), custom_call_target="tpu_custom_call" | custom-call | flops 9437184000 | bytes 1572864 | tf_op jit(solution)/shard_map/swap_do/pallas_call | solution.py:429
  70.7 0.9 copy-done.4
  71.7 35.4 %all-gather.11.cloned.1.call-done = bf16[1,4096,1536]{2,1,0:T(8,128)(2,1)} async-done(((bf16[1,256,1536]{2,1,0:T(8,128)(2,1)}), bf16[1,4096,1536]{2,1,0:T(8,128)(2,1)}) %all-gather.11.cloned.1.call-update) | async-done | bytes 12582928 | tf_op jit(solution)/shard_map/all_gather | solution.py:530
  107.1 0.1 broadcast_in_dim.18.pref_ref
  107.2 87.9 %attention.2 = (bf16[16,3,96,256]{3,2,1,0:T(8,128)(2,1)}, f32[192,1536]{1,0:T(8,128)}, f32[96,1536]{1,0:T(8,128)S(1)}, bf16[16,96,256]{2,1,0:T(8,128)(2,1)S(1)}, bf16[16,96,256]{2,1,0:T(8,128)(2,1)}) custom-call(f32[1]{0:T(128)} %bitcast.slope_ref, bf16[288,1536]{1,0:T(8,128)(2,1)} %bitcast.100, f32[288,1]{1,0:T(8,128)S(1)} %reshape.226.b_ref, ...), custom_call_target="tpu_custom_call" | custom-call | flops 28991029248 | bytes 25165824 | tf_op jit(solution)/shard_map/attention/pallas_call | solution.py:201
  195.1 21.8 %all-gather.13.cloned.1.call-done = bf16[1,4096,1536]{2,1,0:T(8,128)(2,1)} async-done(((bf16[1,256,1536]{2,1,0:T(8,128)(2,1)}), bf16[1,4096,1536]{2,1,0:T(8,128)(2,1)}) %all-gather.13.cloned.1.call-update) | async-done | bytes 12582928 | tf_op jit(solution)/shard_map/all_gather | solution.py:535
  216.9 0.1 broadcast_in_dim.20.pref_ref
  216.9 81.9 %attention.3 = (bf16[16,3,96,256]{3,2,1,0:T(8,128)(2,1)}, f32[192,1536]{1,0:T(8,128)}, f32[96,1536]{1,0:T(8,128)}, bf16[16,96,256]{2,1,0:T(8,128)(2,1)}, bf16[16,3,96,256]{3,2,1,0:T(8,128)(2,1)}) custom-call(f32[1]{0:T(128)} %bitcast.slope_ref, bf16[288,1536]{1,0:T(8,128)(2,1)} %bitcast.101, f32[288,1]{1,0:T(8,128)S(1)} %reshape.226.b_ref, ...), custom_call_target="tpu_custom_call" | custom-call | flops 28991029248 | bytes 25165824 | tf_op jit(solution)/shard_map/attention/pallas_call | solution.py:201
  298.9 0.1 all-gather.9.cloned.1.call-update
  298.9 0.2 all-gather.7.cloned.1.call-start
  299.2 0.3 convert_reduce_fusion.3
  299.5 0.1 all-gather.7.cloned.1.call-update
  299.6 0.4 copy-done.3
  300.0 176.4 %tail.1 = (bf16[16,3,96,256]{3,2,1,0:T(8,128)(2,1)S(1)}, f32[96,1536]{1,0:T(8,128)S(1)}) custom-call(bf16[16,3,96,256]{3,2,1,0:T(8,128)(2,1)} %get-tuple-element.43.dqkv_ref, bf16[16,96,256]{2,1,0:T(8,128)(2,1)S(1)} %get-tuple-element.35.o_old, bf16[16,96,256]{2,1,0:T(8,128)(2,1)S(1)} %copy-done.3, bf16[2,256,1536]{2,1,0:T(8,128)(2,1)S(1)} %copy-done.2), custom_call_target="tpu_custom_call" | custom-call | flops 99999997952 | bytes 67108864 | tf_op jit(solution)/shard_map/tail/pallas_call | solution.py:332
  476.5 7.4 %fusion.10 = f32[256,1536]{1,0:T(8,128)S(1)} fusion(bf16[16,3,96,256]{3,2,1,0:T(8,128)(2,1)S(1)} %get-tuple-element.40, bf16[1536,16,3,96]{0,3,2,1:T(8,128)(2,1)} %param.15), kind=kOutput, calls=%fused_computation.14 | convolution fusion | flops 3623878656 | bytes 18087936 | tf_op jit(solution)/shard_map/dot_general | solution.py:565
  483.9 11.3 %multiply_reduce_fusion.1 = (f32[1536]{0:T(1024)S(1)}, f32[256]{0:T(256)S(1)}, f32[256]{0:T(256)S(1)}, f32[1536]{0:T(1024)S(1)}, f32[256]{0:T(256)S(1)}, /*index...) fusion(f32[2,256,1536]{2,1,0:T(8,128)S(1)} %copy-done.7, f32[1536]{0:T(1024)S(1)} %copy-done.18, ...), kind=kOutput, calls=%fused_computation.30 | convolution fusion | flops 3629376512 | bytes 22841344 | tf_op jit(solution)/shard_map/dot_general | solution.py:565
  495.2 0.0 copy-start.22
  495.2 0.7 convert_reduce_fusion
  496.0 0.1 add.111
  496.1 0.1 stack.41.rows_ref
  496.2 0.0 copy-start.10
  496.2 4.1 fusion.18
  500.3 0.0 copy-start.12
  500.3 0.0 copy-start.13
  500.3 3.9 fusion.17
  504.2 0.0 copy-start.8
  504.2 1.3 pad_maximum_fusion
  505.5 1.2 copy-done.8
  506.7 1.0 fusion.19
  507.6 1.3 pad_maximum_fusion.1
  508.9 13.4 %place.2.refs_1_ = f32[16,3,96,1536]{3,2,1,0:T(8,128)} custom-call(f32[16,2,96,1536]{3,2,1,0:T(8,128)} %bitcast.97), custom_call_target="tpu_custom_call" | custom-call | flops 1000000000 | bytes 37748736 | tf_op jit(solution)/shard_map/place/pallas_call | solution.py:485
  522.3 87.4 %collect.1 = (f32[8,2,96,1536]{3,2,1,0:T(8,128)S(1)}, f32[16,8,1536]{2,1,0:T(8,128)S(1)}) custom-call(f32[96,1536]{1,0:T(8,128)S(1)} %copy-done.6, f32[8,1536]{1,0:T(8,128)S(1)} %stack.41.rows_ref), custom_call_target="tpu_custom_call" | custom-call | flops 49999998976 | bytes 10485760 | tf_op jit(solution)/shard_map/collect/pallas_call | solution.py:405
  609.7 3.8 lay_down.1
  613.4 0.1 slice_reduce_fusion.1
  613.5 0.1 slice_reduce_fusion
  613.6 0.0 all-gather.7.cloned.1.call-done
  613.6 0.6 slice_reduce_fusion.2
  614.3 0.1 reshape_squeeze.2
  614.3 0.6 copy.22
  615.0 7.4 %place.3 = f32[16,3,96,1536]{3,2,1,0:T(8,128)} custom-call(f32[16,1,96,1536]{3,2,1,0:T(8,128)} %bitcast.99, f32[16,3,96,1536]{3,2,1,0:T(8,128)} %place.2.refs_1_), custom_call_target="tpu_custom_call", output_to_operand_aliasing={{}: (1, {})} | custom-call | flops 1000000000 | bytes 18874368 | tf_op jit(solution)/shard_map/place/pallas_call | solution.py:485
  (58 shorter events, 0.3 us)
Async XLA Ops:
  7.2 22.3 %copy-start = (f32[16,3,96]{2,0,1:T(8,128)S(1)}, f32[16,3,96]{2,0,1:T(8,128)}, u32[]{:S(2)}) copy-start(f32[16,3,96]{2,0,1:T(8,128)} %param.16) | copy-start | bytes 55300
  7.2 1.9 copy-start.9
  7.2 2.5 copy-start.17
  7.2 2.5 copy-start.19
  7.2 99.9 %all-gather.11.cloned.1.call-start = ((), (), s32[]{:S(2)}) async-start(), calls=%async_computation.2 | async-start | bytes 13369344 | tf_op jit(solution)/shard_map/all_gather | solution.py:530
  13.3 1.1 copy-start.20
  13.3 1.1 copy-start.21
  13.3 18.7 %copy-start.2 = (bf16[2,256,1536]{2,1,0:T(8,128)(2,1)S(1)}, bf16[2,256,1536]{2,1,0:T(8,128)(2,1)}, u32[]{:S(2)}) copy-start(bf16[2,256,1536]{2,1,0:T(8,128)(2,1)} %dy_ref.1) | copy-start | bytes 4718596
  13.4 203.5 %all-gather.13.cloned.1.call-start = ((), (), s32[]{:S(2)}) async-start(), calls=%async_computation.3 | async-start | bytes 13369344 | tf_op jit(solution)/shard_map/all_gather | solution.py:535
  14.2 494.8 %all-gather.9.cloned.1.call-start = ((), (), s32[]{:S(2)}) async-start(), calls=%async_computation.1 | async-start | bytes 20054016 | tf_op jit(solution)/shard_map/all_gather | solution.py:554
  29.7 7.0 %slice-start = ((s8[4718592]{0:T(1024)(128)(4,1)}), s8[4194304]{0:T(1024)(128)(4,1)S(1)}, s32[]{:S(2)}) async-start(s8[4718592]{0:T(1024)(128)(4,1)} %bitcast.114), calls=%async_computation.4 | async-start | bytes 8388608
  32.0 4.7 slice-start.1
  70.7 0.9 copy-start.4
  298.8 1.1 copy-start.3
  298.9 314.7 %all-gather.7.cloned.1.call-start = ((), (), s32[]{:S(2)}) async-start(), calls=%async_computation | async-start | bytes 10027008 | tf_op jit(solution)/shard_map/all_gather | solution.py:554
  476.4 7.4 %copy-start.5 = (f32[96,1536]{1,0:T(8,128)}, f32[96,1536]{1,0:T(8,128)S(1)}, u32[]{:S(2)}) copy-start(f32[96,1536]{1,0:T(8,128)S(1)} %get-tuple-element.37.part) | copy-start | bytes 1769476
  476.4 7.4 %copy-start.7 = (f32[2,256,1536]{2,1,0:T(8,128)S(1)}, f32[2,256,1536]{2,1,0:T(8,128)}, u32[]{:S(2)}) copy-start(f32[2,256,1536]{2,1,0:T(8,128)} %get-tuple-element.83) | copy-start | bytes 9437188
  476.5 7.4 %copy-start.16 = (bf16[16,3,96,256]{3,2,1,0:T(8,128)(2,1)S(1)}, bf16[16,3,96,256]{3,2,1,0:T(8,128)(2,1)}, u32[]{:S(2)}) copy-start(bf16[16,3,96,256]{3,2,1,0:T(8,128)(2,1)} %get-tuple-element.39) | copy-start | bytes 7077892
  476.5 7.4 %copy-start.18 = (f32[1536]{0:T(1024)S(1)}, f32[1536]{0:T(1024)}, u32[]{:S(2)}) copy-start(f32[1536]{0:T(1024)} %param.13) | copy-start | bytes 18436
  483.8 11.3 %copy-start.11 = (f32[256,1536]{1,0:T(8,128)}, f32[256,1536]{1,0:T(8,128)S(1)}, u32[]{:S(2)}) copy-start(f32[256,1536]{1,0:T(8,128)S(1)} %fusion.10) | copy-start | bytes 4718596
  483.9 11.3 %copy-start.14 = (bf16[16,3,96,256]{3,2,1,0:T(8,128)(2,1)S(1)}, bf16[16,3,96,256]{3,2,1,0:T(8,128)(2,1)}, u32[]{:S(2)}) copy-start(bf16[16,3,96,256]{3,2,1,0:T(8,128)(2,1)} %get-tuple-element.42.refs_2_) | copy-start | bytes 7077892
  483.9 11.3 %copy-start.15 = (bf16[16,3,96,256]{3,2,1,0:T(8,128)(2,1)S(1)}, bf16[16,3,96,256]{3,2,1,0:T(8,128)(2,1)}, u32[]{:S(2)}) copy-start(bf16[16,3,96,256]{3,2,1,0:T(8,128)(2,1)} %get-tuple-element.43.dqkv_ref) | copy-start | bytes 7077892
  495.2 1.0 copy-start.22
  496.2 4.1 copy-start.10
  500.3 5.2 copy-start.12
  500.3 5.2 copy-start.13
  504.2 2.5 copy-start.8
  508.9 13.4 %copy-start.6 = (f32[96,1536]{1,0:T(8,128)S(1)}, f32[96,1536]{1,0:T(8,128)}, u32[]{:S(2)}) copy-start(f32[96,1536]{1,0:T(8,128)} %copy-done.5) | copy-start | bytes 1769476
  615.0 7.4 %copy-start.1 = (f32[16,3,96]{2,0,1:T(8,128)S(1)}, f32[16,3,96]{2,0,1:T(8,128)}, u32[]{:S(2)}) copy-start(f32[16,3,96]{2,0,1:T(8,128)} %param.16) | copy-start | bytes 55300
Sparse Core Ops, SparseCore 0:
  13.5 93.6 all-gather.10
  109.3 107.4 all-gather.12
  299.0 189.7 all-gather.8
  490.3 81.1 all-gather.6

commit v6 on v5

--- a/solution.py
+++ b/solution.py
@@ -14,12 +14,17 @@
 NT = (((1,), (1,)), ((), ()))
 
 
-def attn_body(slope_ref, w_ref, b_ref, x_ref, dot_ref, pos_ref, pref_ref, *refs, blk, tok, n_swap, n_old):
+def attn_body(slope_ref, w_ref, b_ref, x_ref, dot_ref, pos_ref, pref_ref, *refs, blk, tok, n_swap, n_old, send_o):
     peers = dot_ref.shape[0]
     gw_old, old, refs = refs[:n_old], refs[n_old:n_old + n_swap], refs[n_old + n_swap:]
-    (dqkv_ref, gwa_ref, gwb_ref, o_new), got, refs = refs[:4], refs[4:4 + n_swap], refs[4 + n_swap:]
-    x_buf, qkvt_ref, k_tok, v_tok, posk_ref, s_buf, q_pad, do_pad, o_acc, dq_acc, dk_acc, dv_acc, o_ref, x_sem, os_sem, or_sem = refs[:16]
-    swaps = [(old[k], got[k]) + refs[16 + 4 * k:20 + 4 * k] for k in range(n_swap)]
+    (dqkv_ref, gwa_ref, gwb_ref, gb_ref, o_out), got, refs = refs[:5], refs[5:5 + n_swap], refs[5 + n_swap:]
+    x_buf, qkvt_ref, k_tok, v_tok, posk_ref, s_buf, q_pad, do_pad, o_acc, dq_acc, dk_acc, dv_acc, x_sem = refs[:13]
+    swaps = [(old[k], got[k]) + refs[13 + 4 * k:17 + 4 * k] for k in range(n_swap)]
+    if send_o:
+        o_ref, os_sem, or_sem = refs[-3:]
+        o_new = o_out
+    else:
+        o_ref = o_out
     dim = dot_ref.shape[1]
     seq = dot_ref.shape[0] * tok
     pad = k_tok.shape[1] - dim
@@ -82,9 +87,10 @@
                     dst[cols, :] = jnp.transpose(whole).astype(BF16)
                 posk_ref[cols, :] = jnp.transpose(jnp.broadcast_to(pos_ref[:, cols], (128, 128)))
 
-    @pl.when(step > 0)
-    def _():
-        o_start(step - 1)
+    if send_o:
+        @pl.when(step > 0)
+        def _():
+            o_start(step - 1)
 
     qcols = pl.ds(pl.multiple_of(i * blk, blk), blk)
     q_pad[0:dim, :] = qkvt_ref[0:dim, qcols]
@@ -151,75 +157,74 @@
     dq_lo = (dq_acc[...] * scale).astype(BF16)
     for t in range(nq):
         o_ref[i * nq + t] = o_lo[:, t * tok:(t + 1) * tok]
-        dqkv_ref[i * nq + t, 0] = dq_lo[:, t * tok:(t + 1) * tok]
+        dqkv_ref[i * nq + t, 0:dim] = dq_lo[:, t * tok:(t + 1) * tok]
 
     @pl.when(step == steps - 1)
     def _():
         @pl.loop(0, seq // tok)
         def _(t):
             cols = pl.ds(pl.multiple_of(t * tok, tok), tok)
-            dqkv_ref[t, 1] = (dk_acc[:, cols] * scale).astype(BF16)
-            dqkv_ref[t, 2] = dv_acc[:, cols].astype(BF16)
-
-        o_start(step)
-        if n_old:
-            gwa_ref[...] = gw_old[0][...]
-            gwb_ref[...] = gw_old[1][...]
-        else:
-            gwa_ref[...] = jnp.zeros_like(gwa_ref)
-            gwb_ref[...] = jnp.zeros_like(gwb_ref)
+            dqkv_ref[t, dim:2 * dim] = (dk_acc[:, cols] * scale).astype(BF16)
+            dqkv_ref[t, 2 * dim:3 * dim] = dv_acc[:, cols].astype(BF16)
+
+        if send_o:
+            o_start(step)
+        for k, ref in enumerate((gwa_ref, gwb_ref, gb_ref)):
+            ref[...] = gw_old[k][...] if n_old else jnp.zeros_like(ref)
+        ones = jnp.ones((blk, 128), BF16)
 
         @pl.loop(0, steps)
         def _(j):
             rows = pl.ds(pl.multiple_of(j * blk, blk), blk)
-            for ref, lo, n in ((gwa_ref, 0, 2), (gwb_ref, 2, 1)):
-                lhs = jnp.concatenate([dqkv_ref[j * nq + t, lo:lo + n].reshape(n * dim, tok) for t in range(nq)], axis=1)
+            for ref, lo, hi in ((gwa_ref, 0, 2 * dim), (gwb_ref, 2 * dim, 3 * dim)):
+                lhs = jnp.concatenate([dqkv_ref[j * nq + t, lo:hi] for t in range(nq)], axis=1)
                 ref[...] += jnp.dot(lhs, x_buf[rows, :], preferred_element_type=F32)
-
-        o_keep().wait()
-        for d in range(1, peers):
-            o_send(lax.rem(me + d, peers)).wait_send()
-            frm = lax.rem(me + d, peers)
-            pltpu.make_async_remote_copy(
-                src_ref=o_ref.at[frm], dst_ref=o_new.at[frm], send_sem=os_sem.at[frm], recv_sem=or_sem.at[frm],
-                device_id={"sp": frm}, device_id_type=pl.DeviceIdType.MESH).wait_recv()
+                gb_ref[lo:hi, :] += jnp.dot(lhs, ones, preferred_element_type=F32)
+
+        if send_o:
+            o_keep().wait()
+            for d in range(1, peers):
+                frm = lax.rem(me + d, peers)
+                o_send(frm).wait_send()
+                pltpu.make_async_remote_copy(
+                    src_ref=o_ref.at[frm], dst_ref=o_new.at[frm], send_sem=os_sem.at[frm], recv_sem=or_sem.at[frm],
+                    device_id={"sp": frm}, device_id_type=pl.DeviceIdType.MESH).wait_recv()
         for one in swaps:
             swap_wait(*one, peers)
 
 
-def attention(slope2, w_head, b_head, x, dot_, pos, pref, gw, old, *, blk, tok, collective_id):
+def attention(slope2, w_head, b_head, x, dot_, pos, pref, gw, old, *, blk, tok, send_o, collective_id):
     blocks, dim, _ = dot_.shape
     seq, hidden = x.shape
     wide = 128 * pl.cdiv(dim, 128)
     hbm = pl.BlockSpec(memory_space=pltpu.HBM)
     full = lambda a: pl.BlockSpec(a.shape, lambda i: (0,) * len(a.shape), pipeline_mode=pl.Buffered(1))
     like = lambda a: jax.ShapeDtypeStruct(a.shape, a.dtype)
-    outs = [jax.ShapeDtypeStruct((blocks, 3, dim, tok), BF16), jax.ShapeDtypeStruct((2 * dim, hidden), F32),
-            jax.ShapeDtypeStruct((dim, hidden), F32)]
+    outs = [jax.ShapeDtypeStruct((blocks, 3 * dim, tok), BF16), jax.ShapeDtypeStruct((2 * dim, hidden), F32),
+            jax.ShapeDtypeStruct((dim, hidden), F32), jax.ShapeDtypeStruct((3 * dim, 128), F32)]
     pairs = (seq // blk) * (seq // blk + 1) // 2
     dma = pltpu.SemaphoreType.DMA
     res = pl.pallas_call(
-        functools.partial(attn_body, blk=blk, tok=tok, n_swap=len(old), n_old=len(gw)),
+        functools.partial(attn_body, blk=blk, tok=tok, n_swap=len(old), n_old=len(gw), send_o=send_o),
         name="attention",
         out_shape=outs + [like(dot_)] + [like(a) for a in old],
         grid=(seq // blk,),
         in_specs=[pl.BlockSpec(memory_space=pltpu.SMEM), full(w_head), full(b_head), hbm, full(dot_), full(pos), full(pref)]
         + [full(a) for a in gw] + [hbm] * len(old),
-        out_specs=[full(a) for a in outs] + [hbm] * (1 + len(old)),
+        out_specs=[full(a) for a in outs] + [hbm if send_o else full(dot_)] + [hbm] * len(old),
         scratch_shapes=[
             pltpu.VMEM((seq, hidden), BF16), pltpu.VMEM((3 * dim, seq), BF16),
             pltpu.VMEM((seq, wide), BF16), pltpu.VMEM((seq, wide), BF16), pltpu.VMEM((seq, 128), F32),
             pltpu.VMEM((seq, blk), F32),
             pltpu.VMEM((wide, blk), BF16), pltpu.VMEM((wide, blk), BF16),
             pltpu.VMEM((dim, blk), F32), pltpu.VMEM((dim, blk), F32),
-            pltpu.VMEM((dim, seq), F32), pltpu.VMEM((dim, seq), F32), pltpu.VMEM(dot_.shape, BF16),
-            dma((seq // blk,)), dma((blocks,)), dma((blocks,))]
-        + sum((swap_scratch(a) for a in old), []),
+            pltpu.VMEM((dim, seq), F32), pltpu.VMEM((dim, seq), F32), dma((seq // blk,))]
+        + sum((swap_scratch(a) for a in old), []) + ([pltpu.VMEM(dot_.shape, BF16), dma((blocks,)), dma((blocks,))] if send_o else []),
         cost_estimate=pl.CostEstimate(flops=pairs * 6 * 2 * blk * blk * 256, bytes_accessed=24 << 20, transcendentals=pairs * blk * blk),
         compiler_params=pltpu.CompilerParams(dimension_semantics=("arbitrary",), vmem_limit_bytes=52 << 20,
                                              collective_id=collective_id, has_side_effects=True),
     )(slope2, w_head, b_head, x, dot_, pos, pref, *gw, *old)
-    return res[0], res[1:3], res[3], res[4:]
+    return res[0], res[1:4], res[4], res[5:]
 
 
 def peer_at(d, peers):
@@ -263,18 +268,28 @@
             pltpu.SemaphoreType.DMA]
 
 
-def tail_body(dqkv_ref, o_old, o_new, dy_ref, dqkv_new, part, mine, other, pair, landed, own_d, ds_sem, dr_sem, do_sem, ps_sem, pr_sem, rs_sem, rr_sem, *, peers):
+def tail_body(dqkv_ref, d_old, o_old, o_new, dy_ref, x_ref, w_hbm, wo_hbm, gain_ref, bo_ref, y_ref, gx_ref, part, rows_ref,
+              d_new, w_ref, wo_ref, dn, mine, other, pair, landed, sums, own_d, ds_sem, dr_sem, do_sem, ps_sem, pr_sem, rs_sem, rr_sem,
+              w_sem, *, peers):
     ring = peers // 2
     me = lax.axis_index("sp")
     z, c = me // 2, me % 2
-    half = part.shape[-1] // 2
+    _, tok, hidden = x_ref.shape
+    half = hidden // 2
+    wide = hidden // 3
+    group = 8
     cols = (pl.ds(0, half), pl.ds(half, half))
     at = lambda zz, cc: {"sp": 2 * zz + cc}
     turn = lambda k: lax.rem(z + k + 2 * ring, ring)
     step = (1, -1)
     remote = functools.partial(pltpu.make_async_remote_copy, device_id_type=pl.DeviceIdType.MESH)
+    tn = (((0,), (0,)), ((), ()))
+    o_refs, d_refs = (o_old, o_new), (d_old, d_new)
+    loads = [pltpu.make_async_copy(w_hbm, w_ref, w_sem.at[0]), pltpu.make_async_copy(wo_hbm, wo_ref, w_sem.at[1])]
+    for load in loads:
+        load.start()
     meet(peers)
-    swap_start(dqkv_ref, dqkv_new, own_d, ds_sem, dr_sem, do_sem, peers)
+    swap_start(dqkv_ref, d_new, own_d, ds_sem, dr_sem, do_sem, peers)
 
     def product(out, side):
         @pl.loop(0, ring)
@@ -283,10 +298,47 @@
             out[k] = (jnp.dot(o_old[h], dy_ref[0], preferred_element_type=F32)
                       + jnp.dot(o_new[h], dy_ref[1], preferred_element_type=F32))
 
+    def forward(b):
+        o_t = o_refs[b][...].reshape(hidden, tok)
+
+        @pl.loop(0, 3)
+        def _(n):
+            at_n = pl.ds(pl.multiple_of(n * wide, wide), wide)
+            acc = lax.dot_general(o_t, wo_ref[:, at_n], tn, preferred_element_type=F32)
+            y_ref[b, :, at_n] = (x_ref[b, :, at_n].astype(F32) + acc + bo_ref[:, at_n]).astype(BF16)
+
+    def backward(b):
+        @pl.loop(0, 3)
+        def _(n):
+            at_n = pl.ds(pl.multiple_of(n * wide, wide), wide)
+            acc = None
+            for k in range(0, peers, group):
+                lhs = d_refs[b][k:k + group].reshape(-1, tok)
+                one = lax.dot_general(lhs, w_ref[k * lhs.shape[0] // group:(k + group) * lhs.shape[0] // group, at_n], tn, preferred_element_type=F32)
+                acc = one if acc is None else acc + one
+            dn[:, at_n] = acc
+
+        @pl.loop(0, tok // 32)
+        def _(k):
+            rows = pl.ds(pl.multiple_of(k * 32, 32), 32)
+            x = x_ref[b, rows, :].astype(F32)
+            dy = dy_ref[b, rows, :].astype(F32)
+            d = dn[rows, :]
+            cen = x - jnp.mean(x, axis=-1, keepdims=True)
+            inv = lax.rsqrt(jnp.mean(cen * cen, axis=-1, keepdims=True) + NORM_EPS)
+            hat = cen * inv
+            for n, one in enumerate((d * hat, d, dy)):
+                sums[n] += jnp.sum(one.reshape(4, 8, hidden), axis=0)
+            e = d * gain_ref[...]
+            m1 = jnp.mean(e, axis=-1, keepdims=True)
+            m2 = jnp.mean(e * hat, axis=-1, keepdims=True)
+            gx_ref[b, rows, :] = (dy + inv * (e - m1 - hat * m2)).astype(BF16)
+
     product(other, 1 - c)
     to_pair = remote(src_ref=other, dst_ref=pair, send_sem=ps_sem, recv_sem=pr_sem, device_id=at(z, 1 - c))
     product(mine, c)
     to_pair.start()
+    sums[...] = jnp.zeros_like(sums)
     to_pair.wait()
 
     @pl.loop(0, ring)
@@ -301,20 +353,33 @@
         reduce_copy(w, t).wait_recv()
         mine[k, :, cols[w]] = mine[k, :, cols[w]] + landed[w, t]
 
-    for w in range(2):
-        reduce_copy(w, 0).start()
-
-    @pl.loop(1, ring - 1)
-    def _(t):
+    def hop(t):
         for w in range(2):
             add(w, t - 1, turn(-step[w] * (1 + t)))
             reduce_copy(w, t).start()
 
     for w in range(2):
+        reduce_copy(w, 0).start()
+    loads[1].wait()
+    forward(0)
+    hop(1)
+    forward(1)
+    hop(2)
+    loads[0].wait()
+    backward(0)
+
+    @pl.loop(3, ring - 1)
+    def _(t):
+        hop(t)
+
+    swap_wait(dqkv_ref, d_new, own_d, ds_sem, dr_sem, do_sem, peers)
+    backward(1)
+    rows_ref[...] = jnp.zeros_like(rows_ref)
+    for n in range(3):
+        rows_ref[n:n + 1, :] = jnp.sum(sums[n], axis=0, keepdims=True)
+    for w in range(2):
         add(w, ring - 2, z)
-
     part[...] = mine[z]
-    swap_wait(dqkv_ref, dqkv_new, own_d, ds_sem, dr_sem, do_sem, peers)
 
     @pl.loop(0, ring - 1)
     def _(t):
@@ -322,28 +387,31 @@
             reduce_copy(w, t).wait_send()
 
 
-def tail(dqkv, o_old, o_new, dy, collective_id):
+def tail(dqkv, d_old, o_old, o_new, dy, x, w_flat, w_out, gain, b_out, collective_id):
     peers, dim, tok = o_old.shape
     ring = peers // 2
     hidden = dy.shape[-1]
     hbm, vmem = pl.BlockSpec(memory_space=pltpu.HBM), pl.BlockSpec(memory_space=pltpu.VMEM)
     dma = pltpu.SemaphoreType.DMA
     rows = lambda *lead: pltpu.VMEM(lead + (dim, hidden), F32)
+    like = lambda a: jax.ShapeDtypeStruct(a.shape, a.dtype)
     return pl.pallas_call(
         functools.partial(tail_body, peers=peers),
         name="tail",
-        out_shape=[jax.ShapeDtypeStruct(dqkv.shape, BF16), jax.ShapeDtypeStruct((dim, hidden), F32)],
-        in_specs=[hbm, vmem, vmem, vmem],
-        out_specs=[hbm, vmem],
-        scratch_shapes=[rows(ring), rows(ring), rows(ring), pltpu.VMEM((2, ring - 1, dim, hidden // 2), F32),
+        out_shape=[like(x), like(x), jax.ShapeDtypeStruct((dim, hidden), F32), jax.ShapeDtypeStruct((8, hidden), F32)],
+        in_specs=[hbm, vmem, vmem, vmem, vmem, vmem, hbm, hbm, vmem, vmem],
+        out_specs=[vmem] * 4,
+        scratch_shapes=[pltpu.VMEM(dqkv.shape, BF16), pltpu.VMEM(w_flat.shape, BF16), pltpu.VMEM(w_out.shape, BF16),
+                        pltpu.VMEM((tok, hidden), F32), rows(ring), rows(ring), rows(ring),
+                        pltpu.VMEM((2, ring - 1, dim, hidden // 2), F32), pltpu.VMEM((3, 8, hidden), F32),
                         pltpu.VMEM(dqkv.shape[1:], BF16), dma((peers - 1,)), dma((peers - 1,)), dma, dma, dma,
-                        dma((2, ring - 1)), dma((2, ring - 1))],
+                        dma((2, ring - 1)), dma((2, ring - 1)), dma((2,))],
         cost_estimate=pl.CostEstimate(flops=10**11, bytes_accessed=64 << 20, transcendentals=0),
-        compiler_params=pltpu.CompilerParams(collective_id=collective_id, has_side_effects=True, vmem_limit_bytes=48 << 20),
-    )(dqkv, o_old, o_new, dy)
-
-
-def collect_body(part, rows_ref, full, sums, as_sem, ar_sem, fs_sem, fr_sem, xs_sem, xr_sem, *, peers, cuts):
+        compiler_params=pltpu.CompilerParams(collective_id=collective_id, has_side_effects=True, vmem_limit_bytes=47 << 20),
+    )(dqkv, d_old, o_old, o_new, dy, x, w_flat, w_out, gain, b_out)
+
+
+def collect_body(part, rows_ref, gb_ref, full, total, gb_all, stage, as_sem, ar_sem, fs_sem, fr_sem, xs_sem, xr_sem, *, peers, cuts):
     ring = peers // 2
     me = lax.axis_index("sp")
     z, c = me // 2, me % 2
@@ -360,17 +428,52 @@
     gather_copy = lambda w, t, u: block_copy(w, t, u, c, as_sem, ar_sem, 2 * turn(step[w]) + c)
     over_copy = lambda w, t, u, side: block_copy(w, t, u, side, fs_sem, fr_sem, 2 * z + 1 - c)
     parts = [(w, u) for u in range(cuts) for w in range(2)]
+    owners = rows_ref.shape[1] // 128
+    lanes = lambda k: pl.ds(pl.multiple_of(k * 128, 128), 128)
     full[z, c] = part[...]
-    sums[me] = rows_ref[...]
+    gb_all[me] = gb_ref[...]
     meet(peers)
     for w, u in parts:
         gather_copy(w, 0, u).start()
-    small = [remote(src_ref=rows_ref, dst_ref=sums.at[me], send_sem=xs_sem.at[d - 1], recv_sem=xr_sem.at[d - 1],
-                    device_id=peer_at(d, peers)) for d in range(1, peers)]
-    for copy in small:
-        copy.start()
+
+    def small_copy(kind, frm, to):
+        src, dst = ((rows_ref.at[:, lanes(to)], stage.at[frm]), (total.at[:, lanes(frm)],) * 2, (gb_ref, gb_all.at[frm]))[kind]
+        return remote(src_ref=src, dst_ref=dst, send_sem=xs_sem.at[kind, to], recv_sem=xr_sem.at[kind, frm], device_id={"sp": to})
+
+    def each(act, kind, only_to=False, only_from=False):
+        @pl.loop(1, peers)
+        def _(d):
+            other = lax.rem(me + d, peers)
+
+            def go():
+                act(kind, other)
+
+            if only_to:
+                pl.when(other < owners)(go)
+            elif only_from:
+                pl.when(me < owners)(go)
+            else:
+                go()
+
+    send = lambda kind, other: small_copy(kind, me, other).start()
+    sent = lambda kind, other: small_copy(kind, me, other).wait_send()
+    came = lambda kind, other: small_copy(kind, other, me).wait_recv()
+    each(send, 0, only_to=True)
+    each(send, 2)
     for w, u in parts:
         over_copy(w, 0, u, c).start()
+
+    @pl.when(me < owners)
+    def _():
+        stage[me] = rows_ref[:, lanes(me)]
+
+    each(came, 0, only_from=True)
+
+    @pl.when(me < owners)
+    def _():
+        total[:, lanes(me)] = jnp.sum(stage[...], axis=0)
+
+    each(send, 1, only_from=True)
 
     @pl.loop(1, ring)
     def _(t):
@@ -383,8 +486,11 @@
 
             over_copy(w, t, u, c).start()
 
-    for copy in small:
-        copy.wait()
+    each(came, 1, only_to=True)
+    each(came, 2)
+    each(sent, 0, only_to=True)
+    each(sent, 1, only_from=True)
+    each(sent, 2)
 
     @pl.loop(0, ring - 1)
     def _(t):
@@ -398,20 +504,22 @@
             over_copy(w, t, u, 1 - c).wait_recv()
 
 
-def collect(part, rows, peers, collective_id, cuts=3):
+def collect(part, rows, gb, peers, collective_id, cuts=3):
     ring = peers // 2
     vmem = pl.BlockSpec(memory_space=pltpu.VMEM)
     dma = pltpu.SemaphoreType.DMA
     return pl.pallas_call(
         functools.partial(collect_body, peers=peers, cuts=cuts),
         name="collect",
-        out_shape=[jax.ShapeDtypeStruct((ring, 2) + part.shape, F32), jax.ShapeDtypeStruct((peers,) + rows.shape, F32)],
-        in_specs=[vmem, vmem],
-        out_specs=[vmem, vmem],
-        scratch_shapes=[dma((2, ring - 1, cuts)), dma((2, ring - 1, cuts)), dma((2, ring, cuts)), dma((2, ring, cuts)), dma((peers - 1,)), dma((peers - 1,))],
+        out_shape=[jax.ShapeDtypeStruct((ring, 2) + part.shape, F32), jax.ShapeDtypeStruct(rows.shape, F32),
+                   jax.ShapeDtypeStruct((peers,) + gb.shape, F32)],
+        in_specs=[vmem] * 3,
+        out_specs=[vmem] * 3,
+        scratch_shapes=[pltpu.VMEM((peers, rows.shape[0], 128), F32), dma((2, ring - 1, cuts)), dma((2, ring - 1, cuts)),
+                        dma((2, ring, cuts)), dma((2, ring, cuts)), dma((3, peers)), dma((3, peers))],
         cost_estimate=pl.CostEstimate(flops=5 * 10**10, bytes_accessed=10 << 20, transcendentals=0),
         compiler_params=pltpu.CompilerParams(collective_id=collective_id, has_side_effects=True, vmem_limit_bytes=24 << 20),
-    )(part, rows)
+    )(part, rows, gb)
 
 
 def swap_body(*refs, peers, n):
@@ -508,12 +616,24 @@
         compiler_params=pltpu.CompilerParams(vmem_limit_bytes=24 << 20))(x)
 
 
-def norm_forward(x_blk, ln_gain, ln_bias):
-    x_f32 = x_blk.astype(F32)
-    centered = x_f32 - jnp.mean(x_f32, axis=-1, keepdims=True)
-    inv_std = lax.rsqrt(jnp.mean(centered * centered, axis=-1, keepdims=True) + NORM_EPS)
-    x_hat = centered * inv_std
-    return x_f32, x_hat, inv_std, (x_hat * ln_gain + ln_bias).astype(BF16)
+def norm_body(x_ref, gain_ref, bias_ref, *out_refs):
+    for b, out_ref in enumerate(out_refs):
+        @pl.loop(0, x_ref.shape[1] // 32)
+        def _(k):
+            rows = pl.ds(pl.multiple_of(k * 32, 32), 32)
+            x = x_ref[b, rows, :].astype(F32)
+            cen = x - jnp.mean(x, axis=-1, keepdims=True)
+            hat = cen * lax.rsqrt(jnp.mean(cen * cen, axis=-1, keepdims=True) + NORM_EPS)
+            out_ref[rows, :] = (hat * gain_ref[...] + bias_ref[...]).astype(BF16)
+
+
+def norm_forward(x, gain, bias):
+    vmem = pl.BlockSpec(memory_space=pltpu.VMEM)
+    return pl.pallas_call(
+        norm_body, name="norm_forward", out_shape=[jax.ShapeDtypeStruct(x.shape[1:], BF16)] * x.shape[0],
+        in_specs=[vmem] * 3, out_specs=[vmem] * x.shape[0],
+        cost_estimate=pl.CostEstimate(flops=10**8, bytes_accessed=4 * x.size, transcendentals=0),
+        compiler_params=pltpu.CompilerParams(vmem_limit_bytes=8 << 20))(x, gain, bias)
 
 
 def solution(mesh):
@@ -526,7 +646,7 @@
         seq = tok * peers
         blk = 2 * tok
         rank = lax.axis_index("sp")
-        x_f32, x_hat, inv_std, x_norm = norm_forward(x_blk, ln_gain, ln_bias)
+        x_norm = norm_forward(x_blk, ln_gain.reshape(1, hidden), ln_bias.reshape(1, hidden))
         xf = [lax.all_gather(x_norm[0], "sp", axis=0, tiled=True)]
         marks = exchange(jnp.concatenate([pos_blk, keep_blk, jnp.zeros((8 - 2 * batch, tok), jnp.int32)]), peers, 0, "marks")
         do_loc = [lax.dot_general(w_out, dy_blk[b], NT, preferred_element_type=F32).astype(BF16).reshape(heads, dim, tok) for b in range(batch)]
@@ -538,50 +658,33 @@
         b_head = lax.dynamic_index_in_dim(b_qkv, rank, 0, keepdims=False).reshape(3 * dim, 1)
         slope = jnp.exp2(-8.0 * (rank + 1).astype(F32) / heads)
         slope2 = (slope * LOG2E).reshape(1)
-        gw, att, o_got, d_got = (), [], [], []
+        gw, att = (), []
         for b in range(batch):
             pos = marks[:, b].reshape(1, seq).astype(F32)
             keep = marks[:, batch + b].reshape(1, seq)
             pref = jnp.broadcast_to(pos[0, ::blk][:, None], (seq // blk, 128))
-            old = list(do_loc[b + 1:b + 2]) + att[b - 1:b]
-            cur, gw, o_new, swapped = attention(slope2, w_head, b_head, xf[b], do_t[b], jnp.where(keep > 0, pos, MASKED), pref, gw, old,
-                                                blk=blk, tok=tok, collective_id=4 + b)
+            old = list(do_loc[b + 1:b + 2]) if b + 1 < batch else list(att)
+            att_d, gw, att_o, swapped = attention(slope2, w_head, b_head, xf[b], do_t[b], jnp.where(keep > 0, pos, MASKED), pref, gw, old,
+                                                  blk=blk, tok=tok, send_o=b + 1 == batch, collective_id=4 + b)
             if b + 1 < batch:
                 do_t.append(swapped[0])
-            d_got += swapped[-1:] if b else []
-            o_got.append(o_new)
-            att.append(cur)
-        gw_all = [lax.all_gather(one, "sp", axis=0, tiled=True).reshape(heads, -1, dim, hidden) for one in gw]
+            att = [att_o, att_d]
+        o_old, d_old = swapped
+        gw_all = [lax.all_gather(one, "sp", axis=0, tiled=True).reshape(heads, -1, dim, hidden) for one in gw[:2]]
         cut = gw_all[0].shape[1]
-        dqkv_new, part = tail(att[-1], *o_got, dy_blk, 2)
-        d_got.append(dqkv_new)
-        late, x_late, _ = lax.optimization_barrier((att, x_blk, part))
-        gb = sum(jnp.sum(one.astype(F32), axis=(0, 3)).reshape(3 * dim) for one in late)
-        y, gx, gg, gbias = [], [], 0.0, 0.0
-        for b in range(batch):
-            o_t = o_got[b].reshape(hidden, tok)
-            dqkv_t = d_got[b].reshape(3 * hidden, tok)
-            y.append((x_late[b].astype(F32) + lax.dot_general(o_t, w_out, (((0,), (0,)), ((), ())), preferred_element_type=F32) + b_out).astype(BF16))
-            d_norm = lax.dot_general(dqkv_t, w_t.reshape(3 * hidden, hidden), (((0,), (0,)), ((), ())), preferred_element_type=F32)
-            gg += jnp.sum(d_norm * x_hat[b], axis=0)
-            gbias += jnp.sum(d_norm, axis=0)
-            d_hat = d_norm * ln_gain
-            d_mean = jnp.mean(d_hat, axis=-1, keepdims=True)
-            d_proj = jnp.mean(d_hat * x_hat[b], axis=-1, keepdims=True)
-            gx.append((dy_blk[b].astype(F32) + inv_std[b] * (d_hat - d_mean - x_hat[b] * d_proj)).astype(BF16))
-        g_out = jnp.sum(dy_blk.astype(F32), axis=(0, 1))
-        rows = jnp.stack([gg, gbias, g_out, jnp.pad(gb, (0, hidden - 3 * dim))] + [jnp.zeros((hidden,), F32)] * 4)
-        y, gx = jnp.stack(y), jnp.stack(gx)
-        first, _, _ = lax.optimization_barrier((gw_all[0], y, gx))
+        y, gx, part, rows = tail(att_d, d_old, o_old, att_o, dy_blk, x_blk, w_t.reshape(3 * hidden, hidden), w_out,
+                                 ln_gain.reshape(1, hidden), b_out.reshape(1, hidden), 2)
+        gb, _ = lax.optimization_barrier((gw[2], part))
+        gb = jnp.pad(gb[:, 0].reshape(3, dim), ((0, 5), (0, 128 - dim)))
+        first, _ = lax.optimization_barrier((gw_all[0], part))
         gw_out = place(first, None, 3, 0)
-        rows, gw_out = lax.optimization_barrier((rows, gw_out))
-        go_all, sums = collect(part, rows, peers, 3)
+        y, gx = lay_down(y), lay_down(gx)
+        rows, gw_out, y, gx = lax.optimization_barrier((rows, gw_out, y, gx))
+        go_all, total, gb_all = collect(part, rows, gb, peers, 3)
         go_all = lay_down(go_all.reshape(heads, dim, hidden)).reshape(hidden, hidden)
-        total = jnp.sum(sums[:, :3], axis=0)
-        gb_all = sums[:, 3, :3 * dim].reshape(heads, 3, dim)
         second, go_all = lax.optimization_barrier((gw_all[1], go_all))
         gw_out = jnp.transpose(place(second, gw_out, 3, cut), (3, 0, 1, 2))
-        return y, gx, gw_out, gb_all, go_all, total[2], total[0], total[1]
+        return y, gx, gw_out, gb_all[:, :3, :dim], go_all, total[2], total[0], total[1]
 
     act_spec = P("dp", "sp", None)
     tok_spec = P("dp", "sp")

time: 629 us -> 610 us (0.970)
  matrix products: 32.7 us -> 6.17 us
  Pallas kernels: 505 us -> 529 us
  waiting for transfers between devices: 58.2 us -> 44 us
  other arithmetic: 9.49 us -> 0.92 us
    dot_general x4 -> x0, matrix products: 26.6 us -> none  [the longest x2 18.6 us: block_fn(): lax.dot_general(dqkv_t, w_t.reshape(3 * hidden, hidden), (((0,), (0,)), (...]
    all_gather x1, waiting for transfers between devices: 21.8 us -> 5.23 us  [block_fn(): xf.append(lax.all_gather(x_norm[b], 'sp', axis=0, tiled=True))]
  transfers between devices with their start and end apart: 4 -> 4, of which waited for: 2 -> 3; matrix products, arithmetic and copies ran while one was open for 6% -> 2% of each run, Pallas kernels for 66% -> 69%
where the time goes in v6:
time: 610 us; the launch traced here: 609 us
  Pallas kernels  529 us (87%)
  waiting for transfers between devices  44 us (7%)
  local copies, waits for them, and re-layouts  14.6 us (2%)
  between operations  14.1 us (2%)
  matrix products  6.17 us (1%)
    pallas_call x1, Pallas kernels, tail(): pl.pallas_call(functools.partial(tail_body, peers=peers), name='tail', ou...  182 us
    pallas_call x2, Pallas kernels, attention(): pl.pallas_call(functools.partial(attn_body, blk=blk, tok=tok, n_swap=len(...  175 us
    pallas_call x1, Pallas kernels, collect(): pl.pallas_call(functools.partial(collect_body, peers=peers, cuts=cuts), n...  93.6 us
    all_gather x1, waiting for transfers between devices, block_fn(): xf = [lax.all_gather(x_norm[0], 'sp', axis=0, tiled=True)]  34.9 us
    pallas_call x1, Pallas kernels, swap(): pl.pallas_call(functools.partial(swap_body, peers=peers, n=len(xs)), name...  32.4 us
    pallas_call x2, Pallas kernels, place(): pl.pallas_call(functools.partial(place_body, first=first), name='place',...  20.8 us
    pallas_call x1, Pallas kernels, exchange(): pl.pallas_call(functools.partial(exchange_body, peers=peers), name=name,...  14.8 us
  transfers between devices with their start and end apart: 4, of which 3 were waited for; matrix products, arithmetic and copies ran while one was open for 2% of the time, Pallas kernels for 69%

profile of v6, /device:TPU:21, one launch (start us, length us, event | category | flops | bytes accessed | tf_op | source)
XLA Modules:
  0.0 609.5 jit_solution(1173073898772042886)
XLA Ops:
  7.2 0.0 copy-start
  7.2 0.1 all-gather.7.cloned.1.call-start
  7.3 0.7 reshape.133.gain_ref
  8.0 0.7 reshape.134.bias_ref
  8.7 0.0 copy-start.2
  8.7 1.4 copy-done.2
  10.1 4.4 norm_forward.1
  14.5 0.1 all-gather.7.cloned.1.call-update
  14.5 0.1 all-gather.5.cloned.1.call-start
  14.6 0.7 all-gather.5.cloned.1.call-update
  15.4 0.1 all-gather.9.cloned.1.call-start
  15.5 0.1 pad.7.clone
  15.6 0.8 add_add_fusion.x_ref
  16.3 14.8 %marks.1 = s32[16,8,256]{2,1,0:T(8,128)S(1)} custom-call(s32[8,256]{1,0:T(8,128)S(1)} %add_add_fusion.x_ref), custom_call_target="tpu_custom_call" | custom-call | tf_op jit(solution)/shard_map/marks/pallas_call | solution.py:563
  31.2 0.1 slice.42
  31.3 0.1 slice.46
  31.4 0.0 copy-done
  31.4 0.2 reshape.143.b_ref
  31.6 0.1 slice_compare_fusion
  31.7 0.0 slice-start
  31.7 2.3 constant_dynamic-slice_fusion
  34.0 0.0 copy-done.3
  34.0 3.8 convolution_convert_fusion.1
  37.8 0.0 slice-done
  37.8 0.0 slice-done.1
  37.8 2.3 convolution_convert_fusion
  40.2 32.4 %swap_do.1.dot_ref = bf16[16,96,256]{2,1,0:T(8,128)(2,1)S(1)} custom-call(bf16[16,96,256]{2,1,0:T(8,128)(2,1)S(1)} %bitcast.29), custom_call_target="tpu_custom_call" | custom-call | flops 9437184000 | bytes 1572864 | tf_op jit(solution)/shard_map/swap_do/pallas_call | solution.py:537
  72.6 0.0 copy-start.6
  72.6 0.9 copy-done.6
  73.5 34.9 %all-gather.7.cloned.1.call-done.x_ref = bf16[4096,1536]{1,0:T(8,128)(2,1)} async-done(((bf16[256,1536]{1,0:T(8,128)(2,1)}), bf16[4096,1536]{1,0:T(8,128)(2,1)}) %all-gather.7.cloned.1.call-update) | async-done | bytes 12582928 | tf_op jit(solution)/shard_map/all_gather | solution.py:650
  108.4 0.1 broadcast_in_dim.25.pref_ref
  108.5 78.0 %attention.2 = (bf16[16,288,256]{2,1,0:T(8,128)(2,1)}, f32[192,1536]{1,0:T(8,128)}, f32[96,1536]{1,0:T(8,128)S(1)}, f32[288,128]{1,0:T(8,128)S(1)}, bf16[16,96,2...) custom-call(f32[1]{0:T(128)} %bitcast.slope_ref, bf16[288,1536]{1,0:T(8,128)(2,1)} %bitcast.34, ...), custom_call_target="tpu_custom_call" | custom-call | flops 28991029248 | bytes 25165824 | tf_op jit(solution)/shard_map/attention/pallas_call | solution.py:207
  186.4 0.0 copy-start.9
  186.5 0.9 copy-done.9
  187.3 5.2 all-gather.5.cloned.1.call-done.x_ref
  192.6 0.1 broadcast_in_dim.27.pref_ref
  192.6 97.1 %attention.3 = (bf16[16,288,256]{2,1,0:T(8,128)(2,1)}, f32[192,1536]{1,0:T(8,128)}, f32[96,1536]{1,0:T(8,128)}, f32[288,128]{1,0:T(8,128)S(1)}, bf16[16,96,256]{...) custom-call(f32[1]{0:T(128)} %bitcast.slope_ref, bf16[288,1536]{1,0:T(8,128)(2,1)} %bitcast.35, ...), custom_call_target="tpu_custom_call" | custom-call | flops 28991029248 | bytes 25165824 | tf_op jit(solution)/shard_map/attention/pallas_call | solution.py:207
  289.8 0.1 all-gather.9.cloned.1.call-update
  289.8 0.2 all-gather.11.cloned.1.call-start
  290.1 0.4 all-gather.11.cloned.1.call-update
  290.5 0.0 copy-done.12
  290.5 0.0 copy-start.7
  290.5 1.1 copy-done.7
  291.6 1.1 copy-done.8
  292.8 182.0 %tail.1 = (bf16[2,256,1536]{2,1,0:T(8,128)(2,1)S(1)}, bf16[2,256,1536]{2,1,0:T(8,128)(2,1)S(1)}, f32[96,1536]{1,0:T(8,128)S(1)}, f32[8,1536]{1,0:T(8,128)S(1)}) custom-call(bf16[16,288,256]{2,1,0:T(8,128)(2,1)} %get-tuple-element.46.dqkv_ref, bf16[16,288,256]{2,1,0:T(8,128)(2,1)} %get-tuple-element.47.d_old, bf16[16,96,256]{2,1,0:T(8,128)(2,1)S(1)} %copy-done.8, ...), custom_call_target="tpu_custom_call" | custom-call | flops 99999997952 | bytes 67108864 | tf_op jit(solution)/shard_map/tail/pallas_call | solution.py:398
  474.8 0.0 copy-start.4
  474.8 1.1 copy-done.4
  476.0 0.8 copy-done.10
  476.8 0.1 slice_reduce_fusion
  476.9 0.1 reshape_squeeze.2
  477.0 0.0 copy-start.5
  477.0 1.4 copy-done.5
  478.5 1.2 lay_down.3
  479.6 1.2 lay_down.4
  480.8 2.7 all-gather.9.cloned.1.call-done
  483.4 13.4 %place.2.refs_1_ = f32[16,3,96,1536]{3,2,1,0:T(8,128)} custom-call(f32[16,2,96,1536]{3,2,1,0:T(8,128)} %bitcast.31), custom_call_target="tpu_custom_call" | custom-call | flops 1000000000 | bytes 37748736 | tf_op jit(solution)/shard_map/place/pallas_call | solution.py:593
  496.8 0.0 copy-done.11
  496.8 93.6 %collect.1 = (f32[8,2,96,1536]{3,2,1,0:T(8,128)S(1)}, f32[8,1536]{1,0:T(8,128)S(1)}, f32[16,8,128]{2,1,0:T(8,128)S(1)}) custom-call(f32[96,1536]{1,0:T(8,128)S(1)} %copy-done.11, f32[8,1536]{1,0:T(8,128)S(1)} %get-tuple-element.59.rows_ref, f32[8,128]{1,0:T(8,128)S(1)} %pad.4.gb_ref), custom_call_target="tpu_custom_call" | custom-call | flops 49999998976 | bytes 10485760 | tf_op jit(solution)/shard_map/collect/pallas_call | solution.py:511
  590.4 3.8 lay_down.5
  594.2 0.0 all-gather.11.cloned.1.call-done
  594.2 0.6 slice_reduce_fusion.1
  594.9 0.6 copy.22
  595.5 7.4 %place.3 = f32[16,3,96,1536]{3,2,1,0:T(8,128)} custom-call(f32[16,1,96,1536]{3,2,1,0:T(8,128)} %bitcast.33, f32[16,3,96,1536]{3,2,1,0:T(8,128)} %place.2.refs_1_), custom_call_target="tpu_custom_call", output_to_operand_aliasing={{}: (1, {})} | custom-call | flops 1000000000 | bytes 18874368 | tf_op jit(solution)/shard_map/place/pallas_call | solution.py:593
  602.9 0.0 copy-done.1
  (16 shorter events, 0.1 us)
Async XLA Ops:
  7.2 24.2 %copy-start = (f32[16,3,96]{2,0,1:T(8,128)S(1)}, f32[16,3,96]{2,0,1:T(8,128)}, u32[]{:S(2)}) copy-start(f32[16,3,96]{2,0,1:T(8,128)} %param.16) | copy-start | bytes 55300
  7.2 101.2 %all-gather.7.cloned.1.call-start = ((), (), s32[]{:S(2)}) async-start(), calls=%async_computation.1 | async-start | bytes 13369344 | tf_op jit(solution)/shard_map/all_gather | solution.py:650
  8.7 1.4 copy-start.2
  10.1 23.9 %copy-start.3 = (bf16[2,256,1536]{2,1,0:T(8,128)(2,1)S(1)}, bf16[2,256,1536]{2,1,0:T(8,128)(2,1)}, u32[]{:S(2)}) copy-start(bf16[2,256,1536]{2,1,0:T(8,128)(2,1)} %dy_ref.1) | copy-start | bytes 4718596
  14.5 178.0 %all-gather.5.cloned.1.call-start = ((), (), s32[]{:S(2)}) async-start(), calls=%async_computation | async-start | bytes 13369344 | tf_op jit(solution)/shard_map/all_gather | solution.py:655
  15.4 468.1 %all-gather.9.cloned.1.call-start = ((), (), s32[]{:S(2)}) async-start(), calls=%async_computation.2 | async-start | bytes 20054016 | tf_op jit(solution)/shard_map/all_gather | solution.py:673
  31.7 6.2 %slice-start = ((s8[4718592]{0:T(1024)(128)(4,1)}), s8[4194304]{0:T(1024)(128)(4,1)S(1)}, s32[]{:S(2)}) async-start(s8[4718592]{0:T(1024)(128)(4,1)} %bitcast.45), calls=%async_computation.4 | async-start | bytes 8388608
  34.0 3.9 slice-start.1
  72.6 0.9 copy-start.6
  186.4 0.9 copy-start.9
  192.6 97.9 %copy-start.12 = (f32[1536]{0:T(1024)S(1)}, f32[1536]{0:T(1024)}, u32[]{:S(2)}) copy-start(f32[1536]{0:T(1024)} %param.18) | copy-start | bytes 18436
  289.8 304.3 %all-gather.11.cloned.1.call-start = ((), (), s32[]{:S(2)}) async-start(), calls=%async_computation.3 | async-start | bytes 10027008 | tf_op jit(solution)/shard_map/all_gather | solution.py:673
  290.5 1.1 copy-start.7
  291.6 1.1 copy-start.8
  474.8 1.1 copy-start.4
  476.0 0.8 copy-start.10
  477.0 1.4 copy-start.5
  483.4 13.4 %copy-start.11 = (f32[96,1536]{1,0:T(8,128)S(1)}, f32[96,1536]{1,0:T(8,128)}, u32[]{:S(2)}) copy-start(f32[96,1536]{1,0:T(8,128)} %copy-done.10) | copy-start | bytes 1769476
  595.5 7.4 %copy-start.1 = (f32[16,3,96]{2,0,1:T(8,128)S(1)}, f32[16,3,96]{2,0,1:T(8,128)}, u32[]{:S(2)}) copy-start(f32[16,3,96]{2,0,1:T(8,128)} %param.16) | copy-start | bytes 55300
Sparse Core Ops, SparseCore 0:
  14.7 93.6 all-gather.6
  110.6 81.9 all-gather.4
  290.0 193.4 all-gather.8
  484.9 93.8 all-gather.10

commit v7 on v6

--- a/solution.py
+++ b/solution.py
@@ -14,8 +14,9 @@
 NT = (((1,), (1,)), ((), ()))
 
 
-def attn_body(slope_ref, w_ref, b_ref, x_ref, dot_ref, pos_ref, pref_ref, *refs, blk, tok, n_swap, n_old, send_o):
+def attn_body(slope_ref, w_ref, b_ref, dot_ref, pos_ref, pref_ref, *refs, blk, tok, n_swap, n_old, n_x, send_o):
     peers = dot_ref.shape[0]
+    x_refs, refs = refs[:n_x], refs[n_x:]
     gw_old, old, refs = refs[:n_old], refs[n_old:n_old + n_swap], refs[n_old + n_swap:]
     (dqkv_ref, gwa_ref, gwb_ref, gb_ref, o_out), got, refs = refs[:5], refs[5:5 + n_swap], refs[5 + n_swap:]
     x_buf, qkvt_ref, k_tok, v_tok, posk_ref, s_buf, q_pad, do_pad, o_acc, dq_acc, dk_acc, dv_acc, x_sem = refs[:13]
@@ -36,9 +37,12 @@
     i = lax.rem(me // nq + step, steps)
     half = blk // 2
 
-    def x_copy(k):
+    def x_copies(k):
         rows = pl.ds(pl.multiple_of(k * blk, blk), blk)
-        return pltpu.make_async_copy(x_ref.at[rows], x_buf.at[rows], x_sem.at[k])
+        lo = 0
+        for n, x_ref in enumerate(x_refs):
+            yield pltpu.make_async_copy(x_ref.at[rows], x_buf.at[rows, lo:lo + x_ref.shape[1]], x_sem.at[n, k])
+            lo += x_ref.shape[1]
 
     def o_send(to):
         return pltpu.make_async_remote_copy(
@@ -63,7 +67,8 @@
     @pl.when(step == 0)
     def _():
         for k in range(steps):
-            x_copy(k).start()
+            for copy in x_copies(k):
+                copy.start()
         meet(peers)
         for one in swaps:
             swap_start(*one, peers)
@@ -75,7 +80,8 @@
         @pl.loop(0, steps)
         def _(k):
             rows = pl.ds(pl.multiple_of(k * blk, blk), blk)
-            x_copy(k).wait()
+            for copy in x_copies(k):
+                copy.wait()
             qkvt_ref[:, rows] = (lax.dot_general(w_ref[...], x_buf[rows, :], NT, preferred_element_type=F32) + b_ref[...]).astype(BF16)
 
             @pl.loop(0, blk // 128)
@@ -193,9 +199,9 @@
             swap_wait(*one, peers)
 
 
-def attention(slope2, w_head, b_head, x, dot_, pos, pref, gw, old, *, blk, tok, send_o, collective_id):
+def attention(slope2, w_head, b_head, xs, dot_, pos, pref, gw, old, *, blk, tok, send_o, collective_id):
     blocks, dim, _ = dot_.shape
-    seq, hidden = x.shape
+    seq, hidden = xs[0].shape[0], w_head.shape[1]
     wide = 128 * pl.cdiv(dim, 128)
     hbm = pl.BlockSpec(memory_space=pltpu.HBM)
     full = lambda a: pl.BlockSpec(a.shape, lambda i: (0,) * len(a.shape), pipeline_mode=pl.Buffered(1))
@@ -205,12 +211,12 @@
     pairs = (seq // blk) * (seq // blk + 1) // 2
     dma = pltpu.SemaphoreType.DMA
     res = pl.pallas_call(
-        functools.partial(attn_body, blk=blk, tok=tok, n_swap=len(old), n_old=len(gw), send_o=send_o),
+        functools.partial(attn_body, blk=blk, tok=tok, n_swap=len(old), n_old=len(gw), n_x=len(xs), send_o=send_o),
         name="attention",
         out_shape=outs + [like(dot_)] + [like(a) for a in old],
         grid=(seq // blk,),
-        in_specs=[pl.BlockSpec(memory_space=pltpu.SMEM), full(w_head), full(b_head), hbm, full(dot_), full(pos), full(pref)]
-        + [full(a) for a in gw] + [hbm] * len(old),
+        in_specs=[pl.BlockSpec(memory_space=pltpu.SMEM), full(w_head), full(b_head), full(dot_), full(pos), full(pref)]
+        + [hbm] * len(xs) + [full(a) for a in gw] + [hbm] * len(old),
         out_specs=[full(a) for a in outs] + [hbm if send_o else full(dot_)] + [hbm] * len(old),
         scratch_shapes=[
             pltpu.VMEM((seq, hidden), BF16), pltpu.VMEM((3 * dim, seq), BF16),
@@ -218,12 +224,12 @@
             pltpu.VMEM((seq, blk), F32),
             pltpu.VMEM((wide, blk), BF16), pltpu.VMEM((wide, blk), BF16),
             pltpu.VMEM((dim, blk), F32), pltpu.VMEM((dim, blk), F32),
-            pltpu.VMEM((dim, seq), F32), pltpu.VMEM((dim, seq), F32), dma((seq // blk,))]
+            pltpu.VMEM((dim, seq), F32), pltpu.VMEM((dim, seq), F32), dma((len(xs), seq // blk))]
         + sum((swap_scratch(a) for a in old), []) + ([pltpu.VMEM(dot_.shape, BF16), dma((blocks,)), dma((blocks,))] if send_o else []),
         cost_estimate=pl.CostEstimate(flops=pairs * 6 * 2 * blk * blk * 256, bytes_accessed=24 << 20, transcendentals=pairs * blk * blk),
         compiler_params=pltpu.CompilerParams(dimension_semantics=("arbitrary",), vmem_limit_bytes=52 << 20,
                                              collective_id=collective_id, has_side_effects=True),
-    )(slope2, w_head, b_head, x, dot_, pos, pref, *gw, *old)
+    )(slope2, w_head, b_head, dot_, pos, pref, *xs, *gw, *old)
     return res[0], res[1:4], res[4], res[5:]
 
 
@@ -268,9 +274,103 @@
             pltpu.SemaphoreType.DMA]
 
 
-def tail_body(dqkv_ref, d_old, o_old, o_new, dy_ref, x_ref, w_hbm, wo_hbm, gain_ref, bo_ref, y_ref, gx_ref, part, rows_ref,
-              d_new, w_ref, wo_ref, dn, mine, other, pair, landed, sums, own_d, ds_sem, dr_sem, do_sem, ps_sem, pr_sem, rs_sem, rr_sem,
-              w_sem, *, peers):
+def ring_gather(block, send_sem, recv_sem, over_sem, came_sem, peers, cuts):
+    ring = peers // 2
+    me = lax.axis_index("sp")
+    z, c = me // 2, me % 2
+    turn = lambda k: lax.rem(z + k + 2 * ring, ring)
+    step = (1, -1)
+    parts = [(w, u) for u in range(cuts) for w in range(2)]
+
+    def copy(w, t, u, side, sems, to):
+        ref = block(turn(-step[w] * t), side, w, u)
+        return pltpu.make_async_remote_copy(
+            src_ref=ref, dst_ref=ref, send_sem=sems[0].at[w, t, u], recv_sem=sems[1].at[w, t, u],
+            device_id={"sp": to}, device_id_type=pl.DeviceIdType.MESH)
+
+    along = lambda w, t, u: copy(w, t, u, c, (send_sem, recv_sem), 2 * turn(step[w]) + c)
+    across = lambda w, t, u, side: copy(w, t, u, side, (over_sem, came_sem), 2 * z + 1 - c)
+
+    def start():
+        for w, u in parts:
+            along(w, 0, u).start()
+        for w, u in parts:
+            across(w, 0, u, c).start()
+
+    def run():
+        @pl.loop(1, ring)
+        def _(t):
+            for w, u in parts:
+                along(w, t - 1, u).wait_recv()
+
+                @pl.when(t < ring - 1)
+                def _():
+                    along(w, t, u).start()
+
+                across(w, t, u, c).start()
+
+    def finish():
+        @pl.loop(0, ring - 1)
+        def _(t):
+            for w, u in parts:
+                along(w, t, u).wait_send()
+
+        @pl.loop(0, ring)
+        def _(t):
+            for w, u in parts:
+                across(w, t, u, c).wait_send()
+                across(w, t, u, 1 - c).wait_recv()
+
+    return start, run, finish
+
+
+def ring_scratch(peers, cuts):
+    dma = pltpu.SemaphoreType.DMA
+    return [dma((2, peers // 2 - 1, cuts)), dma((2, peers // 2 - 1, cuts)), dma((2, peers // 2, cuts)), dma((2, peers // 2, cuts))]
+
+
+def opening_body(marks_ref, do_ref, xb_ref, marks_all, do_t, x_all, own, ds_sem, dr_sem, do_sem, ms_sem, mr_sem, *ring_sems, peers, cuts):
+    me = lax.axis_index("sp")
+    rows, few = x_all.shape[1] // 2, x_all.shape[1] // 2 // cuts
+    block = lambda k, side, w, u: x_all.at[2 * k + side, pl.ds(w * rows + u * few, few)]
+    start, run, finish = ring_gather(block, *ring_sems, peers, cuts)
+    x_all[me] = xb_ref[...]
+    marks_all[me] = marks_ref[...]
+    meet(peers)
+    start()
+    marks = [pltpu.make_async_remote_copy(
+        src_ref=marks_ref, dst_ref=marks_all.at[me], send_sem=ms_sem.at[d - 1], recv_sem=mr_sem.at[d - 1],
+        device_id=peer_at(d, peers), device_id_type=pl.DeviceIdType.MESH) for d in range(1, peers)]
+    for copy in marks:
+        copy.start()
+    swap_start(do_ref, do_t, own, ds_sem, dr_sem, do_sem, peers)
+    run()
+    for copy in marks:
+        copy.wait()
+    swap_wait(do_ref, do_t, own, ds_sem, dr_sem, do_sem, peers)
+    finish()
+
+
+def opening(marks, do_loc, xb, collective_id, cuts=2):
+    peers = do_loc.shape[0]
+    hbm, vmem = pl.BlockSpec(memory_space=pltpu.HBM), pl.BlockSpec(memory_space=pltpu.VMEM)
+    dma = pltpu.SemaphoreType.DMA
+    return pl.pallas_call(
+        functools.partial(opening_body, peers=peers, cuts=cuts),
+        name="opening",
+        out_shape=[jax.ShapeDtypeStruct((peers,) + marks.shape, marks.dtype), jax.ShapeDtypeStruct(do_loc.shape, BF16),
+                   jax.ShapeDtypeStruct((peers,) + xb.shape, BF16)],
+        in_specs=[vmem, hbm, vmem],
+        out_specs=[vmem, hbm, vmem],
+        scratch_shapes=swap_scratch(do_loc) + [dma((peers - 1,)), dma((peers - 1,))] + ring_scratch(peers, cuts),
+        cost_estimate=pl.CostEstimate(flops=5 * 10**10, bytes_accessed=8 << 20, transcendentals=0),
+        compiler_params=pltpu.CompilerParams(collective_id=collective_id, has_side_effects=True, vmem_limit_bytes=24 << 20),
+    )(marks, do_loc, xb)
+
+
+def tail_body(dqkv_ref, d_old, o_old, o_new, dy_ref, x_ref, w_hbm, wo_hbm, gain_ref, bo_ref, gb_ref, y_ref, gx_ref, full, total, gb_all,
+              d_new, w_ref, wo_ref, dn, mine, landed, sums, rows_ref, stage, own_d, ds_sem, dr_sem, do_sem, ps_sem, pr_sem, rs_sem, rr_sem,
+              w_sem, xs_sem, xr_sem, free_sem, *ring_sems, peers, cuts):
     ring = peers // 2
     me = lax.axis_index("sp")
     z, c = me // 2, me % 2
@@ -291,12 +391,18 @@
     meet(peers)
     swap_start(dqkv_ref, d_new, own_d, ds_sem, dr_sem, do_sem, peers)
 
-    def product(out, side):
+    def product(put, side):
         @pl.loop(0, ring)
         def _(k):
             h = 2 * k + side
-            out[k] = (jnp.dot(o_old[h], dy_ref[0], preferred_element_type=F32)
-                      + jnp.dot(o_new[h], dy_ref[1], preferred_element_type=F32))
+            put(k, jnp.dot(o_old[h], dy_ref[0], preferred_element_type=F32)
+                + jnp.dot(o_new[h], dy_ref[1], preferred_element_type=F32))
+
+    def put_other(k, value):
+        full[k, 1 - c] = value
+
+    def put_mine(k, value):
+        mine[k] = value
 
     def forward(b):
         o_t = o_refs[b][...].reshape(hidden, tok)
@@ -334,16 +440,18 @@
             m2 = jnp.mean(e * hat, axis=-1, keepdims=True)
             gx_ref[b, rows, :] = (dy + inv * (e - m1 - hat * m2)).astype(BF16)
 
-    product(other, 1 - c)
-    to_pair = remote(src_ref=other, dst_ref=pair, send_sem=ps_sem, recv_sem=pr_sem, device_id=at(z, 1 - c))
-    product(mine, c)
-    to_pair.start()
+    product(put_other, 1 - c)
+    pair_copy = lambda side: remote(src_ref=full.at[:, side], dst_ref=full.at[:, side], send_sem=ps_sem, recv_sem=pr_sem, device_id=at(z, 1 - c))
+    product(put_mine, c)
+    pair_copy(1 - c).start()
     sums[...] = jnp.zeros_like(sums)
-    to_pair.wait()
+    pair_copy(1 - c).wait_send()
+    pl.semaphore_signal(free_sem, inc=1, device_id=at(z, 1 - c), device_id_type=pl.DeviceIdType.MESH)
+    pair_copy(c).wait_recv()
 
     @pl.loop(0, ring)
     def _(k):
-        mine[k] = mine[k] + pair[k]
+        mine[k] = mine[k] + full[k, c]
 
     def reduce_copy(w, t):
         return remote(src_ref=mine.at[turn(-step[w] * (1 + t)), :, cols[w]], dst_ref=landed.at[w, t],
@@ -372,154 +480,99 @@
     def _(t):
         hop(t)
 
+    owners = hidden // 128
+    lanes = lambda k: pl.ds(pl.multiple_of(k * 128, 128), 128)
+
+    def small_copy(kind, frm, to):
+        src, dst = ((rows_ref.at[:, lanes(to)], stage.at[frm]), (total.at[:, lanes(frm)],) * 2, (gb_ref, gb_all.at[frm]))[kind]
+        return remote(src_ref=src, dst_ref=dst, send_sem=xs_sem.at[kind, to], recv_sem=xr_sem.at[kind, frm], device_id={"sp": to})
+
+    def each(act, kind, only_to=False, only_from=False):
+        @pl.loop(1, peers)
+        def _(d):
+            far = lax.rem(me + d, peers)
+
+            def go():
+                act(kind, far)
+
+            if only_to:
+                pl.when(far < owners)(go)
+            elif only_from:
+                pl.when(me < owners)(go)
+            else:
+                go()
+
+    send = lambda kind, far: small_copy(kind, me, far).start()
+    sent = lambda kind, far: small_copy(kind, me, far).wait_send()
+    came = lambda kind, far: small_copy(kind, far, me).wait_recv()
+
     swap_wait(dqkv_ref, d_new, own_d, ds_sem, dr_sem, do_sem, peers)
     backward(1)
     rows_ref[...] = jnp.zeros_like(rows_ref)
     for n in range(3):
         rows_ref[n:n + 1, :] = jnp.sum(sums[n], axis=0, keepdims=True)
+    gb_all[me] = gb_ref[...]
     for w in range(2):
         add(w, ring - 2, z)
-    part[...] = mine[z]
+    full[z, c] = mine[z]
+    each(send, 0, only_to=True)
+    each(send, 2)
+    few = full.shape[2] // cuts
+    block = lambda k, side, w, u: full.at[k, side, pl.ds(u * few, few), cols[w]]
+    start, run, finish = ring_gather(block, *ring_sems, peers, cuts)
+    pl.semaphore_wait(free_sem, 1)
+    start()
+
+    @pl.when(me < owners)
+    def _():
+        stage[me] = rows_ref[:, lanes(me)]
+
+    each(came, 0, only_from=True)
+
+    @pl.when(me < owners)
+    def _():
+        total[:, lanes(me)] = jnp.sum(stage[...], axis=0)
+
+    each(send, 1, only_from=True)
+    run()
+    each(came, 1, only_to=True)
+    each(came, 2)
+    each(sent, 0, only_to=True)
+    each(sent, 1, only_from=True)
+    each(sent, 2)
 
     @pl.loop(0, ring - 1)
     def _(t):
         for w in range(2):
             reduce_copy(w, t).wait_send()
 
-
-def tail(dqkv, d_old, o_old, o_new, dy, x, w_flat, w_out, gain, b_out, collective_id):
+    finish()
+
+
+def tail(dqkv, d_old, o_old, o_new, dy, x, w_flat, w_out, gain, b_out, gb, collective_id, cuts=3):
     peers, dim, tok = o_old.shape
     ring = peers // 2
     hidden = dy.shape[-1]
     hbm, vmem = pl.BlockSpec(memory_space=pltpu.HBM), pl.BlockSpec(memory_space=pltpu.VMEM)
     dma = pltpu.SemaphoreType.DMA
-    rows = lambda *lead: pltpu.VMEM(lead + (dim, hidden), F32)
     like = lambda a: jax.ShapeDtypeStruct(a.shape, a.dtype)
     return pl.pallas_call(
-        functools.partial(tail_body, peers=peers),
+        functools.partial(tail_body, peers=peers, cuts=cuts),
         name="tail",
-        out_shape=[like(x), like(x), jax.ShapeDtypeStruct((dim, hidden), F32), jax.ShapeDtypeStruct((8, hidden), F32)],
-        in_specs=[hbm, vmem, vmem, vmem, vmem, vmem, hbm, hbm, vmem, vmem],
-        out_specs=[vmem] * 4,
+        out_shape=[like(x), like(x), jax.ShapeDtypeStruct((ring, 2, dim, hidden), F32), jax.ShapeDtypeStruct((8, hidden), F32),
+                   jax.ShapeDtypeStruct((peers,) + gb.shape, F32)],
+        in_specs=[hbm, vmem, vmem, vmem, vmem, vmem, hbm, hbm, vmem, vmem, vmem],
+        out_specs=[vmem] * 5,
         scratch_shapes=[pltpu.VMEM(dqkv.shape, BF16), pltpu.VMEM(w_flat.shape, BF16), pltpu.VMEM(w_out.shape, BF16),
-                        pltpu.VMEM((tok, hidden), F32), rows(ring), rows(ring), rows(ring),
-                        pltpu.VMEM((2, ring - 1, dim, hidden // 2), F32), pltpu.VMEM((3, 8, hidden), F32),
-                        pltpu.VMEM(dqkv.shape[1:], BF16), dma((peers - 1,)), dma((peers - 1,)), dma, dma, dma,
-                        dma((2, ring - 1)), dma((2, ring - 1)), dma((2,))],
+                        pltpu.VMEM((tok, hidden), F32), pltpu.VMEM((ring, dim, hidden), F32),
+                        pltpu.VMEM((2, ring - 1, dim, hidden // 2), F32), pltpu.VMEM((3, 8, hidden), F32), pltpu.VMEM((8, hidden), F32),
+                        pltpu.VMEM((peers, 8, 128), F32), pltpu.VMEM(dqkv.shape[1:], BF16),
+                        dma((peers - 1,)), dma((peers - 1,)), dma, dma, dma,
+                        dma((2, ring - 1)), dma((2, ring - 1)), dma((2,)), dma((3, peers)), dma((3, peers)), pltpu.SemaphoreType.REGULAR]
+        + ring_scratch(peers, cuts),
         cost_estimate=pl.CostEstimate(flops=10**11, bytes_accessed=64 << 20, transcendentals=0),
-        compiler_params=pltpu.CompilerParams(collective_id=collective_id, has_side_effects=True, vmem_limit_bytes=47 << 20),
-    )(dqkv, d_old, o_old, o_new, dy, x, w_flat, w_out, gain, b_out)
-
-
-def collect_body(part, rows_ref, gb_ref, full, total, gb_all, stage, as_sem, ar_sem, fs_sem, fr_sem, xs_sem, xr_sem, *, peers, cuts):
-    ring = peers // 2
-    me = lax.axis_index("sp")
-    z, c = me // 2, me % 2
-    half = part.shape[-1] // 2
-    few = part.shape[0] // cuts
-    turn = lambda k: lax.rem(z + k + 2 * ring, ring)
-    step = (1, -1)
-    remote = functools.partial(pltpu.make_async_remote_copy, device_id_type=pl.DeviceIdType.MESH)
-
-    def block_copy(w, t, u, side, send_sem, recv_sem, to):
-        ref = full.at[turn(-step[w] * t), side, pl.ds(u * few, few), pl.ds(w * half, half)]
-        return remote(src_ref=ref, dst_ref=ref, send_sem=send_sem.at[w, t, u], recv_sem=recv_sem.at[w, t, u], device_id={"sp": to})
-
-    gather_copy = lambda w, t, u: block_copy(w, t, u, c, as_sem, ar_sem, 2 * turn(step[w]) + c)
-    over_copy = lambda w, t, u, side: block_copy(w, t, u, side, fs_sem, fr_sem, 2 * z + 1 - c)
-    parts = [(w, u) for u in range(cuts) for w in range(2)]
-    owners = rows_ref.shape[1] // 128
-    lanes = lambda k: pl.ds(pl.multiple_of(k * 128, 128), 128)
-    full[z, c] = part[...]
-    gb_all[me] = gb_ref[...]
-    meet(peers)
-    for w, u in parts:
-        gather_copy(w, 0, u).start()
-
-    def small_copy(kind, frm, to):
-        src, dst = ((rows_ref.at[:, lanes(to)], stage.at[frm]), (total.at[:, lanes(frm)],) * 2, (gb_ref, gb_all.at[frm]))[kind]
-        return remote(src_ref=src, dst_ref=dst, send_sem=xs_sem.at[kind, to], recv_sem=xr_sem.at[kind, frm], device_id={"sp": to})
-
-    def each(act, kind, only_to=False, only_from=False):
-        @pl.loop(1, peers)
-        def _(d):
-            other = lax.rem(me + d, peers)
-
-            def go():
-                act(kind, other)
-
-            if only_to:
-                pl.when(other < owners)(go)
-            elif only_from:
-                pl.when(me < owners)(go)
-            else:
-                go()
-
-    send = lambda kind, other: small_copy(kind, me, other).start()
-    sent = lambda kind, other: small_copy(kind, me, other).wait_send()
-    came = lambda kind, other: small_copy(kind, other, me).wait_recv()
-    each(send, 0, only_to=True)
-    each(send, 2)
-    for w, u in parts:
-        over_copy(w, 0, u, c).start()
-
-    @pl.when(me < owners)
-    def _():
-        stage[me] = rows_ref[:, lanes(me)]
-
-    each(came, 0, only_from=True)
-
-    @pl.when(me < owners)
-    def _():
-        total[:, lanes(me)] = jnp.sum(stage[...], axis=0)
-
-    each(send, 1, only_from=True)
-
-    @pl.loop(1, ring)
-    def _(t):
-        for w, u in parts:
-            gather_copy(w, t - 1, u).wait_recv()
-
-            @pl.when(t < ring - 1)
-            def _():
-                gather_copy(w, t, u).start()
-
-            over_copy(w, t, u, c).start()
-
-    each(came, 1, only_to=True)
-    each(came, 2)
-    each(sent, 0, only_to=True)
-    each(sent, 1, only_from=True)
-    each(sent, 2)
-
-    @pl.loop(0, ring - 1)
-    def _(t):
-        for w, u in parts:
-            gather_copy(w, t, u).wait_send()
-
-    @pl.loop(0, ring)
-    def _(t):
-        for w, u in parts:
-            over_copy(w, t, u, c).wait_send()
-            over_copy(w, t, u, 1 - c).wait_recv()
-
-
-def collect(part, rows, gb, peers, collective_id, cuts=3):
-    ring = peers // 2
-    vmem = pl.BlockSpec(memory_space=pltpu.VMEM)
-    dma = pltpu.SemaphoreType.DMA
-    return pl.pallas_call(
-        functools.partial(collect_body, peers=peers, cuts=cuts),
-        name="collect",
-        out_shape=[jax.ShapeDtypeStruct((ring, 2) + part.shape, F32), jax.ShapeDtypeStruct(rows.shape, F32),
-                   jax.ShapeDtypeStruct((peers,) + gb.shape, F32)],
-        in_specs=[vmem] * 3,
-        out_specs=[vmem] * 3,
-        scratch_shapes=[pltpu.VMEM((peers, rows.shape[0], 128), F32), dma((2, ring - 1, cuts)), dma((2, ring - 1, cuts)),
-                        dma((2, ring, cuts)), dma((2, ring, cuts)), dma((3, peers)), dma((3, peers))],
-        cost_estimate=pl.CostEstimate(flops=5 * 10**10, bytes_accessed=10 << 20, transcendentals=0),
-        compiler_params=pltpu.CompilerParams(collective_id=collective_id, has_side_effects=True, vmem_limit_bytes=24 << 20),
-    )(part, rows, gb)
+        compiler_params=pltpu.CompilerParams(collective_id=collective_id, has_side_effects=True, vmem_limit_bytes=44 << 20),
+    )(dqkv, d_old, o_old, o_new, dy, x, w_flat, w_out, gain, b_out, gb)
 
 
 def swap_body(*refs, peers, n):
@@ -546,92 +599,60 @@
     )(*xs)
 
 
-def exchange_body(x_ref, out_ref, send_sem, recv_sem, *, peers):
-    me = lax.axis_index("sp")
-    meet(peers)
-    copies = [pltpu.make_async_remote_copy(
-        src_ref=x_ref, dst_ref=out_ref.at[me], send_sem=send_sem.at[d - 1], recv_sem=recv_sem.at[d - 1],
-        device_id=peer_at(d, peers), device_id_type=pl.DeviceIdType.MESH) for d in range(1, peers)]
-    for copy in copies:
-        copy.start()
-    out_ref[me] = x_ref[...]
-    for copy in copies:
-        copy.wait()
-
-
-def exchange(x, peers, collective_id, name):
-    return pl.pallas_call(
-        functools.partial(exchange_body, peers=peers),
-        name=name,
-        out_shape=jax.ShapeDtypeStruct((peers,) + x.shape, x.dtype),
-        in_specs=[pl.BlockSpec(memory_space=pltpu.VMEM)],
-        out_specs=pl.BlockSpec(memory_space=pltpu.VMEM),
-        scratch_shapes=[pltpu.SemaphoreType.DMA((peers - 1,)), pltpu.SemaphoreType.DMA((peers - 1,))],
-        compiler_params=pltpu.CompilerParams(collective_id=collective_id, has_side_effects=True, vmem_limit_bytes=8 << 20),
-    )(x)
-
-
-def place_body(*refs, first):
-    x_ref, (out_ref, buf, in_sem, out_sem) = refs[0], refs[-4:]
+def settle_body(*refs, n_in, first, n_plain):
+    x_ref, plain, outs = refs[0], refs[1:1 + n_plain], refs[n_in:n_in + 1 + n_plain]
+    buf, in_sem, out_sem, plain_sem = refs[n_in + 1 + n_plain:]
     heads, n = x_ref.shape[:2]
     reads = [pltpu.make_async_copy(x_ref.at[h], buf.at[h], in_sem.at[h]) for h in range(heads)]
-    writes = [pltpu.make_async_copy(buf.at[h], out_ref.at[h, pl.ds(first, n)], out_sem.at[h]) for h in range(heads)]
-    for copy in reads:
+    writes = [pltpu.make_async_copy(buf.at[h], outs[0].at[h, pl.ds(first, n)], out_sem.at[h]) for h in range(heads)]
+    flat = [pltpu.make_async_copy(plain[k], outs[1 + k], plain_sem.at[k]) for k in range(n_plain)]
+    for copy in reads + flat:
         copy.start()
     for read, write in zip(reads, writes):
         read.wait()
         write.start()
-    for copy in writes:
+    for copy in writes + flat:
         copy.wait()
 
 
-def place(x, into, lanes, first):
+def settle(x, into, plain, lanes, first):
     heads, n, dim, hidden = x.shape
-    hbm = pl.BlockSpec(memory_space=pltpu.HBM)
-    args, alias = ((x,), {}) if into is None else ((x, into), {1: 0})
+    hbm, vmem = pl.BlockSpec(memory_space=pltpu.HBM), pl.BlockSpec(memory_space=pltpu.VMEM)
+    args = (x, *plain) + (() if into is None else (into,))
     dma = pltpu.SemaphoreType.DMA
     return pl.pallas_call(
-        functools.partial(place_body, first=first), name="place",
-        out_shape=jax.ShapeDtypeStruct((heads, lanes, dim, hidden), x.dtype),
-        in_specs=[hbm] * len(args), out_specs=hbm, input_output_aliases=alias,
-        scratch_shapes=[pltpu.VMEM(x.shape, x.dtype), dma((heads,)), dma((heads,))],
+        functools.partial(settle_body, n_in=len(args), first=first, n_plain=len(plain)), name="settle",
+        out_shape=[jax.ShapeDtypeStruct((heads, lanes, dim, hidden), x.dtype)] + [jax.ShapeDtypeStruct(a.shape, a.dtype) for a in plain],
+        in_specs=[hbm] + [vmem] * len(plain) + [hbm] * (into is not None), out_specs=[hbm] * (1 + len(plain)),
+        input_output_aliases={} if into is None else {len(args) - 1: 0},
+        scratch_shapes=[pltpu.VMEM(x.shape, x.dtype), dma((heads,)), dma((heads,)), dma((max(len(plain), 1),))],
         cost_estimate=pl.CostEstimate(flops=10**9, bytes_accessed=8 * x.size, transcendentals=0),
-        compiler_params=pltpu.CompilerParams(vmem_limit_bytes=60 << 20))(*args)
-
-
-def lay_body(x_ref, out_ref, sem):
-    copies = [pltpu.make_async_copy(x_ref.at[k], out_ref.at[k], sem.at[k]) for k in range(x_ref.shape[0])]
-    for copy in copies:
-        copy.start()
-    for copy in copies:
-        copy.wait()
-
-
-def lay_down(x):
-    return pl.pallas_call(
-        lay_body, name="lay_down", out_shape=jax.ShapeDtypeStruct(x.shape, x.dtype),
-        in_specs=[pl.BlockSpec(memory_space=pltpu.VMEM)], out_specs=pl.BlockSpec(memory_space=pltpu.HBM),
-        scratch_shapes=[pltpu.SemaphoreType.DMA((x.shape[0],))],
-        cost_estimate=pl.CostEstimate(flops=10**9, bytes_accessed=8 * x.size, transcendentals=0),
-        compiler_params=pltpu.CompilerParams(vmem_limit_bytes=24 << 20))(x)
-
-
-def norm_body(x_ref, gain_ref, bias_ref, *out_refs):
-    for b, out_ref in enumerate(out_refs):
+        compiler_params=pltpu.CompilerParams(vmem_limit_bytes=(60 << 20) - 4 * sum(a.size for a in plain)))(*args)
+
+
+def norm_body(x_ref, gain_ref, bias_ref, *out_refs, pieces):
+    for b in range(x_ref.shape[0]):
         @pl.loop(0, x_ref.shape[1] // 32)
         def _(k):
             rows = pl.ds(pl.multiple_of(k * 32, 32), 32)
             x = x_ref[b, rows, :].astype(F32)
             cen = x - jnp.mean(x, axis=-1, keepdims=True)
             hat = cen * lax.rsqrt(jnp.mean(cen * cen, axis=-1, keepdims=True) + NORM_EPS)
-            out_ref[rows, :] = (hat * gain_ref[...] + bias_ref[...]).astype(BF16)
-
-
-def norm_forward(x, gain, bias):
+            out = (hat * gain_ref[...] + bias_ref[...]).astype(BF16)
+            for (of, lo), out_ref in zip(pieces, out_refs):
+                if of == b:
+                    out_ref[rows, :] = out[:, lo:lo + out_ref.shape[1]]
+
+
+def norm_forward(x, gain, bias, cut):
+    batch, tok, hidden = x.shape
+    pieces = [(0, 0), (0, cut)] + [(b, 0) for b in range(1, batch)]
+    widths = [cut, hidden - cut] + [hidden] * (batch - 1)
     vmem = pl.BlockSpec(memory_space=pltpu.VMEM)
     return pl.pallas_call(
-        norm_body, name="norm_forward", out_shape=[jax.ShapeDtypeStruct(x.shape[1:], BF16)] * x.shape[0],
-        in_specs=[vmem] * 3, out_specs=[vmem] * x.shape[0],
+        functools.partial(norm_body, pieces=pieces), name="norm_forward",
+        out_shape=[jax.ShapeDtypeStruct((tok, wide), BF16) for wide in widths],
+        in_specs=[vmem] * 3, out_specs=[vmem] * len(widths),
         cost_estimate=pl.CostEstimate(flops=10**8, bytes_accessed=4 * x.size, transcendentals=0),
         compiler_params=pltpu.CompilerParams(vmem_limit_bytes=8 << 20))(x, gain, bias)
 
@@ -646,13 +667,14 @@
         seq = tok * peers
         blk = 2 * tok
         rank = lax.axis_index("sp")
-        x_norm = norm_forward(x_blk, ln_gain.reshape(1, hidden), ln_bias.reshape(1, hidden))
-        xf = [lax.all_gather(x_norm[0], "sp", axis=0, tiled=True)]
-        marks = exchange(jnp.concatenate([pos_blk, keep_blk, jnp.zeros((8 - 2 * batch, tok), jnp.int32)]), peers, 0, "marks")
+        cut = 2 * hidden // 3
+        x_lo, x_hi, *x_rest = norm_forward(x_blk, ln_gain.reshape(1, hidden), ln_bias.reshape(1, hidden), cut)
+        xf = [lax.all_gather(one, "sp", axis=0, tiled=True) for one in [x_lo] + x_rest]
         do_loc = [lax.dot_general(w_out, dy_blk[b], NT, preferred_element_type=F32).astype(BF16).reshape(heads, dim, tok) for b in range(batch)]
-        do_t = list(swap(do_loc[:1], 1, "swap_do"))
-        for b in range(1, batch):
-            xf.append(lax.all_gather(x_norm[b], "sp", axis=0, tiled=True))
+        marks_loc = jnp.concatenate([pos_blk, keep_blk, jnp.zeros((8 - 2 * batch, tok), jnp.int32)])
+        marks, do_first, x_hi = opening(marks_loc, do_loc[0], x_hi, 1)
+        do_t = [do_first]
+        xs = [[xf[0], x_hi.reshape(seq, hidden - cut)]] + [[one] for one in xf[1:]]
         w_t = jnp.transpose(w_qkv, (1, 2, 3, 0))
         w_head = lax.dynamic_index_in_dim(w_t, rank, 0, keepdims=False).reshape(3 * dim, hidden)
         b_head = lax.dynamic_index_in_dim(b_qkv, rank, 0, keepdims=False).reshape(3 * dim, 1)
@@ -664,26 +686,21 @@
             keep = marks[:, batch + b].reshape(1, seq)
             pref = jnp.broadcast_to(pos[0, ::blk][:, None], (seq // blk, 128))
             old = list(do_loc[b + 1:b + 2]) if b + 1 < batch else list(att)
-            att_d, gw, att_o, swapped = attention(slope2, w_head, b_head, xf[b], do_t[b], jnp.where(keep > 0, pos, MASKED), pref, gw, old,
+            att_d, gw, att_o, swapped = attention(slope2, w_head, b_head, xs[b], do_t[b], jnp.where(keep > 0, pos, MASKED), pref, gw, old,
                                                   blk=blk, tok=tok, send_o=b + 1 == batch, collective_id=4 + b)
             if b + 1 < batch:
                 do_t.append(swapped[0])
             att = [att_o, att_d]
         o_old, d_old = swapped
         gw_all = [lax.all_gather(one, "sp", axis=0, tiled=True).reshape(heads, -1, dim, hidden) for one in gw[:2]]
-        cut = gw_all[0].shape[1]
-        y, gx, part, rows = tail(att_d, d_old, o_old, att_o, dy_blk, x_blk, w_t.reshape(3 * hidden, hidden), w_out,
-                                 ln_gain.reshape(1, hidden), b_out.reshape(1, hidden), 2)
-        gb, _ = lax.optimization_barrier((gw[2], part))
-        gb = jnp.pad(gb[:, 0].reshape(3, dim), ((0, 5), (0, 128 - dim)))
-        first, _ = lax.optimization_barrier((gw_all[0], part))
-        gw_out = place(first, None, 3, 0)
-        y, gx = lay_down(y), lay_down(gx)
-        rows, gw_out, y, gx = lax.optimization_barrier((rows, gw_out, y, gx))
-        go_all, total, gb_all = collect(part, rows, gb, peers, 3)
-        go_all = lay_down(go_all.reshape(heads, dim, hidden)).reshape(hidden, hidden)
-        second, go_all = lax.optimization_barrier((gw_all[1], go_all))
-        gw_out = jnp.transpose(place(second, gw_out, 3, cut), (3, 0, 1, 2))
+        lead = gw_all[0].shape[1]
+        gb = jnp.pad(gw[2][:, 0].reshape(3, dim), ((0, 5), (0, 128 - dim)))
+        y, gx, go_all, total, gb_all = tail(att_d, d_old, o_old, att_o, dy_blk, x_blk, w_t.reshape(3 * hidden, hidden), w_out,
+                                            ln_gain.reshape(1, hidden), b_out.reshape(1, hidden), gb, 2)
+        first, _ = lax.optimization_barrier((gw_all[0], y))
+        gw_out, y, gx, go_all = settle(first, None, (y, gx, go_all.reshape(hidden, hidden)), 3, 0)
+        second, gw_out = lax.optimization_barrier((gw_all[1], gw_out))
+        gw_out = jnp.transpose(settle(second, gw_out, (), 3, lead)[0], (3, 0, 1, 2))
         return y, gx, gw_out, gb_all[:, :3, :dim], go_all, total[2], total[0], total[1]
 
     act_spec = P("dp", "sp", None)

time: 610 us -> 613 us (level)
  waiting for transfers between devices: 44 us -> 6.49 us
  Pallas kernels: 529 us -> 563 us
    all_gather x2 -> x0, waiting for transfers between devices: 40.1 us -> none  [the longest x1 34.9 us: block_fn(): xf = [lax.all_gather(x_norm[0], 'sp', axis=0, tiled=True)]]
    pallas_call x10 -> x5, Pallas kernels: 354 us -> 387 us  [the longest x1 270 us: tail(): pl.pallas_call(functools.partial(tail_body, peers=peers, cuts=cuts), name...]
  transfers between devices with their start and end apart: 4 -> 4, of which waited for: 3 -> 1; matrix products, arithmetic and copies ran while one was open for 2% -> 2% of each run, Pallas kernels for 69% -> 74%
where the time goes in v7:
time: 613 us; the launch traced here: 612 us
  Pallas kernels  563 us (92%)
  local copies, waits for them, and re-layouts  18.7 us (3%)
  between operations  14.1 us (2%)
  matrix products  8.71 us (1%)
  waiting for transfers between devices  6.49 us (1%)
    pallas_call x1, Pallas kernels, tail(): pl.pallas_call(functools.partial(tail_body, peers=peers, cuts=cuts), name...  270 us
    pallas_call x2, Pallas kernels, attention(): pl.pallas_call(functools.partial(attn_body, blk=blk, tok=tok, n_swap=len(...  176 us
    pallas_call x1, Pallas kernels, opening(): pl.pallas_call(functools.partial(opening_body, peers=peers, cuts=cuts), n...  83.6 us
    pallas_call x2, Pallas kernels, settle(): pl.pallas_call(functools.partial(settle_body, n_in=len(args), first=first...  28.8 us
    unnamed x31, local copies, waits for them, and re-layouts  13.7 us
  transfers between devices with their start and end apart: 4, of which 1 were waited for; matrix products, arithmetic and copies ran while one was open for 2% of the time, Pallas kernels for 74%

profile of v7, /device:TPU:21, one launch (start us, length us, event | category | flops | bytes accessed | tf_op | source)
XLA Modules:
  0.0 612.5 jit_solution(13457253967113869389)
XLA Ops:
  7.2 0.0 copy-start
  7.2 0.1 all-gather.5.cloned.1.call-start
  7.3 0.7 reshape.134.gain_ref
  8.0 0.7 reshape.135.bias_ref
  8.7 0.0 copy-start.2
  8.7 1.4 copy-done.2
  10.1 4.4 norm_forward.1
  14.4 0.1 all-gather.5.cloned.1.call-update
  14.5 0.1 all-gather.7.cloned.1.call-start
  14.6 0.7 all-gather.7.cloned.1.call-update
  15.3 0.1 all-gather.9.cloned.1.call-start
  15.4 0.1 pad.7.clone
  15.5 0.0 copy-done
  15.5 0.2 reshape.143.b_ref
  15.7 0.8 add_add_fusion.marks_ref
  16.5 4.0 convolution_convert_fusion.1
  20.4 0.0 copy-start.6
  20.4 83.6 %opening.1 = (s32[16,8,256]{2,1,0:T(8,128)S(1)}, bf16[16,96,256]{2,1,0:T(8,128)(2,1)S(1)}, bf16[16,256,512]{2,1,0:T(8,128)(2,1)S(1)}) custom-call(s32[8,256]{1,0:T(8,128)S(1)} %add_add_fusion.marks_ref, bf16[16,96,256]{2,1,0:T(8,128)(2,1)S(1)} %bitcast.29, bf16[256,512]{1,0:T(8,128)(2,1)S(1)} %get-tuple-element.39.xb_ref), custom_call_target="tpu_custom_call" | custom-call | flops 49999998976 | bytes 8388608 | tf_op jit(solution)/shard_map/opening/pallas_call | solution.py:358
  104.0 0.0 copy-start.8
  104.0 2.0 copy-done.8
  106.0 0.0 copy-start.13
  106.0 0.9 copy-done.13
  106.9 0.1 slice.42
  107.1 0.1 slice.46
  107.2 0.1 slice_compare_fusion
  107.2 2.1 constant_dynamic-slice_fusion
  109.4 0.0 copy-done.6
  109.4 4.7 convolution_convert_fusion
  114.2 0.0 all-gather.5.cloned.1.call-done.refs_0_
  114.2 0.1 broadcast_in_dim.25.pref_ref
  114.3 77.9 %attention.2 = (bf16[16,288,256]{2,1,0:T(8,128)(2,1)}, f32[192,1536]{1,0:T(8,128)}, f32[96,1536]{1,0:T(8,128)S(1)}, f32[288,128]{1,0:T(8,128)S(1)}, bf16[16,96,2...) custom-call(f32[1]{0:T(128)} %bitcast.slope_ref, bf16[288,1536]{1,0:T(8,128)(2,1)} %bitcast.34, ...), custom_call_target="tpu_custom_call" | custom-call | flops 28991029248 | bytes 25165824 | tf_op jit(solution)/shard_map/attention/pallas_call | solution.py:213
  192.3 0.0 copy-start.12
  192.3 0.9 copy-done.12
  193.1 5.2 all-gather.7.cloned.1.call-done.refs_0_
  198.4 0.1 broadcast_in_dim.27.pref_ref
  198.4 0.0 copy-start.14
  198.4 0.0 copy-start.3
  198.4 98.1 %attention.3 = (bf16[16,288,256]{2,1,0:T(8,128)(2,1)}, f32[192,1536]{1,0:T(8,128)}, f32[96,1536]{1,0:T(8,128)}, f32[288,128]{1,0:T(8,128)S(1)}, bf16[16,96,256]{...) custom-call(f32[1]{0:T(128)} %bitcast.slope_ref, bf16[288,1536]{1,0:T(8,128)(2,1)} %bitcast.35, ...), custom_call_target="tpu_custom_call" | custom-call | flops 28991029248 | bytes 25165824 | tf_op jit(solution)/shard_map/attention/pallas_call | solution.py:213
  296.6 0.1 all-gather.9.cloned.1.call-update
  296.6 0.2 all-gather.11.cloned.1.call-start
  296.9 0.4 all-gather.11.cloned.1.call-update
  297.3 0.0 copy-done.14
  297.3 0.1 slice_reduce_fusion
  297.4 0.1 reshape_squeeze.2
  297.5 0.0 copy-done.3
  297.5 0.0 copy-start.7
  297.5 1.4 copy-done.7
  298.9 0.0 copy-start.9
  298.9 1.7 copy-done.9
  300.6 0.0 copy-start.10
  300.6 1.1 copy-done.10
  301.7 0.0 copy-start.11
  301.7 1.1 copy-done.11
  302.9 270.3 %tail.1 = (bf16[2,256,1536]{2,1,0:T(8,128)(2,1)S(1)}, bf16[2,256,1536]{2,1,0:T(8,128)(2,1)S(1)}, f32[8,2,96,1536]{3,2,1,0:T(8,128)}, f32[8,1536]{1,0:T(8,128)S(1)}, f32[16,8,128]{2,1,0:T(8,128)S(1)}) custom-call(bf16[16,288,256]{2,1,0:T(8,128)(2,1)S(1)} %copy-done.9, bf16[16,288,256]{2,1,0:T(8,128)(2,1)} %get-tuple-element.53.d_old, ...), custom_call_target="tpu_custom_call" | custom-call | flops 99999997952 | bytes 67108864 | tf_op jit(solution)/shard_map/tail/pallas_call | solution.py:559
  573.2 0.0 copy-start.4
  573.2 1.1 copy-done.4
  574.3 0.6 copy.22
  574.9 0.6 slice_reduce_fusion.1
  575.6 1.4 copy-done.5
  577.0 21.4 %settle.2 = (f32[16,3,96,1536]{3,2,1,0:T(8,128)}, bf16[2,256,1536]{2,1,0:T(8,128)(2,1)}, bf16[2,256,1536]{2,1,0:T(8,128)(2,1)}, f32[1536,1536]{1,0:T(8,128)}) custom-call(f32[16,2,96,1536]{3,2,1,0:T(8,128)} %bitcast.31, bf16[2,256,1536]{2,1,0:T(8,128)(2,1)S(1)} %get-tuple-element.57.refs_1_, bf16[2,256,1536]{2,1,0:T(8,128)(2,1)S(1)} %copy-done.5, ...), custom_call_target="tpu_custom_call" | custom-call | flops 1000000000 | bytes 37748736 | tf_op jit(solution)/shard_map/settle/pallas_call | solution.py:623
  598.4 0.0 all-gather.11.cloned.1.call-done
  598.4 0.0 copy-start.1
  598.5 7.4 %settle.3 = f32[16,3,96,1536]{3,2,1,0:T(8,128)} custom-call(f32[16,1,96,1536]{3,2,1,0:T(8,128)} %bitcast.32, f32[16,3,96,1536]{3,2,1,0:T(8,128)} %get-tuple-element.66.refs_1_), custom_call_target="tpu_custom_call", output_to_operand_aliasing={{}: (1, {})} | custom-call | flops 1000000000 | bytes 18874368 | tf_op jit(solution)/shard_map/settle/pallas_call | solution.py:623
  605.9 0.0 copy-done.1
  (10 shorter events, 0.1 us)
Async XLA Ops:
  7.2 8.3 %copy-start = (f32[16,3,96]{2,0,1:T(8,128)S(1)}, f32[16,3,96]{2,0,1:T(8,128)}, u32[]{:S(2)}) copy-start(f32[16,3,96]{2,0,1:T(8,128)} %param.16) | copy-start | bytes 55300
  7.2 107.0 %all-gather.5.cloned.1.call-start = ((), (), s32[]{:S(2)}) async-start(), calls=%async_computation | async-start | bytes 8912896 | tf_op jit(solution)/shard_map/all_gather | solution.py:672
  8.7 1.4 copy-start.2
  14.5 183.9 %all-gather.7.cloned.1.call-start = ((), (), s32[]{:S(2)}) async-start(), calls=%async_computation.1 | async-start | bytes 13369344 | tf_op jit(solution)/shard_map/all_gather | solution.py:672
  15.3 560.3 %all-gather.9.cloned.1.call-start = ((), (), s32[]{:S(2)}) async-start(), calls=%async_computation.2 | async-start | bytes 20054016 | tf_op jit(solution)/shard_map/all_gather | solution.py:695
  20.4 89.0 %copy-start.6 = (bf16[2,256,1536]{2,1,0:T(8,128)(2,1)S(1)}, bf16[2,256,1536]{2,1,0:T(8,128)(2,1)}, u32[]{:S(2)}) copy-start(bf16[2,256,1536]{2,1,0:T(8,128)(2,1)} %dy_ref.1) | copy-start | bytes 4718596
  104.0 2.0 copy-start.8
  106.0 0.9 copy-start.13
  192.3 0.9 copy-start.12
  198.4 98.8 %copy-start.14 = (f32[1536]{0:T(1024)S(1)}, f32[1536]{0:T(1024)}, u32[]{:S(2)}) copy-start(f32[1536]{0:T(1024)} %param.18) | copy-start | bytes 18436
  198.4 99.1 %copy-start.3 = (bf16[2,256,1536]{2,1,0:T(8,128)(2,1)S(1)}, bf16[2,256,1536]{2,1,0:T(8,128)(2,1)}, u32[]{:S(2)}) copy-start(bf16[2,256,1536]{2,1,0:T(8,128)(2,1)} %x_ref.3) | copy-start | bytes 4718596
  296.6 301.8 %all-gather.11.cloned.1.call-start = ((), (), s32[]{:S(2)}) async-start(), calls=%async_computation.3 | async-start | bytes 10027008 | tf_op jit(solution)/shard_map/all_gather | solution.py:695
  297.5 1.4 copy-start.7
  298.9 1.7 copy-start.9
  300.6 1.1 copy-start.10
  301.7 1.1 copy-start.11
  573.2 1.1 copy-start.4
  575.6 1.4 copy-start.5
  598.4 7.4 %copy-start.1 = (f32[16,3,96]{2,0,1:T(8,128)S(1)}, f32[16,3,96]{2,0,1:T(8,128)}, u32[]{:S(2)}) copy-start(f32[16,3,96]{2,0,1:T(8,128)} %param.16) | copy-start | bytes 55300
Sparse Core Ops, SparseCore 0:
  14.6 96.5 all-gather.4
  113.4 84.9 all-gather.6
  296.7 194.5 all-gather.8
  492.8 87.8 all-gather.10

commit v8 on v7

--- a/solution.py
+++ b/solution.py
@@ -14,13 +14,13 @@
 NT = (((1,), (1,)), ((), ()))
 
 
-def attn_body(slope_ref, w_ref, b_ref, dot_ref, pos_ref, pref_ref, *refs, blk, tok, n_swap, n_old, n_x, send_o):
+def attn_body(w_hbm, b_ref, dot_ref, marks_ref, *refs, blk, tok, which, batch, n_swap, n_old, n_x, send_o):
     peers = dot_ref.shape[0]
     x_refs, refs = refs[:n_x], refs[n_x:]
     gw_old, old, refs = refs[:n_old], refs[n_old:n_old + n_swap], refs[n_old + n_swap:]
-    (dqkv_ref, gwa_ref, gwb_ref, gb_ref, o_out), got, refs = refs[:5], refs[5:5 + n_swap], refs[5 + n_swap:]
-    x_buf, qkvt_ref, k_tok, v_tok, posk_ref, s_buf, q_pad, do_pad, o_acc, dq_acc, dk_acc, dv_acc, x_sem = refs[:13]
-    swaps = [(old[k], got[k]) + refs[13 + 4 * k:17 + 4 * k] for k in range(n_swap)]
+    (dqkv_ref, gwa_ref, gwb_ref, gb_ref, gbt_ref, o_out), got, refs = refs[:6], refs[6:6 + n_swap], refs[6 + n_swap:]
+    w_ref, b_rep, x_buf, qkvt_ref, k_tok, v_tok, posk_ref, s_buf, q_pad, do_pad, o_acc, dq_acc, dk_acc, dv_acc, x_sem, w_sem = refs[:16]
+    swaps = [(old[k], got[k]) + refs[16 + 4 * k:20 + 4 * k] for k in range(n_swap)]
     if send_o:
         o_ref, os_sem, or_sem = refs[-3:]
         o_new = o_out
@@ -36,6 +36,10 @@
     step = pl.program_id(0)
     i = lax.rem(me // nq + step, steps)
     half = blk // 2
+    sub = tok // 128
+
+    def spread(row):
+        return jnp.transpose(jnp.broadcast_to(row, (128, 128)))
 
     def x_copies(k):
         rows = pl.ds(pl.multiple_of(k * blk, blk), blk)
@@ -66,6 +70,8 @@
 
     @pl.when(step == 0)
     def _():
+        w_load = pltpu.make_async_copy(w_hbm.at[me], w_ref, w_sem)
+        w_load.start()
         for k in range(steps):
             for copy in x_copies(k):
                 copy.start()
@@ -76,13 +82,17 @@
         dv_acc[...] = jnp.zeros_like(dv_acc)
         q_pad[...] = jnp.zeros_like(q_pad)
         do_pad[...] = jnp.zeros_like(do_pad)
+        for k in range(b_ref.shape[2] // 128):
+            b_rep[k * 128:(k + 1) * 128, :] = spread(b_ref[me, :, k * 128:(k + 1) * 128])
+        w_load.wait()
 
         @pl.loop(0, steps)
         def _(k):
             rows = pl.ds(pl.multiple_of(k * blk, blk), blk)
             for copy in x_copies(k):
                 copy.wait()
-            qkvt_ref[:, rows] = (lax.dot_general(w_ref[...], x_buf[rows, :], NT, preferred_element_type=F32) + b_ref[...]).astype(BF16)
+            shift = jnp.concatenate([b_rep[0:3 * dim, :]] * (blk // 128), axis=1)
+            qkvt_ref[:, rows] = (lax.dot_general(w_ref[...], x_buf[rows, :], NT, preferred_element_type=F32) + shift).astype(BF16)
 
             @pl.loop(0, blk // 128)
             def _(t):
@@ -91,7 +101,10 @@
                     part = qkvt_ref[base:base + dim, cols].astype(F32)
                     whole = jnp.concatenate([part, jnp.zeros((pad, 128), F32)], axis=0)
                     dst[cols, :] = jnp.transpose(whole).astype(BF16)
-                posk_ref[cols, :] = jnp.transpose(jnp.broadcast_to(pos_ref[:, cols], (128, 128)))
+                lanes = pl.ds(pl.multiple_of((t % sub) * 128, 128), 128)
+                pos = marks_ref[k * nq + t // sub, which:which + 1, lanes].astype(F32)
+                keep = marks_ref[k * nq + t // sub, batch + which:batch + which + 1, lanes]
+                posk_ref[cols, :] = spread(jnp.where(keep > 0, pos, MASKED))
 
     if send_o:
         @pl.when(step > 0)
@@ -102,8 +115,8 @@
     q_pad[0:dim, :] = qkvt_ref[0:dim, qcols]
     for t in range(nq):
         do_pad[0:dim, t * tok:(t + 1) * tok] = dot_ref[i * nq + t]
-    slope2 = slope_ref[0]
-    ref_pos = pref_ref[pl.ds(i, 1), :]
+    slope2 = jnp.exp2(jnp.full((1, 128), -8.0 / peers, F32) * (me + 1).astype(F32)) * LOG2E
+    ref_pos = jnp.broadcast_to(marks_ref[i * nq, which:which + 1, 0:128][:, 0:1].astype(F32), (1, 128))
     c = scale * LOG2E
 
     def scores(j, m8, diag):
@@ -187,6 +200,11 @@
                 ref[...] += jnp.dot(lhs, x_buf[rows, :], preferred_element_type=F32)
                 gb_ref[lo:hi, :] += jnp.dot(lhs, ones, preferred_element_type=F32)
 
+        gbt_ref[...] = jnp.zeros_like(gbt_ref)
+        for k in range(3):
+            part = jnp.concatenate([gb_ref[k * dim:(k + 1) * dim, :], jnp.zeros((pad, 128), F32)], axis=0)
+            gbt_ref[k:k + 1, :] = jnp.transpose(part)[0:1, :]
+
         if send_o:
             o_keep().wait()
             for d in range(1, peers):
@@ -199,49 +217,53 @@
             swap_wait(*one, peers)
 
 
-def attention(slope2, w_head, b_head, xs, dot_, pos, pref, gw, old, *, blk, tok, send_o, collective_id):
+def attention(w_all, b_all, dot_, marks, xs, gw, old, *, blk, tok, which, batch, send_o, collective_id):
     blocks, dim, _ = dot_.shape
-    seq, hidden = xs[0].shape[0], w_head.shape[1]
+    seq, hidden = blocks * tok, w_all.shape[2]
     wide = 128 * pl.cdiv(dim, 128)
     hbm = pl.BlockSpec(memory_space=pltpu.HBM)
     full = lambda a: pl.BlockSpec(a.shape, lambda i: (0,) * len(a.shape), pipeline_mode=pl.Buffered(1))
     like = lambda a: jax.ShapeDtypeStruct(a.shape, a.dtype)
     outs = [jax.ShapeDtypeStruct((blocks, 3 * dim, tok), BF16), jax.ShapeDtypeStruct((2 * dim, hidden), F32),
-            jax.ShapeDtypeStruct((dim, hidden), F32), jax.ShapeDtypeStruct((3 * dim, 128), F32)]
+            jax.ShapeDtypeStruct((dim, hidden), F32), jax.ShapeDtypeStruct((3 * dim, 128), F32), jax.ShapeDtypeStruct((8, 128), F32)]
     pairs = (seq // blk) * (seq // blk + 1) // 2
     dma = pltpu.SemaphoreType.DMA
     res = pl.pallas_call(
-        functools.partial(attn_body, blk=blk, tok=tok, n_swap=len(old), n_old=len(gw), n_x=len(xs), send_o=send_o),
+        functools.partial(attn_body, blk=blk, tok=tok, which=which, batch=batch, n_swap=len(old), n_old=len(gw), n_x=len(xs), send_o=send_o),
         name="attention",
         out_shape=outs + [like(dot_)] + [like(a) for a in old],
         grid=(seq // blk,),
-        in_specs=[pl.BlockSpec(memory_space=pltpu.SMEM), full(w_head), full(b_head), full(dot_), full(pos), full(pref)]
-        + [hbm] * len(xs) + [full(a) for a in gw] + [hbm] * len(old),
+        in_specs=[hbm, full(b_all), full(dot_), full(marks)] + [hbm] * len(xs) + [full(a) for a in gw] + [hbm] * len(old),
         out_specs=[full(a) for a in outs] + [hbm if send_o else full(dot_)] + [hbm] * len(old),
         scratch_shapes=[
+            pltpu.VMEM(w_all.shape[1:], BF16), pltpu.VMEM((b_all.shape[2], 128), F32),
             pltpu.VMEM((seq, hidden), BF16), pltpu.VMEM((3 * dim, seq), BF16),
             pltpu.VMEM((seq, wide), BF16), pltpu.VMEM((seq, wide), BF16), pltpu.VMEM((seq, 128), F32),
             pltpu.VMEM((seq, blk), F32),
             pltpu.VMEM((wide, blk), BF16), pltpu.VMEM((wide, blk), BF16),
             pltpu.VMEM((dim, blk), F32), pltpu.VMEM((dim, blk), F32),
-            pltpu.VMEM((dim, seq), F32), pltpu.VMEM((dim, seq), F32), dma((len(xs), seq // blk))]
+            pltpu.VMEM((dim, seq), F32), pltpu.VMEM((dim, seq), F32), dma((len(xs), seq // blk)), dma]
         + sum((swap_scratch(a) for a in old), []) + ([pltpu.VMEM(dot_.shape, BF16), dma((blocks,)), dma((blocks,))] if send_o else []),
         cost_estimate=pl.CostEstimate(flops=pairs * 6 * 2 * blk * blk * 256, bytes_accessed=24 << 20, transcendentals=pairs * blk * blk),
         compiler_params=pltpu.CompilerParams(dimension_semantics=("arbitrary",), vmem_limit_bytes=52 << 20,
                                              collective_id=collective_id, has_side_effects=True),
-    )(slope2, w_head, b_head, dot_, pos, pref, *xs, *gw, *old)
-    return res[0], res[1:4], res[4], res[5:]
+    )(w_all, b_all, dot_, marks, *xs, *gw, *old)
+    return res[0], res[1:4], res[4], res[5], res[6:]
 
 
 def peer_at(d, peers):
     return {"sp": lax.rem(lax.axis_index("sp") + d, peers)}
 
 
-def meet(peers):
+def greet(peers):
     barrier = pltpu.get_barrier_semaphore()
     for d in range(1, peers):
         pl.semaphore_signal(barrier, inc=1, device_id=peer_at(d, peers), device_id_type=pl.DeviceIdType.MESH)
-    pl.semaphore_wait(barrier, peers - 1)
+    return lambda: pl.semaphore_wait(barrier, peers - 1)
+
+
+def meet(peers):
+    greet(peers)()
 
 
 def swap_copies(x_ref, out_ref, send_sem, recv_sem, peers):
@@ -274,122 +296,166 @@
             pltpu.SemaphoreType.DMA]
 
 
-def ring_gather(block, send_sem, recv_sem, over_sem, came_sem, peers, cuts):
+STEP = (1, -1)
+
+
+def hops(ring, s, w):
+    return ring // 2 - (s != w)
+
+
+def ring_gather(block, own, sems, peers, cuts):
     ring = peers // 2
     me = lax.axis_index("sp")
     z, c = me // 2, me % 2
+    send_sem, recv_sem, over_sem, came_sem = sems
     turn = lambda k: lax.rem(z + k + 2 * ring, ring)
-    step = (1, -1)
-    parts = [(w, u) for u in range(cuts) for w in range(2)]
-
-    def copy(w, t, u, side, sems, to):
-        ref = block(turn(-step[w] * t), side, w, u)
-        return pltpu.make_async_remote_copy(
-            src_ref=ref, dst_ref=ref, send_sem=sems[0].at[w, t, u], recv_sem=sems[1].at[w, t, u],
-            device_id={"sp": to}, device_id_type=pl.DeviceIdType.MESH)
-
-    along = lambda w, t, u: copy(w, t, u, c, (send_sem, recv_sem), 2 * turn(step[w]) + c)
-    across = lambda w, t, u, side: copy(w, t, u, side, (over_sem, came_sem), 2 * z + 1 - c)
+    lots = [(s, w, u) for u in range(cuts) for w in range(2) for s in range(2)]
+
+    def copy(src, dst, one, two, to):
+        return pltpu.make_async_remote_copy(src_ref=src, dst_ref=dst, send_sem=one, recv_sem=two, device_id={"sp": to},
+                                            device_id_type=pl.DeviceIdType.MESH)
+
+    def along(s, w, t, u):
+        ref = block(turn(-STEP[s] * t), c, w, u)
+        return copy(own(w, u) if t == 0 else ref, ref, send_sem.at[s, w, t, u], recv_sem.at[s, w, t, u], 2 * turn(STEP[s]) + c)
+
+    def across(s, w, t, u, side):
+        ref = block(turn(-STEP[s] * t), side, w, u)
+        return copy(own(w, u) if t == 0 and side is c else ref, ref, over_sem.at[s, w, t, u], came_sem.at[s, w, t, u], 2 * z + 1 - c)
+
+    home = [(0, w, 0, u) for u in range(cuts) for w in range(2)]
+    moved = [(s, w, t, u) for t in range(1, ring // 2 + 1) for s, w, u in lots if t <= hops(ring, s, w)]
 
     def start():
-        for w, u in parts:
-            along(w, 0, u).start()
-        for w, u in parts:
-            across(w, 0, u, c).start()
+        for s, w, u in lots:
+            along(s, w, 0, u).start()
+        for lot in home:
+            across(*lot, c).start()
 
     def run():
-        @pl.loop(1, ring)
-        def _(t):
-            for w, u in parts:
-                along(w, t - 1, u).wait_recv()
-
-                @pl.when(t < ring - 1)
-                def _():
-                    along(w, t, u).start()
-
-                across(w, t, u, c).start()
+        for s, w, t, u in moved:
+            along(s, w, t - 1, u).wait_recv()
+            if t < hops(ring, s, w):
+                along(s, w, t, u).start()
+            across(s, w, t, u, c).start()
 
     def finish():
-        @pl.loop(0, ring - 1)
-        def _(t):
-            for w, u in parts:
-                along(w, t, u).wait_send()
-
-        @pl.loop(0, ring)
-        def _(t):
-            for w, u in parts:
-                across(w, t, u, c).wait_send()
-                across(w, t, u, 1 - c).wait_recv()
+        for s, w, t, u in moved:
+            along(s, w, t - 1, u).wait_send()
+        for lot in home + moved:
+            across(*lot, c).wait_send()
+            across(*lot, 1 - c).wait_recv()
 
     return start, run, finish
 
 
 def ring_scratch(peers, cuts):
     dma = pltpu.SemaphoreType.DMA
-    return [dma((2, peers // 2 - 1, cuts)), dma((2, peers // 2 - 1, cuts)), dma((2, peers // 2, cuts)), dma((2, peers // 2, cuts))]
-
-
-def opening_body(marks_ref, do_ref, xb_ref, marks_all, do_t, x_all, own, ds_sem, dr_sem, do_sem, ms_sem, mr_sem, *ring_sems, peers, cuts):
+    return [dma((2, 2, peers // 4, cuts))] * 2 + [dma((2, 2, peers // 4 + 1, cuts))] * 2
+
+
+def opening_body(x_ref, dy_ref, wo_hbm, gain_ref, bias_ref, marks_ref, marks_all, do_t, x_all, *refs, peers, batch, cuts):
+    x_out, do_out = refs[:batch - 1], refs[batch - 1:2 * batch - 2]
+    x_own, do_own, wo_ref, own, ds_sem, dr_sem, do_sem, ms_sem, mr_sem, wo_sem, x_sem = refs[2 * batch - 2:2 * batch + 9]
+    ring_sems = refs[2 * batch + 9:]
     me = lax.axis_index("sp")
-    rows, few = x_all.shape[1] // 2, x_all.shape[1] // 2 // cuts
-    block = lambda k, side, w, u: x_all.at[2 * k + side, pl.ds(w * rows + u * few, few)]
-    start, run, finish = ring_gather(block, *ring_sems, peers, cuts)
-    x_all[me] = xb_ref[...]
-    marks_all[me] = marks_ref[...]
-    meet(peers)
+    tok, dim = x_own.shape[0], do_own.shape[1]
+    lot = tok // 2 // cuts
+    rows_of = lambda w, u: pl.ds((w * cuts + u) * lot, lot)
+    arrived = greet(peers)
+    wo_load = pltpu.make_async_copy(wo_hbm, wo_ref, wo_sem)
+    wo_load.start()
+
+    def norm(b, out_ref):
+        @pl.loop(0, tok // 32)
+        def _(k):
+            rows = pl.ds(pl.multiple_of(k * 32, 32), 32)
+            x = x_ref[b, rows, :].astype(F32)
+            cen = x - jnp.mean(x, axis=-1, keepdims=True)
+            hat = cen * lax.rsqrt(jnp.mean(cen * cen, axis=-1, keepdims=True) + NORM_EPS)
+            out_ref[rows, :] = (hat * gain_ref[...] + bias_ref[...]).astype(BF16)
+
+    def product(b, out_ref):
+        @pl.loop(0, peers // 4)
+        def _(g):
+            rows = pl.ds(pl.multiple_of(g * 4 * dim, 4 * dim), 4 * dim)
+            out_ref[pl.ds(g * 4, 4)] = lax.dot_general(wo_ref[rows, :], dy_ref[b], NT, preferred_element_type=F32).astype(BF16).reshape(4, dim, tok)
+
+    norm(0, x_own)
+    block = lambda k, side, w, u: x_all.at[2 * k + side, rows_of(w, u)]
+    start, run, finish = ring_gather(block, lambda w, u: x_own.at[rows_of(w, u)], ring_sems, peers, cuts)
+    arrived()
     start()
+    keep = pltpu.make_async_copy(x_own, x_all.at[me], x_sem)
+    keep.start()
     marks = [pltpu.make_async_remote_copy(
         src_ref=marks_ref, dst_ref=marks_all.at[me], send_sem=ms_sem.at[d - 1], recv_sem=mr_sem.at[d - 1],
         device_id=peer_at(d, peers), device_id_type=pl.DeviceIdType.MESH) for d in range(1, peers)]
     for copy in marks:
         copy.start()
-    swap_start(do_ref, do_t, own, ds_sem, dr_sem, do_sem, peers)
+    marks_all[me] = marks_ref[...]
+    wo_load.wait()
+    product(0, do_own)
+    for b in range(1, batch):
+        norm(b, x_out[b - 1])
+    swap_start(do_own, do_t, own, ds_sem, dr_sem, do_sem, peers)
+    for b in range(1, batch):
+        product(b, do_out[b - 1])
     run()
+    keep.wait()
     for copy in marks:
         copy.wait()
-    swap_wait(do_ref, do_t, own, ds_sem, dr_sem, do_sem, peers)
+    swap_wait(do_own, do_t, own, ds_sem, dr_sem, do_sem, peers)
     finish()
 
 
-def opening(marks, do_loc, xb, collective_id, cuts=2):
-    peers = do_loc.shape[0]
+def opening(x, dy, w_out, gain, bias, marks, peers, collective_id, cuts=4):
+    batch, tok, hidden = x.shape
+    dim = hidden // peers
     hbm, vmem = pl.BlockSpec(memory_space=pltpu.HBM), pl.BlockSpec(memory_space=pltpu.VMEM)
     dma = pltpu.SemaphoreType.DMA
-    return pl.pallas_call(
-        functools.partial(opening_body, peers=peers, cuts=cuts),
+    do_shape, x_shape = jax.ShapeDtypeStruct((peers, dim, tok), BF16), jax.ShapeDtypeStruct((tok, hidden), BF16)
+    res = pl.pallas_call(
+        functools.partial(opening_body, peers=peers, batch=batch, cuts=cuts),
         name="opening",
-        out_shape=[jax.ShapeDtypeStruct((peers,) + marks.shape, marks.dtype), jax.ShapeDtypeStruct(do_loc.shape, BF16),
-                   jax.ShapeDtypeStruct((peers,) + xb.shape, BF16)],
-        in_specs=[vmem, hbm, vmem],
-        out_specs=[vmem, hbm, vmem],
-        scratch_shapes=swap_scratch(do_loc) + [dma((peers - 1,)), dma((peers - 1,))] + ring_scratch(peers, cuts),
-        cost_estimate=pl.CostEstimate(flops=5 * 10**10, bytes_accessed=8 << 20, transcendentals=0),
-        compiler_params=pltpu.CompilerParams(collective_id=collective_id, has_side_effects=True, vmem_limit_bytes=24 << 20),
-    )(marks, do_loc, xb)
-
-
-def tail_body(dqkv_ref, d_old, o_old, o_new, dy_ref, x_ref, w_hbm, wo_hbm, gain_ref, bo_ref, gb_ref, y_ref, gx_ref, full, total, gb_all,
-              d_new, w_ref, wo_ref, dn, mine, landed, sums, rows_ref, stage, own_d, ds_sem, dr_sem, do_sem, ps_sem, pr_sem, rs_sem, rr_sem,
-              w_sem, xs_sem, xr_sem, free_sem, *ring_sems, peers, cuts):
+        out_shape=[jax.ShapeDtypeStruct((peers,) + marks.shape, marks.dtype), do_shape, jax.ShapeDtypeStruct((peers, tok, hidden), BF16)]
+        + [x_shape] * (batch - 1) + [do_shape] * (batch - 1),
+        in_specs=[vmem, vmem, hbm, vmem, vmem, vmem],
+        out_specs=[vmem, hbm, hbm] + [vmem] * (2 * batch - 2),
+        scratch_shapes=[pltpu.VMEM(x_shape.shape, BF16), pltpu.VMEM(do_shape.shape, BF16), pltpu.VMEM(w_out.shape, BF16)] + swap_scratch(do_shape)
+        + [dma((peers - 1,)), dma((peers - 1,)), dma, dma] + ring_scratch(peers, cuts),
+        cost_estimate=pl.CostEstimate(flops=5 * 10**10, bytes_accessed=16 << 20, transcendentals=0),
+        compiler_params=pltpu.CompilerParams(collective_id=collective_id, has_side_effects=True, vmem_limit_bytes=32 << 20),
+    )(x, dy, w_out, gain, bias, marks)
+    return res[0], res[1], res[2], res[3:2 + batch], res[2 + batch:]
+
+
+def tail_body(dqkv_ref, d_hbm, oo_hbm, on_hbm, dy_hbm, x_hbm, w_hbm, wo_hbm, gain_ref, bo_ref, gb_ref, y_ref, gx_ref, full, total, gb_all,
+              d_old, o_old, o_new, dy_ref, x_ref, d_new, w_ref, wo_ref, dn, mine, landed, sums, rows_ref, stage, own_d,
+              ds_sem, dr_sem, do_sem, ps_sem, pr_sem, rs_sem, rr_sem, w_sem, xs_sem, xr_sem, free_sem, *ring_sems, peers, cuts):
     ring = peers // 2
     me = lax.axis_index("sp")
     z, c = me // 2, me % 2
     _, tok, hidden = x_ref.shape
     half = hidden // 2
     wide = hidden // 3
+    few = full.shape[2] // cuts
     group = 8
     cols = (pl.ds(0, half), pl.ds(half, half))
     at = lambda zz, cc: {"sp": 2 * zz + cc}
     turn = lambda k: lax.rem(z + k + 2 * ring, ring)
-    step = (1, -1)
     remote = functools.partial(pltpu.make_async_remote_copy, device_id_type=pl.DeviceIdType.MESH)
     tn = (((0,), (0,)), ((), ()))
     o_refs, d_refs = (o_old, o_new), (d_old, d_new)
-    loads = [pltpu.make_async_copy(w_hbm, w_ref, w_sem.at[0]), pltpu.make_async_copy(wo_hbm, wo_ref, w_sem.at[1])]
+    pairs = ((oo_hbm, o_old), (on_hbm, o_new), (dy_hbm, dy_ref), (x_hbm, x_ref), (wo_hbm, wo_ref), (d_hbm, d_old), (w_hbm, w_ref))
+    loads = [pltpu.make_async_copy(src, dst, w_sem.at[k]) for k, (src, dst) in enumerate(pairs)]
+    arrived = greet(peers)
     for load in loads:
         load.start()
-    meet(peers)
+    arrived()
     swap_start(dqkv_ref, d_new, own_d, ds_sem, dr_sem, do_sem, peers)
+    for load in loads[:3]:
+        load.wait()
 
     def product(put, side):
         @pl.loop(0, ring)
@@ -453,33 +519,44 @@
     def _(k):
         mine[k] = mine[k] + full[k, c]
 
-    def reduce_copy(w, t):
-        return remote(src_ref=mine.at[turn(-step[w] * (1 + t)), :, cols[w]], dst_ref=landed.at[w, t],
-                      send_sem=rs_sem.at[w, t], recv_sem=rr_sem.at[w, t], device_id=at(turn(step[w]), c))
-
-    def add(w, t, k):
-        reduce_copy(w, t).wait_recv()
-        mine[k, :, cols[w]] = mine[k, :, cols[w]] + landed[w, t]
+    lots = [(s, w, u) for u in range(cuts) for w in range(2) for s in range(2)]
+
+    def reduce_copy(s, w, t, u):
+        return remote(src_ref=mine.at[turn(STEP[s] * (hops(ring, s, w) - t)), pl.ds(u * few, few), cols[w]], dst_ref=landed.at[s, w, t, u],
+                      send_sem=rs_sem.at[s, w, t, u], recv_sem=rr_sem.at[s, w, t, u], device_id=at(turn(STEP[s]), c))
+
+    def fold(s, w, t, u):
+        reduce_copy(s, w, t, u).wait_recv()
+        at_k = (turn(STEP[s] * (hops(ring, s, w) - t - 1)), pl.ds(u * few, few), cols[w])
+        mine[at_k] = mine[at_k] + landed[s, w, t, u]
 
     def hop(t):
-        for w in range(2):
-            add(w, t - 1, turn(-step[w] * (1 + t)))
-            reduce_copy(w, t).start()
-
-    for w in range(2):
-        reduce_copy(w, 0).start()
-    loads[1].wait()
+        for s, w, u in lots:
+            if t < hops(ring, s, w):
+                fold(s, w, t - 1, u)
+                reduce_copy(s, w, t, u).start()
+
+    for lot in lots:
+        reduce_copy(*lot[:2], 0, lot[2]).start()
+    loads[3].wait()
+    loads[4].wait()
     forward(0)
-    hop(1)
-    forward(1)
-    hop(2)
-    loads[0].wait()
-    backward(0)
-
-    @pl.loop(3, ring - 1)
-    def _(t):
+    for t in range(1, ring // 2):
         hop(t)
-
+        if t == 1:
+            forward(1)
+        if t == 2:
+            loads[5].wait()
+            loads[6].wait()
+            backward(0)
+    for s, w, u in lots:
+        fold(s, w, hops(ring, s, w) - 1, u)
+    full[z, c] = mine[z]
+    block = lambda k, side, w, u: full.at[k, side, pl.ds(u * few, few), cols[w]]
+    start, run, finish = ring_gather(block, lambda w, u: block(z, c, w, u), ring_sems, peers, cuts)
+    pl.semaphore_wait(free_sem, 1)
+    start()
+    run()
     owners = hidden // 128
     lanes = lambda k: pl.ds(pl.multiple_of(k * 128, 128), 128)
 
@@ -512,21 +589,13 @@
     for n in range(3):
         rows_ref[n:n + 1, :] = jnp.sum(sums[n], axis=0, keepdims=True)
     gb_all[me] = gb_ref[...]
-    for w in range(2):
-        add(w, ring - 2, z)
-    full[z, c] = mine[z]
-    each(send, 0, only_to=True)
     each(send, 2)
-    few = full.shape[2] // cuts
-    block = lambda k, side, w, u: full.at[k, side, pl.ds(u * few, few), cols[w]]
-    start, run, finish = ring_gather(block, *ring_sems, peers, cuts)
-    pl.semaphore_wait(free_sem, 1)
-    start()
 
     @pl.when(me < owners)
     def _():
         stage[me] = rows_ref[:, lanes(me)]
 
+    each(send, 0, only_to=True)
     each(came, 0, only_from=True)
 
     @pl.when(me < owners)
@@ -534,69 +603,42 @@
         total[:, lanes(me)] = jnp.sum(stage[...], axis=0)
 
     each(send, 1, only_from=True)
-    run()
     each(came, 1, only_to=True)
     each(came, 2)
     each(sent, 0, only_to=True)
     each(sent, 1, only_from=True)
     each(sent, 2)
-
-    @pl.loop(0, ring - 1)
-    def _(t):
-        for w in range(2):
-            reduce_copy(w, t).wait_send()
-
+    for s, w, u in lots:
+        for t in range(hops(ring, s, w)):
+            reduce_copy(s, w, t, u).wait_send()
     finish()
 
 
-def tail(dqkv, d_old, o_old, o_new, dy, x, w_flat, w_out, gain, b_out, gb, collective_id, cuts=3):
+def tail(dqkv, d_old, o_old, o_new, dy, x, w_flat, w_out, gain, b_out, gb, collective_id, cuts=2):
     peers, dim, tok = o_old.shape
     ring = peers // 2
     hidden = dy.shape[-1]
     hbm, vmem = pl.BlockSpec(memory_space=pltpu.HBM), pl.BlockSpec(memory_space=pltpu.VMEM)
     dma = pltpu.SemaphoreType.DMA
     like = lambda a: jax.ShapeDtypeStruct(a.shape, a.dtype)
+    held = lambda a: pltpu.VMEM(a.shape, a.dtype)
+    steps = (2, 2, ring // 2, cuts)
     return pl.pallas_call(
         functools.partial(tail_body, peers=peers, cuts=cuts),
         name="tail",
         out_shape=[like(x), like(x), jax.ShapeDtypeStruct((ring, 2, dim, hidden), F32), jax.ShapeDtypeStruct((8, hidden), F32),
                    jax.ShapeDtypeStruct((peers,) + gb.shape, F32)],
-        in_specs=[hbm, vmem, vmem, vmem, vmem, vmem, hbm, hbm, vmem, vmem, vmem],
+        in_specs=[hbm] * 8 + [vmem] * 3,
         out_specs=[vmem] * 5,
-        scratch_shapes=[pltpu.VMEM(dqkv.shape, BF16), pltpu.VMEM(w_flat.shape, BF16), pltpu.VMEM(w_out.shape, BF16),
-                        pltpu.VMEM((tok, hidden), F32), pltpu.VMEM((ring, dim, hidden), F32),
-                        pltpu.VMEM((2, ring - 1, dim, hidden // 2), F32), pltpu.VMEM((3, 8, hidden), F32), pltpu.VMEM((8, hidden), F32),
-                        pltpu.VMEM((peers, 8, 128), F32), pltpu.VMEM(dqkv.shape[1:], BF16),
-                        dma((peers - 1,)), dma((peers - 1,)), dma, dma, dma,
-                        dma((2, ring - 1)), dma((2, ring - 1)), dma((2,)), dma((3, peers)), dma((3, peers)), pltpu.SemaphoreType.REGULAR]
-        + ring_scratch(peers, cuts),
+        scratch_shapes=[held(a) for a in (d_old, o_old, o_new, dy, x, dqkv, w_flat, w_out)]
+        + [pltpu.VMEM((tok, hidden), F32), pltpu.VMEM((ring, dim, hidden), F32),
+           pltpu.VMEM(steps + (dim // cuts, hidden // 2), F32), pltpu.VMEM((3, 8, hidden), F32), pltpu.VMEM((8, hidden), F32),
+           pltpu.VMEM((peers, 8, 128), F32), pltpu.VMEM(dqkv.shape[1:], BF16),
+           dma((peers - 1,)), dma((peers - 1,)), dma, dma, dma, dma(steps), dma(steps), dma((7,)), dma((3, peers)), dma((3, peers)),
+           pltpu.SemaphoreType.REGULAR] + ring_scratch(peers, cuts),
         cost_estimate=pl.CostEstimate(flops=10**11, bytes_accessed=64 << 20, transcendentals=0),
-        compiler_params=pltpu.CompilerParams(collective_id=collective_id, has_side_effects=True, vmem_limit_bytes=44 << 20),
+        compiler_params=pltpu.CompilerParams(collective_id=collective_id, has_side_effects=True, vmem_limit_bytes=56 << 20),
     )(dqkv, d_old, o_old, o_new, dy, x, w_flat, w_out, gain, b_out, gb)
-
-
-def swap_body(*refs, peers, n):
-    ins, outs, scratch = refs[:n], refs[n:2 * n], refs[2 * n:]
-    meet(peers)
-    for k in range(n):
-        swap_start(ins[k], outs[k], *scratch[4 * k:4 * k + 4], peers)
-    for k in range(n):
-        swap_wait(ins[k], outs[k], *scratch[4 * k:4 * k + 4], peers)
-
-
-def swap(xs, collective_id, name):
-    hbm = pl.BlockSpec(memory_space=pltpu.HBM)
-    peers = xs[0].shape[0]
-    return pl.pallas_call(
-        functools.partial(swap_body, peers=peers, n=len(xs)),
-        name=name,
-        out_shape=[jax.ShapeDtypeStruct(x.shape, x.dtype) for x in xs],
-        in_specs=[hbm] * len(xs),
-        out_specs=[hbm] * len(xs),
-        scratch_shapes=sum((swap_scratch(x) for x in xs), []),
-        cost_estimate=pl.CostEstimate(flops=24000 * sum(x.size for x in xs), bytes_accessed=4 * sum(x.size for x in xs), transcendentals=0),
-        compiler_params=pltpu.CompilerParams(collective_id=collective_id, has_side_effects=True, vmem_limit_bytes=48 << 20),
-    )(*xs)
 
 
 def settle_body(*refs, n_in, first, n_plain):
@@ -630,33 +672,6 @@
         compiler_params=pltpu.CompilerParams(vmem_limit_bytes=(60 << 20) - 4 * sum(a.size for a in plain)))(*args)
 
 
-def norm_body(x_ref, gain_ref, bias_ref, *out_refs, pieces):
-    for b in range(x_ref.shape[0]):
-        @pl.loop(0, x_ref.shape[1] // 32)
-        def _(k):
-            rows = pl.ds(pl.multiple_of(k * 32, 32), 32)
-            x = x_ref[b, rows, :].astype(F32)
-            cen = x - jnp.mean(x, axis=-1, keepdims=True)
-            hat = cen * lax.rsqrt(jnp.mean(cen * cen, axis=-1, keepdims=True) + NORM_EPS)
-            out = (hat * gain_ref[...] + bias_ref[...]).astype(BF16)
-            for (of, lo), out_ref in zip(pieces, out_refs):
-                if of == b:
-                    out_ref[rows, :] = out[:, lo:lo + out_ref.shape[1]]
-
-
-def norm_forward(x, gain, bias, cut):
-    batch, tok, hidden = x.shape
-    pieces = [(0, 0), (0, cut)] + [(b, 0) for b in range(1, batch)]
-    widths = [cut, hidden - cut] + [hidden] * (batch - 1)
-    vmem = pl.BlockSpec(memory_space=pltpu.VMEM)
-    return pl.pallas_call(
-        functools.partial(norm_body, pieces=pieces), name="norm_forward",
-        out_shape=[jax.ShapeDtypeStruct((tok, wide), BF16) for wide in widths],
-        in_specs=[vmem] * 3, out_specs=[vmem] * len(widths),
-        cost_estimate=pl.CostEstimate(flops=10**8, bytes_accessed=4 * x.size, transcendentals=0),
-        compiler_params=pltpu.CompilerParams(vmem_limit_bytes=8 << 20))(x, gain, bias)
-
-
 def solution(mesh):
     peers = mesh.shape["sp"]
 
@@ -666,37 +681,26 @@
         assert heads == peers
         seq = tok * peers
         blk = 2 * tok
-        rank = lax.axis_index("sp")
-        cut = 2 * hidden // 3
-        x_lo, x_hi, *x_rest = norm_forward(x_blk, ln_gain.reshape(1, hidden), ln_bias.reshape(1, hidden), cut)
-        xf = [lax.all_gather(one, "sp", axis=0, tiled=True) for one in [x_lo] + x_rest]
-        do_loc = [lax.dot_general(w_out, dy_blk[b], NT, preferred_element_type=F32).astype(BF16).reshape(heads, dim, tok) for b in range(batch)]
+        row = lambda v: v.reshape(1, hidden)
+        w_all = jnp.transpose(w_qkv, (1, 2, 3, 0)).reshape(heads, 3 * dim, hidden)
+        b_all = jnp.pad(b_qkv.reshape(heads, 3 * dim), ((0, 0), (0, -3 * dim % 128)))[:, None]
         marks_loc = jnp.concatenate([pos_blk, keep_blk, jnp.zeros((8 - 2 * batch, tok), jnp.int32)])
-        marks, do_first, x_hi = opening(marks_loc, do_loc[0], x_hi, 1)
+        marks, do_first, x_first, x_rest, do_rest = opening(x_blk, dy_blk, w_out, row(ln_gain), row(ln_bias), marks_loc, peers, 1)
+        xs = [x_first.reshape(seq, hidden)] + [lax.all_gather(one, "sp", axis=0, tiled=True) for one in x_rest]
         do_t = [do_first]
-        xs = [[xf[0], x_hi.reshape(seq, hidden - cut)]] + [[one] for one in xf[1:]]
-        w_t = jnp.transpose(w_qkv, (1, 2, 3, 0))
-        w_head = lax.dynamic_index_in_dim(w_t, rank, 0, keepdims=False).reshape(3 * dim, hidden)
-        b_head = lax.dynamic_index_in_dim(b_qkv, rank, 0, keepdims=False).reshape(3 * dim, 1)
-        slope = jnp.exp2(-8.0 * (rank + 1).astype(F32) / heads)
-        slope2 = (slope * LOG2E).reshape(1)
         gw, att = (), []
         for b in range(batch):
-            pos = marks[:, b].reshape(1, seq).astype(F32)
-            keep = marks[:, batch + b].reshape(1, seq)
-            pref = jnp.broadcast_to(pos[0, ::blk][:, None], (seq // blk, 128))
-            old = list(do_loc[b + 1:b + 2]) if b + 1 < batch else list(att)
-            att_d, gw, att_o, swapped = attention(slope2, w_head, b_head, xs[b], do_t[b], jnp.where(keep > 0, pos, MASKED), pref, gw, old,
-                                                  blk=blk, tok=tok, send_o=b + 1 == batch, collective_id=4 + b)
+            old = list(do_rest[b:b + 1]) if b + 1 < batch else att
+            att_d, gw, gb, att_o, swapped = attention(w_all, b_all, do_t[b], marks, [xs[b]], gw, old, blk=blk, tok=tok, which=b, batch=batch,
+                                                      send_o=b + 1 == batch, collective_id=4 + b)
             if b + 1 < batch:
                 do_t.append(swapped[0])
             att = [att_o, att_d]
         o_old, d_old = swapped
         gw_all = [lax.all_gather(one, "sp", axis=0, tiled=True).reshape(heads, -1, dim, hidden) for one in gw[:2]]
         lead = gw_all[0].shape[1]
-        gb = jnp.pad(gw[2][:, 0].reshape(3, dim), ((0, 5), (0, 128 - dim)))
-        y, gx, go_all, total, gb_all = tail(att_d, d_old, o_old, att_o, dy_blk, x_blk, w_t.reshape(3 * hidden, hidden), w_out,
-                                            ln_gain.reshape(1, hidden), b_out.reshape(1, hidden), gb, 2)
+        y, gx, go_all, total, gb_all = tail(att_d, d_old, o_old, att_o, dy_blk, x_blk, w_all.reshape(3 * hidden, hidden), w_out,
+                                            row(ln_gain), row(b_out), gb, 2)
         first, _ = lax.optimization_barrier((gw_all[0], y))
         gw_out, y, gx, go_all = settle(first, None, (y, gx, go_all.reshape(hidden, hidden)), 3, 0)
         second, gw_out = lax.optimization_barrier((gw_all[1], gw_out))

time: 613 us -> 613 us (level)
  Pallas kernels: 563 us -> 572 us
  matrix products: 8.71 us -> 0 us
    dot_general x2 -> x0, matrix products: 8.71 us -> none  [block_fn(): lax.dot_general(w_out, dy_blk[b], NT, preferred_element_type=F32)]
    pallas_call x4 -> x3, Pallas kernels: 264 us -> 270 us  [the longest x2 174 us: attention(): pl.pallas_call(functools.partial(attn_body, blk=blk, tok=tok, which=which...]
    unnamed x31 -> x28, local copies, waits for them, and re-layouts: 13.7 us -> 16.6 us
  transfers between devices with their start and end apart: 4 -> 3, of which waited for: 1 -> 1; matrix products, arithmetic and copies ran while one was open for 2% -> 1% of each run, Pallas kernels for 74% -> 61%
where the time goes in v8:
time: 613 us; the launch traced here: 612 us
  Pallas kernels  572 us (93%)
  local copies, waits for them, and re-layouts  21.2 us (3%)
  between operations  13.9 us (2%)
    pallas_call x1, Pallas kernels, tail(): pl.pallas_call(functools.partial(tail_body, peers=peers, cuts=cuts), name...  273 us
    pallas_call x2, Pallas kernels, attention(): pl.pallas_call(functools.partial(attn_body, blk=blk, tok=tok, which=which...  174 us
    pallas_call x1, Pallas kernels, opening(): pl.pallas_call(functools.partial(opening_body, peers=peers, batch=batch,...  95.7 us
    pallas_call x2, Pallas kernels, settle(): pl.pallas_call(functools.partial(settle_body, n_in=len(args), first=first...  28.8 us
    unnamed x28, local copies, waits for them, and re-layouts  16.6 us
  transfers between devices with their start and end apart: 3, of which 1 were waited for; matrix products, arithmetic and copies ran while one was open for 1% of the time, Pallas kernels for 61%

profile of v8, /device:TPU:21, one launch (start us, length us, event | category | flops | bytes accessed | tf_op | source)
XLA Modules:
  0.0 612.2 jit_solution(6947533985997370554)
XLA Ops:
  7.2 0.1 all-gather.4.cloned.1.call-start
  7.2 0.7 reshape.46.gain_ref
  8.0 0.0 copy-start.2
  8.0 0.1 pad.7.clone
  8.0 0.7 reshape.47.bias_ref
  8.7 0.8 add_add_fusion.marks_ref
  9.5 0.0 copy-start.3
  9.5 2.3 copy-done.3
  11.8 0.0 copy-start.4
  11.8 1.4 copy-done.4
  13.2 0.0 copy-start.5
  13.3 1.4 copy-done.5
  14.7 0.0 copy-start.11
  14.7 95.7 %opening.1 = (s32[16,8,256]{2,1,0:T(8,128)S(1)}, bf16[16,96,256]{2,1,0:T(8,128)(2,1)S(1)}, bf16[16,256,1536]{2,1,0:T(8,128)(2,1)S(1)}, bf16[256,1536]{1,0:T(8,128)(2,1)}, bf16[16,96,256]{2,1,0:T(8,128)(2,1)S(1)}) custom-call(bf16[2,256,1536]{2,1,0:T(8,128)(2,1)S(1)} %copy-done.4, bf16[2,256,1536]{2,1,0:T(8,128)(2,1)S(1)} %copy-done.5, ...), custom_call_target="tpu_custom_call" | custom-call | flops 49999998976 | bytes 16777216 | tf_op jit(solution)/shard_map/opening/pallas_call | solution.py:418
  110.3 0.0 copy-done.2
  110.4 0.0 copy-start.6
  110.4 4.8 copy-done.6
  115.1 0.0 copy-start.8
  115.1 0.9 copy-done.8
  116.0 0.0 copy-start.9
  116.0 0.9 copy-done.9
  116.9 0.1 all-gather.4.cloned.1.call-update
  117.0 0.2 all-gather.6.cloned.1.call-start
  117.2 0.0 copy-done.11
  117.2 0.1 reshape.45
  117.4 78.3 %attention.2 = (bf16[16,288,256]{2,1,0:T(8,128)(2,1)}, f32[192,1536]{1,0:T(8,128)}, f32[96,1536]{1,0:T(8,128)S(1)}, f32[288,128]{1,0:T(8,128)S(1)}, f32[8,128]{1...) custom-call(bf16[16,288,1536]{2,1,0:T(8,128)(2,1)} %bitcast.15, ...), custom_call_target="tpu_custom_call" | custom-call | flops 28991029248 | bytes 25165824 | tf_op jit(solution)/shard_map/attention/pallas_call | solution.py:231
  195.6 0.0 copy-start.7
  195.6 0.9 copy-done.7
  196.5 3.4 all-gather.4.cloned.1.call-done.refs_0_
  199.9 0.0 copy-start.12
  199.9 95.9 %attention.3 = (bf16[16,288,256]{2,1,0:T(8,128)(2,1)}, f32[192,1536]{1,0:T(8,128)}, f32[96,1536]{1,0:T(8,128)}, f32[288,128]{1,0:T(8,128)}, f32[8,128]{1,0:T(8,1...) custom-call(bf16[16,288,1536]{2,1,0:T(8,128)(2,1)} %bitcast.16, ...), custom_call_target="tpu_custom_call" | custom-call | flops 28991029248 | bytes 25165824 | tf_op jit(solution)/shard_map/attention/pallas_call | solution.py:231
  295.8 0.0 copy-start.10
  295.8 0.6 copy-done.10
  296.4 0.1 all-gather.6.cloned.1.call-update
  296.5 0.3 all-gather.8.cloned.1.call-start
  296.8 0.5 all-gather.8.cloned.1.call-update
  297.3 0.0 copy-done.12
  297.3 0.6 reshape.50.bo_ref
  297.9 273.0 %tail.1 = (bf16[2,256,1536]{2,1,0:T(8,128)(2,1)}, bf16[2,256,1536]{2,1,0:T(8,128)(2,1)}, f32[8,2,96,1536]{3,2,1,0:T(8,128)}, f32[8,1536]{1,0:T(8,128)}, f32[16,8,128]{2,1,0:T(8,128)}) custom-call(bf16[16,288,256]{2,1,0:T(8,128)(2,1)} %get-tuple-element.50.dqkv_ref, bf16[16,288,256]{2,1,0:T(8,128)(2,1)} %get-tuple-element.51.d_hbm, ...), custom_call_target="tpu_custom_call" | custom-call | flops 99999997952 | bytes 67108864 | tf_op jit(solution)/shard_map/tail/pallas_call | solution.py:626
  570.9 0.8 slice.12
  571.8 0.6 copy.22
  572.4 1.6 slice_reduce_fusion
  573.9 0.0 all-gather.6.cloned.1.call-done
  573.9 0.0 copy-start
  573.9 1.4 copy-done
  575.3 0.0 copy-start.1
  575.3 1.4 copy-done.1
  576.8 21.4 %settle.2 = (f32[16,3,96,1536]{3,2,1,0:T(8,128)}, bf16[2,256,1536]{2,1,0:T(8,128)(2,1)}, bf16[2,256,1536]{2,1,0:T(8,128)(2,1)}, f32[1536,1536]{1,0:T(8,128)}) custom-call(f32[16,2,96,1536]{3,2,1,0:T(8,128)} %bitcast.12, bf16[2,256,1536]{2,1,0:T(8,128)(2,1)S(1)} %copy-done, bf16[2,256,1536]{2,1,0:T(8,128)(2,1)S(1)} %copy-done.1, f32[1536,1536]{1,0:T(8,128)} %bitcast.14), custom_call_target="tpu_custom_call" | custom-call | flops 1000000000 | bytes 37748736 | tf_op jit(solution)/shard_map/settle/pallas_call | solution.py:665
  598.2 0.0 all-gather.8.cloned.1.call-done
  598.2 7.4 %settle.3 = f32[16,3,96,1536]{3,2,1,0:T(8,128)} custom-call(f32[16,1,96,1536]{3,2,1,0:T(8,128)} %bitcast.13, f32[16,3,96,1536]{3,2,1,0:T(8,128)} %get-tuple-element.64.refs_1_), custom_call_target="tpu_custom_call", output_to_operand_aliasing={{}: (1, {})} | custom-call | flops 1000000000 | bytes 18874368 | tf_op jit(solution)/shard_map/settle/pallas_call | solution.py:665
  (4 shorter events, 0.0 us)
Async XLA Ops:
  7.2 192.8 %all-gather.4.cloned.1.call-start = ((), (), s32[]{:S(2)}) async-start(), calls=%async_computation | async-start | bytes 13369344 | tf_op jit(solution)/shard_map/all_gather | solution.py:689
  8.0 102.4 %copy-start.2 = (f32[1,1536]{1,0:T(1,128)}, f32[1,1536]{1,0:T(1,128)S(1)}, u32[]{:S(2)}) copy-start(f32[1,1536]{1,0:T(1,128)S(1)} %reshape.46.gain_ref) | copy-start | bytes 18436
  9.5 2.3 copy-start.3
  11.8 1.4 copy-start.4
  13.2 1.4 copy-start.5
  14.7 102.6 %copy-start.11 = (f32[16,3,96]{2,0,1:T(8,128)S(1)}, f32[16,3,96]{2,0,1:T(8,128)}, u32[]{:S(2)}) copy-start(f32[16,3,96]{2,0,1:T(8,128)} %param.16) | copy-start | bytes 55300
  110.4 4.8 copy-start.6
  115.1 0.9 copy-start.8
  116.0 0.9 copy-start.9
  117.0 457.0 %all-gather.6.cloned.1.call-start = ((), (), s32[]{:S(2)}) async-start(), calls=%async_computation.1 | async-start | bytes 20054016 | tf_op jit(solution)/shard_map/all_gather | solution.py:700
  195.6 0.9 copy-start.7
  199.9 97.3 %copy-start.12 = (f32[1536]{0:T(1024)S(1)}, f32[1536]{0:T(1024)}, u32[]{:S(2)}) copy-start(f32[1536]{0:T(1024)} %param.18) | copy-start | bytes 18436
  295.8 0.6 copy-start.10
  296.5 301.7 %all-gather.8.cloned.1.call-start = ((), (), s32[]{:S(2)}) async-start(), calls=%async_computation.2 | async-start | bytes 10027008 | tf_op jit(solution)/shard_map/all_gather | solution.py:700
  573.9 1.4 copy-start
  575.3 1.4 copy-start.1
Sparse Core Ops, SparseCore 0:
  117.1 82.8 all-gather.3
  296.6 210.5 all-gather.5
  508.9 70.4 all-gather.7

commit v9 on v8

--- a/solution.py
+++ b/solution.py
@@ -10,17 +10,18 @@
 
 LOG2E = 1.4426950408889634
 MASKED = -1e30
+VMEM_LIMIT = 62 << 20
 F32, BF16 = jnp.float32, jnp.bfloat16
 NT = (((1,), (1,)), ((), ()))
 
 
-def attn_body(w_hbm, b_ref, dot_ref, marks_ref, *refs, blk, tok, which, batch, n_swap, n_old, n_x, send_o):
+def attn_body(w_hbm, b_ref, dot_ref, marks_ref, x_ref, *refs, blk, tok, which, batch, n_swap, n_old, send_o):
     peers = dot_ref.shape[0]
-    x_refs, refs = refs[:n_x], refs[n_x:]
     gw_old, old, refs = refs[:n_old], refs[n_old:n_old + n_swap], refs[n_old + n_swap:]
     (dqkv_ref, gwa_ref, gwb_ref, gb_ref, gbt_ref, o_out), got, refs = refs[:6], refs[6:6 + n_swap], refs[6 + n_swap:]
-    w_ref, b_rep, x_buf, qkvt_ref, k_tok, v_tok, posk_ref, s_buf, q_pad, do_pad, o_acc, dq_acc, dk_acc, dv_acc, x_sem, w_sem = refs[:16]
-    swaps = [(old[k], got[k]) + refs[16 + 4 * k:20 + 4 * k] for k in range(n_swap)]
+    x_buf, refs = refs[0], refs[1:]
+    w_ref, b_rep, qkvt_ref, k_tok, v_tok, posk_ref, s_buf, q_pad, do_pad, o_acc, dq_acc, dk_acc, dv_acc, x_sem, w_sem = refs[:15]
+    swaps = [(old[k], got[k]) + refs[15 + 4 * k:19 + 4 * k] for k in range(n_swap)]
     if send_o:
         o_ref, os_sem, or_sem = refs[-3:]
         o_new = o_out
@@ -41,12 +42,9 @@
     def spread(row):
         return jnp.transpose(jnp.broadcast_to(row, (128, 128)))
 
-    def x_copies(k):
+    def x_copy(k):
         rows = pl.ds(pl.multiple_of(k * blk, blk), blk)
-        lo = 0
-        for n, x_ref in enumerate(x_refs):
-            yield pltpu.make_async_copy(x_ref.at[rows], x_buf.at[rows, lo:lo + x_ref.shape[1]], x_sem.at[n, k])
-            lo += x_ref.shape[1]
+        return pltpu.make_async_copy(x_ref.at[rows], x_buf.at[rows], x_sem.at[k])
 
     def o_send(to):
         return pltpu.make_async_remote_copy(
@@ -73,8 +71,7 @@
         w_load = pltpu.make_async_copy(w_hbm.at[me], w_ref, w_sem)
         w_load.start()
         for k in range(steps):
-            for copy in x_copies(k):
-                copy.start()
+            x_copy(k).start()
         meet(peers)
         for one in swaps:
             swap_start(*one, peers)
@@ -89,8 +86,7 @@
         @pl.loop(0, steps)
         def _(k):
             rows = pl.ds(pl.multiple_of(k * blk, blk), blk)
-            for copy in x_copies(k):
-                copy.wait()
+            x_copy(k).wait()
             shift = jnp.concatenate([b_rep[0:3 * dim, :]] * (blk // 128), axis=1)
             qkvt_ref[:, rows] = (lax.dot_general(w_ref[...], x_buf[rows, :], NT, preferred_element_type=F32) + shift).astype(BF16)
 
@@ -217,7 +213,7 @@
             swap_wait(*one, peers)
 
 
-def attention(w_all, b_all, dot_, marks, xs, gw, old, *, blk, tok, which, batch, send_o, collective_id):
+def attention(w_all, b_all, dot_, marks, x, gw, old, *, blk, tok, which, batch, send_o, collective_id):
     blocks, dim, _ = dot_.shape
     seq, hidden = blocks * tok, w_all.shape[2]
     wide = 128 * pl.cdiv(dim, 128)
@@ -229,25 +225,25 @@
     pairs = (seq // blk) * (seq // blk + 1) // 2
     dma = pltpu.SemaphoreType.DMA
     res = pl.pallas_call(
-        functools.partial(attn_body, blk=blk, tok=tok, which=which, batch=batch, n_swap=len(old), n_old=len(gw), n_x=len(xs), send_o=send_o),
+        functools.partial(attn_body, blk=blk, tok=tok, which=which, batch=batch, n_swap=len(old), n_old=len(gw), send_o=send_o),
         name="attention",
         out_shape=outs + [like(dot_)] + [like(a) for a in old],
         grid=(seq // blk,),
-        in_specs=[hbm, full(b_all), full(dot_), full(marks)] + [hbm] * len(xs) + [full(a) for a in gw] + [hbm] * len(old),
+        in_specs=[hbm, full(b_all), full(dot_), full(marks), hbm] + [full(a) for a in gw] + [hbm] * len(old),
         out_specs=[full(a) for a in outs] + [hbm if send_o else full(dot_)] + [hbm] * len(old),
         scratch_shapes=[
-            pltpu.VMEM(w_all.shape[1:], BF16), pltpu.VMEM((b_all.shape[2], 128), F32),
-            pltpu.VMEM((seq, hidden), BF16), pltpu.VMEM((3 * dim, seq), BF16),
+            pltpu.VMEM((seq, hidden), BF16),
+            pltpu.VMEM(w_all.shape[1:], BF16), pltpu.VMEM((b_all.shape[2], 128), F32), pltpu.VMEM((3 * dim, seq), BF16),
             pltpu.VMEM((seq, wide), BF16), pltpu.VMEM((seq, wide), BF16), pltpu.VMEM((seq, 128), F32),
             pltpu.VMEM((seq, blk), F32),
             pltpu.VMEM((wide, blk), BF16), pltpu.VMEM((wide, blk), BF16),
             pltpu.VMEM((dim, blk), F32), pltpu.VMEM((dim, blk), F32),
-            pltpu.VMEM((dim, seq), F32), pltpu.VMEM((dim, seq), F32), dma((len(xs), seq // blk)), dma]
+            pltpu.VMEM((dim, seq), F32), pltpu.VMEM((dim, seq), F32), dma((seq // blk,)), dma]
         + sum((swap_scratch(a) for a in old), []) + ([pltpu.VMEM(dot_.shape, BF16), dma((blocks,)), dma((blocks,))] if send_o else []),
         cost_estimate=pl.CostEstimate(flops=pairs * 6 * 2 * blk * blk * 256, bytes_accessed=24 << 20, transcendentals=pairs * blk * blk),
-        compiler_params=pltpu.CompilerParams(dimension_semantics=("arbitrary",), vmem_limit_bytes=52 << 20,
+        compiler_params=pltpu.CompilerParams(dimension_semantics=("arbitrary",), vmem_limit_bytes=VMEM_LIMIT,
                                              collective_id=collective_id, has_side_effects=True),
-    )(w_all, b_all, dot_, marks, *xs, *gw, *old)
+    )(w_all, b_all, dot_, marks, x, *gw, *old)
     return res[0], res[1:4], res[4], res[5], res[6:]
 
 
@@ -332,12 +328,13 @@
         for lot in home:
             across(*lot, c).start()
 
-    def run():
+    def run(lo=1, hi=ring):
         for s, w, t, u in moved:
-            along(s, w, t - 1, u).wait_recv()
-            if t < hops(ring, s, w):
-                along(s, w, t, u).start()
-            across(s, w, t, u, c).start()
+            if lo <= t < hi:
+                along(s, w, t - 1, u).wait_recv()
+                if t < hops(ring, s, w):
+                    along(s, w, t, u).start()
+                across(s, w, t, u, c).start()
 
     def finish():
         for s, w, t, u in moved:
@@ -354,26 +351,30 @@
     return [dma((2, 2, peers // 4, cuts))] * 2 + [dma((2, 2, peers // 4 + 1, cuts))] * 2
 
 
-def opening_body(x_ref, dy_ref, wo_hbm, gain_ref, bias_ref, marks_ref, marks_all, do_t, x_all, *refs, peers, batch, cuts):
+def opening_body(x_hbm, dy_hbm, wo_hbm, vec_ref, marks_ref, marks_all, do_t, x_all, *refs, peers, batch, cuts):
     x_out, do_out = refs[:batch - 1], refs[batch - 1:2 * batch - 2]
-    x_own, do_own, wo_ref, own, ds_sem, dr_sem, do_sem, ms_sem, mr_sem, wo_sem, x_sem = refs[2 * batch - 2:2 * batch + 9]
-    ring_sems = refs[2 * batch + 9:]
+    x_ref, dy_ref, x_own, do_own, wo_ref, own, ds_sem, dr_sem, do_sem, ms_sem, mr_sem, in_sem = refs[2 * batch - 2:2 * batch + 10]
+    ring_sems = refs[2 * batch + 10:]
     me = lax.axis_index("sp")
     tok, dim = x_own.shape[0], do_own.shape[1]
     lot = tok // 2 // cuts
     rows_of = lambda w, u: pl.ds((w * cuts + u) * lot, lot)
     arrived = greet(peers)
-    wo_load = pltpu.make_async_copy(wo_hbm, wo_ref, wo_sem)
-    wo_load.start()
+    loads = [pltpu.make_async_copy(x_hbm.at[b], x_ref.at[b], in_sem.at[b]) for b in range(batch)]
+    loads += [pltpu.make_async_copy(dy_hbm, dy_ref, in_sem.at[batch]), pltpu.make_async_copy(wo_hbm, wo_ref, in_sem.at[batch + 1])]
+    for load in loads:
+        load.start()
 
     def norm(b, out_ref):
+        loads[b].wait()
+
         @pl.loop(0, tok // 32)
         def _(k):
             rows = pl.ds(pl.multiple_of(k * 32, 32), 32)
             x = x_ref[b, rows, :].astype(F32)
             cen = x - jnp.mean(x, axis=-1, keepdims=True)
             hat = cen * lax.rsqrt(jnp.mean(cen * cen, axis=-1, keepdims=True) + NORM_EPS)
-            out_ref[rows, :] = (hat * gain_ref[...] + bias_ref[...]).astype(BF16)
+            out_ref[rows, :] = (hat * vec_ref[0:1, :] + vec_ref[1:2, :]).astype(BF16)
 
     def product(b, out_ref):
         @pl.loop(0, peers // 4)
@@ -386,7 +387,7 @@
     start, run, finish = ring_gather(block, lambda w, u: x_own.at[rows_of(w, u)], ring_sems, peers, cuts)
     arrived()
     start()
-    keep = pltpu.make_async_copy(x_own, x_all.at[me], x_sem)
+    keep = pltpu.make_async_copy(x_own, x_all.at[me], in_sem.at[batch + 2])
     keep.start()
     marks = [pltpu.make_async_remote_copy(
         src_ref=marks_ref, dst_ref=marks_all.at[me], send_sem=ms_sem.at[d - 1], recv_sem=mr_sem.at[d - 1],
@@ -394,7 +395,8 @@
     for copy in marks:
         copy.start()
     marks_all[me] = marks_ref[...]
-    wo_load.wait()
+    loads[-2].wait()
+    loads[-1].wait()
     product(0, do_own)
     for b in range(1, batch):
         norm(b, x_out[b - 1])
@@ -409,7 +411,7 @@
     finish()
 
 
-def opening(x, dy, w_out, gain, bias, marks, peers, collective_id, cuts=4):
+def opening(x, dy, w_out, vecs, marks, peers, collective_id, cuts=4):
     batch, tok, hidden = x.shape
     dim = hidden // peers
     hbm, vmem = pl.BlockSpec(memory_space=pltpu.HBM), pl.BlockSpec(memory_space=pltpu.VMEM)
@@ -420,40 +422,40 @@
         name="opening",
         out_shape=[jax.ShapeDtypeStruct((peers,) + marks.shape, marks.dtype), do_shape, jax.ShapeDtypeStruct((peers, tok, hidden), BF16)]
         + [x_shape] * (batch - 1) + [do_shape] * (batch - 1),
-        in_specs=[vmem, vmem, hbm, vmem, vmem, vmem],
+        in_specs=[hbm, hbm, hbm, vmem, vmem],
         out_specs=[vmem, hbm, hbm] + [vmem] * (2 * batch - 2),
-        scratch_shapes=[pltpu.VMEM(x_shape.shape, BF16), pltpu.VMEM(do_shape.shape, BF16), pltpu.VMEM(w_out.shape, BF16)] + swap_scratch(do_shape)
-        + [dma((peers - 1,)), dma((peers - 1,)), dma, dma] + ring_scratch(peers, cuts),
+        scratch_shapes=[pltpu.VMEM(x.shape, BF16), pltpu.VMEM(dy.shape, BF16), pltpu.VMEM(x_shape.shape, BF16), pltpu.VMEM(do_shape.shape, BF16),
+                        pltpu.VMEM(w_out.shape, BF16)] + swap_scratch(do_shape)
+        + [dma((peers - 1,)), dma((peers - 1,)), dma((batch + 3,))] + ring_scratch(peers, cuts),
         cost_estimate=pl.CostEstimate(flops=5 * 10**10, bytes_accessed=16 << 20, transcendentals=0),
-        compiler_params=pltpu.CompilerParams(collective_id=collective_id, has_side_effects=True, vmem_limit_bytes=32 << 20),
-    )(x, dy, w_out, gain, bias, marks)
+        compiler_params=pltpu.CompilerParams(collective_id=collective_id, has_side_effects=True, vmem_limit_bytes=VMEM_LIMIT),
+    )(x, dy, w_out, vecs, marks)
     return res[0], res[1], res[2], res[3:2 + batch], res[2 + batch:]
 
 
-def tail_body(dqkv_ref, d_hbm, oo_hbm, on_hbm, dy_hbm, x_hbm, w_hbm, wo_hbm, gain_ref, bo_ref, gb_ref, y_ref, gx_ref, full, total, gb_all,
-              d_old, o_old, o_new, dy_ref, x_ref, d_new, w_ref, wo_ref, dn, mine, landed, sums, rows_ref, stage, own_d,
-              ds_sem, dr_sem, do_sem, ps_sem, pr_sem, rs_sem, rr_sem, w_sem, xs_sem, xr_sem, free_sem, *ring_sems, peers, cuts):
+TN = (((0,), (0,)), ((), ()))
+
+
+def tail_a_body(dqkv_ref, oo_hbm, on_hbm, dy_hbm, x_hbm, wo_hbm, vec_ref, y_ref, part, d_out,
+                o_old, o_new, dy_ref, x_ref, wo_ref, both, mine, landed, own_d, ds_sem, dr_sem, do_sem, ps_sem, pr_sem, rs_sem, rr_sem,
+                w_sem, *, peers, cuts, sent):
     ring = peers // 2
     me = lax.axis_index("sp")
     z, c = me // 2, me % 2
     _, tok, hidden = x_ref.shape
-    half = hidden // 2
-    wide = hidden // 3
-    few = full.shape[2] // cuts
-    group = 8
+    half, wide, few = hidden // 2, hidden // 3, part.shape[0] // cuts
     cols = (pl.ds(0, half), pl.ds(half, half))
     at = lambda zz, cc: {"sp": 2 * zz + cc}
     turn = lambda k: lax.rem(z + k + 2 * ring, ring)
     remote = functools.partial(pltpu.make_async_remote_copy, device_id_type=pl.DeviceIdType.MESH)
-    tn = (((0,), (0,)), ((), ()))
-    o_refs, d_refs = (o_old, o_new), (d_old, d_new)
-    pairs = ((oo_hbm, o_old), (on_hbm, o_new), (dy_hbm, dy_ref), (x_hbm, x_ref), (wo_hbm, wo_ref), (d_hbm, d_old), (w_hbm, w_ref))
+    pairs = ((oo_hbm, o_old), (on_hbm, o_new), (dy_hbm, dy_ref), (x_hbm, x_ref), (wo_hbm, wo_ref))
     loads = [pltpu.make_async_copy(src, dst, w_sem.at[k]) for k, (src, dst) in enumerate(pairs)]
+    swap = (dqkv_ref.at[:, pl.ds(0, sent)], d_out, own_d, ds_sem, dr_sem, do_sem, peers)
     arrived = greet(peers)
     for load in loads:
         load.start()
     arrived()
-    swap_start(dqkv_ref, d_new, own_d, ds_sem, dr_sem, do_sem, peers)
+    swap_start(*swap)
     for load in loads[:3]:
         load.wait()
 
@@ -465,28 +467,122 @@
                 + jnp.dot(o_new[h], dy_ref[1], preferred_element_type=F32))
 
     def put_other(k, value):
-        full[k, 1 - c] = value
+        both[k, 1 - c] = value
 
     def put_mine(k, value):
         mine[k] = value
 
-    def forward(b):
-        o_t = o_refs[b][...].reshape(hidden, tok)
+    def forward(b, o_ref):
+        o_t = o_ref[...].reshape(hidden, tok)
 
         @pl.loop(0, 3)
         def _(n):
             at_n = pl.ds(pl.multiple_of(n * wide, wide), wide)
-            acc = lax.dot_general(o_t, wo_ref[:, at_n], tn, preferred_element_type=F32)
-            y_ref[b, :, at_n] = (x_ref[b, :, at_n].astype(F32) + acc + bo_ref[:, at_n]).astype(BF16)
-
-    def backward(b):
+            acc = lax.dot_general(o_t, wo_ref[:, at_n], TN, preferred_element_type=F32)
+            y_ref[b, :, at_n] = (x_ref[b, :, at_n].astype(F32) + acc + vec_ref[2:3, at_n]).astype(BF16)
+
+    product(put_other, 1 - c)
+    pair_copy = lambda side: remote(src_ref=both.at[:, side], dst_ref=both.at[:, side], send_sem=ps_sem, recv_sem=pr_sem, device_id=at(z, 1 - c))
+    product(put_mine, c)
+    pair_copy(1 - c).start()
+    pair_copy(1 - c).wait_send()
+    pair_copy(c).wait_recv()
+
+    @pl.loop(0, ring)
+    def _(k):
+        mine[k] = mine[k] + both[k, c]
+
+    lots = [(s, w, u) for u in range(cuts) for w in range(2) for s in range(2)]
+
+    def reduce_copy(s, w, t, u):
+        return remote(src_ref=mine.at[turn(STEP[s] * (hops(ring, s, w) - t)), pl.ds(u * few, few), cols[w]], dst_ref=landed.at[s, w, t, u],
+                      send_sem=rs_sem.at[s, w, t, u], recv_sem=rr_sem.at[s, w, t, u], device_id=at(turn(STEP[s]), c))
+
+    def fold(s, w, t, u):
+        reduce_copy(s, w, t, u).wait_recv()
+        at_k = (turn(STEP[s] * (hops(ring, s, w) - t - 1)), pl.ds(u * few, few), cols[w])
+        mine[at_k] = mine[at_k] + landed[s, w, t, u]
+
+    def hop(t):
+        for s, w, u in lots:
+            if t < hops(ring, s, w):
+                fold(s, w, t - 1, u)
+                reduce_copy(s, w, t, u).start()
+
+    for s, w, u in lots:
+        reduce_copy(s, w, 0, u).start()
+    loads[3].wait()
+    loads[4].wait()
+    forward(0, o_old)
+    hop(1)
+    forward(1, o_new)
+    for t in range(2, ring // 2):
+        hop(t)
+    for s, w, u in lots:
+        fold(s, w, hops(ring, s, w) - 1, u)
+    part[...] = mine[z]
+    swap_wait(*swap)
+    for s, w, u in lots:
+        for t in range(hops(ring, s, w)):
+            reduce_copy(s, w, t, u).wait_send()
+
+
+def tail_a(dqkv, o_old, o_new, dy, x, w_out, vecs, sent, collective_id, cuts=2):
+    peers, dim, tok = o_old.shape
+    ring = peers // 2
+    hidden = dy.shape[-1]
+    hbm, vmem = pl.BlockSpec(memory_space=pltpu.HBM), pl.BlockSpec(memory_space=pltpu.VMEM)
+    dma = pltpu.SemaphoreType.DMA
+    held = lambda a: pltpu.VMEM(a.shape, a.dtype)
+    steps = (2, 2, ring // 2, cuts)
+    return pl.pallas_call(
+        functools.partial(tail_a_body, peers=peers, cuts=cuts, sent=sent),
+        name="tail_a",
+        out_shape=[jax.ShapeDtypeStruct(x.shape, BF16), jax.ShapeDtypeStruct((dim, hidden), F32),
+                   jax.ShapeDtypeStruct((peers, sent, tok), BF16)],
+        in_specs=[hbm] * 6 + [vmem],
+        out_specs=[vmem, vmem, hbm],
+        scratch_shapes=[held(a) for a in (o_old, o_new, dy, x, w_out)]
+        + [pltpu.VMEM((ring, 2, dim, hidden), F32), pltpu.VMEM((ring, dim, hidden), F32), pltpu.VMEM(steps + (dim // cuts, hidden // 2), F32),
+           pltpu.VMEM((sent, tok), BF16), dma((peers - 1,)), dma((peers - 1,)), dma, dma, dma, dma(steps), dma(steps), dma((5,))],
+        cost_estimate=pl.CostEstimate(flops=10**11, bytes_accessed=64 << 20, transcendentals=0),
+        compiler_params=pltpu.CompilerParams(collective_id=collective_id, has_side_effects=True, vmem_limit_bytes=VMEM_LIMIT),
+    )(dqkv, o_old, o_new, dy, x, w_out, vecs)
+
+
+def tail_b_body(dqkv_ref, da_hbm, d_hbm, dy_hbm, x_hbm, w_hbm, part, vec_ref, gb_ref, gx_ref, full, total, gb_all,
+                d_old, d_new, dy_ref, x_ref, w_ref, dn, sums, rows_ref, stage, own_d, ds_sem, dr_sem, do_sem, w_sem, xs_sem, xr_sem,
+                *ring_sems, peers, cuts):
+    ring = peers // 2
+    me = lax.axis_index("sp")
+    z, c = me // 2, me % 2
+    _, tok, hidden = x_ref.shape
+    half, wide, few = hidden // 2, hidden // 3, full.shape[2] // cuts
+    sent, span = da_hbm.shape[1], d_old.shape[1]
+    rest = pl.ds(sent, span - sent)
+    group = 8
+    cols = (pl.ds(0, half), pl.ds(half, half))
+    remote = functools.partial(pltpu.make_async_remote_copy, device_id_type=pl.DeviceIdType.MESH)
+    pairs = ((w_hbm, w_ref), (d_hbm, d_old), (dy_hbm, dy_ref), (x_hbm, x_ref), (da_hbm, d_new.at[:, pl.ds(0, sent)]))
+    loads = [pltpu.make_async_copy(src, dst, w_sem.at[k]) for k, (src, dst) in enumerate(pairs)]
+    swap = (dqkv_ref.at[:, rest], d_new.at[:, rest], own_d, ds_sem, dr_sem, do_sem, peers)
+    arrived = greet(peers)
+    for load in loads:
+        load.start()
+    full[z, c] = part[...]
+    gb_all[me] = gb_ref[...]
+    sums[...] = jnp.zeros_like(sums)
+    block = lambda k, side, w, u: full.at[k, side, pl.ds(u * few, few), cols[w]]
+    start, run, finish = ring_gather(block, lambda w, u: block(z, c, w, u), ring_sems, peers, cuts)
+
+    def backward(b, d_ref):
         @pl.loop(0, 3)
         def _(n):
             at_n = pl.ds(pl.multiple_of(n * wide, wide), wide)
             acc = None
             for k in range(0, peers, group):
-                lhs = d_refs[b][k:k + group].reshape(-1, tok)
-                one = lax.dot_general(lhs, w_ref[k * lhs.shape[0] // group:(k + group) * lhs.shape[0] // group, at_n], tn, preferred_element_type=F32)
+                lhs = d_ref[k:k + group].reshape(-1, tok)
+                one = lax.dot_general(lhs, w_ref[k * span:(k + group) * span, at_n], TN, preferred_element_type=F32)
                 acc = one if acc is None else acc + one
             dn[:, at_n] = acc
 
@@ -501,62 +597,11 @@
             hat = cen * inv
             for n, one in enumerate((d * hat, d, dy)):
                 sums[n] += jnp.sum(one.reshape(4, 8, hidden), axis=0)
-            e = d * gain_ref[...]
+            e = d * vec_ref[0:1, :]
             m1 = jnp.mean(e, axis=-1, keepdims=True)
             m2 = jnp.mean(e * hat, axis=-1, keepdims=True)
             gx_ref[b, rows, :] = (dy + inv * (e - m1 - hat * m2)).astype(BF16)
 
-    product(put_other, 1 - c)
-    pair_copy = lambda side: remote(src_ref=full.at[:, side], dst_ref=full.at[:, side], send_sem=ps_sem, recv_sem=pr_sem, device_id=at(z, 1 - c))
-    product(put_mine, c)
-    pair_copy(1 - c).start()
-    sums[...] = jnp.zeros_like(sums)
-    pair_copy(1 - c).wait_send()
-    pl.semaphore_signal(free_sem, inc=1, device_id=at(z, 1 - c), device_id_type=pl.DeviceIdType.MESH)
-    pair_copy(c).wait_recv()
-
-    @pl.loop(0, ring)
-    def _(k):
-        mine[k] = mine[k] + full[k, c]
-
-    lots = [(s, w, u) for u in range(cuts) for w in range(2) for s in range(2)]
-
-    def reduce_copy(s, w, t, u):
-        return remote(src_ref=mine.at[turn(STEP[s] * (hops(ring, s, w) - t)), pl.ds(u * few, few), cols[w]], dst_ref=landed.at[s, w, t, u],
-                      send_sem=rs_sem.at[s, w, t, u], recv_sem=rr_sem.at[s, w, t, u], device_id=at(turn(STEP[s]), c))
-
-    def fold(s, w, t, u):
-        reduce_copy(s, w, t, u).wait_recv()
-        at_k = (turn(STEP[s] * (hops(ring, s, w) - t - 1)), pl.ds(u * few, few), cols[w])
-        mine[at_k] = mine[at_k] + landed[s, w, t, u]
-
-    def hop(t):
-        for s, w, u in lots:
-            if t < hops(ring, s, w):
-                fold(s, w, t - 1, u)
-                reduce_copy(s, w, t, u).start()
-
-    for lot in lots:
-        reduce_copy(*lot[:2], 0, lot[2]).start()
-    loads[3].wait()
-    loads[4].wait()
-    forward(0)
-    for t in range(1, ring // 2):
-        hop(t)
-        if t == 1:
-            forward(1)
-        if t == 2:
-            loads[5].wait()
-            loads[6].wait()
-            backward(0)
-    for s, w, u in lots:
-        fold(s, w, hops(ring, s, w) - 1, u)
-    full[z, c] = mine[z]
-    block = lambda k, side, w, u: full.at[k, side, pl.ds(u * few, few), cols[w]]
-    start, run, finish = ring_gather(block, lambda w, u: block(z, c, w, u), ring_sems, peers, cuts)
-    pl.semaphore_wait(free_sem, 1)
-    start()
-    run()
     owners = hidden // 128
     lanes = lambda k: pl.ds(pl.multiple_of(k * 128, 128), 128)
 
@@ -580,16 +625,24 @@
                 go()
 
     send = lambda kind, far: small_copy(kind, me, far).start()
-    sent = lambda kind, far: small_copy(kind, me, far).wait_send()
+    over = lambda kind, far: small_copy(kind, me, far).wait_send()
     came = lambda kind, far: small_copy(kind, far, me).wait_recv()
 
-    swap_wait(dqkv_ref, d_new, own_d, ds_sem, dr_sem, do_sem, peers)
-    backward(1)
+    arrived()
+    start()
+    swap_start(*swap)
+    each(send, 2)
+    run(1, 2)
+    for load in loads[:4]:
+        load.wait()
+    backward(0, d_old)
+    run(2)
+    loads[4].wait()
+    swap_wait(*swap)
+    backward(1, d_new)
     rows_ref[...] = jnp.zeros_like(rows_ref)
     for n in range(3):
         rows_ref[n:n + 1, :] = jnp.sum(sums[n], axis=0, keepdims=True)
-    gb_all[me] = gb_ref[...]
-    each(send, 2)
 
     @pl.when(me < owners)
     def _():
@@ -605,40 +658,32 @@
     each(send, 1, only_from=True)
     each(came, 1, only_to=True)
     each(came, 2)
-    each(sent, 0, only_to=True)
-    each(sent, 1, only_from=True)
-    each(sent, 2)
-    for s, w, u in lots:
-        for t in range(hops(ring, s, w)):
-            reduce_copy(s, w, t, u).wait_send()
+    each(over, 0, only_to=True)
+    each(over, 1, only_from=True)
+    each(over, 2)
     finish()
 
 
-def tail(dqkv, d_old, o_old, o_new, dy, x, w_flat, w_out, gain, b_out, gb, collective_id, cuts=2):
-    peers, dim, tok = o_old.shape
+def tail_b(dqkv, d_part, d_old, dy, x, w_flat, part, vecs, gb, peers, collective_id, cuts=2):
     ring = peers // 2
-    hidden = dy.shape[-1]
+    tok, hidden = x.shape[1:]
     hbm, vmem = pl.BlockSpec(memory_space=pltpu.HBM), pl.BlockSpec(memory_space=pltpu.VMEM)
     dma = pltpu.SemaphoreType.DMA
-    like = lambda a: jax.ShapeDtypeStruct(a.shape, a.dtype)
     held = lambda a: pltpu.VMEM(a.shape, a.dtype)
-    steps = (2, 2, ring // 2, cuts)
     return pl.pallas_call(
-        functools.partial(tail_body, peers=peers, cuts=cuts),
-        name="tail",
-        out_shape=[like(x), like(x), jax.ShapeDtypeStruct((ring, 2, dim, hidden), F32), jax.ShapeDtypeStruct((8, hidden), F32),
-                   jax.ShapeDtypeStruct((peers,) + gb.shape, F32)],
-        in_specs=[hbm] * 8 + [vmem] * 3,
-        out_specs=[vmem] * 5,
-        scratch_shapes=[held(a) for a in (d_old, o_old, o_new, dy, x, dqkv, w_flat, w_out)]
-        + [pltpu.VMEM((tok, hidden), F32), pltpu.VMEM((ring, dim, hidden), F32),
-           pltpu.VMEM(steps + (dim // cuts, hidden // 2), F32), pltpu.VMEM((3, 8, hidden), F32), pltpu.VMEM((8, hidden), F32),
-           pltpu.VMEM((peers, 8, 128), F32), pltpu.VMEM(dqkv.shape[1:], BF16),
-           dma((peers - 1,)), dma((peers - 1,)), dma, dma, dma, dma(steps), dma(steps), dma((7,)), dma((3, peers)), dma((3, peers)),
-           pltpu.SemaphoreType.REGULAR] + ring_scratch(peers, cuts),
+        functools.partial(tail_b_body, peers=peers, cuts=cuts),
+        name="tail_b",
+        out_shape=[jax.ShapeDtypeStruct(x.shape, BF16), jax.ShapeDtypeStruct((ring, 2) + part.shape, F32),
+                   jax.ShapeDtypeStruct((8, hidden), F32), jax.ShapeDtypeStruct((peers,) + gb.shape, F32)],
+        in_specs=[hbm] * 6 + [vmem] * 3,
+        out_specs=[vmem] * 4,
+        scratch_shapes=[held(a) for a in (d_old, d_old, dy, x, w_flat)]
+        + [pltpu.VMEM((tok, hidden), F32), pltpu.VMEM((3, 8, hidden), F32), pltpu.VMEM((8, hidden), F32), pltpu.VMEM((peers, 8, 128), F32),
+           pltpu.VMEM((d_old.shape[1] - d_part.shape[1], tok), BF16), dma((peers - 1,)), dma((peers - 1,)), dma, dma((5,)),
+           dma((3, peers)), dma((3, peers))] + ring_scratch(peers, cuts),
         cost_estimate=pl.CostEstimate(flops=10**11, bytes_accessed=64 << 20, transcendentals=0),
-        compiler_params=pltpu.CompilerParams(collective_id=collective_id, has_side_effects=True, vmem_limit_bytes=56 << 20),
-    )(dqkv, d_old, o_old, o_new, dy, x, w_flat, w_out, gain, b_out, gb)
+        compiler_params=pltpu.CompilerParams(collective_id=collective_id, has_side_effects=True, vmem_limit_bytes=VMEM_LIMIT),
+    )(dqkv, d_part, d_old, dy, x, w_flat, part, vecs, gb)
 
 
 def settle_body(*refs, n_in, first, n_plain):
@@ -681,17 +726,17 @@
         assert heads == peers
         seq = tok * peers
         blk = 2 * tok
-        row = lambda v: v.reshape(1, hidden)
+        vecs = jnp.stack([ln_gain, ln_bias, b_out] + [jnp.zeros_like(b_out)] * 5)
         w_all = jnp.transpose(w_qkv, (1, 2, 3, 0)).reshape(heads, 3 * dim, hidden)
         b_all = jnp.pad(b_qkv.reshape(heads, 3 * dim), ((0, 0), (0, -3 * dim % 128)))[:, None]
         marks_loc = jnp.concatenate([pos_blk, keep_blk, jnp.zeros((8 - 2 * batch, tok), jnp.int32)])
-        marks, do_first, x_first, x_rest, do_rest = opening(x_blk, dy_blk, w_out, row(ln_gain), row(ln_bias), marks_loc, peers, 1)
+        marks, do_first, x_first, x_rest, do_rest = opening(x_blk, dy_blk, w_out, vecs, marks_loc, peers, 1)
         xs = [x_first.reshape(seq, hidden)] + [lax.all_gather(one, "sp", axis=0, tiled=True) for one in x_rest]
         do_t = [do_first]
         gw, att = (), []
         for b in range(batch):
             old = list(do_rest[b:b + 1]) if b + 1 < batch else att
-            att_d, gw, gb, att_o, swapped = attention(w_all, b_all, do_t[b], marks, [xs[b]], gw, old, blk=blk, tok=tok, which=b, batch=batch,
+            att_d, gw, gb, att_o, swapped = attention(w_all, b_all, do_t[b], marks, xs[b], gw, old, blk=blk, tok=tok, which=b, batch=batch,
                                                       send_o=b + 1 == batch, collective_id=4 + b)
             if b + 1 < batch:
                 do_t.append(swapped[0])
@@ -699,12 +744,14 @@
         o_old, d_old = swapped
         gw_all = [lax.all_gather(one, "sp", axis=0, tiled=True).reshape(heads, -1, dim, hidden) for one in gw[:2]]
         lead = gw_all[0].shape[1]
-        y, gx, go_all, total, gb_all = tail(att_d, d_old, o_old, att_o, dy_blk, x_blk, w_all.reshape(3 * hidden, hidden), w_out,
-                                            row(ln_gain), row(b_out), gb, 2)
+        y, part, d_part = tail_a(att_d, o_old, att_o, dy_blk, x_blk, w_out, vecs, 2 * dim, 2)
         first, _ = lax.optimization_barrier((gw_all[0], y))
-        gw_out, y, gx, go_all = settle(first, None, (y, gx, go_all.reshape(hidden, hidden)), 3, 0)
-        second, gw_out = lax.optimization_barrier((gw_all[1], gw_out))
-        gw_out = jnp.transpose(settle(second, gw_out, (), 3, lead)[0], (3, 0, 1, 2))
+        gw_out, y = settle(first, None, (y,), 3, 0)
+        part, gw_out, y = lax.optimization_barrier((part, gw_out, y))
+        gx, go_all, total, gb_all = tail_b(att_d, d_part, d_old, dy_blk, x_blk, w_all.reshape(3 * hidden, hidden), part, vecs, gb, peers, 3)
+        second, gw_out, gx = lax.optimization_barrier((gw_all[1], gw_out, gx))
+        gw_out, gx, go_all = settle(second, gw_out, (gx, go_all.reshape(hidden, hidden)), 3, lead)
+        gw_out = jnp.transpose(gw_out, (3, 0, 1, 2))
         return y, gx, gw_out, gb_all[:, :3, :dim], go_all, total[2], total[0], total[1]
 
     act_spec = P("dp", "sp", None)

time: 613 us -> 637 us (1.039)
  waiting for transfers between devices: 4.05 us -> 34.4 us
  local copies, waits for them, and re-layouts: 21.2 us -> 8.03 us
    all_gather x3, waiting for transfers between devices: 3.44 us -> 33.8 us  [block_fn(): lax.all_gather(one, 'sp', axis=0, tiled=True)]
    unnamed x28 -> x6, local copies, waits for them, and re-layouts: 16.6 us -> 2.04 us
    pallas_call x1 -> x2, Pallas kernels: 273 us -> 275 us  [the longest x1 146 us: tail_a(): pl.pallas_call(functools.partial(tail_a_body, peers=peers, cuts=cuts, sen...]
  transfers between devices with their start and end apart: 3 -> 3, of which waited for: 1 -> 2; matrix products, arithmetic and copies ran while one was open for 1% -> 0% of each run, Pallas kernels for 61% -> 58%
where the time goes in v9:
time: 637 us; the launch traced here: 636 us
  Pallas kernels  578 us (91%)
  waiting for transfers between devices  34.4 us (5%)
  between operations  13.9 us (2%)
  local copies, waits for them, and re-layouts  8.03 us (1%)
    pallas_call x2, Pallas kernels, attention(): pl.pallas_call(functools.partial(attn_body, blk=blk, tok=tok, which=which...  175 us
    pallas_call x1, Pallas kernels, tail_a(): pl.pallas_call(functools.partial(tail_a_body, peers=peers, cuts=cuts, sen...  146 us
    pallas_call x1, Pallas kernels, tail_b(): pl.pallas_call(functools.partial(tail_b_body, peers=peers, cuts=cuts), na...  129 us
    pallas_call x1, Pallas kernels, opening(): pl.pallas_call(functools.partial(opening_body, peers=peers, batch=batch,...  97.3 us
    all_gather x3, waiting for transfers between devices, block_fn(): lax.all_gather(one, 'sp', axis=0, tiled=True)  33.8 us
    pallas_call x2, Pallas kernels, settle(): pl.pallas_call(functools.partial(settle_body, n_in=len(args), first=first...  30.4 us
  transfers between devices with their start and end apart: 3, of which 2 were waited for; matrix products, arithmetic and copies ran while one was open for 0% of the time, Pallas kernels for 58%

profile of v9, /device:TPU:21, one launch (start us, length us, event | category | flops | bytes accessed | tf_op | source)
XLA Modules:
  0.0 635.9 jit_solution(9164652347554947212)
XLA Ops:
  7.2 0.1 all-gather.4.cloned.1.call-start
  7.3 0.1 pad.7.clone
  7.3 0.7 stack.15
  8.0 0.7 stack.16
  8.7 0.7 stack.17
  9.4 1.4 add_add_fusion.marks_ref
  10.8 0.7 stack.19.vec_ref
  11.5 0.0 copy-start.1
  11.5 97.3 %opening.1 = (s32[16,8,256]{2,1,0:T(8,128)}, bf16[16,96,256]{2,1,0:T(8,128)(2,1)}, bf16[16,256,1536]{2,1,0:T(8,128)(2,1)}, bf16[256,1536]{1,0:T(8,128)(2,1)}, bf16[16,96,256]{2,1,0:T(8,128)(2,1)}) custom-call(bf16[2,256,1536]{2,1,0:T(8,128)(2,1)} %x_hbm.5, bf16[2,256,1536]{2,1,0:T(8,128)(2,1)} %dy_hbm.5, bf16[1536,1536]{1,0:T(8,128)(2,1)} %wo_hbm.3, ...), custom_call_target="tpu_custom_call" | custom-call | flops 49999998976 | bytes 16777216 | tf_op jit(solution)/shard_map/opening/pallas_call | solution.py:420
  108.8 0.1 all-gather.4.cloned.1.call-update
  108.9 0.2 all-gather.6.cloned.1.call-start
  109.1 0.0 copy-done.1
  109.2 0.1 reshape.35
  109.3 0.6 broadcast_in_dim.6.b_ref
  109.9 78.9 %attention.2 = (bf16[16,288,256]{2,1,0:T(8,128)(2,1)}, f32[192,1536]{1,0:T(8,128)}, f32[96,1536]{1,0:T(8,128)}, f32[288,128]{1,0:T(8,128)}, f32[8,128]{1,0:T(8,1...) custom-call(bf16[16,288,1536]{2,1,0:T(8,128)(2,1)} %bitcast.14, f32[16,1,384]{2,1,0:T(1,128)} %broadcast_in_dim.6.b_ref, ...), custom_call_target="tpu_custom_call" | custom-call | flops 28991029248 | bytes 25165824 | tf_op jit(solution)/shard_map/attention/pallas_call | solution.py:227
  188.8 4.6 all-gather.4.cloned.1.call-done.x_ref
  193.4 95.8 %attention.3 = (bf16[16,288,256]{2,1,0:T(8,128)(2,1)}, f32[192,1536]{1,0:T(8,128)}, f32[96,1536]{1,0:T(8,128)}, f32[288,128]{1,0:T(8,128)}, f32[8,128]{1,0:T(8,1...) custom-call(bf16[16,288,1536]{2,1,0:T(8,128)(2,1)} %bitcast.15, ...), custom_call_target="tpu_custom_call" | custom-call | flops 28991029248 | bytes 25165824 | tf_op jit(solution)/shard_map/attention/pallas_call | solution.py:227
  289.2 0.1 all-gather.6.cloned.1.call-update
  289.3 0.3 all-gather.8.cloned.1.call-start
  289.6 0.5 all-gather.8.cloned.1.call-update
  290.1 145.9 %tail_a.1 = (bf16[2,256,1536]{2,1,0:T(8,128)(2,1)}, f32[96,1536]{1,0:T(8,128)}, bf16[16,192,256]{2,1,0:T(8,128)(2,1)}) custom-call(bf16[16,288,256]{2,1,0:T(8,128)(2,1)} %get-tuple-element.56.dqkv_ref, bf16[16,96,256]{2,1,0:T(8,128)(2,1)} %get-tuple-element.57.oo_hbm, bf16[16,96,256]{2,1,0:T(8,128)(2,1)} %get-tuple-element.58.on_hbm, ...), custom_call_target="tpu_custom_call" | custom-call | flops 99999997952 | bytes 67108864 | tf_op jit(solution)/shard_map/tail_a/pallas_call | solution.py:538
  435.9 29.2 %all-gather.6.cloned.1.call-done = f32[3072,1536]{1,0:T(8,128)} async-done(((f32[192,1536]{1,0:T(8,128)}), f32[3072,1536]{1,0:T(8,128)}) %all-gather.6.cloned.1.call-update) | async-done | bytes 18874384 | tf_op jit(solution)/shard_map/all_gather | solution.py:745
  465.1 15.3 %settle.2 = (f32[16,3,96,1536]{3,2,1,0:T(8,128)}, bf16[2,256,1536]{2,1,0:T(8,128)(2,1)}) custom-call(f32[16,2,96,1536]{3,2,1,0:T(8,128)} %bitcast.11, bf16[2,256,1536]{2,1,0:T(8,128)(2,1)} %get-tuple-element.61.refs_1_), custom_call_target="tpu_custom_call" | custom-call | flops 1000000000 | bytes 37748736 | tf_op jit(solution)/shard_map/settle/pallas_call | solution.py:710
  480.4 129.3 %tail_b.1 = (bf16[2,256,1536]{2,1,0:T(8,128)(2,1)}, f32[8,2,96,1536]{3,2,1,0:T(8,128)}, f32[8,1536]{1,0:T(8,128)}, f32[16,8,128]{2,1,0:T(8,128)}) custom-call(bf16[16,288,256]{2,1,0:T(8,128)(2,1)} %get-tuple-element.56.dqkv_ref, bf16[16,192,256]{2,1,0:T(8,128)(2,1)} %get-tuple-element.68.da_hbm, bf16[16,288,256]{2,1,0:T(8,128)(2,1)} %get-tuple-element.69.d_hbm, ...), custom_call_target="tpu_custom_call" | custom-call | flops 99999997952 | bytes 67108864 | tf_op jit(solution)/shard_map/tail_b/pallas_call | solution.py:673
  609.7 0.0 all-gather.8.cloned.1.call-done
  609.7 1.6 slice_reduce_fusion
  611.3 0.8 slice.12
  612.1 0.6 copy.22
  612.7 0.0 copy-start
  612.7 1.4 copy-done
  614.1 15.1 %settle.3 = (f32[16,3,96,1536]{3,2,1,0:T(8,128)}, bf16[2,256,1536]{2,1,0:T(8,128)(2,1)}, f32[1536,1536]{1,0:T(8,128)}) custom-call(f32[16,1,96,1536]{3,2,1,0:T(8,128)} %bitcast.12, bf16[2,256,1536]{2,1,0:T(8,128)(2,1)S(1)} %copy-done, f32[1536,1536]{1,0:T(8,128)} %bitcast.13, ...), custom_call_target="tpu_custom_call", output_to_operand_aliasing={{0}: (3, {})} | custom-call | flops 1000000000 | bytes 18874368 | tf_op jit(solution)/shard_map/settle/pallas_call | solution.py:710
  (5 shorter events, 0.0 us)
Async XLA Ops:
  7.2 186.2 %all-gather.4.cloned.1.call-start = ((), (), s32[]{:S(2)}) async-start(), calls=%async_computation | async-start | bytes 13369344 | tf_op jit(solution)/shard_map/all_gather | solution.py:734
  11.5 97.6 %copy-start.1 = (f32[16,3,96]{2,0,1:T(8,128)S(1)}, f32[16,3,96]{2,0,1:T(8,128)}, u32[]{:S(2)}) copy-start(f32[16,3,96]{2,0,1:T(8,128)} %param.16) | copy-start | bytes 55300
  108.9 356.2 %all-gather.6.cloned.1.call-start = ((), (), s32[]{:S(2)}) async-start(), calls=%async_computation.1 | async-start | bytes 20054016 | tf_op jit(solution)/shard_map/all_gather | solution.py:745
  289.3 320.4 %all-gather.8.cloned.1.call-start = ((), (), s32[]{:S(2)}) async-start(), calls=%async_computation.2 | async-start | bytes 10027008 | tf_op jit(solution)/shard_map/all_gather | solution.py:745
  612.7 1.4 copy-start
Sparse Core Ops, SparseCore 0:
  109.0 84.3 all-gather.3
  289.4 175.6 all-gather.5
  466.8 103.3 all-gather.7

commit v10 on v9

--- a/solution.py
+++ b/solution.py
@@ -79,15 +79,17 @@
         dv_acc[...] = jnp.zeros_like(dv_acc)
         q_pad[...] = jnp.zeros_like(q_pad)
         do_pad[...] = jnp.zeros_like(do_pad)
-        for k in range(b_ref.shape[2] // 128):
-            b_rep[k * 128:(k + 1) * 128, :] = spread(b_ref[me, :, k * 128:(k + 1) * 128])
+        mine = lax.broadcasted_iota(jnp.int32, (peers, dim), 0) == me
+        for k in range(3):
+            row = jnp.sum(jnp.where(mine, b_ref[k], 0.0), axis=0, keepdims=True)
+            b_rep[k * dim:(k + 1) * dim, :] = spread(jnp.concatenate([row, jnp.zeros((1, pad), F32)], axis=1))[0:dim]
         w_load.wait()
 
         @pl.loop(0, steps)
         def _(k):
             rows = pl.ds(pl.multiple_of(k * blk, blk), blk)
             x_copy(k).wait()
-            shift = jnp.concatenate([b_rep[0:3 * dim, :]] * (blk // 128), axis=1)
+            shift = jnp.concatenate([b_rep[...]] * (blk // 128), axis=1)
             qkvt_ref[:, rows] = (lax.dot_general(w_ref[...], x_buf[rows, :], NT, preferred_element_type=F32) + shift).astype(BF16)
 
             @pl.loop(0, blk // 128)
@@ -233,7 +235,7 @@
         out_specs=[full(a) for a in outs] + [hbm if send_o else full(dot_)] + [hbm] * len(old),
         scratch_shapes=[
             pltpu.VMEM((seq, hidden), BF16),
-            pltpu.VMEM(w_all.shape[1:], BF16), pltpu.VMEM((b_all.shape[2], 128), F32), pltpu.VMEM((3 * dim, seq), BF16),
+            pltpu.VMEM(w_all.shape[1:], BF16), pltpu.VMEM((3 * dim, 128), F32), pltpu.VMEM((3 * dim, seq), BF16),
             pltpu.VMEM((seq, wide), BF16), pltpu.VMEM((seq, wide), BF16), pltpu.VMEM((seq, 128), F32),
             pltpu.VMEM((seq, blk), F32),
             pltpu.VMEM((wide, blk), BF16), pltpu.VMEM((wide, blk), BF16),
@@ -351,10 +353,11 @@
     return [dma((2, 2, peers // 4, cuts))] * 2 + [dma((2, 2, peers // 4 + 1, cuts))] * 2
 
 
-def opening_body(x_hbm, dy_hbm, wo_hbm, vec_ref, marks_ref, marks_all, do_t, x_all, *refs, peers, batch, cuts):
+def opening_body(x_hbm, dy_hbm, wo_hbm, gain_ref, bias_ref, pos_ref, keep_ref, marks_all, do_t, x_all, *refs, peers, batch, cuts):
     x_out, do_out = refs[:batch - 1], refs[batch - 1:2 * batch - 2]
-    x_ref, dy_ref, x_own, do_own, wo_ref, own, ds_sem, dr_sem, do_sem, ms_sem, mr_sem, in_sem = refs[2 * batch - 2:2 * batch + 10]
-    ring_sems = refs[2 * batch + 10:]
+    x_ref, dy_ref, x_own, do_own, wo_ref, marks_ref, own, ds_sem, dr_sem, do_sem, ms_sem, mr_sem, in_sem = refs[2 * batch - 2:2 * batch + 11]
+    ring_sems = refs[2 * batch + 11:]
+    gain, bias = gain_ref[...].reshape(1, -1), bias_ref[...].reshape(1, -1)
     me = lax.axis_index("sp")
     tok, dim = x_own.shape[0], do_own.shape[1]
     lot = tok // 2 // cuts
@@ -374,7 +377,7 @@
             x = x_ref[b, rows, :].astype(F32)
             cen = x - jnp.mean(x, axis=-1, keepdims=True)
             hat = cen * lax.rsqrt(jnp.mean(cen * cen, axis=-1, keepdims=True) + NORM_EPS)
-            out_ref[rows, :] = (hat * vec_ref[0:1, :] + vec_ref[1:2, :]).astype(BF16)
+            out_ref[rows, :] = (hat * gain + bias).astype(BF16)
 
     def product(b, out_ref):
         @pl.loop(0, peers // 4)
@@ -382,6 +385,9 @@
             rows = pl.ds(pl.multiple_of(g * 4 * dim, 4 * dim), 4 * dim)
             out_ref[pl.ds(g * 4, 4)] = lax.dot_general(wo_ref[rows, :], dy_ref[b], NT, preferred_element_type=F32).astype(BF16).reshape(4, dim, tok)
 
+    marks_ref[...] = jnp.zeros_like(marks_ref)
+    marks_ref[0:batch, :] = pos_ref[...]
+    marks_ref[batch:2 * batch, :] = keep_ref[...]
     norm(0, x_own)
     block = lambda k, side, w, u: x_all.at[2 * k + side, rows_of(w, u)]
     start, run, finish = ring_gather(block, lambda w, u: x_own.at[rows_of(w, u)], ring_sems, peers, cuts)
@@ -411,7 +417,7 @@
     finish()
 
 
-def opening(x, dy, w_out, vecs, marks, peers, collective_id, cuts=4):
+def opening(x, dy, w_out, gain, bias, pos, keep, peers, collective_id, cuts=4):
     batch, tok, hidden = x.shape
     dim = hidden // peers
     hbm, vmem = pl.BlockSpec(memory_space=pltpu.HBM), pl.BlockSpec(memory_space=pltpu.VMEM)
@@ -420,25 +426,25 @@
     res = pl.pallas_call(
         functools.partial(opening_body, peers=peers, batch=batch, cuts=cuts),
         name="opening",
-        out_shape=[jax.ShapeDtypeStruct((peers,) + marks.shape, marks.dtype), do_shape, jax.ShapeDtypeStruct((peers, tok, hidden), BF16)]
+        out_shape=[jax.ShapeDtypeStruct((peers, 8, tok), pos.dtype), do_shape, jax.ShapeDtypeStruct((peers, tok, hidden), BF16)]
         + [x_shape] * (batch - 1) + [do_shape] * (batch - 1),
-        in_specs=[hbm, hbm, hbm, vmem, vmem],
+        in_specs=[hbm, hbm, hbm, vmem, vmem, vmem, vmem],
         out_specs=[vmem, hbm, hbm] + [vmem] * (2 * batch - 2),
         scratch_shapes=[pltpu.VMEM(x.shape, BF16), pltpu.VMEM(dy.shape, BF16), pltpu.VMEM(x_shape.shape, BF16), pltpu.VMEM(do_shape.shape, BF16),
-                        pltpu.VMEM(w_out.shape, BF16)] + swap_scratch(do_shape)
+                        pltpu.VMEM(w_out.shape, BF16), pltpu.VMEM((8, tok), pos.dtype)] + swap_scratch(do_shape)
         + [dma((peers - 1,)), dma((peers - 1,)), dma((batch + 3,))] + ring_scratch(peers, cuts),
         cost_estimate=pl.CostEstimate(flops=5 * 10**10, bytes_accessed=16 << 20, transcendentals=0),
         compiler_params=pltpu.CompilerParams(collective_id=collective_id, has_side_effects=True, vmem_limit_bytes=VMEM_LIMIT),
-    )(x, dy, w_out, vecs, marks)
+    )(x, dy, w_out, gain, bias, pos, keep)
     return res[0], res[1], res[2], res[3:2 + batch], res[2 + batch:]
 
 
 TN = (((0,), (0,)), ((), ()))
 
 
-def tail_a_body(dqkv_ref, oo_hbm, on_hbm, dy_hbm, x_hbm, wo_hbm, vec_ref, y_ref, part, d_out,
-                o_old, o_new, dy_ref, x_ref, wo_ref, both, mine, landed, own_d, ds_sem, dr_sem, do_sem, ps_sem, pr_sem, rs_sem, rr_sem,
-                w_sem, *, peers, cuts, sent):
+def tail_a_body(dqkv_ref, oo_hbm, on_hbm, dy_hbm, x_hbm, wo_hbm, d_hbm, w_hbm, gain_ref, bo_ref, y_ref, gx_ref, part, rows_ref,
+                o_old, o_new, dy_ref, x_ref, wo_ref, d_old, w_ref, d_new, dn, sums, bo_rep, both, mine, landed, own_d,
+                ds_sem, dr_sem, do_sem, ps_sem, pr_sem, rs_sem, rr_sem, w_sem, *, peers, cuts):
     ring = peers // 2
     me = lax.axis_index("sp")
     z, c = me // 2, me % 2
@@ -448,9 +454,11 @@
     at = lambda zz, cc: {"sp": 2 * zz + cc}
     turn = lambda k: lax.rem(z + k + 2 * ring, ring)
     remote = functools.partial(pltpu.make_async_remote_copy, device_id_type=pl.DeviceIdType.MESH)
-    pairs = ((oo_hbm, o_old), (on_hbm, o_new), (dy_hbm, dy_ref), (x_hbm, x_ref), (wo_hbm, wo_ref))
+    span, group = d_old.shape[1], 8
+    gain, b_out = gain_ref[...].reshape(1, hidden), bo_ref[...].reshape(1, hidden)
+    pairs = ((oo_hbm, o_old), (on_hbm, o_new), (dy_hbm, dy_ref), (x_hbm, x_ref), (wo_hbm, wo_ref), (d_hbm, d_old), (w_hbm, w_ref))
     loads = [pltpu.make_async_copy(src, dst, w_sem.at[k]) for k, (src, dst) in enumerate(pairs)]
-    swap = (dqkv_ref.at[:, pl.ds(0, sent)], d_out, own_d, ds_sem, dr_sem, do_sem, peers)
+    swap = (dqkv_ref, d_new, own_d, ds_sem, dr_sem, do_sem, peers)
     arrived = greet(peers)
     for load in loads:
         load.start()
@@ -479,101 +487,7 @@
         def _(n):
             at_n = pl.ds(pl.multiple_of(n * wide, wide), wide)
             acc = lax.dot_general(o_t, wo_ref[:, at_n], TN, preferred_element_type=F32)
-            y_ref[b, :, at_n] = (x_ref[b, :, at_n].astype(F32) + acc + vec_ref[2:3, at_n]).astype(BF16)
-
-    product(put_other, 1 - c)
-    pair_copy = lambda side: remote(src_ref=both.at[:, side], dst_ref=both.at[:, side], send_sem=ps_sem, recv_sem=pr_sem, device_id=at(z, 1 - c))
-    product(put_mine, c)
-    pair_copy(1 - c).start()
-    pair_copy(1 - c).wait_send()
-    pair_copy(c).wait_recv()
-
-    @pl.loop(0, ring)
-    def _(k):
-        mine[k] = mine[k] + both[k, c]
-
-    lots = [(s, w, u) for u in range(cuts) for w in range(2) for s in range(2)]
-
-    def reduce_copy(s, w, t, u):
-        return remote(src_ref=mine.at[turn(STEP[s] * (hops(ring, s, w) - t)), pl.ds(u * few, few), cols[w]], dst_ref=landed.at[s, w, t, u],
-                      send_sem=rs_sem.at[s, w, t, u], recv_sem=rr_sem.at[s, w, t, u], device_id=at(turn(STEP[s]), c))
-
-    def fold(s, w, t, u):
-        reduce_copy(s, w, t, u).wait_recv()
-        at_k = (turn(STEP[s] * (hops(ring, s, w) - t - 1)), pl.ds(u * few, few), cols[w])
-        mine[at_k] = mine[at_k] + landed[s, w, t, u]
-
-    def hop(t):
-        for s, w, u in lots:
-            if t < hops(ring, s, w):
-                fold(s, w, t - 1, u)
-                reduce_copy(s, w, t, u).start()
-
-    for s, w, u in lots:
-        reduce_copy(s, w, 0, u).start()
-    loads[3].wait()
-    loads[4].wait()
-    forward(0, o_old)
-    hop(1)
-    forward(1, o_new)
-    for t in range(2, ring // 2):
-        hop(t)
-    for s, w, u in lots:
-        fold(s, w, hops(ring, s, w) - 1, u)
-    part[...] = mine[z]
-    swap_wait(*swap)
-    for s, w, u in lots:
-        for t in range(hops(ring, s, w)):
-            reduce_copy(s, w, t, u).wait_send()
-
-
-def tail_a(dqkv, o_old, o_new, dy, x, w_out, vecs, sent, collective_id, cuts=2):
-    peers, dim, tok = o_old.shape
-    ring = peers // 2
-    hidden = dy.shape[-1]
-    hbm, vmem = pl.BlockSpec(memory_space=pltpu.HBM), pl.BlockSpec(memory_space=pltpu.VMEM)
-    dma = pltpu.SemaphoreType.DMA
-    held = lambda a: pltpu.VMEM(a.shape, a.dtype)
-    steps = (2, 2, ring // 2, cuts)
-    return pl.pallas_call(
-        functools.partial(tail_a_body, peers=peers, cuts=cuts, sent=sent),
-        name="tail_a",
-        out_shape=[jax.ShapeDtypeStruct(x.shape, BF16), jax.ShapeDtypeStruct((dim, hidden), F32),
-                   jax.ShapeDtypeStruct((peers, sent, tok), BF16)],
-        in_specs=[hbm] * 6 + [vmem],
-        out_specs=[vmem, vmem, hbm],
-        scratch_shapes=[held(a) for a in (o_old, o_new, dy, x, w_out)]
-        + [pltpu.VMEM((ring, 2, dim, hidden), F32), pltpu.VMEM((ring, dim, hidden), F32), pltpu.VMEM(steps + (dim // cuts, hidden // 2), F32),
-           pltpu.VMEM((sent, tok), BF16), dma((peers - 1,)), dma((peers - 1,)), dma, dma, dma, dma(steps), dma(steps), dma((5,))],
-        cost_estimate=pl.CostEstimate(flops=10**11, bytes_accessed=64 << 20, transcendentals=0),
-        compiler_params=pltpu.CompilerParams(collective_id=collective_id, has_side_effects=True, vmem_limit_bytes=VMEM_LIMIT),
-    )(dqkv, o_old, o_new, dy, x, w_out, vecs)
-
-
-def tail_b_body(dqkv_ref, da_hbm, d_hbm, dy_hbm, x_hbm, w_hbm, part, vec_ref, gb_ref, gx_ref, full, total, gb_all,
-                d_old, d_new, dy_ref, x_ref, w_ref, dn, sums, rows_ref, stage, own_d, ds_sem, dr_sem, do_sem, w_sem, xs_sem, xr_sem,
-                *ring_sems, peers, cuts):
-    ring = peers // 2
-    me = lax.axis_index("sp")
-    z, c = me // 2, me % 2
-    _, tok, hidden = x_ref.shape
-    half, wide, few = hidden // 2, hidden // 3, full.shape[2] // cuts
-    sent, span = da_hbm.shape[1], d_old.shape[1]
-    rest = pl.ds(sent, span - sent)
-    group = 8
-    cols = (pl.ds(0, half), pl.ds(half, half))
-    remote = functools.partial(pltpu.make_async_remote_copy, device_id_type=pl.DeviceIdType.MESH)
-    pairs = ((w_hbm, w_ref), (d_hbm, d_old), (dy_hbm, dy_ref), (x_hbm, x_ref), (da_hbm, d_new.at[:, pl.ds(0, sent)]))
-    loads = [pltpu.make_async_copy(src, dst, w_sem.at[k]) for k, (src, dst) in enumerate(pairs)]
-    swap = (dqkv_ref.at[:, rest], d_new.at[:, rest], own_d, ds_sem, dr_sem, do_sem, peers)
-    arrived = greet(peers)
-    for load in loads:
-        load.start()
-    full[z, c] = part[...]
-    gb_all[me] = gb_ref[...]
-    sums[...] = jnp.zeros_like(sums)
-    block = lambda k, side, w, u: full.at[k, side, pl.ds(u * few, few), cols[w]]
-    start, run, finish = ring_gather(block, lambda w, u: block(z, c, w, u), ring_sems, peers, cuts)
+            y_ref[b, :, at_n] = (x_ref[b, :, at_n].astype(F32) + acc + bo_rep[0:1, at_n]).astype(BF16)
 
     def backward(b, d_ref):
         @pl.loop(0, 3)
@@ -597,11 +511,103 @@
             hat = cen * inv
             for n, one in enumerate((d * hat, d, dy)):
                 sums[n] += jnp.sum(one.reshape(4, 8, hidden), axis=0)
-            e = d * vec_ref[0:1, :]
+            e = d * gain
             m1 = jnp.mean(e, axis=-1, keepdims=True)
             m2 = jnp.mean(e * hat, axis=-1, keepdims=True)
             gx_ref[b, rows, :] = (dy + inv * (e - m1 - hat * m2)).astype(BF16)
 
+    bo_rep[...] = jnp.broadcast_to(b_out, bo_rep.shape)
+    sums[...] = jnp.zeros_like(sums)
+    product(put_other, 1 - c)
+    pair_copy = lambda side: remote(src_ref=both.at[:, side], dst_ref=both.at[:, side], send_sem=ps_sem, recv_sem=pr_sem, device_id=at(z, 1 - c))
+    product(put_mine, c)
+    pair_copy(1 - c).start()
+    pair_copy(1 - c).wait_send()
+    pair_copy(c).wait_recv()
+
+    @pl.loop(0, ring)
+    def _(k):
+        mine[k] = mine[k] + both[k, c]
+
+    lots = [(s, w, u) for u in range(cuts) for w in range(2) for s in range(2)]
+
+    def reduce_copy(s, w, t, u):
+        return remote(src_ref=mine.at[turn(STEP[s] * (hops(ring, s, w) - t)), pl.ds(u * few, few), cols[w]], dst_ref=landed.at[s, w, t, u],
+                      send_sem=rs_sem.at[s, w, t, u], recv_sem=rr_sem.at[s, w, t, u], device_id=at(turn(STEP[s]), c))
+
+    def fold(s, w, t, u):
+        reduce_copy(s, w, t, u).wait_recv()
+        at_k = (turn(STEP[s] * (hops(ring, s, w) - t - 1)), pl.ds(u * few, few), cols[w])
+        mine[at_k] = mine[at_k] + landed[s, w, t, u]
+
+    def hop(t):
+        for s, w, u in lots:
+            if t < hops(ring, s, w):
+                fold(s, w, t - 1, u)
+                reduce_copy(s, w, t, u).start()
+
+    for s, w, u in lots:
+        reduce_copy(s, w, 0, u).start()
+    for load in loads[3:5]:
+        load.wait()
+    forward(0, o_old)
+    forward(1, o_new)
+    for load in loads[5:]:
+        load.wait()
+    backward(0, d_old)
+    for t in range(1, ring // 2 - 1):
+        hop(t)
+    swap_wait(*swap)
+    backward(1, d_new)
+    hop(ring // 2 - 1)
+    rows_ref[...] = jnp.zeros_like(rows_ref)
+    for n in range(3):
+        rows_ref[n:n + 1, :] = jnp.sum(sums[n], axis=0, keepdims=True)
+    for s, w, u in lots:
+        fold(s, w, hops(ring, s, w) - 1, u)
+    part[...] = mine[z]
+    for s, w, u in lots:
+        for t in range(hops(ring, s, w)):
+            reduce_copy(s, w, t, u).wait_send()
+
+
+def tail_a(dqkv, d_old, o_old, o_new, dy, x, w_flat, w_out, gain, b_out, collective_id, cuts=2):
+    peers, dim, tok = o_old.shape
+    ring = peers // 2
+    hidden = dy.shape[-1]
+    hbm, vmem = pl.BlockSpec(memory_space=pltpu.HBM), pl.BlockSpec(memory_space=pltpu.VMEM)
+    dma = pltpu.SemaphoreType.DMA
+    held = lambda a: pltpu.VMEM(a.shape, a.dtype)
+    steps = (2, 2, ring // 2, cuts)
+    return pl.pallas_call(
+        functools.partial(tail_a_body, peers=peers, cuts=cuts),
+        name="tail_a",
+        out_shape=[jax.ShapeDtypeStruct(x.shape, BF16), jax.ShapeDtypeStruct(x.shape, BF16), jax.ShapeDtypeStruct((dim, hidden), F32),
+                   jax.ShapeDtypeStruct((8, hidden), F32)],
+        in_specs=[hbm] * 8 + [vmem] * 2,
+        out_specs=[vmem] * 4,
+        scratch_shapes=[held(a) for a in (o_old, o_new, dy, x, w_out, d_old, w_flat, dqkv)]
+        + [pltpu.VMEM((tok, hidden), F32), pltpu.VMEM((3, 8, hidden), F32), pltpu.VMEM((8, hidden), F32),
+           pltpu.VMEM((ring, 2, dim, hidden), F32), pltpu.VMEM((ring, dim, hidden), F32), pltpu.VMEM(steps + (dim // cuts, hidden // 2), F32),
+           pltpu.VMEM(dqkv.shape[1:], BF16), dma((peers - 1,)), dma((peers - 1,)), dma, dma, dma, dma(steps), dma(steps), dma((7,))],
+        cost_estimate=pl.CostEstimate(flops=10**11, bytes_accessed=64 << 20, transcendentals=0),
+        compiler_params=pltpu.CompilerParams(collective_id=collective_id, has_side_effects=True, vmem_limit_bytes=VMEM_LIMIT),
+    )(dqkv, o_old, o_new, dy, x, w_out, d_old, w_flat, gain, b_out)
+
+
+def tail_b_body(part, rows_ref, gb_ref, full, total, gb_all, stage, xs_sem, xr_sem, *ring_sems, peers, cuts):
+    ring = peers // 2
+    me = lax.axis_index("sp")
+    z, c = me // 2, me % 2
+    hidden = part.shape[1]
+    half, few = hidden // 2, part.shape[0] // cuts
+    cols = (pl.ds(0, half), pl.ds(half, half))
+    remote = functools.partial(pltpu.make_async_remote_copy, device_id_type=pl.DeviceIdType.MESH)
+    arrived = greet(peers)
+    full[z, c] = part[...]
+    gb_all[me] = gb_ref[...]
+    block = lambda k, side, w, u: full.at[k, side, pl.ds(u * few, few), cols[w]]
+    start, run, finish = ring_gather(block, lambda w, u: block(z, c, w, u), ring_sems, peers, cuts)
     owners = hidden // 128
     lanes = lambda k: pl.ds(pl.multiple_of(k * 128, 128), 128)
 
@@ -628,27 +634,15 @@
     over = lambda kind, far: small_copy(kind, me, far).wait_send()
     came = lambda kind, far: small_copy(kind, far, me).wait_recv()
 
-    arrived()
-    start()
-    swap_start(*swap)
-    each(send, 2)
-    run(1, 2)
-    for load in loads[:4]:
-        load.wait()
-    backward(0, d_old)
-    run(2)
-    loads[4].wait()
-    swap_wait(*swap)
-    backward(1, d_new)
-    rows_ref[...] = jnp.zeros_like(rows_ref)
-    for n in range(3):
-        rows_ref[n:n + 1, :] = jnp.sum(sums[n], axis=0, keepdims=True)
-
     @pl.when(me < owners)
     def _():
         stage[me] = rows_ref[:, lanes(me)]
 
+    arrived()
+    start()
     each(send, 0, only_to=True)
+    each(send, 2)
+    run(1, 2)
     each(came, 0, only_from=True)
 
     @pl.when(me < owners)
@@ -656,6 +650,7 @@
         total[:, lanes(me)] = jnp.sum(stage[...], axis=0)
 
     each(send, 1, only_from=True)
+    run(2)
     each(came, 1, only_to=True)
     each(came, 2)
     each(over, 0, only_to=True)
@@ -664,31 +659,26 @@
     finish()
 
 
-def tail_b(dqkv, d_part, d_old, dy, x, w_flat, part, vecs, gb, peers, collective_id, cuts=2):
+def tail_b(part, rows, gb, peers, collective_id, cuts=2):
     ring = peers // 2
-    tok, hidden = x.shape[1:]
-    hbm, vmem = pl.BlockSpec(memory_space=pltpu.HBM), pl.BlockSpec(memory_space=pltpu.VMEM)
+    vmem = pl.BlockSpec(memory_space=pltpu.VMEM)
     dma = pltpu.SemaphoreType.DMA
-    held = lambda a: pltpu.VMEM(a.shape, a.dtype)
     return pl.pallas_call(
         functools.partial(tail_b_body, peers=peers, cuts=cuts),
         name="tail_b",
-        out_shape=[jax.ShapeDtypeStruct(x.shape, BF16), jax.ShapeDtypeStruct((ring, 2) + part.shape, F32),
-                   jax.ShapeDtypeStruct((8, hidden), F32), jax.ShapeDtypeStruct((peers,) + gb.shape, F32)],
-        in_specs=[hbm] * 6 + [vmem] * 3,
-        out_specs=[vmem] * 4,
-        scratch_shapes=[held(a) for a in (d_old, d_old, dy, x, w_flat)]
-        + [pltpu.VMEM((tok, hidden), F32), pltpu.VMEM((3, 8, hidden), F32), pltpu.VMEM((8, hidden), F32), pltpu.VMEM((peers, 8, 128), F32),
-           pltpu.VMEM((d_old.shape[1] - d_part.shape[1], tok), BF16), dma((peers - 1,)), dma((peers - 1,)), dma, dma((5,)),
-           dma((3, peers)), dma((3, peers))] + ring_scratch(peers, cuts),
-        cost_estimate=pl.CostEstimate(flops=10**11, bytes_accessed=64 << 20, transcendentals=0),
-        compiler_params=pltpu.CompilerParams(collective_id=collective_id, has_side_effects=True, vmem_limit_bytes=VMEM_LIMIT),
-    )(dqkv, d_part, d_old, dy, x, w_flat, part, vecs, gb)
+        out_shape=[jax.ShapeDtypeStruct((ring, 2) + part.shape, F32), jax.ShapeDtypeStruct(rows.shape, F32),
+                   jax.ShapeDtypeStruct((peers,) + gb.shape, F32)],
+        in_specs=[vmem] * 3,
+        out_specs=[vmem] * 3,
+        scratch_shapes=[pltpu.VMEM((peers, 8, 128), F32), dma((3, peers)), dma((3, peers))] + ring_scratch(peers, cuts),
+        cost_estimate=pl.CostEstimate(flops=5 * 10**10, bytes_accessed=10 << 20, transcendentals=0),
+        compiler_params=pltpu.CompilerParams(collective_id=collective_id, has_side_effects=True, vmem_limit_bytes=32 << 20),
+    )(part, rows, gb)
 
 
 def settle_body(*refs, n_in, first, n_plain):
-    x_ref, plain, outs = refs[0], refs[1:1 + n_plain], refs[n_in:n_in + 1 + n_plain]
-    buf, in_sem, out_sem, plain_sem = refs[n_in + 1 + n_plain:]
+    x_ref, plain = refs[0], refs[1:1 + n_plain]
+    outs, (buf, in_sem, out_sem, plain_sem) = refs[n_in:-4], refs[-4:]
     heads, n = x_ref.shape[:2]
     reads = [pltpu.make_async_copy(x_ref.at[h], buf.at[h], in_sem.at[h]) for h in range(heads)]
     writes = [pltpu.make_async_copy(buf.at[h], outs[0].at[h, pl.ds(first, n)], out_sem.at[h]) for h in range(heads)]
@@ -705,7 +695,7 @@
 def settle(x, into, plain, lanes, first):
     heads, n, dim, hidden = x.shape
     hbm, vmem = pl.BlockSpec(memory_space=pltpu.HBM), pl.BlockSpec(memory_space=pltpu.VMEM)
-    args = (x, *plain) + (() if into is None else (into,))
+    args = (pltpu.with_memory_space_constraint(x, pltpu.HBM), *plain) + (() if into is None else (into,))
     dma = pltpu.SemaphoreType.DMA
     return pl.pallas_call(
         functools.partial(settle_body, n_in=len(args), first=first, n_plain=len(plain)), name="settle",
@@ -714,7 +704,31 @@
         input_output_aliases={} if into is None else {len(args) - 1: 0},
         scratch_shapes=[pltpu.VMEM(x.shape, x.dtype), dma((heads,)), dma((heads,)), dma((max(len(plain), 1),))],
         cost_estimate=pl.CostEstimate(flops=10**9, bytes_accessed=8 * x.size, transcendentals=0),
-        compiler_params=pltpu.CompilerParams(vmem_limit_bytes=(60 << 20) - 4 * sum(a.size for a in plain)))(*args)
+        compiler_params=pltpu.CompilerParams(vmem_limit_bytes=24 << 20))(*args)
+
+
+def lay_body(go_ref, total, gb_all, go_out, gb_out, *refs):
+    vectors, sem = refs[:-1], refs[-1]
+    copies = [pltpu.make_async_copy(go_ref.at[k], go_out.at[k], sem.at[k]) for k in range(go_ref.shape[0])]
+    for copy in copies:
+        copy.start()
+    for k in range(3):
+        gb_out[k] = gb_all[:, k, 0:gb_out.shape[2]]
+        vectors[k][...] = total[k]
+    for copy in copies:
+        copy.wait()
+
+
+def lay_down(go, total, gb_all):
+    hbm, vmem = pl.BlockSpec(memory_space=pltpu.HBM), pl.BlockSpec(memory_space=pltpu.VMEM)
+    ring, _, dim, hidden = go.shape
+    return pl.pallas_call(
+        lay_body, name="lay_down",
+        out_shape=[jax.ShapeDtypeStruct(go.shape, F32), jax.ShapeDtypeStruct((3, 2 * ring, dim), F32)] + [jax.ShapeDtypeStruct((hidden,), F32)] * 3,
+        in_specs=[vmem] * 3, out_specs=[hbm] + [vmem] * 4,
+        scratch_shapes=[pltpu.SemaphoreType.DMA((ring,))],
+        cost_estimate=pl.CostEstimate(flops=10**9, bytes_accessed=8 * go.size, transcendentals=0),
+        compiler_params=pltpu.CompilerParams(vmem_limit_bytes=24 << 20))(go, total, gb_all)
 
 
 def solution(mesh):
@@ -726,11 +740,9 @@
         assert heads == peers
         seq = tok * peers
         blk = 2 * tok
-        vecs = jnp.stack([ln_gain, ln_bias, b_out] + [jnp.zeros_like(b_out)] * 5)
         w_all = jnp.transpose(w_qkv, (1, 2, 3, 0)).reshape(heads, 3 * dim, hidden)
-        b_all = jnp.pad(b_qkv.reshape(heads, 3 * dim), ((0, 0), (0, -3 * dim % 128)))[:, None]
-        marks_loc = jnp.concatenate([pos_blk, keep_blk, jnp.zeros((8 - 2 * batch, tok), jnp.int32)])
-        marks, do_first, x_first, x_rest, do_rest = opening(x_blk, dy_blk, w_out, vecs, marks_loc, peers, 1)
+        b_all = jnp.transpose(b_qkv, (1, 0, 2))
+        marks, do_first, x_first, x_rest, do_rest = opening(x_blk, dy_blk, w_out, ln_gain, ln_bias, pos_blk, keep_blk, peers, 1)
         xs = [x_first.reshape(seq, hidden)] + [lax.all_gather(one, "sp", axis=0, tiled=True) for one in x_rest]
         do_t = [do_first]
         gw, att = (), []
@@ -744,15 +756,15 @@
         o_old, d_old = swapped
         gw_all = [lax.all_gather(one, "sp", axis=0, tiled=True).reshape(heads, -1, dim, hidden) for one in gw[:2]]
         lead = gw_all[0].shape[1]
-        y, part, d_part = tail_a(att_d, o_old, att_o, dy_blk, x_blk, w_out, vecs, 2 * dim, 2)
+        y, gx, part, rows = tail_a(att_d, d_old, o_old, att_o, dy_blk, x_blk, w_all.reshape(3 * hidden, hidden), w_out, ln_gain, b_out, 2)
         first, _ = lax.optimization_barrier((gw_all[0], y))
-        gw_out, y = settle(first, None, (y,), 3, 0)
-        part, gw_out, y = lax.optimization_barrier((part, gw_out, y))
-        gx, go_all, total, gb_all = tail_b(att_d, d_part, d_old, dy_blk, x_blk, w_all.reshape(3 * hidden, hidden), part, vecs, gb, peers, 3)
-        second, gw_out, gx = lax.optimization_barrier((gw_all[1], gw_out, gx))
-        gw_out, gx, go_all = settle(second, gw_out, (gx, go_all.reshape(hidden, hidden)), 3, lead)
-        gw_out = jnp.transpose(gw_out, (3, 0, 1, 2))
-        return y, gx, gw_out, gb_all[:, :3, :dim], go_all, total[2], total[0], total[1]
+        gw_out, y, gx = settle(first, None, (y, gx), 3, 0)
+        part, gw_out, y, gx = lax.optimization_barrier((part, gw_out, y, gx))
+        go_all, gb_all, g_gain, g_bias, g_out = lay_down(*tail_b(part, rows, gb, peers, 3))
+        second, gw_out, go_all = lax.optimization_barrier((gw_all[1], gw_out, go_all))
+        gw_out, = settle(second, gw_out, (), 3, lead)
+        return (y, gx, jnp.transpose(gw_out, (3, 0, 1, 2)), jnp.transpose(gb_all, (1, 0, 2)), go_all.reshape(hidden, hidden),
+                g_out, g_gain, g_bias)
 
     act_spec = P("dp", "sp", None)
     tok_spec = P("dp", "sp")

time: 637 us -> 603 us (0.947)
  Pallas kernels: 578 us -> 560 us
  waiting for transfers between devices: 34.4 us -> 25.4 us
    pallas_call x1, Pallas kernels: 129 us -> 90.2 us  [tail_b(): pl.pallas_call(functools.partial(tail_b_body, peers=peers, cuts=cuts), na...]
    pallas_call x1 -> x2, Pallas kernels: 146 us -> 175 us  [the longest x1 171 us: tail_a(): pl.pallas_call(functools.partial(tail_a_body, peers=peers, cuts=cuts), na...]
    all_gather x3, waiting for transfers between devices: 33.8 us -> 24.8 us  [block_fn(): lax.all_gather(one, 'sp', axis=0, tiled=True)]
    pallas_call x2, Pallas kernels: 30.4 us -> 22 us  [settle(): pl.pallas_call(functools.partial(settle_body, n_in=len(args), first=first...]
  transfers between devices with their start and end apart: 3 -> 3, of which waited for: 2 -> 2; matrix products, arithmetic and copies ran while one was open for 0% -> 0% of each run, Pallas kernels for 58% -> 60%
where the time goes in v10:
time: 603 us; the launch traced here: 602 us
  Pallas kernels  560 us (93%)
  waiting for transfers between devices  25.4 us (4%)
  between operations  13.9 us (2%)
    pallas_call x2, Pallas kernels, attention(): pl.pallas_call(functools.partial(attn_body, blk=blk, tok=tok, which=which...  175 us
    pallas_call x1, Pallas kernels, tail_a(): pl.pallas_call(functools.partial(tail_a_body, peers=peers, cuts=cuts), na...  171 us
    pallas_call x1, Pallas kernels, opening(): pl.pallas_call(functools.partial(opening_body, peers=peers, batch=batch,...  97.3 us
    pallas_call x1, Pallas kernels, tail_b(): pl.pallas_call(functools.partial(tail_b_body, peers=peers, cuts=cuts), na...  90.2 us
    all_gather x3, waiting for transfers between devices, block_fn(): lax.all_gather(one, 'sp', axis=0, tiled=True)  24.8 us
    pallas_call x2, Pallas kernels, settle(): pl.pallas_call(functools.partial(settle_body, n_in=len(args), first=first...  22 us
  transfers between devices with their start and end apart: 3, of which 2 were waited for; matrix products, arithmetic and copies ran while one was open for 0% of the time, Pallas kernels for 60%

profile of v10, /device:TPU:21, one launch (start us, length us, event | category | flops | bytes accessed | tf_op | source)
XLA Modules:
  0.0 602.4 jit_solution(12487839907519159747)
XLA Ops:
  7.2 0.1 all-gather.4.cloned.1.call-start
  7.2 97.3 %opening.1 = (s32[16,8,256]{2,1,0:T(8,128)}, bf16[16,96,256]{2,1,0:T(8,128)(2,1)}, bf16[16,256,1536]{2,1,0:T(8,128)(2,1)}, bf16[256,1536]{1,0:T(8,128)(2,1)}, bf16[16,96,256]{2,1,0:T(8,128)(2,1)}) custom-call(bf16[2,256,1536]{2,1,0:T(8,128)(2,1)} %x_hbm.3, bf16[2,256,1536]{2,1,0:T(8,128)(2,1)} %dy_hbm.3, bf16[1536,1536]{1,0:T(8,128)(2,1)} %wo_hbm.3, ...), custom_call_target="tpu_custom_call" | custom-call | flops 49999998976 | bytes 16777216 | tf_op jit(solution)/shard_map/opening/pallas_call | solution.py:426
  104.6 0.1 all-gather.4.cloned.1.call-update
  104.7 0.2 all-gather.6.cloned.1.call-start
  104.9 78.9 %attention.2 = (bf16[16,288,256]{2,1,0:T(8,128)(2,1)}, f32[192,1536]{1,0:T(8,128)}, f32[96,1536]{1,0:T(8,128)}, f32[288,128]{1,0:T(8,128)}, f32[8,128]{1,0:T(8,1...) custom-call(bf16[16,288,1536]{2,1,0:T(8,128)(2,1)} %bitcast.15, f32[3,16,96]{2,1,0:T(8,128)} %bitcast.19, ...), custom_call_target="tpu_custom_call" | custom-call | flops 28991029248 | bytes 25165824 | tf_op jit(solution)/shard_map/attention/pallas_call | solution.py:229
  183.8 4.6 all-gather.4.cloned.1.call-done.x_ref
  188.4 95.9 %attention.3 = (bf16[16,288,256]{2,1,0:T(8,128)(2,1)}, f32[192,1536]{1,0:T(8,128)}, f32[96,1536]{1,0:T(8,128)}, f32[288,128]{1,0:T(8,128)}, f32[8,128]{1,0:T(8,1...) custom-call(bf16[16,288,1536]{2,1,0:T(8,128)(2,1)} %bitcast.16, ...), custom_call_target="tpu_custom_call" | custom-call | flops 28991029248 | bytes 25165824 | tf_op jit(solution)/shard_map/attention/pallas_call | solution.py:229
  284.3 0.1 all-gather.6.cloned.1.call-update
  284.4 0.3 all-gather.8.cloned.1.call-start
  284.7 0.5 all-gather.8.cloned.1.call-update
  285.2 171.0 %tail_a.1 = (bf16[2,256,1536]{2,1,0:T(8,128)(2,1)}, bf16[2,256,1536]{2,1,0:T(8,128)(2,1)}, f32[96,1536]{1,0:T(8,128)}, f32[8,1536]{1,0:T(8,128)}) custom-call(bf16[16,288,256]{2,1,0:T(8,128)(2,1)} %get-tuple-element.60.dqkv_ref, bf16[16,96,256]{2,1,0:T(8,128)(2,1)} %get-tuple-element.61.oo_hbm, bf16[16,96,256]{2,1,0:T(8,128)(2,1)} %get-tuple-element.62.on_hbm, ...), custom_call_target="tpu_custom_call" | custom-call | flops 99999997952 | bytes 67108864 | tf_op jit(solution)/shard_map/tail_a/pallas_call | solution.py:582
  456.2 20.1 %all-gather.6.cloned.1.call-done = f32[3072,1536]{1,0:T(8,128)} async-done(((f32[192,1536]{1,0:T(8,128)}), f32[3072,1536]{1,0:T(8,128)}) %all-gather.6.cloned.1.call-update) | async-done | bytes 18874384 | tf_op jit(solution)/shard_map/all_gather | solution.py:757
  476.4 0.0 copy-start
  476.4 1.4 copy-done
  477.8 0.0 copy-start.1
  477.8 1.4 copy-done.1
  479.2 0.0 copy-start.2
  479.2 0.0 copy-start.3
  479.2 0.0 copy-start.4
  479.2 14.6 %settle.2 = (f32[16,3,96,1536]{3,2,1,0:T(8,128)}, bf16[2,256,1536]{2,1,0:T(8,128)(2,1)}, bf16[2,256,1536]{2,1,0:T(8,128)(2,1)}) custom-call(f32[16,2,96,1536]{3,2,1,0:T(8,128)} %bitcast.13, bf16[2,256,1536]{2,1,0:T(8,128)(2,1)S(1)} %copy-done, bf16[2,256,1536]{2,1,0:T(8,128)(2,1)S(1)} %copy-done.1), custom_call_target="tpu_custom_call" | custom-call | flops 1000000000 | bytes 37748736 | tf_op jit(solution)/shard_map/settle/pallas_call | solution.py:700
  493.8 0.0 copy-done.2
  493.8 0.0 copy-done.3
  493.8 0.0 copy-done.4
  493.8 90.2 %tail_b.1 = (f32[8,2,96,1536]{3,2,1,0:T(8,128)S(1)}, f32[8,1536]{1,0:T(8,128)S(1)}, f32[16,8,128]{2,1,0:T(8,128)S(1)}) custom-call(f32[96,1536]{1,0:T(8,128)S(1)} %copy-done.2, f32[8,1536]{1,0:T(8,128)S(1)} %copy-done.3, f32[8,128]{1,0:T(8,128)S(1)} %copy-done.4), custom_call_target="tpu_custom_call" | custom-call | flops 49999998976 | bytes 10485760 | tf_op jit(solution)/shard_map/tail_b/pallas_call | solution.py:666
  584.0 4.3 lay_down.1
  588.3 0.0 all-gather.8.cloned.1.call-done
  588.4 7.4 %settle.3 = f32[16,3,96,1536]{3,2,1,0:T(8,128)} custom-call(f32[16,1,96,1536]{3,2,1,0:T(8,128)} %bitcast.14, f32[16,3,96,1536]{3,2,1,0:T(8,128)} %get-tuple-element.84.refs_1_), custom_call_target="tpu_custom_call", output_to_operand_aliasing={{}: (1, {})} | custom-call | flops 1000000000 | bytes 18874368 | tf_op jit(solution)/shard_map/settle/pallas_call | solution.py:700
Async XLA Ops:
  7.2 181.3 %all-gather.4.cloned.1.call-start = ((), (), s32[]{:S(2)}) async-start(), calls=%async_computation | async-start | bytes 13369344 | tf_op jit(solution)/shard_map/all_gather | solution.py:746
  104.7 371.7 %all-gather.6.cloned.1.call-start = ((), (), s32[]{:S(2)}) async-start(), calls=%async_computation.1 | async-start | bytes 20054016 | tf_op jit(solution)/shard_map/all_gather | solution.py:757
  284.4 304.0 %all-gather.8.cloned.1.call-start = ((), (), s32[]{:S(2)}) async-start(), calls=%async_computation.2 | async-start | bytes 10027008 | tf_op jit(solution)/shard_map/all_gather | solution.py:757
  476.4 1.4 copy-start
  477.8 1.4 copy-start.1
  479.2 14.6 %copy-start.2 = (f32[96,1536]{1,0:T(8,128)S(1)}, f32[96,1536]{1,0:T(8,128)}, u32[]{:S(2)}) copy-start(f32[96,1536]{1,0:T(8,128)} %get-tuple-element.76.part) | copy-start | bytes 1769476
  479.2 14.6 %copy-start.3 = (f32[8,1536]{1,0:T(8,128)S(1)}, f32[8,1536]{1,0:T(8,128)}, u32[]{:S(2)}) copy-start(f32[8,1536]{1,0:T(8,128)} %get-tuple-element.77.rows_ref) | copy-start | bytes 147460
  479.2 14.6 %copy-start.4 = (f32[8,128]{1,0:T(8,128)S(1)}, f32[8,128]{1,0:T(8,128)}, u32[]{:S(2)}) copy-start(f32[8,128]{1,0:T(8,128)} %get-tuple-element.78.gb_ref) | copy-start | bytes 12292
Sparse Core Ops, SparseCore 0:
  104.8 83.6 all-gather.3
  284.5 191.7 all-gather.5
  478.0 92.0 all-gather.7

commit v11 on v10

--- a/solution.py
+++ b/solution.py
@@ -20,14 +20,14 @@
     gw_old, old, refs = refs[:n_old], refs[n_old:n_old + n_swap], refs[n_old + n_swap:]
     (dqkv_ref, gwa_ref, gwb_ref, gb_ref, gbt_ref, o_out), got, refs = refs[:6], refs[6:6 + n_swap], refs[6 + n_swap:]
     x_buf, refs = refs[0], refs[1:]
-    w_ref, b_rep, qkvt_ref, k_tok, v_tok, posk_ref, s_buf, q_pad, do_pad, o_acc, dq_acc, dk_acc, dv_acc, x_sem, w_sem = refs[:15]
-    swaps = [(old[k], got[k]) + refs[15 + 4 * k:19 + 4 * k] for k in range(n_swap)]
+    w_ref, b_rep, qkvt_ref, k_tok, v_tok, posk_ref, s_buf, m_buf, q_pad, do_pad, o_acc, dq_acc, dk_acc, dv_acc, x_sem, w_sem = refs[:16]
+    swaps = [(old[k], got[k]) + refs[16 + 4 * k:20 + 4 * k] for k in range(n_swap)]
     if send_o:
         o_ref, os_sem, or_sem = refs[-3:]
         o_new = o_out
     else:
         o_ref = o_out
-    dim = dot_ref.shape[1]
+    dim, lead = dot_ref.shape[1], gwa_ref.shape[0]
     seq = dot_ref.shape[0] * tok
     pad = k_tok.shape[1] - dim
     nq = blk // tok
@@ -117,7 +117,8 @@
     ref_pos = jnp.broadcast_to(marks_ref[i * nq, which:which + 1, 0:128][:, 0:1].astype(F32), (1, 128))
     c = scale * LOG2E
 
-    def scores(j, m8, diag):
+    def scores(j, carry, diag):
+        m, l8 = carry
         for sub in range(2):
             rows = pl.ds(pl.multiple_of(j * blk + sub * half, half), half)
             st = jnp.dot(k_tok[rows, :], q_pad[...], preferred_element_type=F32)
@@ -127,32 +128,29 @@
                 key = lax.broadcasted_iota(jnp.int32, (half, blk), 0) + sub * half
                 qry = lax.broadcasted_iota(jnp.int32, (half, blk), 1)
                 st = jnp.where(key <= qry, st, MASKED)
-            s_buf[rows, :] = st
-            m8 = jnp.maximum(m8, jnp.max(st.reshape(half // 8, 8, blk), axis=0))
-        return m8
-
-    m8 = lax.fori_loop(0, i, lambda j, m: scores(j, m, False), jnp.full((8, blk), MASKED, F32))
-    m8 = scores(i, m8, True)
-    m = jnp.max(m8, axis=0, keepdims=True)
-
-    def exps(j, l8):
-        for sub in range(2):
-            rows = pl.ds(pl.multiple_of(j * blk + sub * half, half), half)
-            e = jnp.exp2(s_buf[rows, :] - m)
+            m_new = jnp.maximum(m, jnp.max(st, axis=0, keepdims=True))
+            e = jnp.exp2(st - m_new)
             s_buf[rows, :] = e
-            l8 = l8 + jnp.sum(e.reshape(half // 8, 8, blk), axis=0)
-        return l8
-
-    l8 = lax.fori_loop(0, i + 1, exps, jnp.zeros((8, blk), F32))
+            m_buf[2 * j + sub] = jnp.broadcast_to(m_new, (8, blk))
+            l8 = l8 * jnp.exp2(m - m_new) + jnp.sum(e.reshape(half // 8, 8, blk), axis=0)
+            m = m_new
+        return m, l8
+
+    start = (jnp.full((1, blk), MASKED, F32), jnp.zeros((8, blk), F32))
+    m, l8 = scores(i, lax.fori_loop(0, i, lambda j, carry: scores(j, carry, False), start), True)
     inv = 1.0 / jnp.sum(l8, axis=0, keepdims=True)
     o_acc[...] = jnp.zeros_like(o_acc)
     dq_acc[...] = jnp.zeros_like(dq_acc)
 
     def values(j, _):
         rows = pl.ds(pl.multiple_of(j * blk, blk), blk)
-        p = s_buf[rows, :] * inv
-        s_buf[rows, :] = p
-        pb = p.astype(BF16)
+        pbs = []
+        for sub in range(2):
+            part = pl.ds(pl.multiple_of(j * blk + sub * half, half), half)
+            p = s_buf[part, :] * (jnp.exp2(m_buf[2 * j + sub][0:1, :] - m) * inv)
+            s_buf[part, :] = p
+            pbs.append(p.astype(BF16))
+        pb = jnp.concatenate(pbs, axis=0)
         o_acc[...] += jnp.dot(qkvt_ref[2 * dim:3 * dim, rows], pb, preferred_element_type=F32)
         dv_acc[:, rows] += lax.dot_general(do_pad[0:dim, :], pb, NT, preferred_element_type=F32)
         return 0
@@ -193,7 +191,7 @@
         @pl.loop(0, steps)
         def _(j):
             rows = pl.ds(pl.multiple_of(j * blk, blk), blk)
-            for ref, lo, hi in ((gwa_ref, 0, 2 * dim), (gwb_ref, 2 * dim, 3 * dim)):
+            for ref, lo, hi in ((gwa_ref, 0, lead), (gwb_ref, lead, 3 * dim)):
                 lhs = jnp.concatenate([dqkv_ref[j * nq + t, lo:hi] for t in range(nq)], axis=1)
                 ref[...] += jnp.dot(lhs, x_buf[rows, :], preferred_element_type=F32)
                 gb_ref[lo:hi, :] += jnp.dot(lhs, ones, preferred_element_type=F32)
@@ -215,15 +213,15 @@
             swap_wait(*one, peers)
 
 
-def attention(w_all, b_all, dot_, marks, x, gw, old, *, blk, tok, which, batch, send_o, collective_id):
+def attention(w_all, b_all, dot_, marks, x, gw, old, *, blk, tok, which, batch, lead, send_o, collective_id):
     blocks, dim, _ = dot_.shape
     seq, hidden = blocks * tok, w_all.shape[2]
     wide = 128 * pl.cdiv(dim, 128)
     hbm = pl.BlockSpec(memory_space=pltpu.HBM)
     full = lambda a: pl.BlockSpec(a.shape, lambda i: (0,) * len(a.shape), pipeline_mode=pl.Buffered(1))
     like = lambda a: jax.ShapeDtypeStruct(a.shape, a.dtype)
-    outs = [jax.ShapeDtypeStruct((blocks, 3 * dim, tok), BF16), jax.ShapeDtypeStruct((2 * dim, hidden), F32),
-            jax.ShapeDtypeStruct((dim, hidden), F32), jax.ShapeDtypeStruct((3 * dim, 128), F32), jax.ShapeDtypeStruct((8, 128), F32)]
+    outs = [jax.ShapeDtypeStruct((blocks, 3 * dim, tok), BF16), jax.ShapeDtypeStruct((lead, hidden), F32),
+            jax.ShapeDtypeStruct((3 * dim - lead, hidden), F32), jax.ShapeDtypeStruct((3 * dim, 128), F32), jax.ShapeDtypeStruct((8, 128), F32)]
     pairs = (seq // blk) * (seq // blk + 1) // 2
     dma = pltpu.SemaphoreType.DMA
     res = pl.pallas_call(
@@ -237,7 +235,7 @@
             pltpu.VMEM((seq, hidden), BF16),
             pltpu.VMEM(w_all.shape[1:], BF16), pltpu.VMEM((3 * dim, 128), F32), pltpu.VMEM((3 * dim, seq), BF16),
             pltpu.VMEM((seq, wide), BF16), pltpu.VMEM((seq, wide), BF16), pltpu.VMEM((seq, 128), F32),
-            pltpu.VMEM((seq, blk), F32),
+            pltpu.VMEM((seq, blk), F32), pltpu.VMEM((2 * seq // blk, 8, blk), F32),
             pltpu.VMEM((wide, blk), BF16), pltpu.VMEM((wide, blk), BF16),
             pltpu.VMEM((dim, blk), F32), pltpu.VMEM((dim, blk), F32),
             pltpu.VMEM((dim, seq), F32), pltpu.VMEM((dim, seq), F32), dma((seq // blk,)), dma]
@@ -324,11 +322,13 @@
     home = [(0, w, 0, u) for u in range(cuts) for w in range(2)]
     moved = [(s, w, t, u) for t in range(1, ring // 2 + 1) for s, w, u in lots if t <= hops(ring, s, w)]
 
-    def start():
+    def start(only=None):
         for s, w, u in lots:
-            along(s, w, 0, u).start()
+            if only in (None, (w, u)):
+                along(s, w, 0, u).start()
         for lot in home:
-            across(*lot, c).start()
+            if only in (None, (lot[1], lot[3])):
+                across(*lot, c).start()
 
     def run(lo=1, hi=ring):
         for s, w, t, u in moved:
@@ -368,16 +368,18 @@
     for load in loads:
         load.start()
 
+    def norm_rows(b, out_ref, rows):
+        x = x_ref[b, rows, :].astype(F32)
+        cen = x - jnp.mean(x, axis=-1, keepdims=True)
+        hat = cen * lax.rsqrt(jnp.mean(cen * cen, axis=-1, keepdims=True) + NORM_EPS)
+        out_ref[rows, :] = (hat * gain + bias).astype(BF16)
+
     def norm(b, out_ref):
         loads[b].wait()
 
         @pl.loop(0, tok // 32)
         def _(k):
-            rows = pl.ds(pl.multiple_of(k * 32, 32), 32)
-            x = x_ref[b, rows, :].astype(F32)
-            cen = x - jnp.mean(x, axis=-1, keepdims=True)
-            hat = cen * lax.rsqrt(jnp.mean(cen * cen, axis=-1, keepdims=True) + NORM_EPS)
-            out_ref[rows, :] = (hat * gain + bias).astype(BF16)
+            norm_rows(b, out_ref, pl.ds(pl.multiple_of(k * 32, 32), 32))
 
     def product(b, out_ref):
         @pl.loop(0, peers // 4)
@@ -388,11 +390,17 @@
     marks_ref[...] = jnp.zeros_like(marks_ref)
     marks_ref[0:batch, :] = pos_ref[...]
     marks_ref[batch:2 * batch, :] = keep_ref[...]
-    norm(0, x_own)
     block = lambda k, side, w, u: x_all.at[2 * k + side, rows_of(w, u)]
     start, run, finish = ring_gather(block, lambda w, u: x_own.at[rows_of(w, u)], ring_sems, peers, cuts)
-    arrived()
-    start()
+    loads[0].wait()
+    pieces = [(w, u) for u in range(cuts) for w in range(2)]
+    for k, piece in enumerate(pieces):
+        norm_rows(0, x_own, rows_of(*piece))
+        if k == 1:
+            arrived()
+        if k:
+            start(pieces[k - 1])
+    start(pieces[-1])
     keep = pltpu.make_async_copy(x_own, x_all.at[me], in_sem.at[batch + 2])
     keep.start()
     marks = [pltpu.make_async_remote_copy(
@@ -676,33 +684,41 @@
     )(part, rows, gb)
 
 
-def settle_body(*refs, n_in, first, n_plain):
-    x_ref, plain = refs[0], refs[1:1 + n_plain]
-    outs, (buf, in_sem, out_sem, plain_sem) = refs[n_in:-4], refs[-4:]
+def settle_body(*refs, n_in, first, n_plain, n_held):
+    x_ref, plain, held = refs[0], refs[1:1 + n_plain], refs[1 + n_plain:1 + n_plain + n_held]
+    outs = refs[n_in:n_in + 1 + n_plain + n_held]
+    buf, in_sem, out_sem, in_plain, out_plain, *rooms = refs[n_in + 1 + n_plain + n_held:]
     heads, n = x_ref.shape[:2]
-    reads = [pltpu.make_async_copy(x_ref.at[h], buf.at[h], in_sem.at[h]) for h in range(heads)]
-    writes = [pltpu.make_async_copy(buf.at[h], outs[0].at[h, pl.ds(first, n)], out_sem.at[h]) for h in range(heads)]
-    flat = [pltpu.make_async_copy(plain[k], outs[1 + k], plain_sem.at[k]) for k in range(n_plain)]
-    for copy in reads + flat:
-        copy.start()
+    copy = pltpu.make_async_copy
+    reads = [copy(x_ref.at[h], buf.at[h], in_sem.at[h]) for h in range(heads)]
+    writes = [copy(buf.at[h], outs[0].at[h, pl.ds(first, n)], out_sem.at[h]) for h in range(heads)]
+    reads += [copy(plain[k], rooms[k], in_plain.at[k]) for k in range(n_plain)]
+    writes += [copy(rooms[k], outs[1 + k], out_plain.at[k]) for k in range(n_plain)]
+    flat = [copy(held[k], outs[1 + n_plain + k], out_plain.at[n_plain + k]) for k in range(n_held)]
+    for one in reads + flat:
+        one.start()
     for read, write in zip(reads, writes):
         read.wait()
         write.start()
-    for copy in writes + flat:
-        copy.wait()
-
-
-def settle(x, into, plain, lanes, first):
-    heads, n, dim, hidden = x.shape
+    for one in writes + flat:
+        one.wait()
+
+
+def settle(x, into, plain, held, span, first):
+    heads, n, hidden = x.shape
     hbm, vmem = pl.BlockSpec(memory_space=pltpu.HBM), pl.BlockSpec(memory_space=pltpu.VMEM)
-    args = (pltpu.with_memory_space_constraint(x, pltpu.HBM), *plain) + (() if into is None else (into,))
+    pin = lambda a: pltpu.with_memory_space_constraint(a, pltpu.HBM)
+    args = (pin(x), *[pin(a) for a in plain], *held) + (() if into is None else (into,))
     dma = pltpu.SemaphoreType.DMA
+    extra = max(len(plain) + len(held), 1)
     return pl.pallas_call(
-        functools.partial(settle_body, n_in=len(args), first=first, n_plain=len(plain)), name="settle",
-        out_shape=[jax.ShapeDtypeStruct((heads, lanes, dim, hidden), x.dtype)] + [jax.ShapeDtypeStruct(a.shape, a.dtype) for a in plain],
-        in_specs=[hbm] + [vmem] * len(plain) + [hbm] * (into is not None), out_specs=[hbm] * (1 + len(plain)),
+        functools.partial(settle_body, n_in=len(args), first=first, n_plain=len(plain), n_held=len(held)), name="settle",
+        out_shape=[jax.ShapeDtypeStruct((heads, span, hidden), x.dtype)] + [jax.ShapeDtypeStruct(a.shape, a.dtype) for a in (*plain, *held)],
+        in_specs=[hbm] * (1 + len(plain)) + [vmem] * len(held) + [hbm] * (into is not None),
+        out_specs=[hbm] * (1 + len(plain) + len(held)),
         input_output_aliases={} if into is None else {len(args) - 1: 0},
-        scratch_shapes=[pltpu.VMEM(x.shape, x.dtype), dma((heads,)), dma((heads,)), dma((max(len(plain), 1),))],
+        scratch_shapes=[pltpu.VMEM(x.shape, x.dtype), dma((heads,)), dma((heads,)), dma((extra,)), dma((extra,))]
+        + [pltpu.VMEM(a.shape, a.dtype) for a in plain],
         cost_estimate=pl.CostEstimate(flops=10**9, bytes_accessed=8 * x.size, transcendentals=0),
         compiler_params=pltpu.CompilerParams(vmem_limit_bytes=24 << 20))(*args)
 
@@ -745,26 +761,26 @@
         marks, do_first, x_first, x_rest, do_rest = opening(x_blk, dy_blk, w_out, ln_gain, ln_bias, pos_blk, keep_blk, peers, 1)
         xs = [x_first.reshape(seq, hidden)] + [lax.all_gather(one, "sp", axis=0, tiled=True) for one in x_rest]
         do_t = [do_first]
+        lead = 5 * dim // 3
         gw, att = (), []
         for b in range(batch):
             old = list(do_rest[b:b + 1]) if b + 1 < batch else att
-            att_d, gw, gb, att_o, swapped = attention(w_all, b_all, do_t[b], marks, xs[b], gw, old, blk=blk, tok=tok, which=b, batch=batch,
+            att_d, gw, gb, att_o, swapped = attention(w_all, b_all, do_t[b], marks, xs[b], gw, old, blk=blk, tok=tok, which=b, batch=batch, lead=lead,
                                                       send_o=b + 1 == batch, collective_id=4 + b)
             if b + 1 < batch:
                 do_t.append(swapped[0])
             att = [att_o, att_d]
         o_old, d_old = swapped
-        gw_all = [lax.all_gather(one, "sp", axis=0, tiled=True).reshape(heads, -1, dim, hidden) for one in gw[:2]]
-        lead = gw_all[0].shape[1]
+        gw_all = [lax.all_gather(one, "sp", axis=0, tiled=True).reshape(heads, -1, hidden) for one in gw[:2]]
         y, gx, part, rows = tail_a(att_d, d_old, o_old, att_o, dy_blk, x_blk, w_all.reshape(3 * hidden, hidden), w_out, ln_gain, b_out, 2)
         first, _ = lax.optimization_barrier((gw_all[0], y))
-        gw_out, y, gx = settle(first, None, (y, gx), 3, 0)
+        gw_out, y, gx = settle(first, None, (y, gx), (), 3 * dim, 0)
         part, gw_out, y, gx = lax.optimization_barrier((part, gw_out, y, gx))
         go_all, gb_all, g_gain, g_bias, g_out = lay_down(*tail_b(part, rows, gb, peers, 3))
         second, gw_out, go_all = lax.optimization_barrier((gw_all[1], gw_out, go_all))
-        gw_out, = settle(second, gw_out, (), 3, lead)
-        return (y, gx, jnp.transpose(gw_out, (3, 0, 1, 2)), jnp.transpose(gb_all, (1, 0, 2)), go_all.reshape(hidden, hidden),
-                g_out, g_gain, g_bias)
+        gw_out, = settle(second, gw_out, (), (), 3 * dim, lead)
+        gw_out = jnp.transpose(gw_out.reshape(heads, 3, dim, hidden), (3, 0, 1, 2))
+        return y, gx, gw_out, jnp.transpose(gb_all, (1, 0, 2)), go_all.reshape(hidden, hidden), g_out, g_gain, g_bias
 
     act_spec = P("dp", "sp", None)
     tok_spec = P("dp", "sp")

time: 603 us -> 597 us (0.990)
  waiting for transfers between devices: 25.4 us -> 10.2 us
  Pallas kernels: 560 us -> 572 us
    all_gather x3 -> x1, waiting for transfers between devices: 24.8 us -> 4.32 us  [block_fn(): lax.all_gather(one, 'sp', axis=0, tiled=True)]
    pallas_call x1, Pallas kernels: 90.2 us -> 104 us  [tail_b(): pl.pallas_call(functools.partial(tail_b_body, peers=peers, cuts=cuts), na...]
  transfers between devices with their start and end apart: 3 -> 3, of which waited for: 2 -> 2; matrix products, arithmetic and copies ran while one was open for 0% -> 0% of each run, Pallas kernels for 60% -> 62%
where the time goes in v11:
time: 597 us
  Pallas kernels  572 us (96%)
  between operations  13.9 us (2%)
  waiting for transfers between devices  10.2 us (2%)
    pallas_call x2, Pallas kernels, attention(): pl.pallas_call(functools.partial(attn_body, blk=blk, tok=tok, which=which...  175 us
    pallas_call x1, Pallas kernels, tail_a(): pl.pallas_call(functools.partial(tail_a_body, peers=peers, cuts=cuts), na...  170 us
    pallas_call x1, Pallas kernels, tail_b(): pl.pallas_call(functools.partial(tail_b_body, peers=peers, cuts=cuts), na...  104 us
    pallas_call x1, Pallas kernels, opening(): pl.pallas_call(functools.partial(opening_body, peers=peers, batch=batch,...  96.5 us
    pallas_call x2, Pallas kernels, settle(): pl.pallas_call(functools.partial(settle_body, n_in=len(args), first=first...  22.5 us
  transfers between devices with their start and end apart: 3, of which 2 were waited for; matrix products, arithmetic and copies ran while one was open for 0% of the time, Pallas kernels for 62%

profile of v11, /device:TPU:21, one launch (start us, length us, event | category | flops | bytes accessed | tf_op | source)
XLA Modules:
  0.0 596.8 jit_solution(9815118988599802423)
XLA Ops:
  7.2 0.1 all-gather.4.cloned.1.call-start
  7.2 96.5 %opening.1 = (s32[16,8,256]{2,1,0:T(8,128)}, bf16[16,96,256]{2,1,0:T(8,128)(2,1)}, bf16[16,256,1536]{2,1,0:T(8,128)(2,1)}, bf16[256,1536]{1,0:T(8,128)(2,1)}, bf16[16,96,256]{2,1,0:T(8,128)(2,1)}) custom-call(bf16[2,256,1536]{2,1,0:T(8,128)(2,1)} %x_hbm.3, bf16[2,256,1536]{2,1,0:T(8,128)(2,1)} %dy_hbm.3, bf16[1536,1536]{1,0:T(8,128)(2,1)} %wo_hbm.3, ...), custom_call_target="tpu_custom_call" | custom-call | flops 49999998976 | bytes 16777216 | tf_op jit(solution)/shard_map/opening/pallas_call | solution.py:434
  103.7 0.1 all-gather.4.cloned.1.call-update
  103.8 0.2 all-gather.6.cloned.1.call-start
  104.0 78.8 %attention.2 = (bf16[16,288,256]{2,1,0:T(8,128)(2,1)}, f32[160,1536]{1,0:T(8,128)}, f32[128,1536]{1,0:T(8,128)}, f32[288,128]{1,0:T(8,128)}, f32[8,128]{1,0:T(8,...) custom-call(bf16[16,288,1536]{2,1,0:T(8,128)(2,1)} %bitcast.17, f32[3,16,96]{2,1,0:T(8,128)} %bitcast.21, ...), custom_call_target="tpu_custom_call" | custom-call | flops 28991029248 | bytes 25165824 | tf_op jit(solution)/shard_map/attention/pallas_call | solution.py:227
  182.9 4.3 all-gather.4.cloned.1.call-done.x_ref
  187.2 95.9 %attention.3 = (bf16[16,288,256]{2,1,0:T(8,128)(2,1)}, f32[160,1536]{1,0:T(8,128)}, f32[128,1536]{1,0:T(8,128)}, f32[288,128]{1,0:T(8,128)}, f32[8,128]{1,0:T(8,...) custom-call(bf16[16,288,1536]{2,1,0:T(8,128)(2,1)} %bitcast.18, ...), custom_call_target="tpu_custom_call" | custom-call | flops 28991029248 | bytes 25165824 | tf_op jit(solution)/shard_map/attention/pallas_call | solution.py:227
  283.1 0.1 all-gather.6.cloned.1.call-update
  283.2 0.3 all-gather.8.cloned.1.call-start
  283.5 0.5 all-gather.8.cloned.1.call-update
  284.0 170.2 %tail_a.1 = (bf16[2,256,1536]{2,1,0:T(8,128)(2,1)}, bf16[2,256,1536]{2,1,0:T(8,128)(2,1)}, f32[96,1536]{1,0:T(8,128)}, f32[8,1536]{1,0:T(8,128)}) custom-call(bf16[16,288,256]{2,1,0:T(8,128)(2,1)} %get-tuple-element.60.dqkv_ref, bf16[16,96,256]{2,1,0:T(8,128)(2,1)} %get-tuple-element.61.oo_hbm, bf16[16,96,256]{2,1,0:T(8,128)(2,1)} %get-tuple-element.62.on_hbm, ...), custom_call_target="tpu_custom_call" | custom-call | flops 99999997952 | bytes 67108864 | tf_op jit(solution)/shard_map/tail_a/pallas_call | solution.py:590
  454.1 5.3 all-gather.6.cloned.1.call-done
  459.4 0.0 copy-start
  459.4 0.0 copy-start.1
  459.4 0.0 copy-start.2
  459.4 13.4 %settle.2 = (f32[16,288,1536]{2,1,0:T(8,128)}, bf16[2,256,1536]{2,1,0:T(8,128)(2,1)}, bf16[2,256,1536]{2,1,0:T(8,128)(2,1)}) custom-call(f32[16,160,1536]{2,1,0:T(8,128)} %bitcast.15, bf16[2,256,1536]{2,1,0:T(8,128)(2,1)} %get-tuple-element.66.refs_1_, bf16[2,256,1536]{2,1,0:T(8,128)(2,1)} %get-tuple-element.68.refs_2_), custom_call_target="tpu_custom_call" | custom-call | flops 1000000000 | bytes 31457280 | tf_op jit(solution)/shard_map/settle/pallas_call | solution.py:714
  472.8 0.0 copy-done
  472.8 0.0 copy-done.1
  472.9 0.0 copy-done.2
  472.9 104.0 %tail_b.1 = (f32[8,2,96,1536]{3,2,1,0:T(8,128)S(1)}, f32[8,1536]{1,0:T(8,128)S(1)}, f32[16,8,128]{2,1,0:T(8,128)S(1)}) custom-call(f32[96,1536]{1,0:T(8,128)S(1)} %copy-done, f32[8,1536]{1,0:T(8,128)S(1)} %copy-done.1, f32[8,128]{1,0:T(8,128)S(1)} %copy-done.2), custom_call_target="tpu_custom_call" | custom-call | flops 49999998976 | bytes 10485760 | tf_op jit(solution)/shard_map/tail_b/pallas_call | solution.py:674
  576.8 4.3 lay_down.1
  581.1 0.0 all-gather.8.cloned.1.call-done
  581.2 9.1 %settle.3 = f32[16,288,1536]{2,1,0:T(8,128)} custom-call(f32[16,128,1536]{2,1,0:T(8,128)} %bitcast.16, f32[16,288,1536]{2,1,0:T(8,128)} %get-tuple-element.84.refs_1_), custom_call_target="tpu_custom_call", output_to_operand_aliasing={{}: (1, {})} | custom-call | flops 1000000000 | bytes 25165824 | tf_op jit(solution)/shard_map/settle/pallas_call | solution.py:714
Async XLA Ops:
  7.2 180.0 %all-gather.4.cloned.1.call-start = ((), (), s32[]{:S(2)}) async-start(), calls=%async_computation | async-start | bytes 13369344 | tf_op jit(solution)/shard_map/all_gather | solution.py:762
  103.8 355.6 %all-gather.6.cloned.1.call-start = ((), (), s32[]{:S(2)}) async-start(), calls=%async_computation.1 | async-start | bytes 16711680 | tf_op jit(solution)/shard_map/all_gather | solution.py:774
  283.2 298.0 %all-gather.8.cloned.1.call-start = ((), (), s32[]{:S(2)}) async-start(), calls=%async_computation.2 | async-start | bytes 13369344 | tf_op jit(solution)/shard_map/all_gather | solution.py:774
  459.4 13.4 %copy-start = (f32[96,1536]{1,0:T(8,128)S(1)}, f32[96,1536]{1,0:T(8,128)}, u32[]{:S(2)}) copy-start(f32[96,1536]{1,0:T(8,128)} %get-tuple-element.76.part) | copy-start | bytes 1769476
  459.4 13.4 %copy-start.1 = (f32[8,1536]{1,0:T(8,128)S(1)}, f32[8,1536]{1,0:T(8,128)}, u32[]{:S(2)}) copy-start(f32[8,1536]{1,0:T(8,128)} %get-tuple-element.77.rows_ref) | copy-start | bytes 147460
  459.4 13.4 %copy-start.2 = (f32[8,128]{1,0:T(8,128)S(1)}, f32[8,128]{1,0:T(8,128)}, u32[]{:S(2)}) copy-start(f32[8,128]{1,0:T(8,128)} %get-tuple-element.78.gb_ref) | copy-start | bytes 12292
Sparse Core Ops, SparseCore 0:
  103.9 83.2 all-gather.3
  283.3 176.0 all-gather.5
  461.0 119.2 all-gather.7

commit v12 on v11

--- a/solution.py
+++ b/solution.py
@@ -74,7 +74,7 @@
             x_copy(k).start()
         meet(peers)
         for one in swaps:
-            swap_start(*one, peers)
+            swap_start(*one, peers, hi=None if send_o else nq)
         dk_acc[...] = jnp.zeros_like(dk_acc)
         dv_acc[...] = jnp.zeros_like(dv_acc)
         q_pad[...] = jnp.zeros_like(q_pad)
@@ -108,6 +108,12 @@
         @pl.when(step > 0)
         def _():
             o_start(step - 1)
+    else:
+        for k in range(1, steps):
+            @pl.when(step == k)
+            def _():
+                for one in swaps:
+                    swap_some(*one, peers, k * nq, (k + 1) * nq)
 
     qcols = pl.ds(pl.multiple_of(i * blk, blk), blk)
     q_pad[0:dim, :] = qkvt_ref[0:dim, qcols]
@@ -262,18 +268,22 @@
     greet(peers)()
 
 
-def swap_copies(x_ref, out_ref, send_sem, recv_sem, peers):
+def swap_copies(x_ref, out_ref, send_sem, recv_sem, peers, lo=0, hi=None):
     me = lax.axis_index("sp")
     order = [d for near in range(peers // 2) for d in sorted({peers // 2 - near, peers // 2 + near})]
     return [pltpu.make_async_remote_copy(
         src_ref=x_ref.at[lax.rem(me + d, peers)], dst_ref=out_ref.at[me], send_sem=send_sem.at[d - 1], recv_sem=recv_sem.at[d - 1],
-        device_id=peer_at(d, peers), device_id_type=pl.DeviceIdType.MESH) for d in order]
-
-
-def swap_start(x_ref, out_ref, own, send_sem, recv_sem, own_sem, peers):
+        device_id=peer_at(d, peers), device_id_type=pl.DeviceIdType.MESH) for d in order[lo:hi]]
+
+
+def swap_some(x_ref, out_ref, own, send_sem, recv_sem, own_sem, peers, lo, hi):
+    for copy in swap_copies(x_ref, out_ref, send_sem, recv_sem, peers, lo, hi):
+        copy.start()
+
+
+def swap_start(x_ref, out_ref, own, send_sem, recv_sem, own_sem, peers, hi=None):
     me = lax.axis_index("sp")
-    for copy in swap_copies(x_ref, out_ref, send_sem, recv_sem, peers):
-        copy.start()
+    swap_some(x_ref, out_ref, own, send_sem, recv_sem, own_sem, peers, 0, hi)
     take = pltpu.make_async_copy(x_ref.at[me], own, own_sem)
     take.start()
     take.wait()
@@ -412,12 +422,17 @@
     loads[-2].wait()
     loads[-1].wait()
     product(0, do_own)
+    swap = (do_own, do_t, own, ds_sem, dr_sem, do_sem, peers)
+    third = (peers + 1) // 3
+    swap_start(*swap, hi=third)
     for b in range(1, batch):
         norm(b, x_out[b - 1])
-    swap_start(do_own, do_t, own, ds_sem, dr_sem, do_sem, peers)
-    for b in range(1, batch):
         product(b, do_out[b - 1])
-    run()
+    run(1, 2)
+    swap_some(*swap, third, 2 * third)
+    run(2, 3)
+    swap_some(*swap, 2 * third, peers)
+    run(3)
     keep.wait()
     for copy in marks:
         copy.wait()
@@ -471,7 +486,8 @@
     for load in loads:
         load.start()
     arrived()
-    swap_start(*swap)
+    third = (peers + 1) // 3
+    swap_start(*swap, hi=third)
     for load in loads[:3]:
         load.wait()
 
@@ -556,14 +572,17 @@
 
     for s, w, u in lots:
         reduce_copy(s, w, 0, u).start()
+    swap_some(*swap, third, 2 * third)
     for load in loads[3:5]:
         load.wait()
     forward(0, o_old)
     forward(1, o_new)
+    hop(1)
+    swap_some(*swap, 2 * third, peers)
     for load in loads[5:]:
         load.wait()
     backward(0, d_old)
-    for t in range(1, ring // 2 - 1):
+    for t in range(2, ring // 2 - 1):
         hop(t)
     swap_wait(*swap)
     backward(1, d_new)

time: 597 us -> 601 us (level)
  transfers between devices with their start and end apart: 3 -> 3, of which waited for: 2 -> 3; matrix products, arithmetic and copies ran while one was open for 0% -> 0% of each run, Pallas kernels for 62% -> 61%
where the time goes in v12:
time: 601 us; the launch traced here: 600 us
  Pallas kernels  571 us (95%)
  waiting for transfers between devices  14.7 us (2%)
  between operations  13.9 us (2%)
    pallas_call x2, Pallas kernels, attention(): pl.pallas_call(functools.partial(attn_body, blk=blk, tok=tok, which=which...  178 us
    pallas_call x1, Pallas kernels, tail_a(): pl.pallas_call(functools.partial(tail_a_body, peers=peers, cuts=cuts), na...  169 us
    pallas_call x1, Pallas kernels, tail_b(): pl.pallas_call(functools.partial(tail_b_body, peers=peers, cuts=cuts), na...  102 us
    pallas_call x1, Pallas kernels, opening(): pl.pallas_call(functools.partial(opening_body, peers=peers, batch=batch,...  96.4 us
    pallas_call x2, Pallas kernels, settle(): pl.pallas_call(functools.partial(settle_body, n_in=len(args), first=first...  22.5 us
  transfers between devices with their start and end apart: 3, of which 3 were waited for; matrix products, arithmetic and copies ran while one was open for 0% of the time, Pallas kernels for 61%

profile of v12, /device:TPU:21, one launch (start us, length us, event | category | flops | bytes accessed | tf_op | source)
XLA Modules:
  0.0 600.3 jit_solution(5682392280316227922)
XLA Ops:
  7.2 0.1 all-gather.4.cloned.1.call-start
  7.2 96.4 %opening.1 = (s32[16,8,256]{2,1,0:T(8,128)}, bf16[16,96,256]{2,1,0:T(8,128)(2,1)}, bf16[16,256,1536]{2,1,0:T(8,128)(2,1)}, bf16[256,1536]{1,0:T(8,128)(2,1)}, bf16[16,96,256]{2,1,0:T(8,128)(2,1)}) custom-call(bf16[2,256,1536]{2,1,0:T(8,128)(2,1)} %x_hbm.3, bf16[2,256,1536]{2,1,0:T(8,128)(2,1)} %dy_hbm.3, bf16[1536,1536]{1,0:T(8,128)(2,1)} %wo_hbm.3, ...), custom_call_target="tpu_custom_call" | custom-call | flops 49999998976 | bytes 16777216 | tf_op jit(solution)/shard_map/opening/pallas_call | solution.py:449
  103.7 0.1 all-gather.4.cloned.1.call-update
  103.8 0.2 all-gather.6.cloned.1.call-start
  104.0 79.6 %attention.2 = (bf16[16,288,256]{2,1,0:T(8,128)(2,1)}, f32[160,1536]{1,0:T(8,128)}, f32[128,1536]{1,0:T(8,128)}, f32[288,128]{1,0:T(8,128)}, f32[8,128]{1,0:T(8,...) custom-call(bf16[16,288,1536]{2,1,0:T(8,128)(2,1)} %bitcast.17, f32[3,16,96]{2,1,0:T(8,128)} %bitcast.21, ...), custom_call_target="tpu_custom_call" | custom-call | flops 28991029248 | bytes 25165824 | tf_op jit(solution)/shard_map/attention/pallas_call | solution.py:233
  183.6 4.2 all-gather.4.cloned.1.call-done.x_ref
  187.9 98.0 %attention.3 = (bf16[16,288,256]{2,1,0:T(8,128)(2,1)}, f32[160,1536]{1,0:T(8,128)}, f32[128,1536]{1,0:T(8,128)}, f32[288,128]{1,0:T(8,128)}, f32[8,128]{1,0:T(8,...) custom-call(bf16[16,288,1536]{2,1,0:T(8,128)(2,1)} %bitcast.18, ...), custom_call_target="tpu_custom_call" | custom-call | flops 28991029248 | bytes 25165824 | tf_op jit(solution)/shard_map/attention/pallas_call | solution.py:233
  285.9 0.1 all-gather.6.cloned.1.call-update
  285.9 0.3 all-gather.8.cloned.1.call-start
  286.2 0.5 all-gather.8.cloned.1.call-update
  286.7 168.6 %tail_a.1 = (bf16[2,256,1536]{2,1,0:T(8,128)(2,1)}, bf16[2,256,1536]{2,1,0:T(8,128)(2,1)}, f32[96,1536]{1,0:T(8,128)}, f32[8,1536]{1,0:T(8,128)}) custom-call(bf16[16,288,256]{2,1,0:T(8,128)(2,1)} %get-tuple-element.60.dqkv_ref, bf16[16,96,256]{2,1,0:T(8,128)(2,1)} %get-tuple-element.61.oo_hbm, bf16[16,96,256]{2,1,0:T(8,128)(2,1)} %get-tuple-element.62.on_hbm, ...), custom_call_target="tpu_custom_call" | custom-call | flops 99999997952 | bytes 67108864 | tf_op jit(solution)/shard_map/tail_a/pallas_call | solution.py:609
  455.3 8.6 %all-gather.6.cloned.1.call-done = f32[2560,1536]{1,0:T(8,128)} async-done(((f32[160,1536]{1,0:T(8,128)}), f32[2560,1536]{1,0:T(8,128)}) %all-gather.6.cloned.1.call-update) | async-done | bytes 15728656 | tf_op jit(solution)/shard_map/all_gather | solution.py:793
  463.9 0.0 copy-start
  463.9 0.0 copy-start.1
  463.9 0.0 copy-start.2
  464.0 13.4 %settle.2 = (f32[16,288,1536]{2,1,0:T(8,128)}, bf16[2,256,1536]{2,1,0:T(8,128)(2,1)}, bf16[2,256,1536]{2,1,0:T(8,128)(2,1)}) custom-call(f32[16,160,1536]{2,1,0:T(8,128)} %bitcast.15, bf16[2,256,1536]{2,1,0:T(8,128)(2,1)} %get-tuple-element.66.refs_1_, bf16[2,256,1536]{2,1,0:T(8,128)(2,1)} %get-tuple-element.68.refs_2_), custom_call_target="tpu_custom_call" | custom-call | flops 1000000000 | bytes 31457280 | tf_op jit(solution)/shard_map/settle/pallas_call | solution.py:733
  477.4 0.0 copy-done
  477.4 0.0 copy-done.1
  477.4 0.0 copy-done.2
  477.4 101.7 %tail_b.1 = (f32[8,2,96,1536]{3,2,1,0:T(8,128)S(1)}, f32[8,1536]{1,0:T(8,128)S(1)}, f32[16,8,128]{2,1,0:T(8,128)S(1)}) custom-call(f32[96,1536]{1,0:T(8,128)S(1)} %copy-done, f32[8,1536]{1,0:T(8,128)S(1)} %copy-done.1, f32[8,128]{1,0:T(8,128)S(1)} %copy-done.2), custom_call_target="tpu_custom_call" | custom-call | flops 49999998976 | bytes 10485760 | tf_op jit(solution)/shard_map/tail_b/pallas_call | solution.py:693
  579.1 4.3 lay_down.1
  583.4 1.2 all-gather.8.cloned.1.call-done
  584.7 9.0 %settle.3 = f32[16,288,1536]{2,1,0:T(8,128)} custom-call(f32[16,128,1536]{2,1,0:T(8,128)} %bitcast.16, f32[16,288,1536]{2,1,0:T(8,128)} %get-tuple-element.84.refs_1_), custom_call_target="tpu_custom_call", output_to_operand_aliasing={{}: (1, {})} | custom-call | flops 1000000000 | bytes 25165824 | tf_op jit(solution)/shard_map/settle/pallas_call | solution.py:733
Async XLA Ops:
  7.2 180.7 %all-gather.4.cloned.1.call-start = ((), (), s32[]{:S(2)}) async-start(), calls=%async_computation | async-start | bytes 13369344 | tf_op jit(solution)/shard_map/all_gather | solution.py:781
  103.8 360.2 %all-gather.6.cloned.1.call-start = ((), (), s32[]{:S(2)}) async-start(), calls=%async_computation.1 | async-start | bytes 16711680 | tf_op jit(solution)/shard_map/all_gather | solution.py:793
  285.9 298.7 %all-gather.8.cloned.1.call-start = ((), (), s32[]{:S(2)}) async-start(), calls=%async_computation.2 | async-start | bytes 13369344 | tf_op jit(solution)/shard_map/all_gather | solution.py:793
  463.9 13.4 %copy-start = (f32[96,1536]{1,0:T(8,128)S(1)}, f32[96,1536]{1,0:T(8,128)}, u32[]{:S(2)}) copy-start(f32[96,1536]{1,0:T(8,128)} %get-tuple-element.76.part) | copy-start | bytes 1769476
  463.9 13.4 %copy-start.1 = (f32[8,1536]{1,0:T(8,128)S(1)}, f32[8,1536]{1,0:T(8,128)}, u32[]{:S(2)}) copy-start(f32[8,1536]{1,0:T(8,128)} %get-tuple-element.77.rows_ref) | copy-start | bytes 147460
  463.9 13.4 %copy-start.2 = (f32[8,128]{1,0:T(8,128)S(1)}, f32[8,128]{1,0:T(8,128)}, u32[]{:S(2)}) copy-start(f32[8,128]{1,0:T(8,128)} %get-tuple-element.78.gb_ref) | copy-start | bytes 12292
Sparse Core Ops, SparseCore 0:
  103.9 83.9 all-gather.3
  286.1 177.8 all-gather.5
  465.6 119.0 all-gather.7

commit v13 on v11

--- a/solution.py
+++ b/solution.py
@@ -92,16 +92,14 @@
             shift = jnp.concatenate([b_rep[...]] * (blk // 128), axis=1)
             qkvt_ref[:, rows] = (lax.dot_general(w_ref[...], x_buf[rows, :], NT, preferred_element_type=F32) + shift).astype(BF16)
 
-            @pl.loop(0, blk // 128)
-            def _(t):
+            for t in range(blk // 128):
                 cols = pl.ds(pl.multiple_of(k * blk + t * 128, 128), 128)
                 for base, dst in ((dim, k_tok), (2 * dim, v_tok)):
                     part = qkvt_ref[base:base + dim, cols].astype(F32)
                     whole = jnp.concatenate([part, jnp.zeros((pad, 128), F32)], axis=0)
                     dst[cols, :] = jnp.transpose(whole).astype(BF16)
-                lanes = pl.ds(pl.multiple_of((t % sub) * 128, 128), 128)
-                pos = marks_ref[k * nq + t // sub, which:which + 1, lanes].astype(F32)
-                keep = marks_ref[k * nq + t // sub, batch + which:batch + which + 1, lanes]
+                mark = marks_ref[k * nq + t // sub, which * sub + t % sub:which * sub + t % sub + 1, :]
+                pos, keep = lax.shift_right_logical(mark, 1).astype(F32), mark & 1
                 posk_ref[cols, :] = spread(jnp.where(keep > 0, pos, MASKED))
 
     if send_o:
@@ -114,7 +112,8 @@
     for t in range(nq):
         do_pad[0:dim, t * tok:(t + 1) * tok] = dot_ref[i * nq + t]
     slope2 = jnp.exp2(jnp.full((1, 128), -8.0 / peers, F32) * (me + 1).astype(F32)) * LOG2E
-    ref_pos = jnp.broadcast_to(marks_ref[i * nq, which:which + 1, 0:128][:, 0:1].astype(F32), (1, 128))
+    first = lax.shift_right_logical(marks_ref[i * nq, which * sub:which * sub + 1, :], 1).astype(F32)
+    ref_pos = jnp.broadcast_to(first[:, 0:1], (1, 128))
     c = scale * LOG2E
 
     def scores(j, carry, diag):
@@ -388,8 +387,11 @@
             out_ref[pl.ds(g * 4, 4)] = lax.dot_general(wo_ref[rows, :], dy_ref[b], NT, preferred_element_type=F32).astype(BF16).reshape(4, dim, tok)
 
     marks_ref[...] = jnp.zeros_like(marks_ref)
-    marks_ref[0:batch, :] = pos_ref[...]
-    marks_ref[batch:2 * batch, :] = keep_ref[...]
+    packed = 2 * pos_ref[...] + keep_ref[...]
+    sub = tok // 128
+    for b in range(batch):
+        for k in range(sub):
+            marks_ref[b * sub + k:b * sub + k + 1, :] = packed[b:b + 1, k * 128:(k + 1) * 128]
     block = lambda k, side, w, u: x_all.at[2 * k + side, rows_of(w, u)]
     start, run, finish = ring_gather(block, lambda w, u: x_own.at[rows_of(w, u)], ring_sems, peers, cuts)
     loads[0].wait()
@@ -434,12 +436,12 @@
     res = pl.pallas_call(
         functools.partial(opening_body, peers=peers, batch=batch, cuts=cuts),
         name="opening",
-        out_shape=[jax.ShapeDtypeStruct((peers, 8, tok), pos.dtype), do_shape, jax.ShapeDtypeStruct((peers, tok, hidden), BF16)]
+        out_shape=[jax.ShapeDtypeStruct((peers, 8, 128), pos.dtype), do_shape, jax.ShapeDtypeStruct((peers, tok, hidden), BF16)]
         + [x_shape] * (batch - 1) + [do_shape] * (batch - 1),
         in_specs=[hbm, hbm, hbm, vmem, vmem, vmem, vmem],
         out_specs=[vmem, hbm, hbm] + [vmem] * (2 * batch - 2),
         scratch_shapes=[pltpu.VMEM(x.shape, BF16), pltpu.VMEM(dy.shape, BF16), pltpu.VMEM(x_shape.shape, BF16), pltpu.VMEM(do_shape.shape, BF16),
-                        pltpu.VMEM(w_out.shape, BF16), pltpu.VMEM((8, tok), pos.dtype)] + swap_scratch(do_shape)
+                        pltpu.VMEM(w_out.shape, BF16), pltpu.VMEM((8, 128), pos.dtype)] + swap_scratch(do_shape)
         + [dma((peers - 1,)), dma((peers - 1,)), dma((batch + 3,))] + ring_scratch(peers, cuts),
         cost_estimate=pl.CostEstimate(flops=5 * 10**10, bytes_accessed=16 << 20, transcendentals=0),
         compiler_params=pltpu.CompilerParams(collective_id=collective_id, has_side_effects=True, vmem_limit_bytes=VMEM_LIMIT),
@@ -761,7 +763,7 @@
         marks, do_first, x_first, x_rest, do_rest = opening(x_blk, dy_blk, w_out, ln_gain, ln_bias, pos_blk, keep_blk, peers, 1)
         xs = [x_first.reshape(seq, hidden)] + [lax.all_gather(one, "sp", axis=0, tiled=True) for one in x_rest]
         do_t = [do_first]
-        lead = 5 * dim // 3
+        lead = 13 * dim // 6
         gw, att = (), []
         for b in range(batch):
             old = list(do_rest[b:b + 1]) if b + 1 < batch else att
@@ -773,10 +775,9 @@
         o_old, d_old = swapped
         gw_all = [lax.all_gather(one, "sp", axis=0, tiled=True).reshape(heads, -1, hidden) for one in gw[:2]]
         y, gx, part, rows = tail_a(att_d, d_old, o_old, att_o, dy_blk, x_blk, w_all.reshape(3 * hidden, hidden), w_out, ln_gain, b_out, 2)
-        first, _ = lax.optimization_barrier((gw_all[0], y))
+        go_all, gb_all, g_gain, g_bias, g_out = lay_down(*tail_b(part, rows, gb, peers, 3))
+        first, y, gx, go_all = lax.optimization_barrier((gw_all[0], y, gx, go_all))
         gw_out, y, gx = settle(first, None, (y, gx), (), 3 * dim, 0)
-        part, gw_out, y, gx = lax.optimization_barrier((part, gw_out, y, gx))
-        go_all, gb_all, g_gain, g_bias, g_out = lay_down(*tail_b(part, rows, gb, peers, 3))
         second, gw_out, go_all = lax.optimization_barrier((gw_all[1], gw_out, go_all))
         gw_out, = settle(second, gw_out, (), (), 3 * dim, lead)
         gw_out = jnp.transpose(gw_out.reshape(heads, 3, dim, hidden), (3, 0, 1, 2))

time: 597 us -> 579 us (0.970)
  Pallas kernels: 572 us -> 556 us
    pallas_call x1, Pallas kernels: 104 us -> 89.6 us  [tail_b(): pl.pallas_call(functools.partial(tail_b_body, peers=peers, cuts=cuts), na...]
  transfers between devices with their start and end apart: 3 -> 3, of which waited for: 2 -> 1; matrix products, arithmetic and copies ran while one was open for 0% -> 0% of each run, Pallas kernels for 62% -> 62%
where the time goes in v13:
time: 579 us; the launch traced here: 578 us
  Pallas kernels  556 us (96%)
  between operations  13.9 us (2%)
    pallas_call x2, Pallas kernels, attention(): pl.pallas_call(functools.partial(attn_body, blk=blk, tok=tok, which=which...  174 us
    pallas_call x1, Pallas kernels, tail_a(): pl.pallas_call(functools.partial(tail_a_body, peers=peers, cuts=cuts), na...  170 us
    pallas_call x1, Pallas kernels, opening(): pl.pallas_call(functools.partial(opening_body, peers=peers, batch=batch,...  95.4 us
    pallas_call x1, Pallas kernels, tail_b(): pl.pallas_call(functools.partial(tail_b_body, peers=peers, cuts=cuts), na...  89.6 us
    pallas_call x2, Pallas kernels, settle(): pl.pallas_call(functools.partial(settle_body, n_in=len(args), first=first...  22.6 us
  transfers between devices with their start and end apart: 3, of which 1 were waited for; matrix products, arithmetic and copies ran while one was open for 0% of the time, Pallas kernels for 62%

profile of v13, /device:TPU:21, one launch (start us, length us, event | category | flops | bytes accessed | tf_op | source)
XLA Modules:
  0.0 577.8 jit_solution(3276405238310906533)
XLA Ops:
  7.2 0.1 all-gather.4.cloned.1.call-start
  7.2 95.4 %opening.1 = (s32[16,8,128]{2,1,0:T(8,128)}, bf16[16,96,256]{2,1,0:T(8,128)(2,1)}, bf16[16,256,1536]{2,1,0:T(8,128)(2,1)}, bf16[256,1536]{1,0:T(8,128)(2,1)}, bf16[16,96,256]{2,1,0:T(8,128)(2,1)}) custom-call(bf16[2,256,1536]{2,1,0:T(8,128)(2,1)} %x_hbm.3, bf16[2,256,1536]{2,1,0:T(8,128)(2,1)} %dy_hbm.3, bf16[1536,1536]{1,0:T(8,128)(2,1)} %wo_hbm.3, ...), custom_call_target="tpu_custom_call" | custom-call | flops 49999998976 | bytes 16777216 | tf_op jit(solution)/shard_map/opening/pallas_call | solution.py:436
  102.7 0.1 all-gather.4.cloned.1.call-update
  102.7 0.2 all-gather.6.cloned.1.call-start
  103.0 78.0 %attention.2 = (bf16[16,288,256]{2,1,0:T(8,128)(2,1)}, f32[208,1536]{1,0:T(8,128)}, f32[80,1536]{1,0:T(8,128)}, f32[288,128]{1,0:T(8,128)}, f32[8,128]{1,0:T(8,1...) custom-call(bf16[16,288,1536]{2,1,0:T(8,128)(2,1)} %bitcast.17, f32[3,16,96]{2,1,0:T(8,128)} %bitcast.21, ...), custom_call_target="tpu_custom_call" | custom-call | flops 28991029248 | bytes 25165824 | tf_op jit(solution)/shard_map/attention/pallas_call | solution.py:226
  180.9 5.0 all-gather.4.cloned.1.call-done.x_ref
  186.0 96.3 %attention.3 = (bf16[16,288,256]{2,1,0:T(8,128)(2,1)}, f32[208,1536]{1,0:T(8,128)}, f32[80,1536]{1,0:T(8,128)}, f32[288,128]{1,0:T(8,128)}, f32[8,128]{1,0:T(8,1...) custom-call(bf16[16,288,1536]{2,1,0:T(8,128)(2,1)} %bitcast.18, ...), custom_call_target="tpu_custom_call" | custom-call | flops 28991029248 | bytes 25165824 | tf_op jit(solution)/shard_map/attention/pallas_call | solution.py:226
  282.3 0.1 all-gather.6.cloned.1.call-update
  282.4 0.3 all-gather.8.cloned.1.call-start
  282.7 0.5 all-gather.8.cloned.1.call-update
  283.2 0.0 copy-start.2
  283.2 169.6 %tail_a.1 = (bf16[2,256,1536]{2,1,0:T(8,128)(2,1)}, bf16[2,256,1536]{2,1,0:T(8,128)(2,1)}, f32[96,1536]{1,0:T(8,128)}, f32[8,1536]{1,0:T(8,128)}) custom-call(bf16[16,288,256]{2,1,0:T(8,128)(2,1)} %get-tuple-element.60.dqkv_ref, bf16[16,96,256]{2,1,0:T(8,128)(2,1)} %get-tuple-element.61.oo_hbm, bf16[16,96,256]{2,1,0:T(8,128)(2,1)} %get-tuple-element.62.on_hbm, ...), custom_call_target="tpu_custom_call" | custom-call | flops 99999997952 | bytes 67108864 | tf_op jit(solution)/shard_map/tail_a/pallas_call | solution.py:592
  452.8 0.0 copy-done.2
  452.8 0.0 copy-start
  452.8 1.1 copy-done
  453.9 0.0 copy-start.1
  453.9 0.8 copy-done.1
  454.7 89.6 %tail_b.1 = (f32[8,2,96,1536]{3,2,1,0:T(8,128)S(1)}, f32[8,1536]{1,0:T(8,128)S(1)}, f32[16,8,128]{2,1,0:T(8,128)S(1)}) custom-call(f32[96,1536]{1,0:T(8,128)S(1)} %copy-done, f32[8,1536]{1,0:T(8,128)S(1)} %copy-done.1, f32[8,128]{1,0:T(8,128)S(1)} %copy-done.2), custom_call_target="tpu_custom_call" | custom-call | flops 49999998976 | bytes 10485760 | tf_op jit(solution)/shard_map/tail_b/pallas_call | solution.py:676
  544.3 4.3 lay_down.1
  548.6 0.0 all-gather.6.cloned.1.call-done
  548.6 16.4 %settle.2 = (f32[16,288,1536]{2,1,0:T(8,128)}, bf16[2,256,1536]{2,1,0:T(8,128)(2,1)}, bf16[2,256,1536]{2,1,0:T(8,128)(2,1)}) custom-call(f32[16,208,1536]{2,1,0:T(8,128)} %bitcast.15, bf16[2,256,1536]{2,1,0:T(8,128)(2,1)} %get-tuple-element.74.refs_1_, bf16[2,256,1536]{2,1,0:T(8,128)(2,1)} %get-tuple-element.75.refs_2_), custom_call_target="tpu_custom_call" | custom-call | flops 1000000000 | bytes 40894464 | tf_op jit(solution)/shard_map/settle/pallas_call | solution.py:716
  565.0 0.0 all-gather.8.cloned.1.call-done
  565.0 6.2 %settle.3 = f32[16,288,1536]{2,1,0:T(8,128)} custom-call(f32[16,80,1536]{2,1,0:T(8,128)} %bitcast.16, f32[16,288,1536]{2,1,0:T(8,128)} %get-tuple-element.82.refs_1_), custom_call_target="tpu_custom_call", output_to_operand_aliasing={{}: (1, {})} | custom-call | flops 1000000000 | bytes 15728640 | tf_op jit(solution)/shard_map/settle/pallas_call | solution.py:716
Async XLA Ops:
  7.2 178.8 %all-gather.4.cloned.1.call-start = ((), (), s32[]{:S(2)}) async-start(), calls=%async_computation | async-start | bytes 13369344 | tf_op jit(solution)/shard_map/all_gather | solution.py:764
  102.7 445.9 %all-gather.6.cloned.1.call-start = ((), (), s32[]{:S(2)}) async-start(), calls=%async_computation.1 | async-start | bytes 21725184 | tf_op jit(solution)/shard_map/all_gather | solution.py:776
  282.4 282.7 %all-gather.8.cloned.1.call-start = ((), (), s32[]{:S(2)}) async-start(), calls=%async_computation.2 | async-start | bytes 8355840 | tf_op jit(solution)/shard_map/all_gather | solution.py:776
  283.2 169.7 %copy-start.2 = (f32[8,128]{1,0:T(8,128)S(1)}, f32[8,128]{1,0:T(8,128)}, u32[]{:S(2)}) copy-start(f32[8,128]{1,0:T(8,128)} %get-tuple-element.68.gb_ref) | copy-start | bytes 12292
  452.8 1.1 copy-start
  453.9 0.8 copy-start.1
Sparse Core Ops, SparseCore 0:
  102.8 83.0 all-gather.3
  282.5 215.9 all-gather.5
  500.1 64.5 all-gather.7

commit v14 on v13

--- a/solution.py
+++ b/solution.py
@@ -427,7 +427,7 @@
     finish()
 
 
-def opening(x, dy, w_out, gain, bias, pos, keep, peers, collective_id, cuts=4):
+def opening(x, dy, w_out, gain, bias, pos, keep, peers, collective_id, cuts=8):
     batch, tok, hidden = x.shape
     dim = hidden // peers
     hbm, vmem = pl.BlockSpec(memory_space=pltpu.HBM), pl.BlockSpec(memory_space=pltpu.VMEM)
@@ -581,7 +581,7 @@
             reduce_copy(s, w, t, u).wait_send()
 
 
-def tail_a(dqkv, d_old, o_old, o_new, dy, x, w_flat, w_out, gain, b_out, collective_id, cuts=2):
+def tail_a(dqkv, d_old, o_old, o_new, dy, x, w_flat, w_out, gain, b_out, collective_id, cuts=4):
     peers, dim, tok = o_old.shape
     ring = peers // 2
     hidden = dy.shape[-1]
@@ -669,7 +669,7 @@
     finish()
 
 
-def tail_b(part, rows, gb, peers, collective_id, cuts=2):
+def tail_b(part, rows, gb, peers, collective_id, cuts=4):
     ring = peers // 2
     vmem = pl.BlockSpec(memory_space=pltpu.VMEM)
     dma = pltpu.SemaphoreType.DMA
@@ -763,7 +763,7 @@
         marks, do_first, x_first, x_rest, do_rest = opening(x_blk, dy_blk, w_out, ln_gain, ln_bias, pos_blk, keep_blk, peers, 1)
         xs = [x_first.reshape(seq, hidden)] + [lax.all_gather(one, "sp", axis=0, tiled=True) for one in x_rest]
         do_t = [do_first]
-        lead = 13 * dim // 6
+        lead = 7 * dim // 3
         gw, att = (), []
         for b in range(batch):
             old = list(do_rest[b:b + 1]) if b + 1 < batch else att

time: 579 us -> 583 us (level)
  no operation moved by 1% of the time
where the time goes in v14:
time: 583 us
  Pallas kernels  561 us (96%)
  between operations  13.9 us (2%)
    pallas_call x2, Pallas kernels, attention(): pl.pallas_call(functools.partial(attn_body, blk=blk, tok=tok, which=which...  174 us
    pallas_call x1, Pallas kernels, tail_a(): pl.pallas_call(functools.partial(tail_a_body, peers=peers, cuts=cuts), na...  171 us
    pallas_call x1, Pallas kernels, opening(): pl.pallas_call(functools.partial(opening_body, peers=peers, batch=batch,...  97.8 us
    pallas_call x1, Pallas kernels, tail_b(): pl.pallas_call(functools.partial(tail_b_body, peers=peers, cuts=cuts), na...  90.5 us
    pallas_call x2, Pallas kernels, settle(): pl.pallas_call(functools.partial(settle_body, n_in=len(args), first=first...  23.1 us
  transfers between devices with their start and end apart: 3, of which 1 were waited for; matrix products, arithmetic and copies ran while one was open for 0% of the time, Pallas kernels for 62%

profile of v14, /device:TPU:21, one launch (start us, length us, event | category | flops | bytes accessed | tf_op | source)
XLA Modules:
  0.0 583.0 jit_solution(16007805422434347878)
XLA Ops:
  7.2 0.1 all-gather.4.cloned.1.call-start
  7.2 97.8 %opening.1 = (s32[16,8,128]{2,1,0:T(8,128)}, bf16[16,96,256]{2,1,0:T(8,128)(2,1)}, bf16[16,256,1536]{2,1,0:T(8,128)(2,1)}, bf16[256,1536]{1,0:T(8,128)(2,1)}, bf16[16,96,256]{2,1,0:T(8,128)(2,1)}) custom-call(bf16[2,256,1536]{2,1,0:T(8,128)(2,1)} %x_hbm.3, bf16[2,256,1536]{2,1,0:T(8,128)(2,1)} %dy_hbm.3, bf16[1536,1536]{1,0:T(8,128)(2,1)} %wo_hbm.3, ...), custom_call_target="tpu_custom_call" | custom-call | flops 49999998976 | bytes 16777216 | tf_op jit(solution)/shard_map/opening/pallas_call | solution.py:436
  105.0 0.1 all-gather.4.cloned.1.call-update
  105.1 0.2 all-gather.6.cloned.1.call-start
  105.4 78.0 %attention.2 = (bf16[16,288,256]{2,1,0:T(8,128)(2,1)}, f32[224,1536]{1,0:T(8,128)}, f32[64,1536]{1,0:T(8,128)}, f32[288,128]{1,0:T(8,128)}, f32[8,128]{1,0:T(8,1...) custom-call(bf16[16,288,1536]{2,1,0:T(8,128)(2,1)} %bitcast.17, f32[3,16,96]{2,1,0:T(8,128)} %bitcast.21, ...), custom_call_target="tpu_custom_call" | custom-call | flops 28991029248 | bytes 25165824 | tf_op jit(solution)/shard_map/attention/pallas_call | solution.py:226
  183.4 4.8 all-gather.4.cloned.1.call-done.x_ref
  188.2 96.2 %attention.3 = (bf16[16,288,256]{2,1,0:T(8,128)(2,1)}, f32[224,1536]{1,0:T(8,128)}, f32[64,1536]{1,0:T(8,128)}, f32[288,128]{1,0:T(8,128)}, f32[8,128]{1,0:T(8,1...) custom-call(bf16[16,288,1536]{2,1,0:T(8,128)(2,1)} %bitcast.18, ...), custom_call_target="tpu_custom_call" | custom-call | flops 28991029248 | bytes 25165824 | tf_op jit(solution)/shard_map/attention/pallas_call | solution.py:226
  284.4 0.1 all-gather.6.cloned.1.call-update
  284.4 0.3 all-gather.8.cloned.1.call-start
  284.7 0.5 all-gather.8.cloned.1.call-update
  285.2 0.0 copy-start.2
  285.2 171.2 %tail_a.1 = (bf16[2,256,1536]{2,1,0:T(8,128)(2,1)}, bf16[2,256,1536]{2,1,0:T(8,128)(2,1)}, f32[96,1536]{1,0:T(8,128)}, f32[8,1536]{1,0:T(8,128)}) custom-call(bf16[16,288,256]{2,1,0:T(8,128)(2,1)} %get-tuple-element.60.dqkv_ref, bf16[16,96,256]{2,1,0:T(8,128)(2,1)} %get-tuple-element.61.oo_hbm, bf16[16,96,256]{2,1,0:T(8,128)(2,1)} %get-tuple-element.62.on_hbm, ...), custom_call_target="tpu_custom_call" | custom-call | flops 99999997952 | bytes 67108864 | tf_op jit(solution)/shard_map/tail_a/pallas_call | solution.py:592
  456.4 0.0 copy-done.2
  456.5 0.0 copy-start
  456.5 1.1 copy-done
  457.5 0.0 copy-start.1
  457.5 0.8 copy-done.1
  458.3 90.5 %tail_b.1 = (f32[8,2,96,1536]{3,2,1,0:T(8,128)S(1)}, f32[8,1536]{1,0:T(8,128)S(1)}, f32[16,8,128]{2,1,0:T(8,128)S(1)}) custom-call(f32[96,1536]{1,0:T(8,128)S(1)} %copy-done, f32[8,1536]{1,0:T(8,128)S(1)} %copy-done.1, f32[8,128]{1,0:T(8,128)S(1)} %copy-done.2), custom_call_target="tpu_custom_call" | custom-call | flops 49999998976 | bytes 10485760 | tf_op jit(solution)/shard_map/tail_b/pallas_call | solution.py:676
  548.9 4.3 lay_down.1
  553.2 0.0 all-gather.6.cloned.1.call-done
  553.2 17.6 %settle.2 = (f32[16,288,1536]{2,1,0:T(8,128)}, bf16[2,256,1536]{2,1,0:T(8,128)(2,1)}, bf16[2,256,1536]{2,1,0:T(8,128)(2,1)}) custom-call(f32[16,224,1536]{2,1,0:T(8,128)} %bitcast.15, bf16[2,256,1536]{2,1,0:T(8,128)(2,1)} %get-tuple-element.74.refs_1_, bf16[2,256,1536]{2,1,0:T(8,128)(2,1)} %get-tuple-element.75.refs_2_), custom_call_target="tpu_custom_call" | custom-call | flops 1000000000 | bytes 44040192 | tf_op jit(solution)/shard_map/settle/pallas_call | solution.py:716
  570.9 0.0 all-gather.8.cloned.1.call-done
  570.9 5.5 settle.3
Async XLA Ops:
  7.2 181.0 %all-gather.4.cloned.1.call-start = ((), (), s32[]{:S(2)}) async-start(), calls=%async_computation | async-start | bytes 13369344 | tf_op jit(solution)/shard_map/all_gather | solution.py:764
  105.1 448.1 %all-gather.6.cloned.1.call-start = ((), (), s32[]{:S(2)}) async-start(), calls=%async_computation.1 | async-start | bytes 23396352 | tf_op jit(solution)/shard_map/all_gather | solution.py:776
  284.4 286.4 %all-gather.8.cloned.1.call-start = ((), (), s32[]{:S(2)}) async-start(), calls=%async_computation.2 | async-start | bytes 6684672 | tf_op jit(solution)/shard_map/all_gather | solution.py:776
  285.2 171.2 %copy-start.2 = (f32[8,128]{1,0:T(8,128)S(1)}, f32[8,128]{1,0:T(8,128)}, u32[]{:S(2)}) copy-start(f32[8,128]{1,0:T(8,128)} %get-tuple-element.68.gb_ref) | copy-start | bytes 12292
  456.5 1.1 copy-start
  457.5 0.8 copy-start.1
Sparse Core Ops, SparseCore 0:
  105.2 82.9 all-gather.3
  284.6 231.4 all-gather.5
  517.7 50.4 all-gather.7

commit v15 on v13

--- a/solution.py
+++ b/solution.py
@@ -23,8 +23,8 @@
     w_ref, b_rep, qkvt_ref, k_tok, v_tok, posk_ref, s_buf, m_buf, q_pad, do_pad, o_acc, dq_acc, dk_acc, dv_acc, x_sem, w_sem = refs[:16]
     swaps = [(old[k], got[k]) + refs[16 + 4 * k:20 + 4 * k] for k in range(n_swap)]
     if send_o:
-        o_ref, os_sem, or_sem = refs[-3:]
-        o_new = o_out
+        o_ref, os_sem, or_sem, out_sem, o_new, *landed = refs[16 + 4 * n_swap:]
+        swaps = [(one[0], land) + one[2:] for one, land in zip(swaps, landed)]
     else:
         o_ref = o_out
     dim, lead = dot_ref.shape[1], gwa_ref.shape[0]
@@ -210,6 +210,12 @@
                     device_id={"sp": frm}, device_id_type=pl.DeviceIdType.MESH).wait_recv()
         for one in swaps:
             swap_wait(*one, peers)
+        if send_o:
+            outs = [pltpu.make_async_copy(src, dst, out_sem.at[k]) for k, (src, dst) in enumerate(zip((o_new, *landed), (o_out, *got)))]
+            for copy in outs:
+                copy.start()
+            for copy in outs:
+                copy.wait()
 
 
 def attention(w_all, b_all, dot_, marks, x, gw, old, *, blk, tok, which, batch, lead, send_o, collective_id):
@@ -238,7 +244,8 @@
             pltpu.VMEM((wide, blk), BF16), pltpu.VMEM((wide, blk), BF16),
             pltpu.VMEM((dim, blk), F32), pltpu.VMEM((dim, blk), F32),
             pltpu.VMEM((dim, seq), F32), pltpu.VMEM((dim, seq), F32), dma((seq // blk,)), dma]
-        + sum((swap_scratch(a) for a in old), []) + ([pltpu.VMEM(dot_.shape, BF16), dma((blocks,)), dma((blocks,))] if send_o else []),
+        + sum((swap_scratch(a) for a in old), []) + ([pltpu.VMEM(dot_.shape, BF16), dma((blocks,)), dma((blocks,)), dma((1 + len(old),)), pltpu.VMEM(dot_.shape, BF16)]
+           + [pltpu.VMEM(a.shape, a.dtype) for a in old] if send_o else []),
         cost_estimate=pl.CostEstimate(flops=pairs * 6 * 2 * blk * blk * 256, bytes_accessed=24 << 20, transcendentals=pairs * blk * blk),
         compiler_params=pltpu.CompilerParams(dimension_semantics=("arbitrary",), vmem_limit_bytes=VMEM_LIMIT,
                                              collective_id=collective_id, has_side_effects=True),
@@ -397,7 +404,10 @@
     loads[0].wait()
     pieces = [(w, u) for u in range(cuts) for w in range(2)]
     for k, piece in enumerate(pieces):
-        norm_rows(0, x_own, rows_of(*piece))
+        @pl.loop(0, lot // 32)
+        def _(n):
+            norm_rows(0, x_own, pl.ds(pl.multiple_of((piece[0] * cuts + piece[1]) * lot + n * 32, 32), 32))
+
         if k == 1:
             arrived()
         if k:
@@ -427,7 +437,7 @@
     finish()
 
 
-def opening(x, dy, w_out, gain, bias, pos, keep, peers, collective_id, cuts=4):
+def opening(x, dy, w_out, gain, bias, pos, keep, peers, collective_id, cuts=2):
     batch, tok, hidden = x.shape
     dim = hidden // peers
     hbm, vmem = pl.BlockSpec(memory_space=pltpu.HBM), pl.BlockSpec(memory_space=pltpu.VMEM)

time: 579 us -> 581 us (level)
  transfers between devices with their start and end apart: 3 -> 3, of which waited for: 1 -> 2; matrix products, arithmetic and copies ran while one was open for 0% -> 0% of each run, Pallas kernels for 62% -> 61%
where the time goes in v15:
time: 581 us; the launch traced here: 579 us
  Pallas kernels  555 us (96%)
  between operations  13.9 us (2%)
  waiting for transfers between devices  7.65 us (1%)
    pallas_call x2, Pallas kernels, attention(): pl.pallas_call(functools.partial(attn_body, blk=blk, tok=tok, which=which...  178 us
    pallas_call x1, Pallas kernels, tail_a(): pl.pallas_call(functools.partial(tail_a_body, peers=peers, cuts=cuts), na...  167 us
    pallas_call x1, Pallas kernels, opening(): pl.pallas_call(functools.partial(opening_body, peers=peers, batch=batch,...  94 us
    pallas_call x1, Pallas kernels, tail_b(): pl.pallas_call(functools.partial(tail_b_body, peers=peers, cuts=cuts), na...  88.6 us
    pallas_call x2, Pallas kernels, settle(): pl.pallas_call(functools.partial(settle_body, n_in=len(args), first=first...  22.6 us
  transfers between devices with their start and end apart: 3, of which 2 were waited for; matrix products, arithmetic and copies ran while one was open for 0% of the time, Pallas kernels for 61%

profile of v15, /device:TPU:21, one launch (start us, length us, event | category | flops | bytes accessed | tf_op | source)
XLA Modules:
  0.0 579.3 jit_solution(2866943541107498771)
XLA Ops:
  7.2 0.1 all-gather.4.cloned.1.call-start
  7.2 94.0 %opening.1 = (s32[16,8,128]{2,1,0:T(8,128)}, bf16[16,96,256]{2,1,0:T(8,128)(2,1)}, bf16[16,256,1536]{2,1,0:T(8,128)(2,1)}, bf16[256,1536]{1,0:T(8,128)(2,1)}, bf16[16,96,256]{2,1,0:T(8,128)(2,1)}) custom-call(bf16[2,256,1536]{2,1,0:T(8,128)(2,1)} %x_hbm.3, bf16[2,256,1536]{2,1,0:T(8,128)(2,1)} %dy_hbm.3, bf16[1536,1536]{1,0:T(8,128)(2,1)} %wo_hbm.3, ...), custom_call_target="tpu_custom_call" | custom-call | flops 49999998976 | bytes 16777216 | tf_op jit(solution)/shard_map/opening/pallas_call | solution.py:446
  101.2 0.1 all-gather.4.cloned.1.call-update
  101.3 0.2 all-gather.6.cloned.1.call-start
  101.5 78.2 %attention.2 = (bf16[16,288,256]{2,1,0:T(8,128)(2,1)}, f32[208,1536]{1,0:T(8,128)}, f32[80,1536]{1,0:T(8,128)}, f32[288,128]{1,0:T(8,128)}, f32[8,128]{1,0:T(8,1...) custom-call(bf16[16,288,1536]{2,1,0:T(8,128)(2,1)} %bitcast.17, f32[3,16,96]{2,1,0:T(8,128)} %bitcast.21, ...), custom_call_target="tpu_custom_call" | custom-call | flops 28991029248 | bytes 25165824 | tf_op jit(solution)/shard_map/attention/pallas_call | solution.py:232
  179.7 5.6 all-gather.4.cloned.1.call-done.x_ref
  185.3 100.3 %attention.3 = (bf16[16,288,256]{2,1,0:T(8,128)(2,1)}, f32[208,1536]{1,0:T(8,128)}, f32[80,1536]{1,0:T(8,128)}, f32[288,128]{1,0:T(8,128)}, f32[8,128]{1,0:T(8,1...) custom-call(bf16[16,288,1536]{2,1,0:T(8,128)(2,1)} %bitcast.18, ...), custom_call_target="tpu_custom_call" | custom-call | flops 28991029248 | bytes 25165824 | tf_op jit(solution)/shard_map/attention/pallas_call | solution.py:232
  285.6 0.1 all-gather.6.cloned.1.call-update
  285.6 0.3 all-gather.8.cloned.1.call-start
  285.9 0.5 all-gather.8.cloned.1.call-update
  286.4 0.0 copy-start.2
  286.4 167.3 %tail_a.1 = (bf16[2,256,1536]{2,1,0:T(8,128)(2,1)}, bf16[2,256,1536]{2,1,0:T(8,128)(2,1)}, f32[96,1536]{1,0:T(8,128)}, f32[8,1536]{1,0:T(8,128)}) custom-call(bf16[16,288,256]{2,1,0:T(8,128)(2,1)} %get-tuple-element.60.dqkv_ref, bf16[16,96,256]{2,1,0:T(8,128)(2,1)} %get-tuple-element.61.oo_hbm, bf16[16,96,256]{2,1,0:T(8,128)(2,1)} %get-tuple-element.62.on_hbm, ...), custom_call_target="tpu_custom_call" | custom-call | flops 99999997952 | bytes 67108864 | tf_op jit(solution)/shard_map/tail_a/pallas_call | solution.py:602
  453.8 0.0 copy-done.2
  453.8 0.0 copy-start
  453.8 1.1 copy-done
  454.8 0.0 copy-start.1
  454.8 0.8 copy-done.1
  455.6 88.6 %tail_b.1 = (f32[8,2,96,1536]{3,2,1,0:T(8,128)S(1)}, f32[8,1536]{1,0:T(8,128)S(1)}, f32[16,8,128]{2,1,0:T(8,128)S(1)}) custom-call(f32[96,1536]{1,0:T(8,128)S(1)} %copy-done, f32[8,1536]{1,0:T(8,128)S(1)} %copy-done.1, f32[8,128]{1,0:T(8,128)S(1)} %copy-done.2), custom_call_target="tpu_custom_call" | custom-call | flops 49999998976 | bytes 10485760 | tf_op jit(solution)/shard_map/tail_b/pallas_call | solution.py:686
  544.3 4.3 lay_down.1
  548.6 0.0 all-gather.6.cloned.1.call-done
  548.6 16.4 %settle.2 = (f32[16,288,1536]{2,1,0:T(8,128)}, bf16[2,256,1536]{2,1,0:T(8,128)(2,1)}, bf16[2,256,1536]{2,1,0:T(8,128)(2,1)}) custom-call(f32[16,208,1536]{2,1,0:T(8,128)} %bitcast.15, bf16[2,256,1536]{2,1,0:T(8,128)(2,1)} %get-tuple-element.74.refs_1_, bf16[2,256,1536]{2,1,0:T(8,128)(2,1)} %get-tuple-element.75.refs_2_), custom_call_target="tpu_custom_call" | custom-call | flops 1000000000 | bytes 40894464 | tf_op jit(solution)/shard_map/settle/pallas_call | solution.py:726
  565.0 1.5 all-gather.8.cloned.1.call-done
  566.5 6.2 %settle.3 = f32[16,288,1536]{2,1,0:T(8,128)} custom-call(f32[16,80,1536]{2,1,0:T(8,128)} %bitcast.16, f32[16,288,1536]{2,1,0:T(8,128)} %get-tuple-element.82.refs_1_), custom_call_target="tpu_custom_call", output_to_operand_aliasing={{}: (1, {})} | custom-call | flops 1000000000 | bytes 15728640 | tf_op jit(solution)/shard_map/settle/pallas_call | solution.py:726
Async XLA Ops:
  7.2 178.1 %all-gather.4.cloned.1.call-start = ((), (), s32[]{:S(2)}) async-start(), calls=%async_computation | async-start | bytes 13369344 | tf_op jit(solution)/shard_map/all_gather | solution.py:774
  101.3 447.3 %all-gather.6.cloned.1.call-start = ((), (), s32[]{:S(2)}) async-start(), calls=%async_computation.1 | async-start | bytes 21725184 | tf_op jit(solution)/shard_map/all_gather | solution.py:786
  285.6 280.8 %all-gather.8.cloned.1.call-start = ((), (), s32[]{:S(2)}) async-start(), calls=%async_computation.2 | async-start | bytes 8355840 | tf_op jit(solution)/shard_map/all_gather | solution.py:786
  286.4 167.3 %copy-start.2 = (f32[8,128]{1,0:T(8,128)S(1)}, f32[8,128]{1,0:T(8,128)}, u32[]{:S(2)}) copy-start(f32[8,128]{1,0:T(8,128)} %get-tuple-element.68.gb_ref) | copy-start | bytes 12292
  453.8 1.1 copy-start
  454.8 0.8 copy-start.1
Sparse Core Ops, SparseCore 0:
  101.4 83.8 all-gather.3
  285.7 214.4 all-gather.5
  501.8 64.5 all-gather.7

commit v16 on v13

--- a/solution.py
+++ b/solution.py
@@ -397,7 +397,10 @@
     loads[0].wait()
     pieces = [(w, u) for u in range(cuts) for w in range(2)]
     for k, piece in enumerate(pieces):
-        norm_rows(0, x_own, rows_of(*piece))
+        @pl.loop(0, lot // 32)
+        def _(n):
+            norm_rows(0, x_own, pl.ds(pl.multiple_of((piece[0] * cuts + piece[1]) * lot + n * 32, 32), 32))
+
         if k == 1:
             arrived()
         if k:
@@ -427,7 +430,7 @@
     finish()
 
 
-def opening(x, dy, w_out, gain, bias, pos, keep, peers, collective_id, cuts=4):
+def opening(x, dy, w_out, gain, bias, pos, keep, peers, collective_id, cuts=2):
     batch, tok, hidden = x.shape
     dim = hidden // peers
     hbm, vmem = pl.BlockSpec(memory_space=pltpu.HBM), pl.BlockSpec(memory_space=pltpu.VMEM)
@@ -581,7 +584,7 @@
             reduce_copy(s, w, t, u).wait_send()
 
 
-def tail_a(dqkv, d_old, o_old, o_new, dy, x, w_flat, w_out, gain, b_out, collective_id, cuts=2):
+def tail_a(dqkv, d_old, o_old, o_new, dy, x, w_flat, w_out, gain, b_out, collective_id, cuts=1):
     peers, dim, tok = o_old.shape
     ring = peers // 2
     hidden = dy.shape[-1]
@@ -669,7 +672,7 @@
     finish()
 
 
-def tail_b(part, rows, gb, peers, collective_id, cuts=2):
+def tail_b(part, rows, gb, peers, collective_id, cuts=1):
     ring = peers // 2
     vmem = pl.BlockSpec(memory_space=pltpu.VMEM)
     dma = pltpu.SemaphoreType.DMA

time: 579 us -> 584 us (level)
    pallas_call x1, Pallas kernels: 89.6 us -> 95.6 us  [tail_b(): pl.pallas_call(functools.partial(tail_b_body, peers=peers, cuts=cuts), na...]
where the time goes in v16:
time: 584 us; the launch traced here: 583 us
  Pallas kernels  560 us (96%)
  between operations  13.9 us (2%)
  waiting for transfers between devices  6.21 us (1%)
    pallas_call x2, Pallas kernels, attention(): pl.pallas_call(functools.partial(attn_body, blk=blk, tok=tok, which=which...  177 us
    pallas_call x1, Pallas kernels, tail_a(): pl.pallas_call(functools.partial(tail_a_body, peers=peers, cuts=cuts), na...  167 us
    pallas_call x1, Pallas kernels, tail_b(): pl.pallas_call(functools.partial(tail_b_body, peers=peers, cuts=cuts), na...  95.6 us
    pallas_call x1, Pallas kernels, opening(): pl.pallas_call(functools.partial(opening_body, peers=peers, batch=batch,...  94 us
    pallas_call x2, Pallas kernels, settle(): pl.pallas_call(functools.partial(settle_body, n_in=len(args), first=first...  22.6 us
  transfers between devices with their start and end apart: 3, of which 1 were waited for; matrix products, arithmetic and copies ran while one was open for 0% of the time, Pallas kernels for 62%

profile of v16, /device:TPU:21, one launch (start us, length us, event | category | flops | bytes accessed | tf_op | source)
XLA Modules:
  0.0 582.6 jit_solution(16444805466703951506)
XLA Ops:
  7.2 0.1 all-gather.4.cloned.1.call-start
  7.2 94.0 %opening.1 = (s32[16,8,128]{2,1,0:T(8,128)}, bf16[16,96,256]{2,1,0:T(8,128)(2,1)}, bf16[16,256,1536]{2,1,0:T(8,128)(2,1)}, bf16[256,1536]{1,0:T(8,128)(2,1)}, bf16[16,96,256]{2,1,0:T(8,128)(2,1)}) custom-call(bf16[2,256,1536]{2,1,0:T(8,128)(2,1)} %x_hbm.3, bf16[2,256,1536]{2,1,0:T(8,128)(2,1)} %dy_hbm.3, bf16[1536,1536]{1,0:T(8,128)(2,1)} %wo_hbm.3, ...), custom_call_target="tpu_custom_call" | custom-call | flops 49999998976 | bytes 16777216 | tf_op jit(solution)/shard_map/opening/pallas_call | solution.py:439
  101.2 0.1 all-gather.4.cloned.1.call-update
  101.3 0.2 all-gather.6.cloned.1.call-start
  101.5 78.2 %attention.2 = (bf16[16,288,256]{2,1,0:T(8,128)(2,1)}, f32[208,1536]{1,0:T(8,128)}, f32[80,1536]{1,0:T(8,128)}, f32[288,128]{1,0:T(8,128)}, f32[8,128]{1,0:T(8,1...) custom-call(bf16[16,288,1536]{2,1,0:T(8,128)(2,1)} %bitcast.17, f32[3,16,96]{2,1,0:T(8,128)} %bitcast.21, ...), custom_call_target="tpu_custom_call" | custom-call | flops 28991029248 | bytes 25165824 | tf_op jit(solution)/shard_map/attention/pallas_call | solution.py:226
  179.7 5.6 all-gather.4.cloned.1.call-done.x_ref
  185.3 98.4 %attention.3 = (bf16[16,288,256]{2,1,0:T(8,128)(2,1)}, f32[208,1536]{1,0:T(8,128)}, f32[80,1536]{1,0:T(8,128)}, f32[288,128]{1,0:T(8,128)}, f32[8,128]{1,0:T(8,1...) custom-call(bf16[16,288,1536]{2,1,0:T(8,128)(2,1)} %bitcast.18, ...), custom_call_target="tpu_custom_call" | custom-call | flops 28991029248 | bytes 25165824 | tf_op jit(solution)/shard_map/attention/pallas_call | solution.py:226
  283.7 0.1 all-gather.6.cloned.1.call-update
  283.7 0.3 all-gather.8.cloned.1.call-start
  284.0 0.5 all-gather.8.cloned.1.call-update
  284.5 0.0 copy-start.2
  284.5 167.0 %tail_a.1 = (bf16[2,256,1536]{2,1,0:T(8,128)(2,1)}, bf16[2,256,1536]{2,1,0:T(8,128)(2,1)}, f32[96,1536]{1,0:T(8,128)}, f32[8,1536]{1,0:T(8,128)}) custom-call(bf16[16,288,256]{2,1,0:T(8,128)(2,1)} %get-tuple-element.60.dqkv_ref, bf16[16,96,256]{2,1,0:T(8,128)(2,1)} %get-tuple-element.61.oo_hbm, bf16[16,96,256]{2,1,0:T(8,128)(2,1)} %get-tuple-element.62.on_hbm, ...), custom_call_target="tpu_custom_call" | custom-call | flops 99999997952 | bytes 67108864 | tf_op jit(solution)/shard_map/tail_a/pallas_call | solution.py:595
  451.6 0.0 copy-done.2
  451.6 0.0 copy-start
  451.6 1.1 copy-done
  452.7 0.0 copy-start.1
  452.7 0.8 copy-done.1
  453.5 95.6 %tail_b.1 = (f32[8,2,96,1536]{3,2,1,0:T(8,128)S(1)}, f32[8,1536]{1,0:T(8,128)S(1)}, f32[16,8,128]{2,1,0:T(8,128)S(1)}) custom-call(f32[96,1536]{1,0:T(8,128)S(1)} %copy-done, f32[8,1536]{1,0:T(8,128)S(1)} %copy-done.1, f32[8,128]{1,0:T(8,128)S(1)} %copy-done.2), custom_call_target="tpu_custom_call" | custom-call | flops 49999998976 | bytes 10485760 | tf_op jit(solution)/shard_map/tail_b/pallas_call | solution.py:679
  549.0 4.3 lay_down.1
  553.4 0.0 all-gather.6.cloned.1.call-done
  553.4 16.4 %settle.2 = (f32[16,288,1536]{2,1,0:T(8,128)}, bf16[2,256,1536]{2,1,0:T(8,128)(2,1)}, bf16[2,256,1536]{2,1,0:T(8,128)(2,1)}) custom-call(f32[16,208,1536]{2,1,0:T(8,128)} %bitcast.15, bf16[2,256,1536]{2,1,0:T(8,128)(2,1)} %get-tuple-element.74.refs_1_, bf16[2,256,1536]{2,1,0:T(8,128)(2,1)} %get-tuple-element.75.refs_2_), custom_call_target="tpu_custom_call" | custom-call | flops 1000000000 | bytes 40894464 | tf_op jit(solution)/shard_map/settle/pallas_call | solution.py:719
  569.8 0.0 all-gather.8.cloned.1.call-done
  569.8 6.2 %settle.3 = f32[16,288,1536]{2,1,0:T(8,128)} custom-call(f32[16,80,1536]{2,1,0:T(8,128)} %bitcast.16, f32[16,288,1536]{2,1,0:T(8,128)} %get-tuple-element.82.refs_1_), custom_call_target="tpu_custom_call", output_to_operand_aliasing={{}: (1, {})} | custom-call | flops 1000000000 | bytes 15728640 | tf_op jit(solution)/shard_map/settle/pallas_call | solution.py:719
Async XLA Ops:
  7.2 178.1 %all-gather.4.cloned.1.call-start = ((), (), s32[]{:S(2)}) async-start(), calls=%async_computation | async-start | bytes 13369344 | tf_op jit(solution)/shard_map/all_gather | solution.py:767
  101.3 452.1 %all-gather.6.cloned.1.call-start = ((), (), s32[]{:S(2)}) async-start(), calls=%async_computation.1 | async-start | bytes 21725184 | tf_op jit(solution)/shard_map/all_gather | solution.py:779
  283.7 286.1 %all-gather.8.cloned.1.call-start = ((), (), s32[]{:S(2)}) async-start(), calls=%async_computation.2 | async-start | bytes 8355840 | tf_op jit(solution)/shard_map/all_gather | solution.py:779
  284.5 167.1 %copy-start.2 = (f32[8,128]{1,0:T(8,128)S(1)}, f32[8,128]{1,0:T(8,128)}, u32[]{:S(2)}) copy-start(f32[8,128]{1,0:T(8,128)} %get-tuple-element.68.gb_ref) | copy-start | bytes 12292
  451.6 1.1 copy-start
  452.7 0.8 copy-start.1
Sparse Core Ops, SparseCore 0:
  101.4 83.8 all-gather.3
  283.9 210.6 all-gather.5
  496.2 68.3 all-gather.7

commit v17 on v16

--- a/solution.py
+++ b/solution.py
@@ -584,7 +584,7 @@
             reduce_copy(s, w, t, u).wait_send()
 
 
-def tail_a(dqkv, d_old, o_old, o_new, dy, x, w_flat, w_out, gain, b_out, collective_id, cuts=1):
+def tail_a(dqkv, d_old, o_old, o_new, dy, x, w_flat, w_out, gain, b_out, collective_id, cuts=2):
     peers, dim, tok = o_old.shape
     ring = peers // 2
     hidden = dy.shape[-1]
@@ -672,7 +672,7 @@
     finish()
 
 
-def tail_b(part, rows, gb, peers, collective_id, cuts=1):
+def tail_b(part, rows, gb, peers, collective_id, cuts=2):
     ring = peers // 2
     vmem = pl.BlockSpec(memory_space=pltpu.VMEM)
     dma = pltpu.SemaphoreType.DMA

time: 584 us -> 579 us (level)
  Pallas kernels: 560 us -> 553 us
    pallas_call x1, Pallas kernels: 95.6 us -> 88.6 us  [tail_b(): pl.pallas_call(functools.partial(tail_b_body, peers=peers, cuts=cuts), na...]
  transfers between devices with their start and end apart: 3 -> 3, of which waited for: 1 -> 2; matrix products, arithmetic and copies ran while one was open for 0% -> 0% of each run, Pallas kernels for 62% -> 61%
where the time goes in v17:
time: 579 us; the launch traced here: 577 us
  Pallas kernels  553 us (96%)
  between operations  13.9 us (2%)
  waiting for transfers between devices  7.65 us (1%)
    pallas_call x2, Pallas kernels, attention(): pl.pallas_call(functools.partial(attn_body, blk=blk, tok=tok, which=which...  177 us
    pallas_call x1, Pallas kernels, tail_a(): pl.pallas_call(functools.partial(tail_a_body, peers=peers, cuts=cuts), na...  167 us
    pallas_call x1, Pallas kernels, opening(): pl.pallas_call(functools.partial(opening_body, peers=peers, batch=batch,...  94 us
    pallas_call x1, Pallas kernels, tail_b(): pl.pallas_call(functools.partial(tail_b_body, peers=peers, cuts=cuts), na...  88.6 us
    pallas_call x2, Pallas kernels, settle(): pl.pallas_call(functools.partial(settle_body, n_in=len(args), first=first...  22.6 us
  transfers between devices with their start and end apart: 3, of which 2 were waited for; matrix products, arithmetic and copies ran while one was open for 0% of the time, Pallas kernels for 61%

profile of v17, /device:TPU:21, one launch (start us, length us, event | category | flops | bytes accessed | tf_op | source)
XLA Modules:
  0.0 577.4 jit_solution(16028075495734282926)
XLA Ops:
  7.2 0.1 all-gather.4.cloned.1.call-start
  7.2 94.0 %opening.1 = (s32[16,8,128]{2,1,0:T(8,128)}, bf16[16,96,256]{2,1,0:T(8,128)(2,1)}, bf16[16,256,1536]{2,1,0:T(8,128)(2,1)}, bf16[256,1536]{1,0:T(8,128)(2,1)}, bf16[16,96,256]{2,1,0:T(8,128)(2,1)}) custom-call(bf16[2,256,1536]{2,1,0:T(8,128)(2,1)} %x_hbm.3, bf16[2,256,1536]{2,1,0:T(8,128)(2,1)} %dy_hbm.3, bf16[1536,1536]{1,0:T(8,128)(2,1)} %wo_hbm.3, ...), custom_call_target="tpu_custom_call" | custom-call | flops 49999998976 | bytes 16777216 | tf_op jit(solution)/shard_map/opening/pallas_call | solution.py:439
  101.2 0.1 all-gather.4.cloned.1.call-update
  101.3 0.2 all-gather.6.cloned.1.call-start
  101.5 78.2 %attention.2 = (bf16[16,288,256]{2,1,0:T(8,128)(2,1)}, f32[208,1536]{1,0:T(8,128)}, f32[80,1536]{1,0:T(8,128)}, f32[288,128]{1,0:T(8,128)}, f32[8,128]{1,0:T(8,1...) custom-call(bf16[16,288,1536]{2,1,0:T(8,128)(2,1)} %bitcast.17, f32[3,16,96]{2,1,0:T(8,128)} %bitcast.21, ...), custom_call_target="tpu_custom_call" | custom-call | flops 28991029248 | bytes 25165824 | tf_op jit(solution)/shard_map/attention/pallas_call | solution.py:226
  179.7 5.6 all-gather.4.cloned.1.call-done.x_ref
  185.3 98.4 %attention.3 = (bf16[16,288,256]{2,1,0:T(8,128)(2,1)}, f32[208,1536]{1,0:T(8,128)}, f32[80,1536]{1,0:T(8,128)}, f32[288,128]{1,0:T(8,128)}, f32[8,128]{1,0:T(8,1...) custom-call(bf16[16,288,1536]{2,1,0:T(8,128)(2,1)} %bitcast.18, ...), custom_call_target="tpu_custom_call" | custom-call | flops 28991029248 | bytes 25165824 | tf_op jit(solution)/shard_map/attention/pallas_call | solution.py:226
  283.7 0.1 all-gather.6.cloned.1.call-update
  283.7 0.3 all-gather.8.cloned.1.call-start
  284.0 0.5 all-gather.8.cloned.1.call-update
  284.5 0.0 copy-start.2
  284.5 167.3 %tail_a.1 = (bf16[2,256,1536]{2,1,0:T(8,128)(2,1)}, bf16[2,256,1536]{2,1,0:T(8,128)(2,1)}, f32[96,1536]{1,0:T(8,128)}, f32[8,1536]{1,0:T(8,128)}) custom-call(bf16[16,288,256]{2,1,0:T(8,128)(2,1)} %get-tuple-element.60.dqkv_ref, bf16[16,96,256]{2,1,0:T(8,128)(2,1)} %get-tuple-element.61.oo_hbm, bf16[16,96,256]{2,1,0:T(8,128)(2,1)} %get-tuple-element.62.on_hbm, ...), custom_call_target="tpu_custom_call" | custom-call | flops 99999997952 | bytes 67108864 | tf_op jit(solution)/shard_map/tail_a/pallas_call | solution.py:595
  451.9 0.0 copy-done.2
  451.9 0.0 copy-start
  451.9 1.1 copy-done
  452.9 0.0 copy-start.1
  453.0 0.8 copy-done.1
  453.7 88.6 %tail_b.1 = (f32[8,2,96,1536]{3,2,1,0:T(8,128)S(1)}, f32[8,1536]{1,0:T(8,128)S(1)}, f32[16,8,128]{2,1,0:T(8,128)S(1)}) custom-call(f32[96,1536]{1,0:T(8,128)S(1)} %copy-done, f32[8,1536]{1,0:T(8,128)S(1)} %copy-done.1, f32[8,128]{1,0:T(8,128)S(1)} %copy-done.2), custom_call_target="tpu_custom_call" | custom-call | flops 49999998976 | bytes 10485760 | tf_op jit(solution)/shard_map/tail_b/pallas_call | solution.py:679
  542.4 4.3 lay_down.1
  546.7 0.0 all-gather.6.cloned.1.call-done
  546.7 16.4 %settle.2 = (f32[16,288,1536]{2,1,0:T(8,128)}, bf16[2,256,1536]{2,1,0:T(8,128)(2,1)}, bf16[2,256,1536]{2,1,0:T(8,128)(2,1)}) custom-call(f32[16,208,1536]{2,1,0:T(8,128)} %bitcast.15, bf16[2,256,1536]{2,1,0:T(8,128)(2,1)} %get-tuple-element.74.refs_1_, bf16[2,256,1536]{2,1,0:T(8,128)(2,1)} %get-tuple-element.75.refs_2_), custom_call_target="tpu_custom_call" | custom-call | flops 1000000000 | bytes 40894464 | tf_op jit(solution)/shard_map/settle/pallas_call | solution.py:719
  563.1 1.5 all-gather.8.cloned.1.call-done
  564.6 6.2 %settle.3 = f32[16,288,1536]{2,1,0:T(8,128)} custom-call(f32[16,80,1536]{2,1,0:T(8,128)} %bitcast.16, f32[16,288,1536]{2,1,0:T(8,128)} %get-tuple-element.82.refs_1_), custom_call_target="tpu_custom_call", output_to_operand_aliasing={{}: (1, {})} | custom-call | flops 1000000000 | bytes 15728640 | tf_op jit(solution)/shard_map/settle/pallas_call | solution.py:719
Async XLA Ops:
  7.2 178.1 %all-gather.4.cloned.1.call-start = ((), (), s32[]{:S(2)}) async-start(), calls=%async_computation | async-start | bytes 13369344 | tf_op jit(solution)/shard_map/all_gather | solution.py:767
  101.3 445.4 %all-gather.6.cloned.1.call-start = ((), (), s32[]{:S(2)}) async-start(), calls=%async_computation.1 | async-start | bytes 21725184 | tf_op jit(solution)/shard_map/all_gather | solution.py:779
  283.7 280.8 %all-gather.8.cloned.1.call-start = ((), (), s32[]{:S(2)}) async-start(), calls=%async_computation.2 | async-start | bytes 8355840 | tf_op jit(solution)/shard_map/all_gather | solution.py:779
  284.5 167.3 %copy-start.2 = (f32[8,128]{1,0:T(8,128)S(1)}, f32[8,128]{1,0:T(8,128)}, u32[]{:S(2)}) copy-start(f32[8,128]{1,0:T(8,128)} %get-tuple-element.68.gb_ref) | copy-start | bytes 12292
  451.9 1.1 copy-start
  452.9 0.8 copy-start.1
Sparse Core Ops, SparseCore 0:
  101.4 83.8 all-gather.3
  283.9 214.4 all-gather.5
  499.9 64.5 all-gather.7
